TPU v7x, 32 devices: a whole 2x2x4 slice. The times are simulated.
32 devices in a mesh: mod: 4 (over y, x), seq: 8 (over z, core).
Axes of the slice: x: 2, y: 2, z: 4, core: 2. Of those that a mesh axis runs over, the one named last changes fastest.
Arguments:
- tokens: bfloat16 [2048, 4096], P(('mod', 'seq')), may hold values from -6 to 6
- norm_gain: float32 [3, 4096], replicated, may hold values from 0.2 to 2.6
- qkv_weight: bfloat16 [3, 4096, 12288], P(None, None, 'seq'), may hold values from -0.45 to 0.45
- out_weight: bfloat16 [3, 4096, 4096], P(None, 'seq'), may hold values from -0.375 to 0.375
- modality: int32 [16], replicated, may hold values from 0 to 2
- doc_lengths: int32 [4], replicated, may hold values from 1 to 1024, 2048 in all
Outputs:
- mixed: bfloat16 [2048, 4096], P(('mod', 'seq'))
Inputs may be any that keep to these rules, and one draw needn't show every extreme that they name: `doc_lengths`: the lengths sum to 2048; documents follow one another from position 0 in the given order.
All inputs are finite; a program needn't handle non-finite values.
Results may differ from a plain program's by a relative error of at most 0.015.
Values may be sent and summed in bfloat16 or wider, within the bound.
No kernel may reach another device: no remote copies, remote signals or barrier semaphores. Data moves between devices by JAX's collectives and lax.ppermute only.
A program may use at most 128 MiB of HBM per device.

v0:
```python
import math

import jax
import jax.numpy as jnp
from jax import lax
from jax.experimental import pallas as pl
from jax.experimental.pallas import tpu as pltpu
from jax.sharding import PartitionSpec as P


HDIM = 128
BLOCK = 128


def modes_of_rows(first_row, row_count, modality):
    block_ids = (first_row + jnp.arange(row_count, dtype=jnp.int32)) // BLOCK
    block_table = jnp.arange(modality.shape[0], dtype=jnp.int32)
    picked = jnp.where(block_ids[:, None] == block_table[None, :], modality[None, :], 0)
    return jnp.sum(picked, axis=1)


def documents(positions, doc_lengths):
    doc_ends = jnp.cumsum(doc_lengths)
    return jnp.sum((positions[:, None] >= doc_ends[None, :]).astype(jnp.int32), axis=1)


def general_body(tokens, norm_gain, qkv_weight, out_weight, modality, doc_lengths):
    row_count = tokens.shape[0]
    seq_count = lax.axis_size("seq")
    mod_count = lax.axis_size("mod")
    group_rows = row_count * seq_count
    mod_index = lax.axis_index("mod")
    own_first = (mod_index * seq_count + lax.axis_index("seq")) * row_count
    row_modes = modes_of_rows(own_first, row_count, modality)
    choose = (
        row_modes[:, None, None] == jnp.arange(norm_gain.shape[0], dtype=jnp.int32)[None, :, None]
    )
    gain_rows = jnp.sum(jnp.where(choose, norm_gain[None, :, :], 0.0), axis=1)
    values = tokens.astype(jnp.float32)
    mean_square = jnp.mean(values * values, axis=1, keepdims=True)
    normed = (values * lax.rsqrt(mean_square + 1e-05) * gain_rows).astype(jnp.bfloat16)
    gathered = lax.all_gather(normed, "seq", axis=0, tiled=True)
    group_first = mod_index * group_rows
    block_count = group_rows // BLOCK
    block_modes = lax.dynamic_slice_in_dim(modality, group_first // BLOCK, block_count)
    heads_here = qkv_weight.shape[2] // (3 * HDIM)

    def project(block_pair):
        row_block, block_mode = block_pair
        weight = lax.dynamic_index_in_dim(qkv_weight, block_mode, 0, keepdims=False)
        return jnp.dot(row_block, weight, preferred_element_type=jnp.float32).astype(jnp.bfloat16)

    projected = lax.map(
        project, (gathered.reshape(block_count, BLOCK, gathered.shape[1]), block_modes)
    )
    projected = projected.reshape(group_rows, heads_here, 3, HDIM)
    queries = projected[:, :, 0, :]
    keys_here = projected[:, :, 1, :]
    values_here = projected[:, :, 2, :]
    quarter = group_rows // mod_count
    local_rows = jnp.arange(group_rows, dtype=jnp.int32)
    query_pos = group_first + local_rows
    query_docs = documents(query_pos, doc_lengths)
    block_size = min(512, quarter)
    block_total = group_rows // block_size
    score_scale = 1.0 / math.sqrt(HDIM)
    query_blocks = queries.reshape(block_total, block_size, heads_here, HDIM)
    pos_blocks = query_pos.reshape(block_total, block_size)
    doc_blocks = query_docs.reshape(block_total, block_size)
    piece_keys = lax.all_gather(keys_here, "mod", axis=0, tiled=True)
    piece_values = lax.all_gather(values_here, "mod", axis=0, tiled=True)
    key_pos = jnp.arange(piece_keys.shape[0], dtype=jnp.int32)
    key_docs = documents(key_pos, doc_lengths)

    def one_block(block_state):
        query_block, block_pos, block_docs = block_state
        scores = (
            jnp.einsum("qhc,khc->hqk", query_block, piece_keys, preferred_element_type=jnp.float32)
            * score_scale
        )
        allowed = (
            (key_pos[None, :] <= block_pos[:, None]) & (key_docs[None, :] == block_docs[:, None])
        )[None, :, :]
        row_max = jnp.max(jnp.where(allowed, scores, -1e30), axis=2)
        weights = jnp.where(allowed, jnp.exp(scores - row_max[:, :, None]), 0.0)
        totals = jnp.sum(weights, axis=2)
        rows = jnp.einsum(
            "hqk,khc->qhc",
            weights.astype(jnp.bfloat16),
            piece_values,
            preferred_element_type=jnp.float32,
        )
        return (rows / jnp.transpose(totals)[:, :, None]).astype(jnp.bfloat16)

    attended = lax.map(one_block, (query_blocks, pos_blocks, doc_blocks))
    attended = attended.reshape(group_rows, heads_here * HDIM)

    def output(block_pair):
        row_block, block_mode = block_pair
        weight = lax.dynamic_index_in_dim(out_weight, block_mode, 0, keepdims=False)
        return jnp.dot(row_block, weight, preferred_element_type=jnp.float32)

    partial_value = lax.map(
        output, (attended.reshape(block_count, BLOCK, attended.shape[1]), block_modes)
    )
    head_sums = lax.psum_scatter(
        partial_value.reshape(group_rows, partial_value.shape[2]).astype(jnp.bfloat16),
        "seq",
        scatter_dimension=0,
        tiled=True,
    ).astype(jnp.float32)
    return (tokens.astype(jnp.float32) + head_sums).astype(jnp.bfloat16)


SMEM = pl.BlockSpec(memory_space=pltpu.SMEM)
VMEM = pl.BlockSpec(memory_space=pltpu.VMEM)
HBM = pl.BlockSpec(memory_space=pltpu.HBM)
PIECES = 4


def mode_of(ids, modality, chips, slot):
    return modality[ids[0] * chips + jnp.bitwise_xor(ids[1], slot)]


def params(mib):
    return pltpu.CompilerParams(vmem_limit_bytes=mib << 20)


def norm_rows(ids, modality, tokens, norm_gain, chips):
    rows, width = tokens.shape

    def kernel(ids_ref, modality_ref, tokens_ref, gain_ref, out_ref):
        gain = gain_ref[pl.ds(mode_of(ids_ref, modality_ref, chips, 0), 1), :]
        step = 16
        for first in range(0, rows, step):
            values = tokens_ref[first : first + step, :].astype(jnp.float32)
            mean_square = jnp.sum(values * values, axis=1, keepdims=True) * (1.0 / width)
            scaled = values * lax.rsqrt(mean_square + 1e-05) * gain
            out_ref[first : first + step, :] = scaled.astype(jnp.bfloat16)

    return pl.pallas_call(
        kernel,
        out_shape=pltpu.VMEM((rows, width), jnp.bfloat16),
        in_specs=[SMEM, SMEM, VMEM, VMEM],
        out_specs=VMEM,
        compiler_params=params(8),
        cost_estimate=pl.CostEstimate(flops=4_000_000, bytes_accessed=1 << 20, transcendentals=64),
        name="norm_rows",
    )(ids, modality, tokens, norm_gain)


def fetch_weights(ids, modality, qkv_weight, out_weight, chips, slot):
    modes, width, cols = qkv_weight.shape
    pairs = 2
    pair_cols = cols // pairs
    piece = width // PIECES

    def kernel(ids_ref, modality_ref, qkv_ref, out_ref, late_ref, kept_ref, late_sems, kept_sems):
        mode = mode_of(ids_ref, modality_ref, chips, slot)
        copies = []
        for p in range(pairs):
            first = jnp.bitwise_xor(ids_ref[0] // 2, p) * pair_cols
            for k in range(PIECES):
                copies.append(
                    pltpu.make_async_copy(
                        qkv_ref.at[
                            mode,
                            pl.ds(k * piece, piece),
                            pl.ds(pl.multiple_of(first, 128), pair_cols),
                        ],
                        late_ref.at[p, k],
                        late_sems.at[p, k],
                    )
                )
        for m in range(modes):
            copies.append(pltpu.make_async_copy(out_ref.at[m], kept_ref.at[m], kept_sems.at[m]))
        for copy in copies:
            copy.start()
        for copy in copies:
            copy.wait()

    return pl.pallas_call(
        kernel,
        out_shape=[
            pltpu.VMEM((pairs, PIECES, piece, pair_cols), jnp.bfloat16),
            pltpu.VMEM(out_weight.shape, jnp.bfloat16),
        ],
        in_specs=[SMEM, SMEM, HBM, HBM],
        out_specs=[VMEM, VMEM],
        scratch_shapes=[
            pltpu.SemaphoreType.DMA((pairs, PIECES)),
            pltpu.SemaphoreType.DMA((modes,)),
        ],
        compiler_params=params(1),
        cost_estimate=pl.CostEstimate(
            flops=6_000_000_000, bytes_accessed=25 << 20, transcendentals=0
        ),
        name="fetch_weights",
    )(ids, modality, qkv_weight, out_weight)


def store_pair(ids_ref, outs, rows, p, result):
    result = result.astype(jnp.bfloat16)
    cols = result.shape[1] // 2
    odd = ids_ref[0] % 2 == 1
    for e in range(2):
        first, last = result[:, e * cols : (e + 1) * cols], result[:, (1 - e) * cols : (2 - e) * cols]
        outs[2 * p + e][rows, :] = jnp.where(odd, last, first)


def project_slots(ids, modality, parts, weight, chips, slots):
    half, width = parts[0][0].shape
    block = 2 * half
    cols = 3 * HDIM
    heads = weight.shape[2] // cols
    pairs = 2
    pair_cols = weight.shape[2] // pairs
    piece = width // PIECES
    count = len(slots)

    def kernel(ids_ref, modality_ref, *refs):
        ins = refs[: 2 * count]
        weight_ref = refs[2 * count]
        outs = refs[2 * count + 1 : 2 * count + 1 + heads]
        buffer_ref, sems = refs[2 * count + 1 + heads :]

        def copy_of(n, p, k):
            first = jnp.bitwise_xor(ids_ref[0] // 2, p) * pair_cols
            return pltpu.make_async_copy(
                weight_ref.at[
                    mode_of(ids_ref, modality_ref, chips, slots[n]),
                    pl.ds(k * piece, piece),
                    pl.ds(pl.multiple_of(first, 128), pair_cols),
                ],
                buffer_ref.at[p, k],
                sems.at[p, k],
            )

        for p in range(pairs):
            for k in range(PIECES):
                copy_of(0, p, k).start()
        for n in range(count):
            for p in range(pairs):
                result = None
                for k in range(PIECES):
                    copy_of(n, p, k).wait()
                    rows = jnp.concatenate(
                        [ins[2 * n + i][:, k * piece : (k + 1) * piece] for i in range(2)], axis=0
                    )
                    part = jnp.dot(rows, buffer_ref[p, k], preferred_element_type=jnp.float32)
                    result = part if result is None else result + part
                    if n + 1 < count:
                        copy_of(n + 1, p, k).start()
                store_pair(ids_ref, outs, pl.ds(n * block, block), p, result)

    return pl.pallas_call(
        kernel,
        out_shape=[pltpu.VMEM((count * block, cols), jnp.bfloat16)] * heads,
        in_specs=[SMEM, SMEM] + [VMEM] * (2 * count) + [HBM],
        out_specs=[VMEM] * heads,
        scratch_shapes=[
            pltpu.VMEM((pairs, PIECES, piece, pair_cols), jnp.bfloat16),
            pltpu.SemaphoreType.DMA((pairs, PIECES)),
        ],
        compiler_params=params(16),
        cost_estimate=pl.CostEstimate(
            flops=2 * count * block * width * cols * heads,
            bytes_accessed=count * width * cols * heads * 2,
            transcendentals=0,
        ),
        name="project_slots",
    )(ids, modality, *[piece for pair in parts for piece in pair], weight)


def project_late(ids, inner, relayed, weight, cols, chips):
    half, width = inner[0].shape
    block = 2 * half
    pairs, pieces, piece, pair_cols = weight.shape
    heads = pairs * pair_cols // cols

    def kernel(ids_ref, inner_own, inner_partner, relayed_own, relayed_partner, weight_ref, *refs):
        outs, rows_ref = refs[:heads], refs[heads]
        chip = ids_ref[1]
        middle = (chip > 0) & (chip < chips - 1)

        @pl.when(middle)
        def _():
            rows_ref[:half, :] = inner_own[...]
            rows_ref[half:, :] = inner_partner[...]

        @pl.when(jnp.logical_not(middle))
        def _():
            rows_ref[:half, :] = relayed_own[...]
            rows_ref[half:, :] = relayed_partner[...]

        for p in range(pairs):
            result = None
            for k in range(pieces):
                part = jnp.dot(
                    rows_ref[:, k * piece : (k + 1) * piece],
                    weight_ref[p, k],
                    preferred_element_type=jnp.float32,
                )
                result = part if result is None else result + part
            store_pair(ids_ref, outs, pl.ds(0, block), p, result)

    return pl.pallas_call(
        kernel,
        out_shape=[pltpu.VMEM((block, cols), jnp.bfloat16)] * heads,
        in_specs=[SMEM] + [VMEM] * 5,
        out_specs=[VMEM] * heads,
        scratch_shapes=[pltpu.VMEM((block, width), jnp.bfloat16)],
        compiler_params=params(8),
        cost_estimate=pl.CostEstimate(
            flops=2 * block * width * cols * heads,
            bytes_accessed=width * cols * heads * 2,
            transcendentals=0,
        ),
        name="project_late",
    )(ids, *inner, *relayed, weight)


def attend_slots(ids, doc_lengths, sets, query_slots, chips):
    count = len(sets[0][1])
    block = sets[0][1][0].shape[0] // len(sets[0][0])
    total = count * chips * block
    window = min(total // 2 + block, total)
    scale = 1.0 / math.sqrt(HDIM)
    docs = doc_lengths.shape[0]

    def kernel(ids_ref, docs_ref, *refs):
        ins = refs[: len(sets) * count]
        outs = refs[len(sets) * count : (len(sets) + 1) * count]
        keys_ref, values_ref = refs[(len(sets) + 1) * count :]
        mu, chip, own_first = ids_ref[0], ids_ref[1], ids_ref[2] * (block // 2)

        def slot_rows(d, slot, part):
            for i, (slots, _) in enumerate(sets):
                if slot in slots:
                    at = slots.index(slot) * block
                    return ins[i * count + d][at : at + block, part * HDIM : (part + 1) * HDIM]

        for d in range(count):
            for slot in range(chips):
                index = jnp.bitwise_xor(mu, d) * chips + jnp.bitwise_xor(chip, slot)
                place = pl.ds(pl.multiple_of(index * block, block), block)
                keys_ref[place, :] = slot_rows(d, slot, 1)
                values_ref[place, :] = slot_rows(d, slot, 2)

        ends = []
        end = jnp.int32(0)
        for i in range(docs):
            end = end + docs_ref[i]
            ends.append(end)
        row_place = lax.broadcasted_iota(jnp.int32, (block, 1), 0) + own_first
        row_place = jnp.where(row_place >= block, row_place - block, row_place)
        key_iota = lax.broadcasted_iota(jnp.int32, (1, window), 1)
        key_in_block = key_iota % block + own_first
        key_in_block = jnp.where(key_in_block >= block, key_in_block - block, key_in_block)
        key_place = (key_iota // block) * block + key_in_block
        for n, slot in enumerate(query_slots):
            for d in range(count):
                index = jnp.bitwise_xor(mu, d) * chips + jnp.bitwise_xor(chip, slot)
                first_row = index * block
                doc_first = jnp.int32(0)
                for e in ends:
                    doc_first = jnp.where(first_row >= e, e, doc_first)
                start = jnp.minimum(doc_first // block, (total - window) // block) * block
                start = pl.multiple_of(start, block)
                row_pos = row_place + first_row
                row_first = jnp.zeros((block, 1), jnp.int32)
                for e in ends:
                    row_first = jnp.where(row_pos >= e, e, row_first)
                key_pos = key_place + start
                allowed = (key_pos <= row_pos) & (key_pos >= row_first)
                scores = lax.dot_general(
                    slot_rows(d, slot, 0),
                    keys_ref[pl.ds(start, window), :],
                    (((1,), (1,)), ((), ())),
                    preferred_element_type=jnp.float32,
                )
                scores = jnp.where(allowed, scores * scale, -1e30)
                row_max = jnp.max(scores, axis=1, keepdims=True)
                weights = jnp.where(allowed, jnp.exp(scores - row_max), 0.0)
                totals = jnp.sum(weights, axis=1, keepdims=True)
                summed = jnp.dot(
                    weights.astype(jnp.bfloat16),
                    values_ref[pl.ds(start, window), :],
                    preferred_element_type=jnp.float32,
                )
                outs[d][n * block : (n + 1) * block, :] = (summed / totals).astype(jnp.bfloat16)

    n_queries = len(query_slots) * count
    return pl.pallas_call(
        kernel,
        out_shape=[pltpu.VMEM((len(query_slots) * block, HDIM), jnp.bfloat16)] * count,
        in_specs=[SMEM, SMEM] + [VMEM] * (len(sets) * count),
        out_specs=[VMEM] * count,
        scratch_shapes=[
            pltpu.VMEM((total, HDIM), jnp.bfloat16),
            pltpu.VMEM((total, HDIM), jnp.bfloat16),
        ],
        compiler_params=params(18),
        cost_estimate=pl.CostEstimate(
            flops=n_queries * block * window * HDIM * 8,
            bytes_accessed=3 * total * HDIM * 2,
            transcendentals=n_queries * block * window,
        ),
        name="attend_slots",
    )(ids, doc_lengths, *[piece for _, pieces in sets for piece in pieces])


def output_rows(ids, modality, pieces, weight, chips, slots, slot):
    count = len(pieces)
    block = pieces[0].shape[0] // len(slots)
    half = block // 2
    at = slots.index(slot) * block
    depth, width = weight.shape[1:]
    tile = min(1024, width)

    def kernel(ids_ref, modality_ref, *refs):
        ins = refs[:count]
        weight_ref, own_ref, partner_ref, heads_ref = refs[count:]
        mode = mode_of(ids_ref, modality_ref, chips, slot)
        for d in range(count):
            heads_ref[jnp.bitwise_xor(ids_ref[0], d)] = ins[d][at : at + block, :]
        rows = jnp.concatenate([heads_ref[h] for h in range(count)], axis=1)
        for first in range(0, width, tile):
            cols = slice(first, first + tile)
            result = jnp.dot(rows, weight_ref[mode, :, cols], preferred_element_type=jnp.float32)
            result = result.astype(jnp.bfloat16)
            own_ref[:, cols] = result[:half]
            partner_ref[:, cols] = result[half:]

    return pl.pallas_call(
        kernel,
        out_shape=[pltpu.VMEM((half, width), jnp.bfloat16)] * 2,
        in_specs=[SMEM, SMEM] + [VMEM] * (count + 1),
        out_specs=[VMEM] * 2,
        scratch_shapes=[pltpu.VMEM((count, block, HDIM), jnp.bfloat16)],
        compiler_params=params(8),
        cost_estimate=pl.CostEstimate(
            flops=2 * block * depth * width,
            bytes_accessed=depth * width * 2,
            transcendentals=0,
        ),
        name="output_rows",
    )(ids, modality, *pieces, weight)


def chip_pairs(pairs):
    return [(2 * a + core, 2 * b + core) for a, b in pairs for core in range(2)]


def line_body(tokens, norm_gain, qkv_weight, out_weight, modality, doc_lengths):
    seq_count = lax.axis_size("seq")
    mod_count = lax.axis_size("mod")
    chips = seq_count // 2
    mu = lax.axis_index("mod").astype(jnp.int32)
    seq = lax.axis_index("seq").astype(jnp.int32)
    ids = jnp.stack([mu, seq // 2, seq % 2])
    qkv_weight = pltpu.with_memory_space_constraint(qkv_weight, pltpu.HBM)
    out_weight = pltpu.with_memory_space_constraint(out_weight, pltpu.HBM)

    def along(value, pairs):
        return lax.ppermute(value, "seq", chip_pairs(pairs))

    def swap(value):
        return lax.ppermute(value, "seq", [(i, i ^ 1) for i in range(seq_count)])

    def exchange(pieces):
        moved = [pieces[0]]
        for d in range(1, mod_count):
            moved.append(lax.ppermute(pieces[d], "mod", [(i, i ^ d) for i in range(mod_count)]))
        return moved

    normed = norm_rows(ids, modality, tokens, norm_gain, chips)
    two = along(normed, [(i, i ^ 2) for i in range(chips)])
    one = along(normed, [(i, i ^ 1) for i in range(chips)])
    inner = along(normed, [(1, 2), (2, 1)])
    relayed = along(two, [(2, 3), (1, 0)])
    own_pair = (normed, swap(normed))
    two_pair = (two, swap(two))
    one_pair = (one, swap(one))
    inner_pair = (inner, swap(inner))
    relayed_pair = (relayed, swap(relayed))

    own = project_slots(ids, modality, [own_pair], qkv_weight, chips, (0,))
    own = exchange(own)
    late_weight, kept_weight = fetch_weights(ids, modality, qkv_weight, out_weight, chips, 3)
    mid = project_slots(ids, modality, [two_pair, one_pair], qkv_weight, chips, (2, 1))
    mid = exchange(mid)
    late = project_late(ids, inner_pair, relayed_pair, late_weight, 3 * HDIM, chips)
    late = exchange(late)
    sets = (((0,), own), ((2, 1), mid), ((3,), late))

    def add(*shares):
        total = shares[0].astype(jnp.float32)
        for share in shares[1:]:
            total = total + share.astype(jnp.float32)
        return total.astype(jnp.bfloat16)

    def finish(pieces, slots, slot):
        own_share, partner_share = output_rows(
            ids, modality, pieces, kept_weight, chips, slots, slot
        )
        return own_share, swap(partner_share)

    first = attend_slots(ids, doc_lengths, sets, (3,), chips)
    first = exchange(first)
    sum3 = add(*finish(first, (3,), 3))
    from_end = along(sum3, [(3, 2), (0, 1)])
    from_inner = along(sum3, [(1, 2), (2, 1)])
    rest = attend_slots(ids, doc_lengths, sets, (2, 1, 0), chips)
    rest = exchange(rest)
    sum2 = add(*finish(rest, (2, 1, 0), 2))
    from_two_end = along(sum2, [(3, 1), (0, 2)])
    from_two_inner = along(add(sum2, from_end), [(2, 0), (1, 3)])
    sum1 = add(*finish(rest, (2, 1, 0), 1))
    from_one = along(sum1, [(i, i ^ 1) for i in range(chips)])
    shares0 = finish(rest, (2, 1, 0), 0)
    return add(tokens, *shares0, from_inner, from_one, from_two_end, from_two_inner)


def solution(mesh):
    fits = mesh.shape["seq"] == 8 and mesh.shape["mod"] == 4

    def body(tokens, norm_gain, qkv_weight, out_weight, modality, doc_lengths):
        whole = tokens.shape[0] * 2 == BLOCK and qkv_weight.shape[2] == 12 * HDIM
        chosen = line_body if fits and whole else general_body
        return chosen(tokens, norm_gain, qkv_weight, out_weight, modality, doc_lengths)

    return jax.shard_map(
        body,
        mesh=mesh,
        in_specs=(
            P(("mod", "seq"), None),
            P(),
            P(None, None, "seq"),
            P(None, "seq", None),
            P(),
            P(),
        ),
        out_specs=P(("mod", "seq"), None),
        check_vma=False,
    )
```

profile of v0, /device:TPU:0, one launch (start us, length us, event | category | flops | bytes accessed | tf_op | source)
XLA Modules:
  0.0 160.3 jit_solution(16902624249243670886)
XLA Ops:
  0.0 0.1 pad_add_fusion.ids_ref
  0.1 1.0 copy-done
  1.1 0.8 copy-done.2
  2.0 0.7 copy-done.3
  2.6 0.8 norm_rows.1.refs_0_
  3.4 4.1 %collective-permute-start.4 = (bf16[64,4096]{1,0:T(8,128)(2,1)S(1)}, bf16[64,4096]{1,0:T(8,128)(2,1)S(1)}, u32[]{:S(2)}, u32[]{:S(2)}) collective-permute-start(bf16[64,4096]{1,0:T(8,128)(2,1)S(1)} %norm_rows.1.refs_0_), channel_id=1, source_target_pairs={{0,4},{1,5},{2,6},{3,7},{4,0},{5,1},{6,2},{7,3},{8,12},{9,13},{10,... | collective-permute-start | bytes 1572872 | tf_op jit(solution)/shard_map/ppermute | solution.py:466
  7.6 1.6 collective-permute-start.6
  9.1 0.7 collective-permute-start.11
  9.8 21.8 %collective-permute-done.4.refs_0_ = bf16[64,4096]{1,0:T(8,128)(2,1)S(1)} collective-permute-done((bf16[64,4096]{1,0:T(8,128)(2,1)S(1)}, bf16[64,4096]{1,0:T(8,128)(2,1)S(1)}, u32[]{:S(2)}, u32[]{:S(2)}) %collective-permute-start.4) | collective-permute-done | bytes 524320 | tf_op jit(solution)/shard_map/ppermute | solution.py:466
  31.6 0.5 collective-permute-start.7
  32.1 1.3 collective-permute-start.13
  33.4 0.6 copy-done.4
  34.1 6.4 %project_slots.2 = (bf16[128,384]{1,0:T(8,128)(2,1)S(1)}, bf16[128,384]{1,0:T(8,128)(2,1)S(1)}, bf16[128,384]{1,0:T(8,128)(2,1)S(1)}, bf16[128,384]{1,0:T(8,128)(2,1)S(1)}) custom-call(s32[3]{0:T(128)S(1)} %pad_add_fusion.ids_ref, s32[16]{0:T(128)S(1)} %copy-done.4, bf16[64,4096]{1,0:T(8,128)(2,1)S(1)} %norm_rows.1.refs_0_, ...), custom_call_target="tpu_custom_call" | custom-call | flops 1610612736 | bytes 12582912 | tf_op jit(solution)/shard_map/project_slots/pallas_call | solution.py:256
  40.5 1.9 %collective-permute-start.1 = (bf16[128,384]{1,0:T(8,128)(2,1)S(1)}, bf16[128,384]{1,0:T(8,128)(2,1)S(1)}, u32[]{:S(2)}, u32[]{:S(2)}) collective-permute-start(bf16[128,384]{1,0:T(8,128)(2,1)S(1)} %get-tuple-element.36), channel_id=1, source_target_pairs={{0,8},{8,0},{16,24},{24,16},{1,9},{9,1},{17,25},{25,17},{2,10},{10... | collective-permute-start | bytes 294920 | tf_op jit(solution)/shard_map/ppermute | solution.py:474
  42.3 10.4 %project_slots.3 = (bf16[256,384]{1,0:T(8,128)(2,1)S(1)}, bf16[256,384]{1,0:T(8,128)(2,1)S(1)}, bf16[256,384]{1,0:T(8,128)(2,1)S(1)}, bf16[256,384]{1,0:T(8,128)(2,1)S(1)}) custom-call(s32[3]{0:T(128)S(1)} %pad_add_fusion.ids_ref, s32[16]{0:T(128)S(1)} %copy-done.4, bf16[64,4096]{1,0:T(8,128)(2,1)S(1)} %collective-permute-done.4.refs_0_, ...), custom_call_target="tpu_custom_call" | custom-call | flops 3221225472 | bytes 25165824 | tf_op jit(solution)/shard_map/project_slots/pallas_call | solution.py:256
  52.7 1.6 collective-permute-start.10
  54.3 0.2 collective-permute-start.14
  54.5 8.9 %fetch_weights.1 = (bf16[2,4,1024,768]{3,2,1,0:T(8,128)(2,1)S(1)}, bf16[3,512,4096]{2,1,0:T(8,128)(2,1)S(1)}) custom-call(s32[3]{0:T(128)S(1)} %pad_add_fusion.ids_ref, s32[16]{0:T(128)S(1)} %copy-done.5, bf16[3,4096,1536]{2,1,0:T(8,128)(2,1)} %qkv_ref.1, bf16[3,512,4096]{2,1,0:T(8,128)(2,1)} %out_ref.1), custom_call_target="tpu_custom_call" | custom-call | flops 6000000000 | bytes 26214400 | tf_op jit(solution)/shard_map/fetch_weights/pallas_call | solution.py:182
  63.4 0.5 collective-permute-start.2
  63.9 2.6 %collective-permute-start.3 = (bf16[128,384]{1,0:T(8,128)(2,1)S(1)}, bf16[128,384]{1,0:T(8,128)(2,1)S(1)}, u32[]{:S(2)}, u32[]{:S(2)}) collective-permute-start(bf16[128,384]{1,0:T(8,128)(2,1)S(1)} %get-tuple-element.38), channel_id=1, source_target_pairs={{0,24},{8,16},{16,8},{24,0},{1,25},{9,17},{17,9},{25,1},{2,26},{10... | collective-permute-start | bytes 294920 | tf_op jit(solution)/shard_map/ppermute | solution.py:474
  66.4 0.5 collective-permute-start.8
  67.0 0.4 collective-permute-start.9
  67.4 2.6 %project_late.1 = (bf16[128,384]{1,0:T(8,128)(2,1)S(1)}, bf16[128,384]{1,0:T(8,128)(2,1)S(1)}, bf16[128,384]{1,0:T(8,128)(2,1)S(1)}, bf16[128,384]{1,0:T(8,128)(2,1)S(1)}) custom-call(s32[3]{0:T(128)S(1)} %pad_add_fusion.ids_ref, bf16[64,4096]{1,0:T(8,128)(2,1)S(1)} %collective-permute-done.11.inner_own, ...), custom_call_target="tpu_custom_call" | custom-call | flops 1610612736 | bytes 12582912 | tf_op jit(solution)/shard_map/project_late/pallas_call | solution.py:307
  70.0 1.3 collective-permute-done.2.refs_2_
  71.2 1.5 collective-permute-start.15
  72.7 0.5 collective-permute-start.16
  73.2 1.5 collective-permute-start.17
  74.8 0.9 collective-permute-done.9.refs_6_
  75.6 1.3 collective-permute-done.15.refs_9_
  76.9 2.1 %collective-permute-done.16.refs_10_ = bf16[128,384]{1,0:T(8,128)(2,1)S(1)} collective-permute-done((bf16[128,384]{1,0:T(8,128)(2,1)S(1)}, bf16[128,384]{1,0:T(8,128)(2,1)S(1)}, u32[]{:S(2)}, u32[]{:S(2)}) %collective-permute-start.16) | collective-permute-done | bytes 98336 | tf_op jit(solution)/shard_map/ppermute | solution.py:474
  79.0 2.7 %attend_slots.3 = (bf16[128,128]{1,0:T(8,128)(2,1)S(1)}, bf16[128,128]{1,0:T(8,128)(2,1)S(1)}, bf16[128,128]{1,0:T(8,128)(2,1)S(1)}, bf16[128,128]{1,0:T(8,128)(2,1)S(1)}) custom-call(s32[3]{0:T(128)S(1)} %pad_add_fusion.ids_ref, s32[4]{0:T(128)S(1)} %copy-done.6, bf16[128,384]{1,0:T(8,128)(2,1)S(1)} %get-tuple-element.35.refs_0_, ...), custom_call_target="tpu_custom_call" | custom-call | flops 603979776 | bytes 1572864 | tf_op jit(solution)/shard_map/attend_slots/pallas_call | solution.py:394
  81.7 1.6 collective-permute-start.22
  83.3 0.5 collective-permute-start.23
  83.8 1.4 collective-permute-start.24
  85.3 0.4 collective-permute-done.22.refs_1_
  85.7 1.5 collective-permute-done.23.refs_2_
  87.2 1.4 collective-permute-done.24.refs_3_
  88.6 1.3 output_rows.5
  90.0 0.1 collective-permute-start.25
  90.0 6.3 %attend_slots.2 = (bf16[384,128]{1,0:T(8,128)(2,1)S(1)}, bf16[384,128]{1,0:T(8,128)(2,1)S(1)}, bf16[384,128]{1,0:T(8,128)(2,1)S(1)}, bf16[384,128]{1,0:T(8,128)(2,1)S(1)}) custom-call(s32[3]{0:T(128)S(1)} %pad_add_fusion.ids_ref, s32[4]{0:T(128)S(1)} %copy-done.6, bf16[128,384]{1,0:T(8,128)(2,1)S(1)} %get-tuple-element.35.refs_0_, ...), custom_call_target="tpu_custom_call" | custom-call | flops 1811939328 | bytes 1572864 | tf_op jit(solution)/shard_map/attend_slots/pallas_call | solution.py:394
  96.3 1.4 collective-permute-start.18
  97.7 0.7 collective-permute-start.19
  98.4 1.5 collective-permute-start.20
  99.9 1.7 %collective-permute-done.18.refs_1_ = bf16[384,128]{1,0:T(8,128)(2,1)S(1)} collective-permute-done((bf16[384,128]{1,0:T(8,128)(2,1)S(1)}, bf16[384,128]{1,0:T(8,128)(2,1)S(1)}, u32[]{:S(2)}, u32[]{:S(2)}) %collective-permute-start.18) | collective-permute-done | bytes 98336 | tf_op jit(solution)/shard_map/ppermute | solution.py:474
  101.6 1.5 collective-permute-done.19.refs_2_
  103.1 1.6 %collective-permute-done.20.refs_3_ = bf16[384,128]{1,0:T(8,128)(2,1)S(1)} collective-permute-done((bf16[384,128]{1,0:T(8,128)(2,1)S(1)}, bf16[384,128]{1,0:T(8,128)(2,1)S(1)}, u32[]{:S(2)}, u32[]{:S(2)}) %collective-permute-start.20) | collective-permute-done | bytes 98336 | tf_op jit(solution)/shard_map/ppermute | solution.py:474
  104.7 1.3 output_rows.4
  106.1 1.5 output_rows.6
  107.6 0.6 collective-permute-start.27
  108.2 1.3 output_rows.7
  109.5 0.1 collective-permute-start.29
  109.6 0.1 add_convert_fusion.4
  109.7 4.6 %collective-permute-start.31 = (bf16[64,4096]{1,0:T(8,128)(2,1)S(1)}, bf16[64,4096]{1,0:T(8,128)(2,1)S(1)}, u32[]{:S(2)}, u32[]{:S(2)}) collective-permute-start(bf16[64,4096]{1,0:T(8,128)(2,1)S(1)} %add_convert_fusion.4), channel_id=1, source_target_pairs={{6,4},{7,5},{0,2},{1,3},{14,12},{15,13},{8,10},{9,11},{22,20},{23,... | collective-permute-start | bytes 1572872 | tf_op jit(solution)/shard_map/ppermute | solution.py:466
  114.4 0.7 collective-permute-start.26
  115.1 0.1 add_convert_fusion.3
  115.2 2.2 %collective-permute-start.28 = (bf16[64,4096]{1,0:T(8,128)(2,1)S(1)}, bf16[64,4096]{1,0:T(8,128)(2,1)S(1)}, u32[]{:S(2)}, u32[]{:S(2)}) collective-permute-start(bf16[64,4096]{1,0:T(8,128)(2,1)S(1)} %add_convert_fusion.3), channel_id=1, source_target_pairs={{0,2},{1,3},{2,0},{3,1},{4,6},{5,7},{6,4},{7,5},{8,10},{9,11},{10,... | collective-permute-start | bytes 1572872 | tf_op jit(solution)/shard_map/ppermute | solution.py:466
  117.4 9.3 %collective-permute-done.31 = bf16[64,4096]{1,0:T(8,128)(2,1)S(1)} collective-permute-done((bf16[64,4096]{1,0:T(8,128)(2,1)S(1)}, bf16[64,4096]{1,0:T(8,128)(2,1)S(1)}, u32[]{:S(2)}, u32[]{:S(2)}) %collective-permute-start.31) | collective-permute-done | bytes 524320 | tf_op jit(solution)/shard_map/ppermute | solution.py:466
  126.6 0.2 add_convert_fusion.1
  126.9 5.4 %collective-permute-start.30 = (bf16[64,4096]{1,0:T(8,128)(2,1)S(1)}, bf16[64,4096]{1,0:T(8,128)(2,1)S(1)}, u32[]{:S(2)}, u32[]{:S(2)}) collective-permute-start(bf16[64,4096]{1,0:T(8,128)(2,1)S(1)} %get-tuple-element.66), channel_id=1, source_target_pairs={{6,2},{7,3},{0,4},{1,5},{14,10},{15,11},{8,12},{9,13},{22,18},{23,... | collective-permute-start | bytes 1572872 | tf_op jit(solution)/shard_map/ppermute | solution.py:466
  132.2 1.3 collective-permute-start.32
  133.6 4.3 %collective-permute-done.28 = bf16[64,4096]{1,0:T(8,128)(2,1)S(1)} collective-permute-done((bf16[64,4096]{1,0:T(8,128)(2,1)S(1)}, bf16[64,4096]{1,0:T(8,128)(2,1)S(1)}, u32[]{:S(2)}, u32[]{:S(2)}) %collective-permute-start.28) | collective-permute-done | bytes 524320 | tf_op jit(solution)/shard_map/ppermute | solution.py:466
  137.9 10.8 %collective-permute-done.30 = bf16[64,4096]{1,0:T(8,128)(2,1)S(1)} collective-permute-done((bf16[64,4096]{1,0:T(8,128)(2,1)S(1)}, bf16[64,4096]{1,0:T(8,128)(2,1)S(1)}, u32[]{:S(2)}, u32[]{:S(2)}) %collective-permute-start.30) | collective-permute-done | bytes 524320 | tf_op jit(solution)/shard_map/ppermute | solution.py:466
  148.7 10.3 %collective-permute-done.32 = bf16[64,4096]{1,0:T(8,128)(2,1)S(1)} collective-permute-done((bf16[64,4096]{1,0:T(8,128)(2,1)S(1)}, bf16[64,4096]{1,0:T(8,128)(2,1)S(1)}, u32[]{:S(2)}, u32[]{:S(2)}) %collective-permute-start.32) | collective-permute-done | bytes 524320 | tf_op jit(solution)/shard_map/ppermute | solution.py:466
  159.0 1.3 add_convert_fusion
  (32 shorter events, 0.2 us)
Async XLA Ops:
  0.1 1.0 copy-start
  1.1 0.8 copy-start.2
  2.0 0.7 copy-start.3
  3.4 28.2 %collective-permute-start.4 = (bf16[64,4096]{1,0:T(8,128)(2,1)S(1)}, bf16[64,4096]{1,0:T(8,128)(2,1)S(1)}, u32[]{:S(2)}, u32[]{:S(2)}) collective-permute-start(bf16[64,4096]{1,0:T(8,128)(2,1)S(1)} %norm_rows.1.refs_0_), channel_id=1, source_target_pairs={{0,4},{1,5},{2,6},{3,7},{4,0},{5,1},{6,2},{7,3},{8,12},{9,13},{10,... | collective-permute-start | bytes 1572872 | tf_op jit(solution)/shard_map/ppermute | solution.py:466
  7.6 24.1 %collective-permute-start.6 = (bf16[64,4096]{1,0:T(8,128)(2,1)S(1)}, bf16[64,4096]{1,0:T(8,128)(2,1)S(1)}, u32[]{:S(2)}, u32[]{:S(2)}) collective-permute-start(bf16[64,4096]{1,0:T(8,128)(2,1)S(1)} %norm_rows.1.refs_0_), channel_id=1, source_target_pairs={{0,2},{1,3},{2,0},{3,1},{4,6},{5,7},{6,4},{7,5},{8,10},{9,11},{10,... | collective-permute-start | bytes 1572872 | tf_op jit(solution)/shard_map/ppermute | solution.py:466
  9.1 24.3 %collective-permute-start = (bf16[64,4096]{1,0:T(8,128)(2,1)S(1)}, bf16[64,4096]{1,0:T(8,128)(2,1)S(1)}, u32[]{:S(2)}, u32[]{:S(2)}) collective-permute-start(bf16[64,4096]{1,0:T(8,128)(2,1)S(1)} %norm_rows.1.refs_0_), channel_id=1, source_target_pairs={{0,1},{1,0},{2,3},{3,2},{4,5},{5,4},{6,7},{7,6},{8,9},{9,8},{10,11... | collective-permute-start | bytes 1572872 | tf_op jit(solution)/shard_map/ppermute | solution.py:469
  9.1 33.2 %collective-permute-start.11 = (bf16[64,4096]{1,0:T(8,128)(2,1)S(1)}, bf16[64,4096]{1,0:T(8,128)(2,1)S(1)}, u32[]{:S(2)}, u32[]{:S(2)}) collective-permute-start(bf16[64,4096]{1,0:T(8,128)(2,1)S(1)} %norm_rows.1.refs_0_), channel_id=1, source_target_pairs={{2,4},{3,5},{4,2},{5,3},{10,12},{11,13},{12,10},{13,11},{18,20},{1... | collective-permute-start | bytes 1572872 | tf_op jit(solution)/shard_map/ppermute | solution.py:466
  31.6 10.7 %collective-permute-start.5 = (bf16[64,4096]{1,0:T(8,128)(2,1)S(1)}, bf16[64,4096]{1,0:T(8,128)(2,1)S(1)}, u32[]{:S(2)}, u32[]{:S(2)}) collective-permute-start(bf16[64,4096]{1,0:T(8,128)(2,1)S(1)} %collective-permute-done.4.refs_0_), channel_id=1, source_target_pairs={{0,1},{1,0},{2,3},{3,2},{4,5},{5,4},{6,7},{7,6},{8,9},{9,8},{10,11... | collective-permute-start | bytes 1572872 | tf_op jit(solution)/shard_map/ppermute | solution.py:469
  31.6 10.7 %collective-permute-start.7 = (bf16[64,4096]{1,0:T(8,128)(2,1)S(1)}, bf16[64,4096]{1,0:T(8,128)(2,1)S(1)}, u32[]{:S(2)}, u32[]{:S(2)}) collective-permute-start(bf16[64,4096]{1,0:T(8,128)(2,1)S(1)} %collective-permute-done.6.refs_2_), channel_id=1, source_target_pairs={{0,1},{1,0},{2,3},{3,2},{4,5},{5,4},{6,7},{7,6},{8,9},{9,8},{10,11... | collective-permute-start | bytes 1572872 | tf_op jit(solution)/shard_map/ppermute | solution.py:469
  32.1 22.1 %collective-permute-start.13 = (bf16[64,4096]{1,0:T(8,128)(2,1)S(1)}, bf16[64,4096]{1,0:T(8,128)(2,1)S(1)}, u32[]{:S(2)}, u32[]{:S(2)}) collective-permute-start(bf16[64,4096]{1,0:T(8,128)(2,1)S(1)} %collective-permute-done.4.refs_0_), channel_id=1, source_target_pairs={{4,6},{5,7},{2,0},{3,1},{12,14},{13,15},{10,8},{11,9},{20,22},{21,... | collective-permute-start | bytes 1572872 | tf_op jit(solution)/shard_map/ppermute | solution.py:466
  33.4 0.7 copy-start.4
  40.4 14.0 %copy-start.5 = (s32[16]{0:T(128)S(1)}, s32[16]{0:T(128)}, u32[]{:S(2)}) copy-start(s32[16]{0:T(128)} %modality_ref.15) | copy-start | bytes 196
  40.5 23.4 %collective-permute-start.1 = (bf16[128,384]{1,0:T(8,128)(2,1)S(1)}, bf16[128,384]{1,0:T(8,128)(2,1)S(1)}, u32[]{:S(2)}, u32[]{:S(2)}) collective-permute-start(bf16[128,384]{1,0:T(8,128)(2,1)S(1)} %get-tuple-element.36), channel_id=1, source_target_pairs={{0,8},{8,0},{16,24},{24,16},{1,9},{9,1},{17,25},{25,17},{2,10},{10... | collective-permute-start | bytes 294920 | tf_op jit(solution)/shard_map/ppermute | solution.py:474
  42.3 24.1 %collective-permute-start.12 = (bf16[64,4096]{1,0:T(8,128)(2,1)S(1)}, bf16[64,4096]{1,0:T(8,128)(2,1)S(1)}, u32[]{:S(2)}, u32[]{:S(2)}) collective-permute-start(bf16[64,4096]{1,0:T(8,128)(2,1)S(1)} %collective-permute-done.11.inner_own), channel_id=1, source_target_pairs={{0,1},{1,0},{2,3},{3,2},{4,5},{5,4},{6,7},{7,6},{8,9},{9,8},{10,11... | collective-permute-start | bytes 1572872 | tf_op jit(solution)/shard_map/ppermute | solution.py:469
  52.7 20.5 %collective-permute-start.10 = (bf16[256,384]{1,0:T(8,128)(2,1)S(1)}, bf16[256,384]{1,0:T(8,128)(2,1)S(1)}, u32[]{:S(2)}, u32[]{:S(2)}) collective-permute-start(bf16[256,384]{1,0:T(8,128)(2,1)S(1)} %get-tuple-element.42), channel_id=1, source_target_pairs={{0,24},{8,16},{16,8},{24,0},{1,25},{9,17},{17,9},{25,1},{2,26},{10... | collective-permute-start | bytes 589832 | tf_op jit(solution)/shard_map/ppermute | solution.py:474
  54.3 12.7 %collective-permute-start.14 = (bf16[64,4096]{1,0:T(8,128)(2,1)S(1)}, bf16[64,4096]{1,0:T(8,128)(2,1)S(1)}, u32[]{:S(2)}, u32[]{:S(2)}) collective-permute-start(bf16[64,4096]{1,0:T(8,128)(2,1)S(1)} %collective-permute-done.13.relayed_own), channel_id=1, source_target_pairs={{0,1},{1,0},{2,3},{3,2},{4,5},{5,4},{6,7},{7,6},{8,9},{9,8},{10,11... | collective-permute-start | bytes 1572872 | tf_op jit(solution)/shard_map/ppermute | solution.py:469
  63.4 15.6 %copy-start.6 = (s32[4]{0:T(128)S(1)}, s32[4]{0:T(128)}, u32[]{:S(2)}) copy-start(s32[4]{0:T(128)} %docs_ref.3) | copy-start | bytes 52
  63.4 7.8 %collective-permute-start.2 = (bf16[128,384]{1,0:T(8,128)(2,1)S(1)}, bf16[128,384]{1,0:T(8,128)(2,1)S(1)}, u32[]{:S(2)}, u32[]{:S(2)}) collective-permute-start(bf16[128,384]{1,0:T(8,128)(2,1)S(1)} %get-tuple-element.37), channel_id=1, source_target_pairs={{0,16},{8,24},{16,0},{24,8},{1,17},{9,25},{17,1},{25,9},{2,18},{10... | collective-permute-start | bytes 294920 | tf_op jit(solution)/shard_map/ppermute | solution.py:474
  63.9 8.9 %collective-permute-start.3 = (bf16[128,384]{1,0:T(8,128)(2,1)S(1)}, bf16[128,384]{1,0:T(8,128)(2,1)S(1)}, u32[]{:S(2)}, u32[]{:S(2)}) collective-permute-start(bf16[128,384]{1,0:T(8,128)(2,1)S(1)} %get-tuple-element.38), channel_id=1, source_target_pairs={{0,24},{8,16},{16,8},{24,0},{1,25},{9,17},{17,9},{25,1},{2,26},{10... | collective-permute-start | bytes 294920 | tf_op jit(solution)/shard_map/ppermute | solution.py:474
  66.4 8.3 %collective-permute-start.8 = (bf16[256,384]{1,0:T(8,128)(2,1)S(1)}, bf16[256,384]{1,0:T(8,128)(2,1)S(1)}, u32[]{:S(2)}, u32[]{:S(2)}) collective-permute-start(bf16[256,384]{1,0:T(8,128)(2,1)S(1)} %get-tuple-element.40), channel_id=1, source_target_pairs={{0,8},{8,0},{16,24},{24,16},{1,9},{9,1},{17,25},{25,17},{2,10},{10... | collective-permute-start | bytes 589832 | tf_op jit(solution)/shard_map/ppermute | solution.py:474
  67.0 8.6 %collective-permute-start.9 = (bf16[256,384]{1,0:T(8,128)(2,1)S(1)}, bf16[256,384]{1,0:T(8,128)(2,1)S(1)}, u32[]{:S(2)}, u32[]{:S(2)}) collective-permute-start(bf16[256,384]{1,0:T(8,128)(2,1)S(1)} %get-tuple-element.41), channel_id=1, source_target_pairs={{0,16},{8,24},{16,0},{24,8},{1,17},{9,25},{17,1},{25,9},{2,18},{10... | collective-permute-start | bytes 589832 | tf_op jit(solution)/shard_map/ppermute | solution.py:474
  71.2 5.7 %collective-permute-start.15 = (bf16[128,384]{1,0:T(8,128)(2,1)S(1)}, bf16[128,384]{1,0:T(8,128)(2,1)S(1)}, u32[]{:S(2)}, u32[]{:S(2)}) collective-permute-start(bf16[128,384]{1,0:T(8,128)(2,1)S(1)} %get-tuple-element.45), channel_id=1, source_target_pairs={{0,8},{8,0},{16,24},{24,16},{1,9},{9,1},{17,25},{25,17},{2,10},{10... | collective-permute-start | bytes 294920 | tf_op jit(solution)/shard_map/ppermute | solution.py:474
  72.7 6.3 %collective-permute-start.16 = (bf16[128,384]{1,0:T(8,128)(2,1)S(1)}, bf16[128,384]{1,0:T(8,128)(2,1)S(1)}, u32[]{:S(2)}, u32[]{:S(2)}) collective-permute-start(bf16[128,384]{1,0:T(8,128)(2,1)S(1)} %get-tuple-element.46), channel_id=1, source_target_pairs={{0,16},{8,24},{16,0},{24,8},{1,17},{9,25},{17,1},{25,9},{2,18},{10... | collective-permute-start | bytes 294920 | tf_op jit(solution)/shard_map/ppermute | solution.py:474
  73.2 5.8 %collective-permute-start.17 = (bf16[128,384]{1,0:T(8,128)(2,1)S(1)}, bf16[128,384]{1,0:T(8,128)(2,1)S(1)}, u32[]{:S(2)}, u32[]{:S(2)}) collective-permute-start(bf16[128,384]{1,0:T(8,128)(2,1)S(1)} %get-tuple-element.47), channel_id=1, source_target_pairs={{0,24},{8,16},{16,8},{24,0},{1,25},{9,17},{17,9},{25,1},{2,26},{10... | collective-permute-start | bytes 294920 | tf_op jit(solution)/shard_map/ppermute | solution.py:474
  81.7 4.0 %collective-permute-start.22 = (bf16[128,128]{1,0:T(8,128)(2,1)S(1)}, bf16[128,128]{1,0:T(8,128)(2,1)S(1)}, u32[]{:S(2)}, u32[]{:S(2)}) collective-permute-start(bf16[128,128]{1,0:T(8,128)(2,1)S(1)} %get-tuple-element.56), channel_id=1, source_target_pairs={{0,8},{8,0},{16,24},{24,16},{1,9},{9,1},{17,25},{25,17},{2,10},{10... | collective-permute-start | bytes 98312 | tf_op jit(solution)/shard_map/ppermute | solution.py:474
  83.3 3.9 %collective-permute-start.23 = (bf16[128,128]{1,0:T(8,128)(2,1)S(1)}, bf16[128,128]{1,0:T(8,128)(2,1)S(1)}, u32[]{:S(2)}, u32[]{:S(2)}) collective-permute-start(bf16[128,128]{1,0:T(8,128)(2,1)S(1)} %get-tuple-element.57), channel_id=1, source_target_pairs={{0,16},{8,24},{16,0},{24,8},{1,17},{9,25},{17,1},{25,9},{2,18},{10... | collective-permute-start | bytes 98312 | tf_op jit(solution)/shard_map/ppermute | solution.py:474
  83.8 4.8 %collective-permute-start.24 = (bf16[128,128]{1,0:T(8,128)(2,1)S(1)}, bf16[128,128]{1,0:T(8,128)(2,1)S(1)}, u32[]{:S(2)}, u32[]{:S(2)}) collective-permute-start(bf16[128,128]{1,0:T(8,128)(2,1)S(1)} %get-tuple-element.58), channel_id=1, source_target_pairs={{0,24},{8,16},{16,8},{24,0},{1,25},{9,17},{17,9},{25,1},{2,26},{10... | collective-permute-start | bytes 98312 | tf_op jit(solution)/shard_map/ppermute | solution.py:474
  90.0 19.7 %collective-permute-start.25 = (bf16[64,4096]{1,0:T(8,128)(2,1)S(1)}, bf16[64,4096]{1,0:T(8,128)(2,1)S(1)}, u32[]{:S(2)}, u32[]{:S(2)}) collective-permute-start(bf16[64,4096]{1,0:T(8,128)(2,1)S(1)} %get-tuple-element.60), channel_id=1, source_target_pairs={{0,1},{1,0},{2,3},{3,2},{4,5},{5,4},{6,7},{7,6},{8,9},{9,8},{10,11... | collective-permute-start | bytes 1572872 | tf_op jit(solution)/shard_map/ppermute | solution.py:469
  96.3 5.2 %collective-permute-start.18 = (bf16[384,128]{1,0:T(8,128)(2,1)S(1)}, bf16[384,128]{1,0:T(8,128)(2,1)S(1)}, u32[]{:S(2)}, u32[]{:S(2)}) collective-permute-start(bf16[384,128]{1,0:T(8,128)(2,1)S(1)} %get-tuple-element.49), channel_id=1, source_target_pairs={{0,8},{8,0},{16,24},{24,16},{1,9},{9,1},{17,25},{25,17},{2,10},{10... | collective-permute-start | bytes 294920 | tf_op jit(solution)/shard_map/ppermute | solution.py:474
  97.7 5.4 %collective-permute-start.19 = (bf16[384,128]{1,0:T(8,128)(2,1)S(1)}, bf16[384,128]{1,0:T(8,128)(2,1)S(1)}, u32[]{:S(2)}, u32[]{:S(2)}) collective-permute-start(bf16[384,128]{1,0:T(8,128)(2,1)S(1)} %get-tuple-element.50), channel_id=1, source_target_pairs={{0,16},{8,24},{16,0},{24,8},{1,17},{9,25},{17,1},{25,9},{2,18},{10... | collective-permute-start | bytes 294920 | tf_op jit(solution)/shard_map/ppermute | solution.py:474
  98.4 6.3 %collective-permute-start.20 = (bf16[384,128]{1,0:T(8,128)(2,1)S(1)}, bf16[384,128]{1,0:T(8,128)(2,1)S(1)}, u32[]{:S(2)}, u32[]{:S(2)}) collective-permute-start(bf16[384,128]{1,0:T(8,128)(2,1)S(1)} %get-tuple-element.51), channel_id=1, source_target_pairs={{0,24},{8,16},{16,8},{24,0},{1,25},{9,17},{17,9},{25,1},{2,26},{10... | collective-permute-start | bytes 294920 | tf_op jit(solution)/shard_map/ppermute | solution.py:474
  106.0 27.5 %collective-permute-start.21 = (bf16[64,4096]{1,0:T(8,128)(2,1)S(1)}, bf16[64,4096]{1,0:T(8,128)(2,1)S(1)}, u32[]{:S(2)}, u32[]{:S(2)}) collective-permute-start(bf16[64,4096]{1,0:T(8,128)(2,1)S(1)} %get-tuple-element.54), channel_id=1, source_target_pairs={{0,1},{1,0},{2,3},{3,2},{4,5},{5,4},{6,7},{7,6},{8,9},{9,8},{10,11... | collective-permute-start | bytes 1572872 | tf_op jit(solution)/shard_map/ppermute | solution.py:469
  107.6 51.3 %copy-start.1 = (bf16[64,4096]{1,0:T(8,128)(2,1)S(1)}, bf16[64,4096]{1,0:T(8,128)(2,1)}, u32[]{:S(2)}) copy-start(bf16[64,4096]{1,0:T(8,128)(2,1)} %tokens_ref.1) | copy-start | bytes 1572868
  107.6 7.4 %collective-permute-start.27 = (bf16[64,4096]{1,0:T(8,128)(2,1)S(1)}, bf16[64,4096]{1,0:T(8,128)(2,1)S(1)}, u32[]{:S(2)}, u32[]{:S(2)}) collective-permute-start(bf16[64,4096]{1,0:T(8,128)(2,1)S(1)} %get-tuple-element.62), channel_id=1, source_target_pairs={{0,1},{1,0},{2,3},{3,2},{4,5},{5,4},{6,7},{7,6},{8,9},{9,8},{10,11... | collective-permute-start | bytes 1572872 | tf_op jit(solution)/shard_map/ppermute | solution.py:469
  109.5 7.8 %collective-permute-start.29 = (bf16[64,4096]{1,0:T(8,128)(2,1)S(1)}, bf16[64,4096]{1,0:T(8,128)(2,1)S(1)}, u32[]{:S(2)}, u32[]{:S(2)}) collective-permute-start(bf16[64,4096]{1,0:T(8,128)(2,1)S(1)} %get-tuple-element.64), channel_id=1, source_target_pairs={{0,1},{1,0},{2,3},{3,2},{4,5},{5,4},{6,7},{7,6},{8,9},{9,8},{10,11... | collective-permute-start | bytes 1572872 | tf_op jit(solution)/shard_map/ppermute | solution.py:469
  109.7 16.9 %collective-permute-start.31 = (bf16[64,4096]{1,0:T(8,128)(2,1)S(1)}, bf16[64,4096]{1,0:T(8,128)(2,1)S(1)}, u32[]{:S(2)}, u32[]{:S(2)}) collective-permute-start(bf16[64,4096]{1,0:T(8,128)(2,1)S(1)} %add_convert_fusion.4), channel_id=1, source_target_pairs={{6,4},{7,5},{0,2},{1,3},{14,12},{15,13},{8,10},{9,11},{22,20},{23,... | collective-permute-start | bytes 1572872 | tf_op jit(solution)/shard_map/ppermute | solution.py:466
  114.4 19.2 %collective-permute-start.26 = (bf16[64,4096]{1,0:T(8,128)(2,1)S(1)}, bf16[64,4096]{1,0:T(8,128)(2,1)S(1)}, u32[]{:S(2)}, u32[]{:S(2)}) collective-permute-start(bf16[64,4096]{1,0:T(8,128)(2,1)S(1)} %add_convert_fusion.4), channel_id=1, source_target_pairs={{2,4},{3,5},{4,2},{5,3},{10,12},{11,13},{12,10},{13,11},{18,20},{1... | collective-permute-start | bytes 1572872 | tf_op jit(solution)/shard_map/ppermute | solution.py:466
  115.2 22.7 %collective-permute-start.28 = (bf16[64,4096]{1,0:T(8,128)(2,1)S(1)}, bf16[64,4096]{1,0:T(8,128)(2,1)S(1)}, u32[]{:S(2)}, u32[]{:S(2)}) collective-permute-start(bf16[64,4096]{1,0:T(8,128)(2,1)S(1)} %add_convert_fusion.3), channel_id=1, source_target_pairs={{0,2},{1,3},{2,0},{3,1},{4,6},{5,7},{6,4},{7,5},{8,10},{9,11},{10,... | collective-permute-start | bytes 1572872 | tf_op jit(solution)/shard_map/ppermute | solution.py:466
  126.9 21.8 %collective-permute-start.30 = (bf16[64,4096]{1,0:T(8,128)(2,1)S(1)}, bf16[64,4096]{1,0:T(8,128)(2,1)S(1)}, u32[]{:S(2)}, u32[]{:S(2)}) collective-permute-start(bf16[64,4096]{1,0:T(8,128)(2,1)S(1)} %get-tuple-element.66), channel_id=1, source_target_pairs={{6,2},{7,3},{0,4},{1,5},{14,10},{15,11},{8,12},{9,13},{22,18},{23,... | collective-permute-start | bytes 1572872 | tf_op jit(solution)/shard_map/ppermute | solution.py:466
  132.2 26.7 %collective-permute-start.32 = (bf16[64,4096]{1,0:T(8,128)(2,1)S(1)}, bf16[64,4096]{1,0:T(8,128)(2,1)S(1)}, u32[]{:S(2)}, u32[]{:S(2)}) collective-permute-start(bf16[64,4096]{1,0:T(8,128)(2,1)S(1)} %get-tuple-element.65), channel_id=1, source_target_pairs={{4,0},{5,1},{2,6},{3,7},{12,8},{13,9},{10,14},{11,15},{20,16},{21,... | collective-permute-start | bytes 1572872 | tf_op jit(solution)/shard_map/ppermute | solution.py:466
where the time goes:
time: 161 us; the launch traced here: 160 us
  waiting for transfers between devices  70.2 us (44%)
  Pallas kernels  43.5 us (27%)
  starting transfers between devices  41.3 us (26%)
  local copies, waits for them, and re-layouts  3.21 us (2%)
  other arithmetic  1.88 us (1%)
    ppermute x9, waiting for transfers between devices, along(): return lax.ppermute(value, 'seq', chip_pairs(pairs))  56.4 us
    ppermute x9, starting transfers between devices, along(): return lax.ppermute(value, 'seq', chip_pairs(pairs))  21.8 us
    ppermute x15, starting transfers between devices, exchange(): lax.ppermute(pieces[d], 'mod', [(i, i ^ d) for i in range(mod_count)])  18 us
    pallas_call x2, Pallas kernels, project_slots(): pl.pallas_call(kernel, out_shape=[pltpu.VMEM((count * block, cols), jnp.b...  16.7 us
    ppermute x15, waiting for transfers between devices, exchange(): lax.ppermute(pieces[d], 'mod', [(i, i ^ d) for i in range(mod_count)])  13.7 us
    pallas_call x2, Pallas kernels, attend_slots(): pl.pallas_call(kernel, out_shape=[pltpu.VMEM((len(query_slots) * block, H...  9 us
    pallas_call x1, Pallas kernels, fetch_weights(): pl.pallas_call(kernel, out_shape=[pltpu.VMEM((pairs, PIECES, piece, pair_...  8.9 us
    pallas_call x4, Pallas kernels, output_rows(): pl.pallas_call(kernel, out_shape=[pltpu.VMEM((half, width), jnp.bfloat16)...  5.46 us
  transfers between devices with their start and end apart: 33, of which 15 were waited for; matrix products, arithmetic and copies ran while one was open for 0% of the time, Pallas kernels for 24%

commit v1 on v0

--- a/solution.py
+++ b/solution.py
@@ -118,8 +118,8 @@
 PIECES = 4
 
 
-def mode_of(ids, modality, chips, slot):
-    return modality[ids[0] * chips + jnp.bitwise_xor(ids[1], slot)]
+def mode_of(info, slot):
+    return info[3 + slot]
 
 
 def params(mib):
@@ -128,38 +128,76 @@
 
 def norm_rows(ids, modality, tokens, norm_gain, chips):
     rows, width = tokens.shape
-
-    def kernel(ids_ref, modality_ref, tokens_ref, gain_ref, out_ref):
-        gain = gain_ref[pl.ds(mode_of(ids_ref, modality_ref, chips, 0), 1), :]
-        step = 16
-        for first in range(0, rows, step):
-            values = tokens_ref[first : first + step, :].astype(jnp.float32)
-            mean_square = jnp.sum(values * values, axis=1, keepdims=True) * (1.0 / width)
-            scaled = values * lax.rsqrt(mean_square + 1e-05) * gain
-            out_ref[first : first + step, :] = scaled.astype(jnp.bfloat16)
+    modes = norm_gain.shape[0]
+    step = 16
+    parts = 4
+    part = rows // parts
+
+    def kernel(ids_ref, modality_ref, tokens_ref, gain_ref, out_ref, info_ref, *scratch):
+        rows_ref, gains_ref, table_ref, row_sems, sems = scratch
+        table_copy = pltpu.make_async_copy(modality_ref, table_ref, sems.at[0])
+        table_copy.start()
+        gain_copy = pltpu.make_async_copy(gain_ref, gains_ref, sems.at[1])
+        gain_copy.start()
+        row_copies = [
+            pltpu.make_async_copy(
+                tokens_ref.at[pl.ds(i * part, part)],
+                rows_ref.at[pl.ds(i * part, part)],
+                row_sems.at[i],
+            )
+            for i in range(parts)
+        ]
+        for copy in row_copies:
+            copy.start()
+        table_copy.wait()
+        for i in range(3):
+            info_ref[i] = ids_ref[i]
+        for slot in range(chips):
+            at = ids_ref[0] * chips + jnp.bitwise_xor(ids_ref[1], slot)
+            info_ref[3 + slot] = table_ref[at]
+        mode = table_ref[ids_ref[0] * chips + ids_ref[1]]
+        gain_copy.wait()
+        gain = gains_ref[pl.ds(mode, 1), :]
+        for i in range(parts):
+            row_copies[i].wait()
+            for first in range(i * part, (i + 1) * part, step):
+                values = rows_ref[first : first + step, :].astype(jnp.float32)
+                mean_square = jnp.sum(values * values, axis=1, keepdims=True) * (1.0 / width)
+                scaled = values * lax.rsqrt(mean_square + 1e-05) * gain
+                out_ref[first : first + step, :] = scaled.astype(jnp.bfloat16)
 
     return pl.pallas_call(
         kernel,
-        out_shape=pltpu.VMEM((rows, width), jnp.bfloat16),
-        in_specs=[SMEM, SMEM, VMEM, VMEM],
-        out_specs=VMEM,
+        out_shape=[
+            pltpu.VMEM((rows, width), jnp.bfloat16),
+            jax.ShapeDtypeStruct((3 + chips,), jnp.int32),
+        ],
+        in_specs=[SMEM, HBM, HBM, HBM],
+        out_specs=[VMEM, SMEM],
+        scratch_shapes=[
+            pltpu.VMEM((rows, width), jnp.bfloat16),
+            pltpu.VMEM((modes, width), jnp.float32),
+            pltpu.SMEM(modality.shape, jnp.int32),
+            pltpu.SemaphoreType.DMA((parts,)),
+            pltpu.SemaphoreType.DMA((2,)),
+        ],
         compiler_params=params(8),
         cost_estimate=pl.CostEstimate(flops=4_000_000, bytes_accessed=1 << 20, transcendentals=64),
         name="norm_rows",
     )(ids, modality, tokens, norm_gain)
 
 
-def fetch_weights(ids, modality, qkv_weight, out_weight, chips, slot):
-    modes, width, cols = qkv_weight.shape
+def fetch_weights(info, qkv_weight, slot):
+    _, width, cols = qkv_weight.shape
     pairs = 2
     pair_cols = cols // pairs
     piece = width // PIECES
 
-    def kernel(ids_ref, modality_ref, qkv_ref, out_ref, late_ref, kept_ref, late_sems, kept_sems):
-        mode = mode_of(ids_ref, modality_ref, chips, slot)
+    def kernel(info_ref, qkv_ref, late_ref, late_sems):
+        mode = mode_of(info_ref, slot)
         copies = []
         for p in range(pairs):
-            first = jnp.bitwise_xor(ids_ref[0] // 2, p) * pair_cols
+            first = jnp.bitwise_xor(info_ref[0] // 2, p) * pair_cols
             for k in range(PIECES):
                 copies.append(
                     pltpu.make_async_copy(
@@ -172,8 +210,6 @@
                         late_sems.at[p, k],
                     )
                 )
-        for m in range(modes):
-            copies.append(pltpu.make_async_copy(out_ref.at[m], kept_ref.at[m], kept_sems.at[m]))
         for copy in copies:
             copy.start()
         for copy in copies:
@@ -181,34 +217,41 @@
 
     return pl.pallas_call(
         kernel,
-        out_shape=[
-            pltpu.VMEM((pairs, PIECES, piece, pair_cols), jnp.bfloat16),
-            pltpu.VMEM(out_weight.shape, jnp.bfloat16),
-        ],
-        in_specs=[SMEM, SMEM, HBM, HBM],
-        out_specs=[VMEM, VMEM],
-        scratch_shapes=[
-            pltpu.SemaphoreType.DMA((pairs, PIECES)),
-            pltpu.SemaphoreType.DMA((modes,)),
-        ],
+        out_shape=pltpu.VMEM((pairs, PIECES, piece, pair_cols), jnp.bfloat16),
+        in_specs=[SMEM, HBM],
+        out_specs=VMEM,
+        scratch_shapes=[pltpu.SemaphoreType.DMA((pairs, PIECES))],
         compiler_params=params(1),
         cost_estimate=pl.CostEstimate(
-            flops=6_000_000_000, bytes_accessed=25 << 20, transcendentals=0
+            flops=3_000_000_000, bytes_accessed=12 << 20, transcendentals=0
         ),
         name="fetch_weights",
-    )(ids, modality, qkv_weight, out_weight)
-
-
-def store_pair(ids_ref, outs, rows, p, result):
+    )(info, qkv_weight)
+
+
+class Prefetch:
+    def __init__(self, out_weight, slots):
+        self.weight, self.slots = out_weight, slots
+        self.shapes = [pltpu.VMEM(out_weight.shape[1:], jnp.bfloat16)] * len(slots)
+        self.scratch = pltpu.SemaphoreType.DMA((len(slots),))
+
+    def copies(self, info_ref, weight_ref, kept_refs, sems):
+        return [
+            pltpu.make_async_copy(weight_ref.at[mode_of(info_ref, slot)], kept_refs[i], sems.at[i])
+            for i, slot in enumerate(self.slots)
+        ]
+
+
+def store_pair(info_ref, outs, rows, p, result):
     result = result.astype(jnp.bfloat16)
     cols = result.shape[1] // 2
-    odd = ids_ref[0] % 2 == 1
+    odd = info_ref[0] % 2 == 1
     for e in range(2):
         first, last = result[:, e * cols : (e + 1) * cols], result[:, (1 - e) * cols : (2 - e) * cols]
         outs[2 * p + e][rows, :] = jnp.where(odd, last, first)
 
 
-def project_slots(ids, modality, parts, weight, chips, slots):
+def project_slots(info, parts, weight, slots):
     half, width = parts[0][0].shape
     block = 2 * half
     cols = 3 * HDIM
@@ -218,17 +261,17 @@
     piece = width // PIECES
     count = len(slots)
 
-    def kernel(ids_ref, modality_ref, *refs):
+    def kernel(info_ref, *refs):
         ins = refs[: 2 * count]
         weight_ref = refs[2 * count]
         outs = refs[2 * count + 1 : 2 * count + 1 + heads]
         buffer_ref, sems = refs[2 * count + 1 + heads :]
 
         def copy_of(n, p, k):
-            first = jnp.bitwise_xor(ids_ref[0] // 2, p) * pair_cols
+            first = jnp.bitwise_xor(info_ref[0] // 2, p) * pair_cols
             return pltpu.make_async_copy(
                 weight_ref.at[
-                    mode_of(ids_ref, modality_ref, chips, slots[n]),
+                    mode_of(info_ref, slots[n]),
                     pl.ds(k * piece, piece),
                     pl.ds(pl.multiple_of(first, 128), pair_cols),
                 ],
@@ -251,12 +294,12 @@
                     result = part if result is None else result + part
                     if n + 1 < count:
                         copy_of(n + 1, p, k).start()
-                store_pair(ids_ref, outs, pl.ds(n * block, block), p, result)
+                store_pair(info_ref, outs, pl.ds(n * block, block), p, result)
 
     return pl.pallas_call(
         kernel,
         out_shape=[pltpu.VMEM((count * block, cols), jnp.bfloat16)] * heads,
-        in_specs=[SMEM, SMEM] + [VMEM] * (2 * count) + [HBM],
+        in_specs=[SMEM] + [VMEM] * (2 * count) + [HBM],
         out_specs=[VMEM] * heads,
         scratch_shapes=[
             pltpu.VMEM((pairs, PIECES, piece, pair_cols), jnp.bfloat16),
@@ -269,18 +312,24 @@
             transcendentals=0,
         ),
         name="project_slots",
-    )(ids, modality, *[piece for pair in parts for piece in pair], weight)
-
-
-def project_late(ids, inner, relayed, weight, cols, chips):
+    )(info, *[piece for pair in parts for piece in pair], weight)
+
+
+def project_late(info, inner, relayed, weight, cols, chips, prefetch):
     half, width = inner[0].shape
     block = 2 * half
     pairs, pieces, piece, pair_cols = weight.shape
     heads = pairs * pair_cols // cols
 
-    def kernel(ids_ref, inner_own, inner_partner, relayed_own, relayed_partner, weight_ref, *refs):
-        outs, rows_ref = refs[:heads], refs[heads]
-        chip = ids_ref[1]
+    kept = len(prefetch.slots)
+
+    def kernel(info_ref, inner_own, inner_partner, relayed_own, relayed_partner, weight_ref, *refs):
+        next_ref, outs, kept_refs = refs[0], refs[1 : 1 + heads], refs[1 + heads : 1 + heads + kept]
+        rows_ref, sems = refs[1 + heads + kept :]
+        copies = prefetch.copies(info_ref, next_ref, kept_refs, sems)
+        for copy in copies:
+            copy.start()
+        chip = info_ref[1]
         middle = (chip > 0) & (chip < chips - 1)
 
         @pl.when(middle)
@@ -302,14 +351,16 @@
                     preferred_element_type=jnp.float32,
                 )
                 result = part if result is None else result + part
-            store_pair(ids_ref, outs, pl.ds(0, block), p, result)
+            store_pair(info_ref, outs, pl.ds(0, block), p, result)
+        for copy in copies:
+            copy.wait()
 
     return pl.pallas_call(
         kernel,
-        out_shape=[pltpu.VMEM((block, cols), jnp.bfloat16)] * heads,
-        in_specs=[SMEM] + [VMEM] * 5,
-        out_specs=[VMEM] * heads,
-        scratch_shapes=[pltpu.VMEM((block, width), jnp.bfloat16)],
+        out_shape=[pltpu.VMEM((block, cols), jnp.bfloat16)] * heads + prefetch.shapes,
+        in_specs=[SMEM] + [VMEM] * 5 + [HBM],
+        out_specs=[VMEM] * (heads + kept),
+        scratch_shapes=[pltpu.VMEM((block, width), jnp.bfloat16), prefetch.scratch],
         compiler_params=params(8),
         cost_estimate=pl.CostEstimate(
             flops=2 * block * width * cols * heads,
@@ -317,10 +368,10 @@
             transcendentals=0,
         ),
         name="project_late",
-    )(ids, *inner, *relayed, weight)
-
-
-def attend_slots(ids, doc_lengths, sets, query_slots, chips):
+    )(info, *inner, *relayed, weight, prefetch.weight)
+
+
+def attend_slots(info, doc_lengths, sets, query_slots, chips, prefetch):
     count = len(sets[0][1])
     block = sets[0][1][0].shape[0] // len(sets[0][0])
     total = count * chips * block
@@ -328,11 +379,16 @@
     scale = 1.0 / math.sqrt(HDIM)
     docs = doc_lengths.shape[0]
 
-    def kernel(ids_ref, docs_ref, *refs):
-        ins = refs[: len(sets) * count]
-        outs = refs[len(sets) * count : (len(sets) + 1) * count]
-        keys_ref, values_ref = refs[(len(sets) + 1) * count :]
-        mu, chip, own_first = ids_ref[0], ids_ref[1], ids_ref[2] * (block // 2)
+    kept = len(prefetch.slots)
+
+    def kernel(info_ref, docs_ref, *refs):
+        ins, refs = refs[: len(sets) * count], refs[len(sets) * count :]
+        next_ref, outs, kept_refs = refs[0], refs[1 : 1 + count], refs[1 + count : 1 + count + kept]
+        keys_ref, values_ref, sems = refs[1 + count + kept :]
+        copies = prefetch.copies(info_ref, next_ref, kept_refs, sems)
+        for copy in copies:
+            copy.start()
+        mu, chip, own_first = info_ref[0], info_ref[1], info_ref[2] * (block // 2)
 
         def slot_rows(d, slot, part):
             for i, (slots, _) in enumerate(sets):
@@ -389,16 +445,20 @@
                     preferred_element_type=jnp.float32,
                 )
                 outs[d][n * block : (n + 1) * block, :] = (summed / totals).astype(jnp.bfloat16)
+        for copy in copies:
+            copy.wait()
 
     n_queries = len(query_slots) * count
     return pl.pallas_call(
         kernel,
-        out_shape=[pltpu.VMEM((len(query_slots) * block, HDIM), jnp.bfloat16)] * count,
-        in_specs=[SMEM, SMEM] + [VMEM] * (len(sets) * count),
-        out_specs=[VMEM] * count,
+        out_shape=[pltpu.VMEM((len(query_slots) * block, HDIM), jnp.bfloat16)] * count
+        + prefetch.shapes,
+        in_specs=[SMEM, SMEM] + [VMEM] * (len(sets) * count) + [HBM],
+        out_specs=[VMEM] * (count + kept),
         scratch_shapes=[
             pltpu.VMEM((total, HDIM), jnp.bfloat16),
             pltpu.VMEM((total, HDIM), jnp.bfloat16),
+            prefetch.scratch,
         ],
         compiler_params=params(18),
         cost_estimate=pl.CostEstimate(
@@ -407,27 +467,26 @@
             transcendentals=n_queries * block * window,
         ),
         name="attend_slots",
-    )(ids, doc_lengths, *[piece for _, pieces in sets for piece in pieces])
-
-
-def output_rows(ids, modality, pieces, weight, chips, slots, slot):
+    )(info, doc_lengths, *[piece for _, pieces in sets for piece in pieces], prefetch.weight)
+
+
+def output_rows(info, pieces, weight, slots, slot):
     count = len(pieces)
     block = pieces[0].shape[0] // len(slots)
     half = block // 2
     at = slots.index(slot) * block
-    depth, width = weight.shape[1:]
+    depth, width = weight.shape
     tile = min(1024, width)
 
-    def kernel(ids_ref, modality_ref, *refs):
+    def kernel(info_ref, *refs):
         ins = refs[:count]
         weight_ref, own_ref, partner_ref, heads_ref = refs[count:]
-        mode = mode_of(ids_ref, modality_ref, chips, slot)
         for d in range(count):
-            heads_ref[jnp.bitwise_xor(ids_ref[0], d)] = ins[d][at : at + block, :]
+            heads_ref[jnp.bitwise_xor(info_ref[0], d)] = ins[d][at : at + block, :]
         rows = jnp.concatenate([heads_ref[h] for h in range(count)], axis=1)
         for first in range(0, width, tile):
             cols = slice(first, first + tile)
-            result = jnp.dot(rows, weight_ref[mode, :, cols], preferred_element_type=jnp.float32)
+            result = jnp.dot(rows, weight_ref[:, cols], preferred_element_type=jnp.float32)
             result = result.astype(jnp.bfloat16)
             own_ref[:, cols] = result[:half]
             partner_ref[:, cols] = result[half:]
@@ -435,7 +494,7 @@
     return pl.pallas_call(
         kernel,
         out_shape=[pltpu.VMEM((half, width), jnp.bfloat16)] * 2,
-        in_specs=[SMEM, SMEM] + [VMEM] * (count + 1),
+        in_specs=[SMEM] + [VMEM] * (count + 1),
         out_specs=[VMEM] * 2,
         scratch_shapes=[pltpu.VMEM((count, block, HDIM), jnp.bfloat16)],
         compiler_params=params(8),
@@ -445,7 +504,7 @@
             transcendentals=0,
         ),
         name="output_rows",
-    )(ids, modality, *pieces, weight)
+    )(info, *pieces, weight)
 
 
 def chip_pairs(pairs):
@@ -474,7 +533,17 @@
             moved.append(lax.ppermute(pieces[d], "mod", [(i, i ^ d) for i in range(mod_count)]))
         return moved
 
-    normed = norm_rows(ids, modality, tokens, norm_gain, chips)
+    def add(*shares):
+        total = shares[0].astype(jnp.float32)
+        for share in shares[1:]:
+            total = total + share.astype(jnp.float32)
+        return total.astype(jnp.bfloat16)
+
+    in_hbm = [
+        pltpu.with_memory_space_constraint(value, pltpu.HBM)
+        for value in (modality, tokens, norm_gain)
+    ]
+    normed, info = norm_rows(ids, *in_hbm, chips)
     two = along(normed, [(i, i ^ 2) for i in range(chips)])
     one = along(normed, [(i, i ^ 1) for i in range(chips)])
     inner = along(normed, [(1, 2), (2, 1)])
@@ -485,40 +554,46 @@
     inner_pair = (inner, swap(inner))
     relayed_pair = (relayed, swap(relayed))
 
-    own = project_slots(ids, modality, [own_pair], qkv_weight, chips, (0,))
+    own = project_slots(info, [own_pair], qkv_weight, (0,))
     own = exchange(own)
-    late_weight, kept_weight = fetch_weights(ids, modality, qkv_weight, out_weight, chips, 3)
-    mid = project_slots(ids, modality, [two_pair, one_pair], qkv_weight, chips, (2, 1))
+    late_weight = fetch_weights(info, qkv_weight, 3)
+    mid = project_slots(info, [two_pair, one_pair], qkv_weight, (2, 1))
     mid = exchange(mid)
-    late = project_late(ids, inner_pair, relayed_pair, late_weight, 3 * HDIM, chips)
+    kept = {}
+    *late, kept[3] = project_late(
+        info,
+        inner_pair,
+        relayed_pair,
+        late_weight,
+        3 * HDIM,
+        chips,
+        Prefetch(out_weight, (3,)),
+    )
     late = exchange(late)
     sets = (((0,), own), ((2, 1), mid), ((3,), late))
 
-    def add(*shares):
-        total = shares[0].astype(jnp.float32)
-        for share in shares[1:]:
-            total = total + share.astype(jnp.float32)
-        return total.astype(jnp.bfloat16)
-
     def finish(pieces, slots, slot):
-        own_share, partner_share = output_rows(
-            ids, modality, pieces, kept_weight, chips, slots, slot
-        )
+        own_share, partner_share = output_rows(info, pieces, kept[slot], slots, slot)
         return own_share, swap(partner_share)
 
-    first = attend_slots(ids, doc_lengths, sets, (3,), chips)
+    *first, kept[2], kept[1] = attend_slots(
+        info, doc_lengths, sets, (3, 2), chips, Prefetch(out_weight, (2, 1))
+    )
     first = exchange(first)
-    sum3 = add(*finish(first, (3,), 3))
+    sum3 = add(*finish(first, (3, 2), 3))
     from_end = along(sum3, [(3, 2), (0, 1)])
     from_inner = along(sum3, [(1, 2), (2, 1)])
-    rest = attend_slots(ids, doc_lengths, sets, (2, 1, 0), chips)
+    sum2 = add(*finish(first, (3, 2), 2))
+    from_two_end = along(sum2, [(3, 1), (0, 2)])
+    *rest, kept[0] = attend_slots(
+        info, doc_lengths, sets, (1, 0), chips, Prefetch(out_weight, (0,))
+    )
     rest = exchange(rest)
-    sum2 = add(*finish(rest, (2, 1, 0), 2))
-    from_two_end = along(sum2, [(3, 1), (0, 2)])
-    from_two_inner = along(add(sum2, from_end), [(2, 0), (1, 3)])
-    sum1 = add(*finish(rest, (2, 1, 0), 1))
+    both2 = add(lax.optimization_barrier(sum2), from_end)
+    from_two_inner = along(both2, [(2, 0), (1, 3)])
+    sum1 = add(*finish(rest, (1, 0), 1))
     from_one = along(sum1, [(i, i ^ 1) for i in range(chips)])
-    shares0 = finish(rest, (2, 1, 0), 0)
+    shares0 = finish(rest, (1, 0), 0)
     return add(tokens, *shares0, from_inner, from_one, from_two_end, from_two_inner)
 
 

time: 161 us -> 160 us (level)
  starting transfers between devices: 41.3 us -> 37.2 us
  Pallas kernels: 43.5 us -> 47.3 us
  local copies, waits for them, and re-layouts: 3.21 us -> 0.01 us
  waiting for transfers between devices: 70.2 us -> 72.5 us
    pallas_call x2, Pallas kernels: 9 us -> 14.6 us  [attend_slots(): pl.pallas_call(kernel, out_shape=[pltpu.VMEM((len(query_slots) * block, H...]
    ppermute x9, starting transfers between devices: 21.8 us -> 17.1 us  [along(): return lax.ppermute(value, 'seq', chip_pairs(pairs))]
    ppermute x9, waiting for transfers between devices: 56.4 us -> 59.9 us  [along(): return lax.ppermute(value, 'seq', chip_pairs(pairs))]
    unnamed x14 -> x4, local copies, waits for them, and re-layouts: 3.21 us -> 0.01 us
    pallas_call x2, Pallas kernels: 9.7 us -> 7.91 us  [the longest x1 5.25 us: fetch_weights(): pl.pallas_call(kernel, out_shape=pltpu.VMEM((pairs, PIECES, piece, pair_c...]
  transfers between devices with their start and end apart: 33 -> 33, of which waited for: 15 -> 16; matrix products, arithmetic and copies ran while one was open for 0% -> 0% of each run, Pallas kernels for 24% -> 22%
where the time goes in v1:
time: 160 us; the launch traced here: 159 us
  waiting for transfers between devices  72.5 us (45%)
  Pallas kernels  47.3 us (30%)
  starting transfers between devices  37.2 us (23%)
  other arithmetic  1.9 us (1%)
    ppermute x9, waiting for transfers between devices, along(): return lax.ppermute(value, 'seq', chip_pairs(pairs))  59.9 us
    ppermute x15, starting transfers between devices, exchange(): lax.ppermute(pieces[d], 'mod', [(i, i ^ d) for i in range(mod_count)])  18.8 us
    ppermute x9, starting transfers between devices, along(): return lax.ppermute(value, 'seq', chip_pairs(pairs))  17.1 us
    pallas_call x2, Pallas kernels, project_slots(): pl.pallas_call(kernel, out_shape=[pltpu.VMEM((count * block, cols), jnp.b...  16.7 us
    pallas_call x2, Pallas kernels, attend_slots(): pl.pallas_call(kernel, out_shape=[pltpu.VMEM((len(query_slots) * block, H...  14.6 us
    ppermute x15, waiting for transfers between devices, exchange(): lax.ppermute(pieces[d], 'mod', [(i, i ^ d) for i in range(mod_count)])  12.6 us
    pallas_call x4, Pallas kernels, output_rows(): pl.pallas_call(kernel, out_shape=[pltpu.VMEM((half, width), jnp.bfloat16)...  5.41 us
    pallas_call x1, Pallas kernels, fetch_weights(): pl.pallas_call(kernel, out_shape=pltpu.VMEM((pairs, PIECES, piece, pair_c...  5.25 us
  transfers between devices with their start and end apart: 33, of which 16 were waited for; matrix products, arithmetic and copies ran while one was open for 0% of the time, Pallas kernels for 22%

profile of v1, /device:TPU:0, one launch (start us, length us, event | category | flops | bytes accessed | tf_op | source)
XLA Modules:
  0.0 159.2 jit_solution(10162780245155846169)
XLA Ops:
  0.0 0.1 pad_add_fusion.ids_ref
  0.1 2.7 %norm_rows.1 = (bf16[64,4096]{1,0:T(8,128)(2,1)S(1)}, s32[7]{0:T(128)S(1)}) custom-call(s32[3]{0:T(128)S(1)} %pad_add_fusion.ids_ref, s32[16]{0:T(128)} %modality_ref.1, bf16[64,4096]{1,0:T(8,128)(2,1)} %tokens_ref.1, f32[3,4096]{1,0:T(4,128)} %gain_ref.1), custom_call_target="tpu_custom_call" | custom-call | flops 4000000 | bytes 1048576 | tf_op jit(solution)/shard_map/norm_rows/pallas_call | solution.py:169
  2.7 4.1 %collective-permute-start.4 = (bf16[64,4096]{1,0:T(8,128)(2,1)S(1)}, bf16[64,4096]{1,0:T(8,128)(2,1)S(1)}, u32[]{:S(2)}, u32[]{:S(2)}) collective-permute-start(bf16[64,4096]{1,0:T(8,128)(2,1)S(1)} %get-tuple-element.40.refs_0_), channel_id=1, source_target_pairs={{0,4},{1,5},{2,6},{3,7},{4,0},{5,1},{6,2},{7,3},{8,12},{9,13},{10,... | collective-permute-start | bytes 1572872 | tf_op jit(solution)/shard_map/ppermute | solution.py:525
  6.9 1.6 collective-permute-start.6
  8.5 0.7 collective-permute-start.11
  9.1 21.8 %collective-permute-done.4.refs_0_ = bf16[64,4096]{1,0:T(8,128)(2,1)S(1)} collective-permute-done((bf16[64,4096]{1,0:T(8,128)(2,1)S(1)}, bf16[64,4096]{1,0:T(8,128)(2,1)S(1)}, u32[]{:S(2)}, u32[]{:S(2)}) %collective-permute-start.4) | collective-permute-done | bytes 524320 | tf_op jit(solution)/shard_map/ppermute | solution.py:525
  30.9 1.3 collective-permute-start.13
  32.2 0.1 collective-permute-start.5
  32.3 0.5 collective-permute-start.7
  32.8 6.3 %project_slots.2 = (bf16[128,384]{1,0:T(8,128)(2,1)S(1)}, bf16[128,384]{1,0:T(8,128)(2,1)S(1)}, bf16[128,384]{1,0:T(8,128)(2,1)S(1)}, bf16[128,384]{1,0:T(8,128)(2,1)S(1)}) custom-call(s32[7]{0:T(128)S(1)} %get-tuple-element.39.info_ref, bf16[64,4096]{1,0:T(8,128)(2,1)S(1)} %get-tuple-element.40.refs_0_, bf16[64,4096]{1,0:T(8,128)(2,1)S(1)} %collective-permute-done.refs_1_, ...), custom_call_target="tpu_custom_call" | custom-call | flops 1610612736 | bytes 12582912 | tf_op jit(solution)/shard_map/project_slots/pallas_call | solution.py:299
  39.1 1.9 %collective-permute-start.1 = (bf16[128,384]{1,0:T(8,128)(2,1)S(1)}, bf16[128,384]{1,0:T(8,128)(2,1)S(1)}, u32[]{:S(2)}, u32[]{:S(2)}) collective-permute-start(bf16[128,384]{1,0:T(8,128)(2,1)S(1)} %get-tuple-element.42), channel_id=1, source_target_pairs={{0,8},{8,0},{16,24},{24,16},{1,9},{9,1},{17,25},{25,17},{2,10},{10... | collective-permute-start | bytes 294920 | tf_op jit(solution)/shard_map/ppermute | solution.py:533
  41.0 4.0 %collective-permute-done.13.relayed_own = bf16[64,4096]{1,0:T(8,128)(2,1)S(1)} collective-permute-done((bf16[64,4096]{1,0:T(8,128)(2,1)S(1)}, bf16[64,4096]{1,0:T(8,128)(2,1)S(1)}, u32[]{:S(2)}, u32[]{:S(2)}) %collective-permute-start.13) | collective-permute-done | bytes 524320 | tf_op jit(solution)/shard_map/ppermute | solution.py:525
  45.1 10.3 %project_slots.3 = (bf16[256,384]{1,0:T(8,128)(2,1)S(1)}, bf16[256,384]{1,0:T(8,128)(2,1)S(1)}, bf16[256,384]{1,0:T(8,128)(2,1)S(1)}, bf16[256,384]{1,0:T(8,128)(2,1)S(1)}) custom-call(s32[7]{0:T(128)S(1)} %get-tuple-element.39.info_ref, bf16[64,4096]{1,0:T(8,128)(2,1)S(1)} %collective-permute-done.4.refs_0_, ...), custom_call_target="tpu_custom_call" | custom-call | flops 3221225472 | bytes 25165824 | tf_op jit(solution)/shard_map/project_slots/pallas_call | solution.py:299
  55.4 2.3 %collective-permute-start.10 = (bf16[256,384]{1,0:T(8,128)(2,1)S(1)}, bf16[256,384]{1,0:T(8,128)(2,1)S(1)}, u32[]{:S(2)}, u32[]{:S(2)}) collective-permute-start(bf16[256,384]{1,0:T(8,128)(2,1)S(1)} %get-tuple-element.48), channel_id=1, source_target_pairs={{0,24},{8,16},{16,8},{24,0},{1,25},{9,17},{17,9},{25,1},{2,26},{10... | collective-permute-start | bytes 589832 | tf_op jit(solution)/shard_map/ppermute | solution.py:533
  57.7 5.3 %fetch_weights.1.weight_ref = bf16[2,4,1024,768]{3,2,1,0:T(8,128)(2,1)S(1)} custom-call(s32[7]{0:T(128)S(1)} %get-tuple-element.39.info_ref, bf16[3,4096,1536]{2,1,0:T(8,128)(2,1)} %qkv_ref.1), custom_call_target="tpu_custom_call" | custom-call | flops 3000000000 | bytes 12582912 | tf_op jit(solution)/shard_map/fetch_weights/pallas_call | solution.py:218
  63.0 0.6 collective-permute-start.2
  63.5 1.5 collective-permute-start.3
  65.0 1.5 collective-permute-start.8
  66.5 0.5 collective-permute-start.9
  67.0 2.7 %project_late.1 = (bf16[128,384]{1,0:T(8,128)(2,1)S(1)}, bf16[128,384]{1,0:T(8,128)(2,1)S(1)}, bf16[128,384]{1,0:T(8,128)(2,1)S(1)}, bf16[128,384]{1,0:T(8,128)(2,1)S(1)}, bf16[512,4096]{1,0:T(8,128)(2,1)S(1)}) custom-call(s32[7]{0:T(128)S(1)} %get-tuple-element.39.info_ref, bf16[64,4096]{1,0:T(8,128)(2,1)S(1)} %collective-permute-done.11.inner_own, ...), custom_call_target="tpu_custom_call" | custom-call | flops 1610612736 | bytes 12582912 | tf_op jit(solution)/shard_map/project_late/pallas_call | solution.py:358
  69.8 1.0 collective-permute-done.2.refs_2_
  70.8 0.4 collective-permute-start.15
  71.2 0.7 collective-permute-start.16
  71.9 2.4 %collective-permute-start.17 = (bf16[128,384]{1,0:T(8,128)(2,1)S(1)}, bf16[128,384]{1,0:T(8,128)(2,1)S(1)}, u32[]{:S(2)}, u32[]{:S(2)}) collective-permute-start(bf16[128,384]{1,0:T(8,128)(2,1)S(1)} %get-tuple-element.52), channel_id=1, source_target_pairs={{0,24},{8,16},{16,8},{24,0},{1,25},{9,17},{17,9},{25,1},{2,26},{10... | collective-permute-start | bytes 294920 | tf_op jit(solution)/shard_map/ppermute | solution.py:533
  74.3 0.1 collective-permute-done.8.refs_5_
  74.4 1.2 collective-permute-done.9.refs_6_
  75.6 0.9 collective-permute-done.15.refs_9_
  76.5 2.0 %collective-permute-done.16.refs_10_ = bf16[128,384]{1,0:T(8,128)(2,1)S(1)} collective-permute-done((bf16[128,384]{1,0:T(8,128)(2,1)S(1)}, bf16[128,384]{1,0:T(8,128)(2,1)S(1)}, u32[]{:S(2)}, u32[]{:S(2)}) %collective-permute-start.16) | collective-permute-done | bytes 98336 | tf_op jit(solution)/shard_map/ppermute | solution.py:533
  78.5 7.9 %attend_slots.3 = (bf16[256,128]{1,0:T(8,128)(2,1)S(1)}, bf16[256,128]{1,0:T(8,128)(2,1)S(1)}, bf16[256,128]{1,0:T(8,128)(2,1)S(1)}, bf16[256,128]{1,0:T(8,128)(...) custom-call(s32[7]{0:T(128)S(1)} %get-tuple-element.39.info_ref, s32[4]{0:T(128)S(1)} %copy-done, ...), custom_call_target="tpu_custom_call" | custom-call | flops 1207959552 | bytes 1572864 | tf_op jit(solution)/shard_map/attend_slots/pallas_call | solution.py:452
  86.4 0.7 collective-permute-start.22
  87.1 1.3 collective-permute-start.23
  88.4 1.6 %collective-permute-start.24 = (bf16[256,128]{1,0:T(8,128)(2,1)S(1)}, bf16[256,128]{1,0:T(8,128)(2,1)S(1)}, u32[]{:S(2)}, u32[]{:S(2)}) collective-permute-start(bf16[256,128]{1,0:T(8,128)(2,1)S(1)} %get-tuple-element.63), channel_id=1, source_target_pairs={{0,24},{8,16},{16,8},{24,0},{1,25},{9,17},{17,9},{25,1},{2,26},{10... | collective-permute-start | bytes 196616 | tf_op jit(solution)/shard_map/ppermute | solution.py:533
  90.0 1.1 collective-permute-done.22.refs_1_
  91.1 0.2 collective-permute-done.23.refs_2_
  91.4 2.2 %collective-permute-done.24.refs_3_ = bf16[256,128]{1,0:T(8,128)(2,1)S(1)} collective-permute-done((bf16[256,128]{1,0:T(8,128)(2,1)S(1)}, bf16[256,128]{1,0:T(8,128)(2,1)S(1)}, u32[]{:S(2)}, u32[]{:S(2)}) %collective-permute-start.24) | collective-permute-done | bytes 65568 | tf_op jit(solution)/shard_map/ppermute | solution.py:533
  93.5 1.3 output_rows.7
  94.8 0.1 collective-permute-start.29
  94.9 6.6 %attend_slots.2 = (bf16[256,128]{1,0:T(8,128)(2,1)S(1)}, bf16[256,128]{1,0:T(8,128)(2,1)S(1)}, bf16[256,128]{1,0:T(8,128)(2,1)S(1)}, bf16[256,128]{1,0:T(8,128)(2,1)S(1)}, bf16[512,4096]{1,0:T(8,128)(2,1)S(1)}) custom-call(s32[7]{0:T(128)S(1)} %get-tuple-element.39.info_ref, s32[4]{0:T(128)S(1)} %copy-done, bf16[128,384]{1,0:T(8,128)(2,1)S(1)} %get-tuple-element.41.refs_0_, ...), custom_call_target="tpu_custom_call" | custom-call | flops 1207959552 | bytes 1572864 | tf_op jit(solution)/shard_map/attend_slots/pallas_call | solution.py:452
  101.6 0.7 collective-permute-start.18
  102.3 1.5 collective-permute-start.19
  103.8 1.3 collective-permute-start.20
  105.1 1.0 collective-permute-done.18.refs_1_
  106.1 0.5 collective-permute-done.19.refs_2_
  106.6 2.4 %collective-permute-done.20.refs_3_ = bf16[256,128]{1,0:T(8,128)(2,1)S(1)} collective-permute-done((bf16[256,128]{1,0:T(8,128)(2,1)S(1)}, bf16[256,128]{1,0:T(8,128)(2,1)S(1)}, u32[]{:S(2)}, u32[]{:S(2)}) %collective-permute-start.20) | collective-permute-done | bytes 65568 | tf_op jit(solution)/shard_map/ppermute | solution.py:533
  109.0 1.3 output_rows.4
  110.3 0.1 collective-permute-start.21
  110.4 1.5 output_rows.6
  111.9 0.6 collective-permute-start.27
  112.5 1.3 output_rows.5
  113.8 0.0 copy-start.1
  113.8 0.1 collective-permute-start.25
  113.9 0.1 add_convert_fusion.2
  114.0 4.5 %collective-permute-start.30 = (bf16[64,4096]{1,0:T(8,128)(2,1)S(1)}, bf16[64,4096]{1,0:T(8,128)(2,1)S(1)}, u32[]{:S(2)}, u32[]{:S(2)}) collective-permute-start(bf16[64,4096]{1,0:T(8,128)(2,1)S(1)} %add_convert_fusion.2), channel_id=1, source_target_pairs={{6,2},{7,3},{0,4},{1,5},{14,10},{15,11},{8,12},{9,13},{22,18},{23,... | collective-permute-start | bytes 1572872 | tf_op jit(solution)/shard_map/ppermute | solution.py:525
  118.5 0.1 add_convert_fusion.4
  118.6 1.3 collective-permute-start.31
  119.9 0.7 collective-permute-start.26
  120.7 0.1 add_convert_fusion.3
  120.8 1.6 %collective-permute-start.28 = (bf16[64,4096]{1,0:T(8,128)(2,1)S(1)}, bf16[64,4096]{1,0:T(8,128)(2,1)S(1)}, u32[]{:S(2)}, u32[]{:S(2)}) collective-permute-start(bf16[64,4096]{1,0:T(8,128)(2,1)S(1)} %add_convert_fusion.3), channel_id=1, source_target_pairs={{0,2},{1,3},{2,0},{3,1},{4,6},{5,7},{6,4},{7,5},{8,10},{9,11},{10,... | collective-permute-start | bytes 1572872 | tf_op jit(solution)/shard_map/ppermute | solution.py:525
  122.4 19.6 %collective-permute-done.31 = bf16[64,4096]{1,0:T(8,128)(2,1)S(1)} collective-permute-done((bf16[64,4096]{1,0:T(8,128)(2,1)S(1)}, bf16[64,4096]{1,0:T(8,128)(2,1)S(1)}, u32[]{:S(2)}, u32[]{:S(2)}) %collective-permute-start.31) | collective-permute-done | bytes 524320 | tf_op jit(solution)/shard_map/ppermute | solution.py:525
  142.0 0.1 add_convert_fusion.1
  142.1 1.3 collective-permute-start.32
  143.5 9.3 %collective-permute-done.28 = bf16[64,4096]{1,0:T(8,128)(2,1)S(1)} collective-permute-done((bf16[64,4096]{1,0:T(8,128)(2,1)S(1)}, bf16[64,4096]{1,0:T(8,128)(2,1)S(1)}, u32[]{:S(2)}, u32[]{:S(2)}) %collective-permute-start.28) | collective-permute-done | bytes 524320 | tf_op jit(solution)/shard_map/ppermute | solution.py:525
  152.8 5.1 %collective-permute-done.32 = bf16[64,4096]{1,0:T(8,128)(2,1)S(1)} collective-permute-done((bf16[64,4096]{1,0:T(8,128)(2,1)S(1)}, bf16[64,4096]{1,0:T(8,128)(2,1)S(1)}, u32[]{:S(2)}, u32[]{:S(2)}) %collective-permute-start.32) | collective-permute-done | bytes 524320 | tf_op jit(solution)/shard_map/ppermute | solution.py:525
  157.9 1.3 add_convert_fusion
  (23 shorter events, 0.1 us)
Async XLA Ops:
  2.7 28.2 %collective-permute-start.4 = (bf16[64,4096]{1,0:T(8,128)(2,1)S(1)}, bf16[64,4096]{1,0:T(8,128)(2,1)S(1)}, u32[]{:S(2)}, u32[]{:S(2)}) collective-permute-start(bf16[64,4096]{1,0:T(8,128)(2,1)S(1)} %get-tuple-element.40.refs_0_), channel_id=1, source_target_pairs={{0,4},{1,5},{2,6},{3,7},{4,0},{5,1},{6,2},{7,3},{8,12},{9,13},{10,... | collective-permute-start | bytes 1572872 | tf_op jit(solution)/shard_map/ppermute | solution.py:525
  6.9 25.4 %collective-permute-start.6 = (bf16[64,4096]{1,0:T(8,128)(2,1)S(1)}, bf16[64,4096]{1,0:T(8,128)(2,1)S(1)}, u32[]{:S(2)}, u32[]{:S(2)}) collective-permute-start(bf16[64,4096]{1,0:T(8,128)(2,1)S(1)} %get-tuple-element.40.refs_0_), channel_id=1, source_target_pairs={{0,2},{1,3},{2,0},{3,1},{4,6},{5,7},{6,4},{7,5},{8,10},{9,11},{10,... | collective-permute-start | bytes 1572872 | tf_op jit(solution)/shard_map/ppermute | solution.py:525
  8.5 24.3 %collective-permute-start = (bf16[64,4096]{1,0:T(8,128)(2,1)S(1)}, bf16[64,4096]{1,0:T(8,128)(2,1)S(1)}, u32[]{:S(2)}, u32[]{:S(2)}) collective-permute-start(bf16[64,4096]{1,0:T(8,128)(2,1)S(1)} %get-tuple-element.40.refs_0_), channel_id=1, source_target_pairs={{0,1},{1,0},{2,3},{3,2},{4,5},{5,4},{6,7},{7,6},{8,9},{9,8},{10,11... | collective-permute-start | bytes 1572872 | tf_op jit(solution)/shard_map/ppermute | solution.py:528
  8.5 32.6 %collective-permute-start.11 = (bf16[64,4096]{1,0:T(8,128)(2,1)S(1)}, bf16[64,4096]{1,0:T(8,128)(2,1)S(1)}, u32[]{:S(2)}, u32[]{:S(2)}) collective-permute-start(bf16[64,4096]{1,0:T(8,128)(2,1)S(1)} %get-tuple-element.40.refs_0_), channel_id=1, source_target_pairs={{2,4},{3,5},{4,2},{5,3},{10,12},{11,13},{12,10},{13,11},{18,20},{1... | collective-permute-start | bytes 1572872 | tf_op jit(solution)/shard_map/ppermute | solution.py:525
  30.9 14.1 %collective-permute-start.13 = (bf16[64,4096]{1,0:T(8,128)(2,1)S(1)}, bf16[64,4096]{1,0:T(8,128)(2,1)S(1)}, u32[]{:S(2)}, u32[]{:S(2)}) collective-permute-start(bf16[64,4096]{1,0:T(8,128)(2,1)S(1)} %collective-permute-done.4.refs_0_), channel_id=1, source_target_pairs={{4,6},{5,7},{2,0},{3,1},{12,14},{13,15},{10,8},{11,9},{20,22},{21,... | collective-permute-start | bytes 1572872 | tf_op jit(solution)/shard_map/ppermute | solution.py:525
  32.2 12.8 %collective-permute-start.5 = (bf16[64,4096]{1,0:T(8,128)(2,1)S(1)}, bf16[64,4096]{1,0:T(8,128)(2,1)S(1)}, u32[]{:S(2)}, u32[]{:S(2)}) collective-permute-start(bf16[64,4096]{1,0:T(8,128)(2,1)S(1)} %collective-permute-done.4.refs_0_), channel_id=1, source_target_pairs={{0,1},{1,0},{2,3},{3,2},{4,5},{5,4},{6,7},{7,6},{8,9},{9,8},{10,11... | collective-permute-start | bytes 1572872 | tf_op jit(solution)/shard_map/ppermute | solution.py:528
  32.3 12.8 %collective-permute-start.7 = (bf16[64,4096]{1,0:T(8,128)(2,1)S(1)}, bf16[64,4096]{1,0:T(8,128)(2,1)S(1)}, u32[]{:S(2)}, u32[]{:S(2)}) collective-permute-start(bf16[64,4096]{1,0:T(8,128)(2,1)S(1)} %collective-permute-done.6.refs_2_), channel_id=1, source_target_pairs={{0,1},{1,0},{2,3},{3,2},{4,5},{5,4},{6,7},{7,6},{8,9},{9,8},{10,11... | collective-permute-start | bytes 1572872 | tf_op jit(solution)/shard_map/ppermute | solution.py:528
  39.1 24.4 %collective-permute-start.1 = (bf16[128,384]{1,0:T(8,128)(2,1)S(1)}, bf16[128,384]{1,0:T(8,128)(2,1)S(1)}, u32[]{:S(2)}, u32[]{:S(2)}) collective-permute-start(bf16[128,384]{1,0:T(8,128)(2,1)S(1)} %get-tuple-element.42), channel_id=1, source_target_pairs={{0,8},{8,0},{16,24},{24,16},{1,9},{9,1},{17,25},{25,17},{2,10},{10... | collective-permute-start | bytes 294920 | tf_op jit(solution)/shard_map/ppermute | solution.py:533
  41.0 24.0 %collective-permute-start.12 = (bf16[64,4096]{1,0:T(8,128)(2,1)S(1)}, bf16[64,4096]{1,0:T(8,128)(2,1)S(1)}, u32[]{:S(2)}, u32[]{:S(2)}) collective-permute-start(bf16[64,4096]{1,0:T(8,128)(2,1)S(1)} %collective-permute-done.11.inner_own), channel_id=1, source_target_pairs={{0,1},{1,0},{2,3},{3,2},{4,5},{5,4},{6,7},{7,6},{8,9},{9,8},{10,11... | collective-permute-start | bytes 1572872 | tf_op jit(solution)/shard_map/ppermute | solution.py:528
  45.1 21.5 %collective-permute-start.14 = (bf16[64,4096]{1,0:T(8,128)(2,1)S(1)}, bf16[64,4096]{1,0:T(8,128)(2,1)S(1)}, u32[]{:S(2)}, u32[]{:S(2)}) collective-permute-start(bf16[64,4096]{1,0:T(8,128)(2,1)S(1)} %collective-permute-done.13.relayed_own), channel_id=1, source_target_pairs={{0,1},{1,0},{2,3},{3,2},{4,5},{5,4},{6,7},{7,6},{8,9},{9,8},{10,11... | collective-permute-start | bytes 1572872 | tf_op jit(solution)/shard_map/ppermute | solution.py:528
  55.4 16.5 %collective-permute-start.10 = (bf16[256,384]{1,0:T(8,128)(2,1)S(1)}, bf16[256,384]{1,0:T(8,128)(2,1)S(1)}, u32[]{:S(2)}, u32[]{:S(2)}) collective-permute-start(bf16[256,384]{1,0:T(8,128)(2,1)S(1)} %get-tuple-element.48), channel_id=1, source_target_pairs={{0,24},{8,16},{16,8},{24,0},{1,25},{9,17},{17,9},{25,1},{2,26},{10... | collective-permute-start | bytes 589832 | tf_op jit(solution)/shard_map/ppermute | solution.py:533
  63.0 7.8 %collective-permute-start.2 = (bf16[128,384]{1,0:T(8,128)(2,1)S(1)}, bf16[128,384]{1,0:T(8,128)(2,1)S(1)}, u32[]{:S(2)}, u32[]{:S(2)}) collective-permute-start(bf16[128,384]{1,0:T(8,128)(2,1)S(1)} %get-tuple-element.43), channel_id=1, source_target_pairs={{0,16},{8,24},{16,0},{24,8},{1,17},{9,25},{17,1},{25,9},{2,18},{10... | collective-permute-start | bytes 294920 | tf_op jit(solution)/shard_map/ppermute | solution.py:533
  63.5 7.7 %collective-permute-start.3 = (bf16[128,384]{1,0:T(8,128)(2,1)S(1)}, bf16[128,384]{1,0:T(8,128)(2,1)S(1)}, u32[]{:S(2)}, u32[]{:S(2)}) collective-permute-start(bf16[128,384]{1,0:T(8,128)(2,1)S(1)} %get-tuple-element.44), channel_id=1, source_target_pairs={{0,24},{8,16},{16,8},{24,0},{1,25},{9,17},{17,9},{25,1},{2,26},{10... | collective-permute-start | bytes 294920 | tf_op jit(solution)/shard_map/ppermute | solution.py:533
  65.0 9.3 %collective-permute-start.8 = (bf16[256,384]{1,0:T(8,128)(2,1)S(1)}, bf16[256,384]{1,0:T(8,128)(2,1)S(1)}, u32[]{:S(2)}, u32[]{:S(2)}) collective-permute-start(bf16[256,384]{1,0:T(8,128)(2,1)S(1)} %get-tuple-element.46), channel_id=1, source_target_pairs={{0,8},{8,0},{16,24},{24,16},{1,9},{9,1},{17,25},{25,17},{2,10},{10... | collective-permute-start | bytes 589832 | tf_op jit(solution)/shard_map/ppermute | solution.py:533
  66.5 12.0 %copy-start = (s32[4]{0:T(128)S(1)}, s32[4]{0:T(128)}, u32[]{:S(2)}) copy-start(s32[4]{0:T(128)} %docs_ref.3) | copy-start | bytes 52
  66.5 9.1 %collective-permute-start.9 = (bf16[256,384]{1,0:T(8,128)(2,1)S(1)}, bf16[256,384]{1,0:T(8,128)(2,1)S(1)}, u32[]{:S(2)}, u32[]{:S(2)}) collective-permute-start(bf16[256,384]{1,0:T(8,128)(2,1)S(1)} %get-tuple-element.47), channel_id=1, source_target_pairs={{0,16},{8,24},{16,0},{24,8},{1,17},{9,25},{17,1},{25,9},{2,18},{10... | collective-permute-start | bytes 589832 | tf_op jit(solution)/shard_map/ppermute | solution.py:533
  70.8 5.7 %collective-permute-start.15 = (bf16[128,384]{1,0:T(8,128)(2,1)S(1)}, bf16[128,384]{1,0:T(8,128)(2,1)S(1)}, u32[]{:S(2)}, u32[]{:S(2)}) collective-permute-start(bf16[128,384]{1,0:T(8,128)(2,1)S(1)} %get-tuple-element.50), channel_id=1, source_target_pairs={{0,8},{8,0},{16,24},{24,16},{1,9},{9,1},{17,25},{25,17},{2,10},{10... | collective-permute-start | bytes 294920 | tf_op jit(solution)/shard_map/ppermute | solution.py:533
  71.2 7.2 %collective-permute-start.16 = (bf16[128,384]{1,0:T(8,128)(2,1)S(1)}, bf16[128,384]{1,0:T(8,128)(2,1)S(1)}, u32[]{:S(2)}, u32[]{:S(2)}) collective-permute-start(bf16[128,384]{1,0:T(8,128)(2,1)S(1)} %get-tuple-element.51), channel_id=1, source_target_pairs={{0,16},{8,24},{16,0},{24,8},{1,17},{9,25},{17,1},{25,9},{2,18},{10... | collective-permute-start | bytes 294920 | tf_op jit(solution)/shard_map/ppermute | solution.py:533
  71.9 6.6 %collective-permute-start.17 = (bf16[128,384]{1,0:T(8,128)(2,1)S(1)}, bf16[128,384]{1,0:T(8,128)(2,1)S(1)}, u32[]{:S(2)}, u32[]{:S(2)}) collective-permute-start(bf16[128,384]{1,0:T(8,128)(2,1)S(1)} %get-tuple-element.52), channel_id=1, source_target_pairs={{0,24},{8,16},{16,8},{24,0},{1,25},{9,17},{17,9},{25,1},{2,26},{10... | collective-permute-start | bytes 294920 | tf_op jit(solution)/shard_map/ppermute | solution.py:533
  86.4 4.7 %collective-permute-start.22 = (bf16[256,128]{1,0:T(8,128)(2,1)S(1)}, bf16[256,128]{1,0:T(8,128)(2,1)S(1)}, u32[]{:S(2)}, u32[]{:S(2)}) collective-permute-start(bf16[256,128]{1,0:T(8,128)(2,1)S(1)} %get-tuple-element.61), channel_id=1, source_target_pairs={{0,8},{8,0},{16,24},{24,16},{1,9},{9,1},{17,25},{25,17},{2,10},{10... | collective-permute-start | bytes 196616 | tf_op jit(solution)/shard_map/ppermute | solution.py:533
  87.1 4.3 %collective-permute-start.23 = (bf16[256,128]{1,0:T(8,128)(2,1)S(1)}, bf16[256,128]{1,0:T(8,128)(2,1)S(1)}, u32[]{:S(2)}, u32[]{:S(2)}) collective-permute-start(bf16[256,128]{1,0:T(8,128)(2,1)S(1)} %get-tuple-element.62), channel_id=1, source_target_pairs={{0,16},{8,24},{16,0},{24,8},{1,17},{9,25},{17,1},{25,9},{2,18},{10... | collective-permute-start | bytes 196616 | tf_op jit(solution)/shard_map/ppermute | solution.py:533
  88.4 5.2 %collective-permute-start.24 = (bf16[256,128]{1,0:T(8,128)(2,1)S(1)}, bf16[256,128]{1,0:T(8,128)(2,1)S(1)}, u32[]{:S(2)}, u32[]{:S(2)}) collective-permute-start(bf16[256,128]{1,0:T(8,128)(2,1)S(1)} %get-tuple-element.63), channel_id=1, source_target_pairs={{0,24},{8,16},{16,8},{24,0},{1,25},{9,17},{17,9},{25,1},{2,26},{10... | collective-permute-start | bytes 196616 | tf_op jit(solution)/shard_map/ppermute | solution.py:533
  94.8 19.0 %collective-permute-start.29 = (bf16[64,4096]{1,0:T(8,128)(2,1)S(1)}, bf16[64,4096]{1,0:T(8,128)(2,1)S(1)}, u32[]{:S(2)}, u32[]{:S(2)}) collective-permute-start(bf16[64,4096]{1,0:T(8,128)(2,1)S(1)} %get-tuple-element.72), channel_id=1, source_target_pairs={{0,1},{1,0},{2,3},{3,2},{4,5},{5,4},{6,7},{7,6},{8,9},{9,8},{10,11... | collective-permute-start | bytes 1572872 | tf_op jit(solution)/shard_map/ppermute | solution.py:528
  101.6 4.5 %collective-permute-start.18 = (bf16[256,128]{1,0:T(8,128)(2,1)S(1)}, bf16[256,128]{1,0:T(8,128)(2,1)S(1)}, u32[]{:S(2)}, u32[]{:S(2)}) collective-permute-start(bf16[256,128]{1,0:T(8,128)(2,1)S(1)} %get-tuple-element.54), channel_id=1, source_target_pairs={{0,8},{8,0},{16,24},{24,16},{1,9},{9,1},{17,25},{25,17},{2,10},{10... | collective-permute-start | bytes 196616 | tf_op jit(solution)/shard_map/ppermute | solution.py:533
  102.3 4.3 %collective-permute-start.19 = (bf16[256,128]{1,0:T(8,128)(2,1)S(1)}, bf16[256,128]{1,0:T(8,128)(2,1)S(1)}, u32[]{:S(2)}, u32[]{:S(2)}) collective-permute-start(bf16[256,128]{1,0:T(8,128)(2,1)S(1)} %get-tuple-element.55), channel_id=1, source_target_pairs={{0,16},{8,24},{16,0},{24,8},{1,17},{9,25},{17,1},{25,9},{2,18},{10... | collective-permute-start | bytes 196616 | tf_op jit(solution)/shard_map/ppermute | solution.py:533
  103.8 5.2 %collective-permute-start.20 = (bf16[256,128]{1,0:T(8,128)(2,1)S(1)}, bf16[256,128]{1,0:T(8,128)(2,1)S(1)}, u32[]{:S(2)}, u32[]{:S(2)}) collective-permute-start(bf16[256,128]{1,0:T(8,128)(2,1)S(1)} %get-tuple-element.56), channel_id=1, source_target_pairs={{0,24},{8,16},{16,8},{24,0},{1,25},{9,17},{17,9},{25,1},{2,26},{10... | collective-permute-start | bytes 196616 | tf_op jit(solution)/shard_map/ppermute | solution.py:533
  110.3 33.2 %collective-permute-start.21 = (bf16[64,4096]{1,0:T(8,128)(2,1)S(1)}, bf16[64,4096]{1,0:T(8,128)(2,1)S(1)}, u32[]{:S(2)}, u32[]{:S(2)}) collective-permute-start(bf16[64,4096]{1,0:T(8,128)(2,1)S(1)} %get-tuple-element.59), channel_id=1, source_target_pairs={{0,1},{1,0},{2,3},{3,2},{4,5},{5,4},{6,7},{7,6},{8,9},{9,8},{10,11... | collective-permute-start | bytes 1572872 | tf_op jit(solution)/shard_map/ppermute | solution.py:528
  111.9 8.8 %collective-permute-start.27 = (bf16[64,4096]{1,0:T(8,128)(2,1)S(1)}, bf16[64,4096]{1,0:T(8,128)(2,1)S(1)}, u32[]{:S(2)}, u32[]{:S(2)}) collective-permute-start(bf16[64,4096]{1,0:T(8,128)(2,1)S(1)} %get-tuple-element.69), channel_id=1, source_target_pairs={{0,1},{1,0},{2,3},{3,2},{4,5},{5,4},{6,7},{7,6},{8,9},{9,8},{10,11... | collective-permute-start | bytes 1572872 | tf_op jit(solution)/shard_map/ppermute | solution.py:528
  113.8 44.2 %copy-start.1 = (bf16[64,4096]{1,0:T(8,128)(2,1)S(1)}, bf16[64,4096]{1,0:T(8,128)(2,1)}, u32[]{:S(2)}) copy-start(bf16[64,4096]{1,0:T(8,128)(2,1)} %tokens_ref.1) | copy-start | bytes 1572868
  113.8 4.7 %collective-permute-start.25 = (bf16[64,4096]{1,0:T(8,128)(2,1)S(1)}, bf16[64,4096]{1,0:T(8,128)(2,1)S(1)}, u32[]{:S(2)}, u32[]{:S(2)}) collective-permute-start(bf16[64,4096]{1,0:T(8,128)(2,1)S(1)} %get-tuple-element.66), channel_id=1, source_target_pairs={{0,1},{1,0},{2,3},{3,2},{4,5},{5,4},{6,7},{7,6},{8,9},{9,8},{10,11... | collective-permute-start | bytes 1572872 | tf_op jit(solution)/shard_map/ppermute | solution.py:528
  114.0 38.8 %collective-permute-start.30 = (bf16[64,4096]{1,0:T(8,128)(2,1)S(1)}, bf16[64,4096]{1,0:T(8,128)(2,1)S(1)}, u32[]{:S(2)}, u32[]{:S(2)}) collective-permute-start(bf16[64,4096]{1,0:T(8,128)(2,1)S(1)} %add_convert_fusion.2), channel_id=1, source_target_pairs={{6,2},{7,3},{0,4},{1,5},{14,10},{15,11},{8,12},{9,13},{22,18},{23,... | collective-permute-start | bytes 1572872 | tf_op jit(solution)/shard_map/ppermute | solution.py:525
  118.6 23.4 %collective-permute-start.31 = (bf16[64,4096]{1,0:T(8,128)(2,1)S(1)}, bf16[64,4096]{1,0:T(8,128)(2,1)S(1)}, u32[]{:S(2)}, u32[]{:S(2)}) collective-permute-start(bf16[64,4096]{1,0:T(8,128)(2,1)S(1)} %add_convert_fusion.4), channel_id=1, source_target_pairs={{6,4},{7,5},{0,2},{1,3},{14,12},{15,13},{8,10},{9,11},{22,20},{23,... | collective-permute-start | bytes 1572872 | tf_op jit(solution)/shard_map/ppermute | solution.py:525
  119.9 32.8 %collective-permute-start.26 = (bf16[64,4096]{1,0:T(8,128)(2,1)S(1)}, bf16[64,4096]{1,0:T(8,128)(2,1)S(1)}, u32[]{:S(2)}, u32[]{:S(2)}) collective-permute-start(bf16[64,4096]{1,0:T(8,128)(2,1)S(1)} %add_convert_fusion.4), channel_id=1, source_target_pairs={{2,4},{3,5},{4,2},{5,3},{10,12},{11,13},{12,10},{13,11},{18,20},{1... | collective-permute-start | bytes 1572872 | tf_op jit(solution)/shard_map/ppermute | solution.py:525
  120.8 32.0 %collective-permute-start.28 = (bf16[64,4096]{1,0:T(8,128)(2,1)S(1)}, bf16[64,4096]{1,0:T(8,128)(2,1)S(1)}, u32[]{:S(2)}, u32[]{:S(2)}) collective-permute-start(bf16[64,4096]{1,0:T(8,128)(2,1)S(1)} %add_convert_fusion.3), channel_id=1, source_target_pairs={{0,2},{1,3},{2,0},{3,1},{4,6},{5,7},{6,4},{7,5},{8,10},{9,11},{10,... | collective-permute-start | bytes 1572872 | tf_op jit(solution)/shard_map/ppermute | solution.py:525
  142.1 15.8 %collective-permute-start.32 = (bf16[64,4096]{1,0:T(8,128)(2,1)S(1)}, bf16[64,4096]{1,0:T(8,128)(2,1)S(1)}, u32[]{:S(2)}, u32[]{:S(2)}) collective-permute-start(bf16[64,4096]{1,0:T(8,128)(2,1)S(1)} %add_convert_fusion.1), channel_id=1, source_target_pairs={{4,0},{5,1},{2,6},{3,7},{12,8},{13,9},{10,14},{11,15},{20,16},{21,... | collective-permute-start | bytes 1572872 | tf_op jit(solution)/shard_map/ppermute | solution.py:525

commit v2 on v1

--- a/solution.py
+++ b/solution.py
@@ -116,6 +116,10 @@
 VMEM = pl.BlockSpec(memory_space=pltpu.VMEM)
 HBM = pl.BlockSpec(memory_space=pltpu.HBM)
 PIECES = 4
+
+
+def is_middle(info, chips):
+    return (info[1] > 0) & (info[1] < chips - 1)
 
 
 def mode_of(info, slot):
@@ -187,29 +191,38 @@
     )(ids, modality, tokens, norm_gain)
 
 
-def fetch_weights(info, qkv_weight, slot):
-    _, width, cols = qkv_weight.shape
-    pairs = 2
-    pair_cols = cols // pairs
-    piece = width // PIECES
-
-    def kernel(info_ref, qkv_ref, late_ref, late_sems):
-        mode = mode_of(info_ref, slot)
+def weight_copies(info_ref, weight_ref, buffer_ref, sems, slot):
+    pairs, pieces, piece, pair_cols = buffer_ref.shape
+    copies = {}
+    for p in range(pairs):
+        first = jnp.bitwise_xor(info_ref[0] // 2, p) * pair_cols
+        for k in range(pieces):
+            copies[p, k] = pltpu.make_async_copy(
+                weight_ref.at[
+                    mode_of(info_ref, slot),
+                    pl.ds(k * piece, piece),
+                    pl.ds(pl.multiple_of(first, 128), pair_cols),
+                ],
+                buffer_ref.at[p, k],
+                sems.at[p, k],
+            )
+    return copies
+
+
+def weight_shape(weight):
+    width, cols = weight.shape[1:]
+    return (2, PIECES, width // PIECES, cols // 2)
+
+
+def fetch_weights(info, qkv_weight, slots):
+    shape = weight_shape(qkv_weight)
+    count = len(slots)
+
+    def kernel(info_ref, qkv_ref, *refs):
+        sems = refs[count]
         copies = []
-        for p in range(pairs):
-            first = jnp.bitwise_xor(info_ref[0] // 2, p) * pair_cols
-            for k in range(PIECES):
-                copies.append(
-                    pltpu.make_async_copy(
-                        qkv_ref.at[
-                            mode,
-                            pl.ds(k * piece, piece),
-                            pl.ds(pl.multiple_of(first, 128), pair_cols),
-                        ],
-                        late_ref.at[p, k],
-                        late_sems.at[p, k],
-                    )
-                )
+        for i, slot in enumerate(slots):
+            copies += weight_copies(info_ref, qkv_ref, refs[i], sems.at[i], slot).values()
         for copy in copies:
             copy.start()
         for copy in copies:
@@ -217,29 +230,46 @@
 
     return pl.pallas_call(
         kernel,
-        out_shape=pltpu.VMEM((pairs, PIECES, piece, pair_cols), jnp.bfloat16),
+        out_shape=[pltpu.VMEM(shape, jnp.bfloat16)] * count,
         in_specs=[SMEM, HBM],
-        out_specs=VMEM,
-        scratch_shapes=[pltpu.SemaphoreType.DMA((pairs, PIECES))],
+        out_specs=[VMEM] * count,
+        scratch_shapes=[pltpu.SemaphoreType.DMA((count, *shape[:2]))],
         compiler_params=params(1),
         cost_estimate=pl.CostEstimate(
-            flops=3_000_000_000, bytes_accessed=12 << 20, transcendentals=0
+            flops=6_000_000_000, bytes_accessed=25 << 20, transcendentals=0
         ),
         name="fetch_weights",
     )(info, qkv_weight)
 
 
 class Prefetch:
-    def __init__(self, out_weight, slots):
-        self.weight, self.slots = out_weight, slots
-        self.shapes = [pltpu.VMEM(out_weight.shape[1:], jnp.bfloat16)] * len(slots)
-        self.scratch = pltpu.SemaphoreType.DMA((len(slots),))
+    def __init__(self, out_weight, turns, chips):
+        self.weight, self.turns, self.chips = out_weight, turns, chips
+        self.shapes = [pltpu.VMEM(out_weight.shape[1:], jnp.bfloat16)] * len(turns)
+        self.scratch = pltpu.SemaphoreType.DMA((len(turns),))
 
     def copies(self, info_ref, weight_ref, kept_refs, sems):
+        middle = is_middle(info_ref, self.chips)
         return [
-            pltpu.make_async_copy(weight_ref.at[mode_of(info_ref, slot)], kept_refs[i], sems.at[i])
-            for i, slot in enumerate(self.slots)
+            pltpu.make_async_copy(
+                weight_ref.at[mode_of(info_ref, jnp.where(middle, turn[1], turn[0]))],
+                kept_refs[i],
+                sems.at[i],
+            )
+            for i, turn in enumerate(self.turns)
         ]
+
+    def start(self, *refs):
+        @pl.when(refs[0][1] >= 0)
+        def _():
+            for copy in self.copies(*refs):
+                copy.start()
+
+    def wait(self, *refs):
+        @pl.when(refs[0][1] >= 0)
+        def _():
+            for copy in self.copies(*refs):
+                copy.wait()
 
 
 def store_pair(info_ref, outs, rows, p, result):
@@ -251,59 +281,48 @@
         outs[2 * p + e][rows, :] = jnp.where(odd, last, first)
 
 
-def project_slots(info, parts, weight, slots):
+def project_slots(info, parts, weight, slots, ready=()):
     half, width = parts[0][0].shape
     block = 2 * half
     cols = 3 * HDIM
     heads = weight.shape[2] // cols
-    pairs = 2
-    pair_cols = weight.shape[2] // pairs
-    piece = width // PIECES
-    count = len(slots)
+    shape = weight_shape(weight)
+    pairs, pieces, piece, _ = shape
+    count, given = len(slots), len(ready)
 
     def kernel(info_ref, *refs):
-        ins = refs[: 2 * count]
-        weight_ref = refs[2 * count]
-        outs = refs[2 * count + 1 : 2 * count + 1 + heads]
-        buffer_ref, sems = refs[2 * count + 1 + heads :]
-
-        def copy_of(n, p, k):
-            first = jnp.bitwise_xor(info_ref[0] // 2, p) * pair_cols
-            return pltpu.make_async_copy(
-                weight_ref.at[
-                    mode_of(info_ref, slots[n]),
-                    pl.ds(k * piece, piece),
-                    pl.ds(pl.multiple_of(first, 128), pair_cols),
-                ],
-                buffer_ref.at[p, k],
-                sems.at[p, k],
-            )
-
-        for p in range(pairs):
-            for k in range(PIECES):
-                copy_of(0, p, k).start()
+        ins, refs = refs[: 2 * count], refs[2 * count :]
+        ready_refs, weight_ref, refs = refs[:given], refs[given], refs[given + 1 :]
+        outs, (buffer_ref, sems) = refs[:heads], refs[heads:]
+        fetched = [
+            weight_copies(info_ref, weight_ref, buffer_ref, sems, slot) for slot in slots[given:]
+        ]
+        for copy in fetched[0].values():
+            copy.start()
         for n in range(count):
+            source_ref = ready_refs[n] if n < given else buffer_ref
             for p in range(pairs):
                 result = None
-                for k in range(PIECES):
-                    copy_of(n, p, k).wait()
+                for k in range(pieces):
+                    if n >= given:
+                        fetched[n - given][p, k].wait()
                     rows = jnp.concatenate(
                         [ins[2 * n + i][:, k * piece : (k + 1) * piece] for i in range(2)], axis=0
                     )
-                    part = jnp.dot(rows, buffer_ref[p, k], preferred_element_type=jnp.float32)
+                    part = jnp.dot(rows, source_ref[p, k], preferred_element_type=jnp.float32)
                     result = part if result is None else result + part
-                    if n + 1 < count:
-                        copy_of(n + 1, p, k).start()
+                    if given <= n < count - 1:
+                        fetched[n - given + 1][p, k].start()
                 store_pair(info_ref, outs, pl.ds(n * block, block), p, result)
 
     return pl.pallas_call(
         kernel,
         out_shape=[pltpu.VMEM((count * block, cols), jnp.bfloat16)] * heads,
-        in_specs=[SMEM] + [VMEM] * (2 * count) + [HBM],
+        in_specs=[SMEM] + [VMEM] * (2 * count + given) + [HBM],
         out_specs=[VMEM] * heads,
         scratch_shapes=[
-            pltpu.VMEM((pairs, PIECES, piece, pair_cols), jnp.bfloat16),
-            pltpu.SemaphoreType.DMA((pairs, PIECES)),
+            pltpu.VMEM(shape, jnp.bfloat16),
+            pltpu.SemaphoreType.DMA(shape[:2]),
         ],
         compiler_params=params(16),
         cost_estimate=pl.CostEstimate(
@@ -312,7 +331,7 @@
             transcendentals=0,
         ),
         name="project_slots",
-    )(info, *[piece for pair in parts for piece in pair], weight)
+    )(info, *[piece for pair in parts for piece in pair], *ready, weight)
 
 
 def project_late(info, inner, relayed, weight, cols, chips, prefetch):
@@ -321,16 +340,13 @@
     pairs, pieces, piece, pair_cols = weight.shape
     heads = pairs * pair_cols // cols
 
-    kept = len(prefetch.slots)
+    kept = len(prefetch.turns)
 
     def kernel(info_ref, inner_own, inner_partner, relayed_own, relayed_partner, weight_ref, *refs):
         next_ref, outs, kept_refs = refs[0], refs[1 : 1 + heads], refs[1 + heads : 1 + heads + kept]
         rows_ref, sems = refs[1 + heads + kept :]
-        copies = prefetch.copies(info_ref, next_ref, kept_refs, sems)
-        for copy in copies:
-            copy.start()
-        chip = info_ref[1]
-        middle = (chip > 0) & (chip < chips - 1)
+        prefetch.start(info_ref, next_ref, kept_refs, sems)
+        middle = is_middle(info_ref, chips)
 
         @pl.when(middle)
         def _():
@@ -352,8 +368,7 @@
                 )
                 result = part if result is None else result + part
             store_pair(info_ref, outs, pl.ds(0, block), p, result)
-        for copy in copies:
-            copy.wait()
+        prefetch.wait(info_ref, next_ref, kept_refs, sems)
 
     return pl.pallas_call(
         kernel,
@@ -371,7 +386,7 @@
     )(info, *inner, *relayed, weight, prefetch.weight)
 
 
-def attend_slots(info, doc_lengths, sets, query_slots, chips, prefetch):
+def attend_slots(info, doc_lengths, sets, turns, chips, prefetch):
     count = len(sets[0][1])
     block = sets[0][1][0].shape[0] // len(sets[0][0])
     total = count * chips * block
@@ -379,15 +394,14 @@
     scale = 1.0 / math.sqrt(HDIM)
     docs = doc_lengths.shape[0]
 
-    kept = len(prefetch.slots)
+    kept = len(prefetch.turns)
 
     def kernel(info_ref, docs_ref, *refs):
         ins, refs = refs[: len(sets) * count], refs[len(sets) * count :]
         next_ref, outs, kept_refs = refs[0], refs[1 : 1 + count], refs[1 + count : 1 + count + kept]
         keys_ref, values_ref, sems = refs[1 + count + kept :]
-        copies = prefetch.copies(info_ref, next_ref, kept_refs, sems)
-        for copy in copies:
-            copy.start()
+        prefetch.start(info_ref, next_ref, kept_refs, sems)
+        middle = is_middle(info_ref, chips)
         mu, chip, own_first = info_ref[0], info_ref[1], info_ref[2] * (block // 2)
 
         def slot_rows(d, slot, part):
@@ -414,7 +428,8 @@
         key_in_block = key_iota % block + own_first
         key_in_block = jnp.where(key_in_block >= block, key_in_block - block, key_in_block)
         key_place = (key_iota // block) * block + key_in_block
-        for n, slot in enumerate(query_slots):
+        for n, turn in enumerate(turns):
+            slot = jnp.where(middle, turn[1], turn[0])
             for d in range(count):
                 index = jnp.bitwise_xor(mu, d) * chips + jnp.bitwise_xor(chip, slot)
                 first_row = index * block
@@ -429,8 +444,11 @@
                     row_first = jnp.where(row_pos >= e, e, row_first)
                 key_pos = key_place + start
                 allowed = (key_pos <= row_pos) & (key_pos >= row_first)
+                query = slot_rows(d, turn[0], 0)
+                if turn[1] != turn[0]:
+                    query = jnp.where(middle, slot_rows(d, turn[1], 0), query)
                 scores = lax.dot_general(
-                    slot_rows(d, slot, 0),
+                    query,
                     keys_ref[pl.ds(start, window), :],
                     (((1,), (1,)), ((), ())),
                     preferred_element_type=jnp.float32,
@@ -445,13 +463,12 @@
                     preferred_element_type=jnp.float32,
                 )
                 outs[d][n * block : (n + 1) * block, :] = (summed / totals).astype(jnp.bfloat16)
-        for copy in copies:
-            copy.wait()
-
-    n_queries = len(query_slots) * count
+        prefetch.wait(info_ref, next_ref, kept_refs, sems)
+
+    n_queries = len(turns) * count
     return pl.pallas_call(
         kernel,
-        out_shape=[pltpu.VMEM((len(query_slots) * block, HDIM), jnp.bfloat16)] * count
+        out_shape=[pltpu.VMEM((len(turns) * block, HDIM), jnp.bfloat16)] * count
         + prefetch.shapes,
         in_specs=[SMEM, SMEM] + [VMEM] * (len(sets) * count) + [HBM],
         out_specs=[VMEM] * (count + kept),
@@ -470,33 +487,53 @@
     )(info, doc_lengths, *[piece for _, pieces in sets for piece in pieces], prefetch.weight)
 
 
-def output_rows(info, pieces, weight, slots, slot):
+def output_rows(info, pieces, weight, index, turns, slot=None):
     count = len(pieces)
-    block = pieces[0].shape[0] // len(slots)
+    block = pieces[0].shape[0] // turns
     half = block // 2
-    at = slots.index(slot) * block
-    depth, width = weight.shape
+    at = index * block
+    depth, width = weight.shape[-2:]
     tile = min(1024, width)
+    firsts = range(0, width, tile)
 
     def kernel(info_ref, *refs):
         ins = refs[:count]
-        weight_ref, own_ref, partner_ref, heads_ref = refs[count:]
+        weight_ref, own_ref, partner_ref, heads_ref = refs[count : count + 4]
+        copies = []
+        if slot is not None:
+            buffer_ref, sems = refs[count + 4 :]
+            for i, first in enumerate(firsts):
+                part = weight_ref.at[mode_of(info_ref, slot), :, pl.ds(first, tile)]
+                copies.append(pltpu.make_async_copy(part, buffer_ref.at[i], sems.at[i]))
+            for copy in copies:
+                copy.start()
         for d in range(count):
             heads_ref[jnp.bitwise_xor(info_ref[0], d)] = ins[d][at : at + block, :]
         rows = jnp.concatenate([heads_ref[h] for h in range(count)], axis=1)
-        for first in range(0, width, tile):
+        for i, first in enumerate(firsts):
             cols = slice(first, first + tile)
-            result = jnp.dot(rows, weight_ref[:, cols], preferred_element_type=jnp.float32)
+            if slot is None:
+                part = weight_ref[:, cols]
+            else:
+                copies[i].wait()
+                part = buffer_ref[i]
+            result = jnp.dot(rows, part, preferred_element_type=jnp.float32)
             result = result.astype(jnp.bfloat16)
             own_ref[:, cols] = result[:half]
             partner_ref[:, cols] = result[half:]
 
+    streamed = []
+    if slot is not None:
+        streamed = [
+            pltpu.VMEM((len(firsts), depth, tile), jnp.bfloat16),
+            pltpu.SemaphoreType.DMA((len(firsts),)),
+        ]
     return pl.pallas_call(
         kernel,
         out_shape=[pltpu.VMEM((half, width), jnp.bfloat16)] * 2,
-        in_specs=[SMEM] + [VMEM] * (count + 1),
+        in_specs=[SMEM] + [VMEM] * count + [VMEM if slot is None else HBM],
         out_specs=[VMEM] * 2,
-        scratch_shapes=[pltpu.VMEM((count, block, HDIM), jnp.bfloat16)],
+        scratch_shapes=[pltpu.VMEM((count, block, HDIM), jnp.bfloat16)] + streamed,
         compiler_params=params(8),
         cost_estimate=pl.CostEstimate(
             flops=2 * block * depth * width,
@@ -520,6 +557,7 @@
     ids = jnp.stack([mu, seq // 2, seq % 2])
     qkv_weight = pltpu.with_memory_space_constraint(qkv_weight, pltpu.HBM)
     out_weight = pltpu.with_memory_space_constraint(out_weight, pltpu.HBM)
+    alone = lax.optimization_barrier
 
     def along(value, pairs):
         return lax.ppermute(value, "seq", chip_pairs(pairs))
@@ -547,54 +585,71 @@
     two = along(normed, [(i, i ^ 2) for i in range(chips)])
     one = along(normed, [(i, i ^ 1) for i in range(chips)])
     inner = along(normed, [(1, 2), (2, 1)])
-    relayed = along(two, [(2, 3), (1, 0)])
+    relayed = along(two, [(i, i ^ 1) for i in range(chips)])
     own_pair = (normed, swap(normed))
     two_pair = (two, swap(two))
     one_pair = (one, swap(one))
     inner_pair = (inner, swap(inner))
     relayed_pair = (relayed, swap(relayed))
+    turn_a, turn_b, turn_c, turn_d = (3, 1), (2, 3), (1, 2), (0, 0)
 
     own = project_slots(info, [own_pair], qkv_weight, (0,))
     own = exchange(own)
-    late_weight = fetch_weights(info, qkv_weight, 3)
-    mid = project_slots(info, [two_pair, one_pair], qkv_weight, (2, 1))
+    late_weight, two_weight = fetch_weights(info, qkv_weight, (3, 2))
+    mid = project_slots(
+        info, [two_pair, one_pair], qkv_weight, (2, 1), ready=(two_weight,)
+    )
     mid = exchange(mid)
-    kept = {}
-    *late, kept[3] = project_late(
+    *late, kept_a = project_late(
         info,
         inner_pair,
         relayed_pair,
         late_weight,
         3 * HDIM,
         chips,
-        Prefetch(out_weight, (3,)),
+        Prefetch(out_weight, (turn_a,), chips),
     )
     late = exchange(late)
     sets = (((0,), own), ((2, 1), mid), ((3,), late))
 
-    def finish(pieces, slots, slot):
-        own_share, partner_share = output_rows(info, pieces, kept[slot], slots, slot)
+    def finish(pieces, kept, index, slot=None):
+        own_share, partner_share = output_rows(info, pieces, kept, index, 2, slot)
         return own_share, swap(partner_share)
 
-    *first, kept[2], kept[1] = attend_slots(
-        info, doc_lengths, sets, (3, 2), chips, Prefetch(out_weight, (2, 1))
+    *first, kept_b = attend_slots(
+        info,
+        doc_lengths,
+        sets,
+        (turn_a, turn_b),
+        chips,
+        Prefetch(out_weight, (turn_b,), chips),
     )
     first = exchange(first)
-    sum3 = add(*finish(first, (3, 2), 3))
-    from_end = along(sum3, [(3, 2), (0, 1)])
-    from_inner = along(sum3, [(1, 2), (2, 1)])
-    sum2 = add(*finish(first, (3, 2), 2))
-    from_two_end = along(sum2, [(3, 1), (0, 2)])
-    *rest, kept[0] = attend_slots(
-        info, doc_lengths, sets, (1, 0), chips, Prefetch(out_weight, (0,))
+    sum_a = alone(add(*finish(first, kept_a, 0)))
+    own_b, partner_b = finish(first, kept_b, 1)
+    own_b, sum_a = alone((own_b, sum_a))
+    from_one = along(sum_a, [(i, i ^ 1) for i in range(chips)])
+    sum_b = alone(add(own_b, partner_b))
+    from_inner = along(sum_b, [(1, 2), (2, 1)])
+    *rest, kept_c = attend_slots(
+        info,
+        doc_lengths,
+        sets,
+        (turn_c, turn_d),
+        chips,
+        Prefetch(out_weight, (turn_c,), chips),
     )
     rest = exchange(rest)
-    both2 = add(lax.optimization_barrier(sum2), from_end)
-    from_two_inner = along(both2, [(2, 0), (1, 3)])
-    sum1 = add(*finish(rest, (1, 0), 1))
-    from_one = along(sum1, [(i, i ^ 1) for i in range(chips)])
-    shares0 = finish(rest, (1, 0), 0)
-    return add(tokens, *shares0, from_inner, from_one, from_two_end, from_two_inner)
+    sum_c = alone(add(*finish(rest, kept_c, 0)))
+    chip = seq // 2
+    middle = (chip > 0) & (chip < chips - 1)
+    relay_sum = jnp.where(middle, add(sum_c, from_one), sum_b)
+    from_two = along(relay_sum, [(i, i ^ 2) for i in range(chips)])
+    from_end = along(sum_c, [(i, i ^ 1) for i in range(chips)])
+    shares_d = finish(rest, out_weight, 1, slot=0)
+    near = jnp.where(middle, from_inner, from_one)
+    far = jnp.where(middle, from_end, jnp.zeros_like(from_end))
+    return add(tokens, *shares_d, near, from_two, far)
 
 
 def solution(mesh):

time: 160 us -> 171 us (1.069)
  waiting for transfers between devices: 72.5 us -> 81.2 us
  local copies, waits for them, and re-layouts: 0.01 us -> 6.4 us
  starting transfers between devices: 37.2 us -> 32 us
    ppermute x9 -> x8, waiting for transfers between devices: 59.9 us -> 68.5 us  [along(): return lax.ppermute(value, 'seq', chip_pairs(pairs))]
    unnamed x4 -> x12, local copies, waits for them, and re-layouts: 0.01 us -> 6.4 us
    ppermute x9 -> x8, starting transfers between devices: 17.1 us -> 12.7 us  [along(): return lax.ppermute(value, 'seq', chip_pairs(pairs))]
    pallas_call x2, Pallas kernels: 16.7 us -> 14.3 us  [project_slots(): pl.pallas_call(kernel, out_shape=[pltpu.VMEM((count * block, cols), jnp.b...]
    pallas_call x3, Pallas kernels: 19.8 us -> 22.1 us  [the longest x2 13.2 us: attend_slots(): pl.pallas_call(kernel, out_shape=[pltpu.VMEM((len(turns) * block, HDIM),...]
  transfers between devices with their start and end apart: 33 -> 32, of which waited for: 16 -> 11; matrix products, arithmetic and copies ran while one was open for 0% -> 0% of each run, Pallas kernels for 22% -> 22%
where the time goes in v2:
time: 171 us
  waiting for transfers between devices  81.2 us (47%)
  Pallas kernels  48.8 us (29%)
  starting transfers between devices  32 us (19%)
  local copies, waits for them, and re-layouts  6.4 us (4%)
  other arithmetic  2.01 us (1%)
    ppermute x8, waiting for transfers between devices, along(): return lax.ppermute(value, 'seq', chip_pairs(pairs))  68.5 us
    ppermute x15, starting transfers between devices, exchange(): lax.ppermute(pieces[d], 'mod', [(i, i ^ d) for i in range(mod_count)])  17.6 us
    pallas_call x2, Pallas kernels, project_slots(): pl.pallas_call(kernel, out_shape=[pltpu.VMEM((count * block, cols), jnp.b...  14.3 us
    pallas_call x2, Pallas kernels, attend_slots(): pl.pallas_call(kernel, out_shape=[pltpu.VMEM((len(turns) * block, HDIM),...  13.2 us
    ppermute x15, waiting for transfers between devices, exchange(): lax.ppermute(pieces[d], 'mod', [(i, i ^ d) for i in range(mod_count)])  12.7 us
    ppermute x8, starting transfers between devices, along(): return lax.ppermute(value, 'seq', chip_pairs(pairs))  12.7 us
    pallas_call x1, Pallas kernels, fetch_weights(): pl.pallas_call(kernel, out_shape=[pltpu.VMEM(shape, jnp.bfloat16)] * coun...  8.91 us
    pallas_call x4, Pallas kernels, output_rows(): pl.pallas_call(kernel, out_shape=[pltpu.VMEM((half, width), jnp.bfloat16)...  6.95 us
  transfers between devices with their start and end apart: 32, of which 11 were waited for; matrix products, arithmetic and copies ran while one was open for 0% of the time, Pallas kernels for 22%

profile of v2, /device:TPU:0, one launch (start us, length us, event | category | flops | bytes accessed | tf_op | source)
XLA Modules:
  0.0 170.7 jit_solution(14888933051428179808)
XLA Ops:
  0.0 0.1 pad_add_fusion.ids_ref
  0.1 2.7 %norm_rows.1 = (bf16[64,4096]{1,0:T(8,128)(2,1)S(1)}, s32[7]{0:T(128)S(1)}) custom-call(s32[3]{0:T(128)S(1)} %pad_add_fusion.ids_ref, s32[16]{0:T(128)} %modality_ref.1, bf16[64,4096]{1,0:T(8,128)(2,1)} %tokens_ref.1, f32[3,4096]{1,0:T(4,128)} %gain_ref.1), custom_call_target="tpu_custom_call" | custom-call | flops 4000000 | bytes 1048576 | tf_op jit(solution)/shard_map/norm_rows/pallas_call | solution.py:173
  2.7 4.1 %collective-permute-start.4 = (bf16[64,4096]{1,0:T(8,128)(2,1)S(1)}, bf16[64,4096]{1,0:T(8,128)(2,1)S(1)}, u32[]{:S(2)}, u32[]{:S(2)}) collective-permute-start(bf16[64,4096]{1,0:T(8,128)(2,1)S(1)} %get-tuple-element.43.refs_0_), channel_id=1, source_target_pairs={{0,4},{1,5},{2,6},{3,7},{4,0},{5,1},{6,2},{7,3},{8,12},{9,13},{10,... | collective-permute-start | bytes 1572872 | tf_op jit(solution)/shard_map/ppermute | solution.py:563
  6.9 1.6 collective-permute-start.6
  8.5 0.7 collective-permute-start.11
  9.1 21.8 %collective-permute-done.4.refs_0_ = bf16[64,4096]{1,0:T(8,128)(2,1)S(1)} collective-permute-done((bf16[64,4096]{1,0:T(8,128)(2,1)S(1)}, bf16[64,4096]{1,0:T(8,128)(2,1)S(1)}, u32[]{:S(2)}, u32[]{:S(2)}) %collective-permute-start.4) | collective-permute-done | bytes 524320 | tf_op jit(solution)/shard_map/ppermute | solution.py:563
  30.9 0.0 collective-permute-start.13
  30.9 0.5 collective-permute-start.5
  31.4 0.0 collective-permute-start.7
  31.5 0.0 collective-permute-done.11.inner_own
  31.5 0.5 collective-permute-start.12
  32.0 11.2 %collective-permute-done.13.relayed_own = bf16[64,4096]{1,0:T(8,128)(2,1)S(1)} collective-permute-done((bf16[64,4096]{1,0:T(8,128)(2,1)S(1)}, bf16[64,4096]{1,0:T(8,128)(2,1)S(1)}, u32[]{:S(2)}, u32[]{:S(2)}) %collective-permute-start.13) | collective-permute-done | bytes 524320 | tf_op jit(solution)/shard_map/ppermute | solution.py:563
  43.2 0.0 collective-permute-start.14
  43.2 8.9 %fetch_weights.1 = (bf16[2,4,1024,768]{3,2,1,0:T(8,128)(2,1)S(1)}, bf16[2,4,1024,768]{3,2,1,0:T(8,128)(2,1)S(1)}) custom-call(s32[7]{0:T(128)S(1)} %get-tuple-element.42.info_ref, bf16[3,4096,1536]{2,1,0:T(8,128)(2,1)} %refs_5_.1), custom_call_target="tpu_custom_call" | custom-call | flops 6000000000 | bytes 26214400 | tf_op jit(solution)/shard_map/fetch_weights/pallas_call | solution.py:231
  52.1 6.3 %project_slots.2 = (bf16[128,384]{1,0:T(8,128)(2,1)S(1)}, bf16[128,384]{1,0:T(8,128)(2,1)S(1)}, bf16[128,384]{1,0:T(8,128)(2,1)S(1)}, bf16[128,384]{1,0:T(8,128)(2,1)S(1)}) custom-call(s32[7]{0:T(128)S(1)} %get-tuple-element.42.info_ref, bf16[64,4096]{1,0:T(8,128)(2,1)S(1)} %get-tuple-element.43.refs_0_, bf16[64,4096]{1,0:T(8,128)(2,1)S(1)} %collective-permute-done.refs_1_, ...), custom_call_target="tpu_custom_call" | custom-call | flops 1610612736 | bytes 12582912 | tf_op jit(solution)/shard_map/project_slots/pallas_call | solution.py:318
  58.4 1.3 collective-permute-start.1
  59.8 0.0 collective-permute-done.5.refs_1_
  59.8 8.0 %project_slots.3 = (bf16[256,384]{1,0:T(8,128)(2,1)S(1)}, bf16[256,384]{1,0:T(8,128)(2,1)S(1)}, bf16[256,384]{1,0:T(8,128)(2,1)S(1)}, bf16[256,384]{1,0:T(8,128)(2,1)S(1)}) custom-call(s32[7]{0:T(128)S(1)} %get-tuple-element.42.info_ref, bf16[64,4096]{1,0:T(8,128)(2,1)S(1)} %collective-permute-done.4.refs_0_, ...), custom_call_target="tpu_custom_call" | custom-call | flops 3221225472 | bytes 25165824 | tf_op jit(solution)/shard_map/project_slots/pallas_call | solution.py:318
  67.8 0.8 collective-permute-start.8
  68.6 1.4 collective-permute-start.2
  70.0 1.3 collective-permute-start.3
  71.4 1.5 collective-permute-start.9
  72.9 0.7 collective-permute-start.10
  73.6 2.7 %project_late.1 = (bf16[128,384]{1,0:T(8,128)(2,1)S(1)}, bf16[128,384]{1,0:T(8,128)(2,1)S(1)}, bf16[128,384]{1,0:T(8,128)(2,1)S(1)}, bf16[128,384]{1,0:T(8,128)(2,1)S(1)}, bf16[512,4096]{1,0:T(8,128)(2,1)S(1)}) custom-call(s32[7]{0:T(128)S(1)} %get-tuple-element.42.info_ref, bf16[64,4096]{1,0:T(8,128)(2,1)S(1)} %collective-permute-done.11.inner_own, ...), custom_call_target="tpu_custom_call" | custom-call | flops 1610612736 | bytes 12582912 | tf_op jit(solution)/shard_map/project_late/pallas_call | solution.py:373
  76.4 1.4 collective-permute-start.15
  77.7 1.1 collective-permute-done.3.refs_3_
  78.8 0.5 collective-permute-start.16
  79.3 1.6 collective-permute-start.17
  80.9 6.1 %collective-permute-done.9.refs_6_ = bf16[256,384]{1,0:T(8,128)(2,1)S(1)} collective-permute-done((bf16[256,384]{1,0:T(8,128)(2,1)S(1)}, bf16[256,384]{1,0:T(8,128)(2,1)S(1)}, u32[]{:S(2)}, u32[]{:S(2)}) %collective-permute-start.9) | collective-permute-done | bytes 196640 | tf_op jit(solution)/shard_map/ppermute | solution.py:571
  87.1 1.0 collective-permute-done.16.refs_10_
  88.1 6.6 %attend_slots.3 = (bf16[256,128]{1,0:T(8,128)(2,1)S(1)}, bf16[256,128]{1,0:T(8,128)(2,1)S(1)}, bf16[256,128]{1,0:T(8,128)(2,1)S(1)}, bf16[256,128]{1,0:T(8,128)(2,1)S(1)}, bf16[512,4096]{1,0:T(8,128)(2,1)S(1)}) custom-call(s32[7]{0:T(128)S(1)} %get-tuple-element.42.info_ref, s32[4]{0:T(128)S(1)} %copy-done.4, ...), custom_call_target="tpu_custom_call" | custom-call | flops 1207959552 | bytes 1572864 | tf_op jit(solution)/shard_map/attend_slots/pallas_call | solution.py:469
  94.7 1.3 collective-permute-start.22
  96.0 1.5 collective-permute-start.23
  97.5 0.8 collective-permute-start.24
  98.3 1.1 collective-permute-done.22.refs_1_
  99.4 1.5 collective-permute-done.23.refs_2_
  100.9 1.7 %collective-permute-done.24.refs_3_ = bf16[256,128]{1,0:T(8,128)(2,1)S(1)} collective-permute-done((bf16[256,128]{1,0:T(8,128)(2,1)S(1)}, bf16[256,128]{1,0:T(8,128)(2,1)S(1)}, u32[]{:S(2)}, u32[]{:S(2)}) %collective-permute-start.24) | collective-permute-done | bytes 65568 | tf_op jit(solution)/shard_map/ppermute | solution.py:571
  102.6 1.3 output_rows.6
  104.0 0.1 collective-permute-start.25
  104.0 6.6 %attend_slots.2 = (bf16[256,128]{1,0:T(8,128)(2,1)S(1)}, bf16[256,128]{1,0:T(8,128)(2,1)S(1)}, bf16[256,128]{1,0:T(8,128)(2,1)S(1)}, bf16[256,128]{1,0:T(8,128)(2,1)S(1)}, bf16[512,4096]{1,0:T(8,128)(2,1)S(1)}) custom-call(s32[7]{0:T(128)S(1)} %get-tuple-element.42.info_ref, s32[4]{0:T(128)S(1)} %copy-done.4, ...), custom_call_target="tpu_custom_call" | custom-call | flops 1207959552 | bytes 1572864 | tf_op jit(solution)/shard_map/attend_slots/pallas_call | solution.py:469
  110.7 2.0 %copy-done.2 = bf16[512,4096]{1,0:T(8,128)(2,1)} copy-done((bf16[512,4096]{1,0:T(8,128)(2,1)}, bf16[512,4096]{1,0:T(8,128)(2,1)S(1)}, u32[]{:S(2)}) %copy-start.2) | copy-done | bytes 4194328
  112.7 0.8 collective-permute-start.18
  113.5 0.5 collective-permute-start.19
  114.0 2.1 %collective-permute-start.20 = (bf16[256,128]{1,0:T(8,128)(2,1)S(1)}, bf16[256,128]{1,0:T(8,128)(2,1)S(1)}, u32[]{:S(2)}, u32[]{:S(2)}) collective-permute-start(bf16[256,128]{1,0:T(8,128)(2,1)S(1)} %get-tuple-element.61), channel_id=1, source_target_pairs={{0,24},{8,16},{16,8},{24,0},{1,25},{9,17},{17,9},{25,1},{2,26},{10... | collective-permute-start | bytes 196616 | tf_op jit(solution)/shard_map/ppermute | solution.py:571
  116.2 2.2 %copy-done.1 = bf16[512,4096]{1,0:T(8,128)(2,1)S(1)} copy-done((bf16[512,4096]{1,0:T(8,128)(2,1)S(1)}, bf16[512,4096]{1,0:T(8,128)(2,1)}, u32[]{:S(2)}) %copy-start.1) | copy-done | bytes 4194328
  118.4 1.3 output_rows.5
  119.7 0.1 collective-permute-start.26
  119.8 2.2 %copy-done.3 = bf16[512,4096]{1,0:T(8,128)(2,1)S(1)} copy-done((bf16[512,4096]{1,0:T(8,128)(2,1)S(1)}, bf16[512,4096]{1,0:T(8,128)(2,1)}, u32[]{:S(2)}) %copy-start.3) | copy-done | bytes 4194328
  122.0 1.3 output_rows.7
  123.3 0.5 collective-permute-start.29
  123.8 3.1 %output_rows.4 = (bf16[64,4096]{1,0:T(8,128)(2,1)S(1)}, bf16[64,4096]{1,0:T(8,128)(2,1)S(1)}) custom-call(s32[7]{0:T(128)S(1)} %get-tuple-element.42.info_ref, bf16[256,128]{1,0:T(8,128)(2,1)S(1)} %get-tuple-element.58.refs_0_, bf16[256,128]{1,0:T(8,128)(2,1)S(1)} %collective-permute-done.18.refs_1_, bf16[256,128]{1,0:T(8,128)(2,1)S(1)} %collective-permute-done.19.refs_2_, ...), custom_call_target="tpu_custom_call" | custom-call | flops 536870912 | bytes 4194304 | tf_op jit(solution)/shard_map/output_rows/pallas_call | solution.py:531
  126.9 0.1 collective-permute-start.21
  127.0 0.1 add_convert_fusion.4
  127.1 0.1 add_convert_fusion.3
  127.3 1.7 %collective-permute-start.28 = (bf16[64,4096]{1,0:T(8,128)(2,1)S(1)}, bf16[64,4096]{1,0:T(8,128)(2,1)S(1)}, u32[]{:S(2)}, u32[]{:S(2)}) collective-permute-start(bf16[64,4096]{1,0:T(8,128)(2,1)S(1)} %add_convert_fusion.4), channel_id=1, source_target_pairs={{0,2},{1,3},{2,0},{3,1},{4,6},{5,7},{6,4},{7,5},{8,10},{9,11},{10,... | collective-permute-start | bytes 1572872 | tf_op jit(solution)/shard_map/ppermute | solution.py:563
  129.0 0.1 add_convert_fusion.2
  129.1 0.4 collective-permute-start.31
  129.6 0.7 collective-permute-start.27
  130.3 11.9 %collective-permute-done.28 = bf16[64,4096]{1,0:T(8,128)(2,1)S(1)} collective-permute-done((bf16[64,4096]{1,0:T(8,128)(2,1)S(1)}, bf16[64,4096]{1,0:T(8,128)(2,1)S(1)}, u32[]{:S(2)}, u32[]{:S(2)}) %collective-permute-start.28) | collective-permute-done | bytes 524320 | tf_op jit(solution)/shard_map/ppermute | solution.py:563
  142.1 0.2 fusion
  142.3 3.4 %collective-permute-start.30 = (bf16[64,4096]{1,0:T(8,128)(2,1)S(1)}, bf16[64,4096]{1,0:T(8,128)(2,1)S(1)}, u32[]{:S(2)}, u32[]{:S(2)}) collective-permute-start(bf16[64,4096]{1,0:T(8,128)(2,1)S(1)} %fusion), channel_id=1, source_target_pairs={{0,4},{1,5},{2,6},{3,7},{4,0},{5,1},{6,2},{7,3},{8,12},{9,13},{10,... | collective-permute-start | bytes 1572872 | tf_op jit(solution)/shard_map/ppermute | solution.py:563
  145.8 16.0 %collective-permute-done.31 = bf16[64,4096]{1,0:T(8,128)(2,1)S(1)} collective-permute-done((bf16[64,4096]{1,0:T(8,128)(2,1)S(1)}, bf16[64,4096]{1,0:T(8,128)(2,1)S(1)}, u32[]{:S(2)}, u32[]{:S(2)}) %collective-permute-start.31) | collective-permute-done | bytes 524320 | tf_op jit(solution)/shard_map/ppermute | solution.py:563
  161.8 7.6 %collective-permute-done.30 = bf16[64,4096]{1,0:T(8,128)(2,1)S(1)} collective-permute-done((bf16[64,4096]{1,0:T(8,128)(2,1)S(1)}, bf16[64,4096]{1,0:T(8,128)(2,1)S(1)}, u32[]{:S(2)}, u32[]{:S(2)}) %collective-permute-start.30) | collective-permute-done | bytes 524320 | tf_op jit(solution)/shard_map/ppermute | solution.py:563
  169.4 1.4 add_convert_fusion
  (29 shorter events, 0.1 us)
Async XLA Ops:
  2.7 28.2 %collective-permute-start.4 = (bf16[64,4096]{1,0:T(8,128)(2,1)S(1)}, bf16[64,4096]{1,0:T(8,128)(2,1)S(1)}, u32[]{:S(2)}, u32[]{:S(2)}) collective-permute-start(bf16[64,4096]{1,0:T(8,128)(2,1)S(1)} %get-tuple-element.43.refs_0_), channel_id=1, source_target_pairs={{0,4},{1,5},{2,6},{3,7},{4,0},{5,1},{6,2},{7,3},{8,12},{9,13},{10,... | collective-permute-start | bytes 1572872 | tf_op jit(solution)/shard_map/ppermute | solution.py:563
  6.9 24.6 %collective-permute-start.6 = (bf16[64,4096]{1,0:T(8,128)(2,1)S(1)}, bf16[64,4096]{1,0:T(8,128)(2,1)S(1)}, u32[]{:S(2)}, u32[]{:S(2)}) collective-permute-start(bf16[64,4096]{1,0:T(8,128)(2,1)S(1)} %get-tuple-element.43.refs_0_), channel_id=1, source_target_pairs={{0,2},{1,3},{2,0},{3,1},{4,6},{5,7},{6,4},{7,5},{8,10},{9,11},{10,... | collective-permute-start | bytes 1572872 | tf_op jit(solution)/shard_map/ppermute | solution.py:563
  8.5 23.0 %collective-permute-start.11 = (bf16[64,4096]{1,0:T(8,128)(2,1)S(1)}, bf16[64,4096]{1,0:T(8,128)(2,1)S(1)}, u32[]{:S(2)}, u32[]{:S(2)}) collective-permute-start(bf16[64,4096]{1,0:T(8,128)(2,1)S(1)} %get-tuple-element.43.refs_0_), channel_id=1, source_target_pairs={{2,4},{3,5},{4,2},{5,3},{10,12},{11,13},{12,10},{13,11},{18,20},{1... | collective-permute-start | bytes 1572872 | tf_op jit(solution)/shard_map/ppermute | solution.py:563
  30.9 12.2 %collective-permute-start.13 = (bf16[64,4096]{1,0:T(8,128)(2,1)S(1)}, bf16[64,4096]{1,0:T(8,128)(2,1)S(1)}, u32[]{:S(2)}, u32[]{:S(2)}) collective-permute-start(bf16[64,4096]{1,0:T(8,128)(2,1)S(1)} %collective-permute-done.4.refs_0_), channel_id=1, source_target_pairs={{0,2},{1,3},{2,0},{3,1},{4,6},{5,7},{6,4},{7,5},{8,10},{9,11},{10,... | collective-permute-start | bytes 1572872 | tf_op jit(solution)/shard_map/ppermute | solution.py:563
  30.9 21.2 %collective-permute-start = (bf16[64,4096]{1,0:T(8,128)(2,1)S(1)}, bf16[64,4096]{1,0:T(8,128)(2,1)S(1)}, u32[]{:S(2)}, u32[]{:S(2)}) collective-permute-start(bf16[64,4096]{1,0:T(8,128)(2,1)S(1)} %get-tuple-element.43.refs_0_), channel_id=1, source_target_pairs={{0,1},{1,0},{2,3},{3,2},{4,5},{5,4},{6,7},{7,6},{8,9},{9,8},{10,11... | collective-permute-start | bytes 1572872 | tf_op jit(solution)/shard_map/ppermute | solution.py:566
  30.9 28.9 %collective-permute-start.5 = (bf16[64,4096]{1,0:T(8,128)(2,1)S(1)}, bf16[64,4096]{1,0:T(8,128)(2,1)S(1)}, u32[]{:S(2)}, u32[]{:S(2)}) collective-permute-start(bf16[64,4096]{1,0:T(8,128)(2,1)S(1)} %collective-permute-done.4.refs_0_), channel_id=1, source_target_pairs={{0,1},{1,0},{2,3},{3,2},{4,5},{5,4},{6,7},{7,6},{8,9},{9,8},{10,11... | collective-permute-start | bytes 1572872 | tf_op jit(solution)/shard_map/ppermute | solution.py:566
  31.4 28.3 %collective-permute-start.7 = (bf16[64,4096]{1,0:T(8,128)(2,1)S(1)}, bf16[64,4096]{1,0:T(8,128)(2,1)S(1)}, u32[]{:S(2)}, u32[]{:S(2)}) collective-permute-start(bf16[64,4096]{1,0:T(8,128)(2,1)S(1)} %collective-permute-done.6.refs_2_), channel_id=1, source_target_pairs={{0,1},{1,0},{2,3},{3,2},{4,5},{5,4},{6,7},{7,6},{8,9},{9,8},{10,11... | collective-permute-start | bytes 1572872 | tf_op jit(solution)/shard_map/ppermute | solution.py:566
  31.5 39.9 %collective-permute-start.12 = (bf16[64,4096]{1,0:T(8,128)(2,1)S(1)}, bf16[64,4096]{1,0:T(8,128)(2,1)S(1)}, u32[]{:S(2)}, u32[]{:S(2)}) collective-permute-start(bf16[64,4096]{1,0:T(8,128)(2,1)S(1)} %collective-permute-done.11.inner_own), channel_id=1, source_target_pairs={{0,1},{1,0},{2,3},{3,2},{4,5},{5,4},{6,7},{7,6},{8,9},{9,8},{10,11... | collective-permute-start | bytes 1572872 | tf_op jit(solution)/shard_map/ppermute | solution.py:566
  43.2 29.7 %collective-permute-start.14 = (bf16[64,4096]{1,0:T(8,128)(2,1)S(1)}, bf16[64,4096]{1,0:T(8,128)(2,1)S(1)}, u32[]{:S(2)}, u32[]{:S(2)}) collective-permute-start(bf16[64,4096]{1,0:T(8,128)(2,1)S(1)} %collective-permute-done.13.relayed_own), channel_id=1, source_target_pairs={{0,1},{1,0},{2,3},{3,2},{4,5},{5,4},{6,7},{7,6},{8,9},{9,8},{10,11... | collective-permute-start | bytes 1572872 | tf_op jit(solution)/shard_map/ppermute | solution.py:566
  58.4 11.6 %collective-permute-start.1 = (bf16[128,384]{1,0:T(8,128)(2,1)S(1)}, bf16[128,384]{1,0:T(8,128)(2,1)S(1)}, u32[]{:S(2)}, u32[]{:S(2)}) collective-permute-start(bf16[128,384]{1,0:T(8,128)(2,1)S(1)} %get-tuple-element.45), channel_id=1, source_target_pairs={{0,8},{8,0},{16,24},{24,16},{1,9},{9,1},{17,25},{25,17},{2,10},{10... | collective-permute-start | bytes 294920 | tf_op jit(solution)/shard_map/ppermute | solution.py:571
  67.8 11.5 %collective-permute-start.8 = (bf16[256,384]{1,0:T(8,128)(2,1)S(1)}, bf16[256,384]{1,0:T(8,128)(2,1)S(1)}, u32[]{:S(2)}, u32[]{:S(2)}) collective-permute-start(bf16[256,384]{1,0:T(8,128)(2,1)S(1)} %get-tuple-element.50), channel_id=1, source_target_pairs={{0,8},{8,0},{16,24},{24,16},{1,9},{9,1},{17,25},{25,17},{2,10},{10... | collective-permute-start | bytes 589832 | tf_op jit(solution)/shard_map/ppermute | solution.py:571
  68.6 7.7 %collective-permute-start.2 = (bf16[128,384]{1,0:T(8,128)(2,1)S(1)}, bf16[128,384]{1,0:T(8,128)(2,1)S(1)}, u32[]{:S(2)}, u32[]{:S(2)}) collective-permute-start(bf16[128,384]{1,0:T(8,128)(2,1)S(1)} %get-tuple-element.46), channel_id=1, source_target_pairs={{0,16},{8,24},{16,0},{24,8},{1,17},{9,25},{17,1},{25,9},{2,18},{10... | collective-permute-start | bytes 294920 | tf_op jit(solution)/shard_map/ppermute | solution.py:571
  70.0 8.8 %collective-permute-start.3 = (bf16[128,384]{1,0:T(8,128)(2,1)S(1)}, bf16[128,384]{1,0:T(8,128)(2,1)S(1)}, u32[]{:S(2)}, u32[]{:S(2)}) collective-permute-start(bf16[128,384]{1,0:T(8,128)(2,1)S(1)} %get-tuple-element.47), channel_id=1, source_target_pairs={{0,24},{8,16},{16,8},{24,0},{1,25},{9,17},{17,9},{25,1},{2,26},{10... | collective-permute-start | bytes 294920 | tf_op jit(solution)/shard_map/ppermute | solution.py:571
  71.4 15.7 %collective-permute-start.9 = (bf16[256,384]{1,0:T(8,128)(2,1)S(1)}, bf16[256,384]{1,0:T(8,128)(2,1)S(1)}, u32[]{:S(2)}, u32[]{:S(2)}) collective-permute-start(bf16[256,384]{1,0:T(8,128)(2,1)S(1)} %get-tuple-element.51), channel_id=1, source_target_pairs={{0,16},{8,24},{16,0},{24,8},{1,17},{9,25},{17,1},{25,9},{2,18},{10... | collective-permute-start | bytes 589832 | tf_op jit(solution)/shard_map/ppermute | solution.py:571
  72.9 14.2 %collective-permute-start.10 = (bf16[256,384]{1,0:T(8,128)(2,1)S(1)}, bf16[256,384]{1,0:T(8,128)(2,1)S(1)}, u32[]{:S(2)}, u32[]{:S(2)}) collective-permute-start(bf16[256,384]{1,0:T(8,128)(2,1)S(1)} %get-tuple-element.52), channel_id=1, source_target_pairs={{0,24},{8,16},{16,8},{24,0},{1,25},{9,17},{17,9},{25,1},{2,26},{10... | collective-permute-start | bytes 589832 | tf_op jit(solution)/shard_map/ppermute | solution.py:571
  73.6 14.5 %copy-start.4 = (s32[4]{0:T(128)S(1)}, s32[4]{0:T(128)}, u32[]{:S(2)}) copy-start(s32[4]{0:T(128)} %docs_ref.3) | copy-start | bytes 52
  76.4 10.7 %collective-permute-start.15 = (bf16[128,384]{1,0:T(8,128)(2,1)S(1)}, bf16[128,384]{1,0:T(8,128)(2,1)S(1)}, u32[]{:S(2)}, u32[]{:S(2)}) collective-permute-start(bf16[128,384]{1,0:T(8,128)(2,1)S(1)} %get-tuple-element.55), channel_id=1, source_target_pairs={{0,8},{8,0},{16,24},{24,16},{1,9},{9,1},{17,25},{25,17},{2,10},{10... | collective-permute-start | bytes 294920 | tf_op jit(solution)/shard_map/ppermute | solution.py:571
  78.8 9.3 %collective-permute-start.16 = (bf16[128,384]{1,0:T(8,128)(2,1)S(1)}, bf16[128,384]{1,0:T(8,128)(2,1)S(1)}, u32[]{:S(2)}, u32[]{:S(2)}) collective-permute-start(bf16[128,384]{1,0:T(8,128)(2,1)S(1)} %get-tuple-element.56), channel_id=1, source_target_pairs={{0,16},{8,24},{16,0},{24,8},{1,17},{9,25},{17,1},{25,9},{2,18},{10... | collective-permute-start | bytes 294920 | tf_op jit(solution)/shard_map/ppermute | solution.py:571
  79.3 8.8 %collective-permute-start.17 = (bf16[128,384]{1,0:T(8,128)(2,1)S(1)}, bf16[128,384]{1,0:T(8,128)(2,1)S(1)}, u32[]{:S(2)}, u32[]{:S(2)}) collective-permute-start(bf16[128,384]{1,0:T(8,128)(2,1)S(1)} %get-tuple-element.57), channel_id=1, source_target_pairs={{0,24},{8,16},{16,8},{24,0},{1,25},{9,17},{17,9},{25,1},{2,26},{10... | collective-permute-start | bytes 294920 | tf_op jit(solution)/shard_map/ppermute | solution.py:571
  94.7 9.3 %copy-start = (bf16[512,4096]{1,0:T(8,128)(2,1)}, bf16[512,4096]{1,0:T(8,128)(2,1)S(1)}, u32[]{:S(2)}) copy-start(bf16[512,4096]{1,0:T(8,128)(2,1)S(1)} %get-tuple-element.68.refs_4_) | copy-start | bytes 12582916
  94.7 4.7 %collective-permute-start.22 = (bf16[256,128]{1,0:T(8,128)(2,1)S(1)}, bf16[256,128]{1,0:T(8,128)(2,1)S(1)}, u32[]{:S(2)}, u32[]{:S(2)}) collective-permute-start(bf16[256,128]{1,0:T(8,128)(2,1)S(1)} %get-tuple-element.65), channel_id=1, source_target_pairs={{0,8},{8,0},{16,24},{24,16},{1,9},{9,1},{17,25},{25,17},{2,10},{10... | collective-permute-start | bytes 196616 | tf_op jit(solution)/shard_map/ppermute | solution.py:571
  96.0 5.0 %collective-permute-start.23 = (bf16[256,128]{1,0:T(8,128)(2,1)S(1)}, bf16[256,128]{1,0:T(8,128)(2,1)S(1)}, u32[]{:S(2)}, u32[]{:S(2)}) collective-permute-start(bf16[256,128]{1,0:T(8,128)(2,1)S(1)} %get-tuple-element.66), channel_id=1, source_target_pairs={{0,16},{8,24},{16,0},{24,8},{1,17},{9,25},{17,1},{25,9},{2,18},{10... | collective-permute-start | bytes 196616 | tf_op jit(solution)/shard_map/ppermute | solution.py:571
  97.5 5.2 %collective-permute-start.24 = (bf16[256,128]{1,0:T(8,128)(2,1)S(1)}, bf16[256,128]{1,0:T(8,128)(2,1)S(1)}, u32[]{:S(2)}, u32[]{:S(2)}) collective-permute-start(bf16[256,128]{1,0:T(8,128)(2,1)S(1)} %get-tuple-element.67), channel_id=1, source_target_pairs={{0,24},{8,16},{16,8},{24,0},{1,25},{9,17},{17,9},{25,1},{2,26},{10... | collective-permute-start | bytes 196616 | tf_op jit(solution)/shard_map/ppermute | solution.py:571
  104.0 23.0 %collective-permute-start.25 = (bf16[64,4096]{1,0:T(8,128)(2,1)S(1)}, bf16[64,4096]{1,0:T(8,128)(2,1)S(1)}, u32[]{:S(2)}, u32[]{:S(2)}) collective-permute-start(bf16[64,4096]{1,0:T(8,128)(2,1)S(1)} %get-tuple-element.72), channel_id=1, source_target_pairs={{0,1},{1,0},{2,3},{3,2},{4,5},{5,4},{6,7},{7,6},{8,9},{9,8},{10,11... | collective-permute-start | bytes 1572872 | tf_op jit(solution)/shard_map/ppermute | solution.py:566
  110.7 2.0 %copy-start.2 = (bf16[512,4096]{1,0:T(8,128)(2,1)}, bf16[512,4096]{1,0:T(8,128)(2,1)S(1)}, u32[]{:S(2)}) copy-start(bf16[512,4096]{1,0:T(8,128)(2,1)S(1)} %get-tuple-element.76.refs_4_) | copy-start | bytes 12582916
  112.7 7.1 %collective-permute-start.18 = (bf16[256,128]{1,0:T(8,128)(2,1)S(1)}, bf16[256,128]{1,0:T(8,128)(2,1)S(1)}, u32[]{:S(2)}, u32[]{:S(2)}) collective-permute-start(bf16[256,128]{1,0:T(8,128)(2,1)S(1)} %get-tuple-element.59), channel_id=1, source_target_pairs={{0,8},{8,0},{16,24},{24,16},{1,9},{9,1},{17,25},{25,17},{2,10},{10... | collective-permute-start | bytes 196616 | tf_op jit(solution)/shard_map/ppermute | solution.py:571
  113.5 6.2 %collective-permute-start.19 = (bf16[256,128]{1,0:T(8,128)(2,1)S(1)}, bf16[256,128]{1,0:T(8,128)(2,1)S(1)}, u32[]{:S(2)}, u32[]{:S(2)}) collective-permute-start(bf16[256,128]{1,0:T(8,128)(2,1)S(1)} %get-tuple-element.60), channel_id=1, source_target_pairs={{0,16},{8,24},{16,0},{24,8},{1,17},{9,25},{17,1},{25,9},{2,18},{10... | collective-permute-start | bytes 196616 | tf_op jit(solution)/shard_map/ppermute | solution.py:571
  114.0 5.7 %collective-permute-start.20 = (bf16[256,128]{1,0:T(8,128)(2,1)S(1)}, bf16[256,128]{1,0:T(8,128)(2,1)S(1)}, u32[]{:S(2)}, u32[]{:S(2)}) collective-permute-start(bf16[256,128]{1,0:T(8,128)(2,1)S(1)} %get-tuple-element.61), channel_id=1, source_target_pairs={{0,24},{8,16},{16,8},{24,0},{1,25},{9,17},{17,9},{25,1},{2,26},{10... | collective-permute-start | bytes 196616 | tf_op jit(solution)/shard_map/ppermute | solution.py:571
  116.2 2.2 %copy-start.1 = (bf16[512,4096]{1,0:T(8,128)(2,1)S(1)}, bf16[512,4096]{1,0:T(8,128)(2,1)}, u32[]{:S(2)}) copy-start(bf16[512,4096]{1,0:T(8,128)(2,1)} %copy-done) | copy-start | bytes 12582916
  118.4 51.0 %copy-start.5 = (bf16[64,4096]{1,0:T(8,128)(2,1)S(1)}, bf16[64,4096]{1,0:T(8,128)(2,1)}, u32[]{:S(2)}) copy-start(bf16[64,4096]{1,0:T(8,128)(2,1)} %tokens_ref.1) | copy-start | bytes 1572868
  119.7 7.5 %collective-permute-start.26 = (bf16[64,4096]{1,0:T(8,128)(2,1)S(1)}, bf16[64,4096]{1,0:T(8,128)(2,1)S(1)}, u32[]{:S(2)}, u32[]{:S(2)}) collective-permute-start(bf16[64,4096]{1,0:T(8,128)(2,1)S(1)} %get-tuple-element.74), channel_id=1, source_target_pairs={{0,1},{1,0},{2,3},{3,2},{4,5},{5,4},{6,7},{7,6},{8,9},{9,8},{10,11... | collective-permute-start | bytes 1572872 | tf_op jit(solution)/shard_map/ppermute | solution.py:566
  119.8 2.2 %copy-start.3 = (bf16[512,4096]{1,0:T(8,128)(2,1)S(1)}, bf16[512,4096]{1,0:T(8,128)(2,1)}, u32[]{:S(2)}) copy-start(bf16[512,4096]{1,0:T(8,128)(2,1)} %copy-done.2) | copy-start | bytes 12582916
  123.3 5.7 %collective-permute-start.29 = (bf16[64,4096]{1,0:T(8,128)(2,1)S(1)}, bf16[64,4096]{1,0:T(8,128)(2,1)S(1)}, u32[]{:S(2)}, u32[]{:S(2)}) collective-permute-start(bf16[64,4096]{1,0:T(8,128)(2,1)S(1)} %get-tuple-element.78), channel_id=1, source_target_pairs={{0,1},{1,0},{2,3},{3,2},{4,5},{5,4},{6,7},{7,6},{8,9},{9,8},{10,11... | collective-permute-start | bytes 1572872 | tf_op jit(solution)/shard_map/ppermute | solution.py:566
  126.9 18.9 %collective-permute-start.21 = (bf16[64,4096]{1,0:T(8,128)(2,1)S(1)}, bf16[64,4096]{1,0:T(8,128)(2,1)S(1)}, u32[]{:S(2)}, u32[]{:S(2)}) collective-permute-start(bf16[64,4096]{1,0:T(8,128)(2,1)S(1)} %get-tuple-element.63), channel_id=1, source_target_pairs={{0,1},{1,0},{2,3},{3,2},{4,5},{5,4},{6,7},{7,6},{8,9},{9,8},{10,11... | collective-permute-start | bytes 1572872 | tf_op jit(solution)/shard_map/ppermute | solution.py:566
  127.3 14.9 %collective-permute-start.28 = (bf16[64,4096]{1,0:T(8,128)(2,1)S(1)}, bf16[64,4096]{1,0:T(8,128)(2,1)S(1)}, u32[]{:S(2)}, u32[]{:S(2)}) collective-permute-start(bf16[64,4096]{1,0:T(8,128)(2,1)S(1)} %add_convert_fusion.4), channel_id=1, source_target_pairs={{0,2},{1,3},{2,0},{3,1},{4,6},{5,7},{6,4},{7,5},{8,10},{9,11},{10,... | collective-permute-start | bytes 1572872 | tf_op jit(solution)/shard_map/ppermute | solution.py:563
  129.1 32.7 %collective-permute-start.31 = (bf16[64,4096]{1,0:T(8,128)(2,1)S(1)}, bf16[64,4096]{1,0:T(8,128)(2,1)S(1)}, u32[]{:S(2)}, u32[]{:S(2)}) collective-permute-start(bf16[64,4096]{1,0:T(8,128)(2,1)S(1)} %add_convert_fusion.2), channel_id=1, source_target_pairs={{0,2},{1,3},{2,0},{3,1},{4,6},{5,7},{6,4},{7,5},{8,10},{9,11},{10,... | collective-permute-start | bytes 1572872 | tf_op jit(solution)/shard_map/ppermute | solution.py:563
  129.6 32.2 %collective-permute-start.27 = (bf16[64,4096]{1,0:T(8,128)(2,1)S(1)}, bf16[64,4096]{1,0:T(8,128)(2,1)S(1)}, u32[]{:S(2)}, u32[]{:S(2)}) collective-permute-start(bf16[64,4096]{1,0:T(8,128)(2,1)S(1)} %add_convert_fusion.3), channel_id=1, source_target_pairs={{2,4},{3,5},{4,2},{5,3},{10,12},{11,13},{12,10},{13,11},{18,20},{1... | collective-permute-start | bytes 1572872 | tf_op jit(solution)/shard_map/ppermute | solution.py:563
  142.3 27.0 %collective-permute-start.30 = (bf16[64,4096]{1,0:T(8,128)(2,1)S(1)}, bf16[64,4096]{1,0:T(8,128)(2,1)S(1)}, u32[]{:S(2)}, u32[]{:S(2)}) collective-permute-start(bf16[64,4096]{1,0:T(8,128)(2,1)S(1)} %fusion), channel_id=1, source_target_pairs={{0,4},{1,5},{2,6},{3,7},{4,0},{5,1},{6,2},{7,3},{8,12},{9,13},{10,... | collective-permute-start | bytes 1572872 | tf_op jit(solution)/shard_map/ppermute | solution.py:563

commit v3 on v2

--- a/solution.py
+++ b/solution.py
@@ -259,17 +259,14 @@
             for i, turn in enumerate(self.turns)
         ]
 
+
     def start(self, *refs):
-        @pl.when(refs[0][1] >= 0)
-        def _():
-            for copy in self.copies(*refs):
-                copy.start()
+        for copy in self.copies(*refs):
+            copy.start()
 
     def wait(self, *refs):
-        @pl.when(refs[0][1] >= 0)
-        def _():
-            for copy in self.copies(*refs):
-                copy.wait()
+        for copy in self.copies(*refs):
+            copy.wait()
 
 
 def store_pair(info_ref, outs, rows, p, result):
@@ -299,7 +296,8 @@
         ]
         for copy in fetched[0].values():
             copy.start()
-        for n in range(count):
+
+        def project(n):
             source_ref = ready_refs[n] if n < given else buffer_ref
             for p in range(pairs):
                 result = None
@@ -314,6 +312,12 @@
                     if given <= n < count - 1:
                         fetched[n - given + 1][p, k].start()
                 store_pair(info_ref, outs, pl.ds(n * block, block), p, result)
+
+        for n in range(count):
+            if n < given:
+                pl.when(info_ref[1] >= 0)(lambda: project(n))
+            else:
+                project(n)
 
     return pl.pallas_call(
         kernel,
@@ -401,68 +405,72 @@
         next_ref, outs, kept_refs = refs[0], refs[1 : 1 + count], refs[1 + count : 1 + count + kept]
         keys_ref, values_ref, sems = refs[1 + count + kept :]
         prefetch.start(info_ref, next_ref, kept_refs, sems)
-        middle = is_middle(info_ref, chips)
-        mu, chip, own_first = info_ref[0], info_ref[1], info_ref[2] * (block // 2)
-
-        def slot_rows(d, slot, part):
-            for i, (slots, _) in enumerate(sets):
-                if slot in slots:
-                    at = slots.index(slot) * block
-                    return ins[i * count + d][at : at + block, part * HDIM : (part + 1) * HDIM]
-
-        for d in range(count):
-            for slot in range(chips):
-                index = jnp.bitwise_xor(mu, d) * chips + jnp.bitwise_xor(chip, slot)
-                place = pl.ds(pl.multiple_of(index * block, block), block)
-                keys_ref[place, :] = slot_rows(d, slot, 1)
-                values_ref[place, :] = slot_rows(d, slot, 2)
-
-        ends = []
-        end = jnp.int32(0)
-        for i in range(docs):
-            end = end + docs_ref[i]
-            ends.append(end)
-        row_place = lax.broadcasted_iota(jnp.int32, (block, 1), 0) + own_first
-        row_place = jnp.where(row_place >= block, row_place - block, row_place)
-        key_iota = lax.broadcasted_iota(jnp.int32, (1, window), 1)
-        key_in_block = key_iota % block + own_first
-        key_in_block = jnp.where(key_in_block >= block, key_in_block - block, key_in_block)
-        key_place = (key_iota // block) * block + key_in_block
-        for n, turn in enumerate(turns):
-            slot = jnp.where(middle, turn[1], turn[0])
+
+        @pl.when(info_ref[1] >= 0)
+        def _():
+            middle = is_middle(info_ref, chips)
+            mu, chip, own_first = info_ref[0], info_ref[1], info_ref[2] * (block // 2)
+
+            def slot_rows(d, slot, part):
+                for i, (slots, _) in enumerate(sets):
+                    if slot in slots:
+                        at = slots.index(slot) * block
+                        return ins[i * count + d][at : at + block, part * HDIM : (part + 1) * HDIM]
+
             for d in range(count):
-                index = jnp.bitwise_xor(mu, d) * chips + jnp.bitwise_xor(chip, slot)
-                first_row = index * block
-                doc_first = jnp.int32(0)
-                for e in ends:
-                    doc_first = jnp.where(first_row >= e, e, doc_first)
-                start = jnp.minimum(doc_first // block, (total - window) // block) * block
-                start = pl.multiple_of(start, block)
-                row_pos = row_place + first_row
-                row_first = jnp.zeros((block, 1), jnp.int32)
-                for e in ends:
-                    row_first = jnp.where(row_pos >= e, e, row_first)
-                key_pos = key_place + start
-                allowed = (key_pos <= row_pos) & (key_pos >= row_first)
-                query = slot_rows(d, turn[0], 0)
-                if turn[1] != turn[0]:
-                    query = jnp.where(middle, slot_rows(d, turn[1], 0), query)
-                scores = lax.dot_general(
-                    query,
-                    keys_ref[pl.ds(start, window), :],
-                    (((1,), (1,)), ((), ())),
-                    preferred_element_type=jnp.float32,
-                )
-                scores = jnp.where(allowed, scores * scale, -1e30)
-                row_max = jnp.max(scores, axis=1, keepdims=True)
-                weights = jnp.where(allowed, jnp.exp(scores - row_max), 0.0)
-                totals = jnp.sum(weights, axis=1, keepdims=True)
-                summed = jnp.dot(
-                    weights.astype(jnp.bfloat16),
-                    values_ref[pl.ds(start, window), :],
-                    preferred_element_type=jnp.float32,
-                )
-                outs[d][n * block : (n + 1) * block, :] = (summed / totals).astype(jnp.bfloat16)
+                for slot in range(chips):
+                    index = jnp.bitwise_xor(mu, d) * chips + jnp.bitwise_xor(chip, slot)
+                    place = pl.ds(pl.multiple_of(index * block, block), block)
+                    keys_ref[place, :] = slot_rows(d, slot, 1)
+                    values_ref[place, :] = slot_rows(d, slot, 2)
+
+            ends = []
+            end = jnp.int32(0)
+            for i in range(docs):
+                end = end + docs_ref[i]
+                ends.append(end)
+            row_place = lax.broadcasted_iota(jnp.int32, (block, 1), 0) + own_first
+            row_place = jnp.where(row_place >= block, row_place - block, row_place)
+            key_iota = lax.broadcasted_iota(jnp.int32, (1, window), 1)
+            key_in_block = key_iota % block + own_first
+            key_in_block = jnp.where(key_in_block >= block, key_in_block - block, key_in_block)
+            key_place = (key_iota // block) * block + key_in_block
+            for n, turn in enumerate(turns):
+                slot = jnp.where(middle, turn[1], turn[0])
+                for d in range(count):
+                    index = jnp.bitwise_xor(mu, d) * chips + jnp.bitwise_xor(chip, slot)
+                    first_row = index * block
+                    doc_first = jnp.int32(0)
+                    for e in ends:
+                        doc_first = jnp.where(first_row >= e, e, doc_first)
+                    start = jnp.minimum(doc_first // block, (total - window) // block) * block
+                    start = pl.multiple_of(start, block)
+                    row_pos = row_place + first_row
+                    row_first = jnp.zeros((block, 1), jnp.int32)
+                    for e in ends:
+                        row_first = jnp.where(row_pos >= e, e, row_first)
+                    key_pos = key_place + start
+                    allowed = (key_pos <= row_pos) & (key_pos >= row_first)
+                    query = slot_rows(d, turn[0], 0)
+                    if turn[1] != turn[0]:
+                        query = jnp.where(middle, slot_rows(d, turn[1], 0), query)
+                    scores = lax.dot_general(
+                        query,
+                        keys_ref[pl.ds(start, window), :],
+                        (((1,), (1,)), ((), ())),
+                        preferred_element_type=jnp.float32,
+                    )
+                    scores = jnp.where(allowed, scores * scale, -1e30)
+                    row_max = jnp.max(scores, axis=1, keepdims=True)
+                    weights = jnp.where(allowed, jnp.exp(scores - row_max), 0.0)
+                    totals = jnp.sum(weights, axis=1, keepdims=True)
+                    summed = jnp.dot(
+                        weights.astype(jnp.bfloat16),
+                        values_ref[pl.ds(start, window), :],
+                        preferred_element_type=jnp.float32,
+                    )
+                    outs[d][n * block : (n + 1) * block, :] = (summed / totals).astype(jnp.bfloat16)
+
         prefetch.wait(info_ref, next_ref, kept_refs, sems)
 
     n_queries = len(turns) * count
@@ -477,7 +485,7 @@
             pltpu.VMEM((total, HDIM), jnp.bfloat16),
             prefetch.scratch,
         ],
-        compiler_params=params(18),
+        compiler_params=params(14),
         cost_estimate=pl.CostEstimate(
             flops=n_queries * block * window * HDIM * 8,
             bytes_accessed=3 * total * HDIM * 2,
@@ -487,53 +495,33 @@
     )(info, doc_lengths, *[piece for _, pieces in sets for piece in pieces], prefetch.weight)
 
 
-def output_rows(info, pieces, weight, index, turns, slot=None):
+def output_rows(info, pieces, weight, index, turns):
     count = len(pieces)
     block = pieces[0].shape[0] // turns
     half = block // 2
     at = index * block
-    depth, width = weight.shape[-2:]
+    depth, width = weight.shape
     tile = min(1024, width)
-    firsts = range(0, width, tile)
 
     def kernel(info_ref, *refs):
         ins = refs[:count]
-        weight_ref, own_ref, partner_ref, heads_ref = refs[count : count + 4]
-        copies = []
-        if slot is not None:
-            buffer_ref, sems = refs[count + 4 :]
-            for i, first in enumerate(firsts):
-                part = weight_ref.at[mode_of(info_ref, slot), :, pl.ds(first, tile)]
-                copies.append(pltpu.make_async_copy(part, buffer_ref.at[i], sems.at[i]))
-            for copy in copies:
-                copy.start()
+        weight_ref, own_ref, partner_ref, heads_ref = refs[count:]
         for d in range(count):
             heads_ref[jnp.bitwise_xor(info_ref[0], d)] = ins[d][at : at + block, :]
         rows = jnp.concatenate([heads_ref[h] for h in range(count)], axis=1)
-        for i, first in enumerate(firsts):
+        for first in range(0, width, tile):
             cols = slice(first, first + tile)
-            if slot is None:
-                part = weight_ref[:, cols]
-            else:
-                copies[i].wait()
-                part = buffer_ref[i]
-            result = jnp.dot(rows, part, preferred_element_type=jnp.float32)
+            result = jnp.dot(rows, weight_ref[:, cols], preferred_element_type=jnp.float32)
             result = result.astype(jnp.bfloat16)
             own_ref[:, cols] = result[:half]
             partner_ref[:, cols] = result[half:]
 
-    streamed = []
-    if slot is not None:
-        streamed = [
-            pltpu.VMEM((len(firsts), depth, tile), jnp.bfloat16),
-            pltpu.SemaphoreType.DMA((len(firsts),)),
-        ]
     return pl.pallas_call(
         kernel,
         out_shape=[pltpu.VMEM((half, width), jnp.bfloat16)] * 2,
-        in_specs=[SMEM] + [VMEM] * count + [VMEM if slot is None else HBM],
+        in_specs=[SMEM] + [VMEM] * (count + 1),
         out_specs=[VMEM] * 2,
-        scratch_shapes=[pltpu.VMEM((count, block, HDIM), jnp.bfloat16)] + streamed,
+        scratch_shapes=[pltpu.VMEM((count, block, HDIM), jnp.bfloat16)],
         compiler_params=params(8),
         cost_estimate=pl.CostEstimate(
             flops=2 * block * depth * width,
@@ -542,6 +530,70 @@
         ),
         name="output_rows",
     )(info, *pieces, weight)
+
+
+def add_rows(info, chips, first, second, otherwise=None):
+    values = [first, second] + ([] if otherwise is None else [otherwise])
+    values = [pltpu.with_memory_space_constraint(value, pltpu.VMEM) for value in values]
+
+    def kernel(info_ref, first_ref, second_ref, *refs):
+        def add():
+            total = first_ref[...].astype(jnp.float32) + second_ref[...].astype(jnp.float32)
+            refs[-1][...] = total.astype(jnp.bfloat16)
+
+        if otherwise is None:
+            add()
+            return
+        middle = is_middle(info_ref, chips)
+        pl.when(middle)(lambda: add())
+
+        @pl.when(jnp.logical_not(middle))
+        def _():
+            refs[-1][...] = refs[0][...]
+
+    return pl.pallas_call(
+        kernel,
+        out_shape=pltpu.VMEM(first.shape, jnp.bfloat16),
+        in_specs=[SMEM] + [VMEM] * len(values),
+        out_specs=VMEM,
+        compiler_params=params(4),
+        cost_estimate=pl.CostEstimate(
+            flops=4 * first.size, bytes_accessed=6 * first.size, transcendentals=0
+        ),
+        name="add_rows",
+    )(info, *values)
+
+
+def last_rows(info, chips, early, far, middle_only):
+    values = [
+        pltpu.with_memory_space_constraint(value, pltpu.VMEM)
+        for value in (early, far, middle_only)
+    ]
+
+    def kernel(info_ref, early_ref, far_ref, middle_ref, out_ref):
+        middle = is_middle(info_ref, chips)
+
+        @pl.when(middle)
+        def _():
+            total = early_ref[...] + far_ref[...].astype(jnp.float32)
+            out_ref[...] = (total + middle_ref[...].astype(jnp.float32)).astype(jnp.bfloat16)
+
+        @pl.when(jnp.logical_not(middle))
+        def _():
+            total = early_ref[...] + far_ref[...].astype(jnp.float32)
+            out_ref[...] = total.astype(jnp.bfloat16)
+
+    return pl.pallas_call(
+        kernel,
+        out_shape=jax.ShapeDtypeStruct(far.shape, jnp.bfloat16),
+        in_specs=[SMEM, VMEM, VMEM, VMEM],
+        out_specs=VMEM,
+        compiler_params=params(6),
+        cost_estimate=pl.CostEstimate(
+            flops=4 * far.size, bytes_accessed=10 * far.size, transcendentals=0
+        ),
+        name="last_rows",
+    )(info, *values)
 
 
 def chip_pairs(pairs):
@@ -557,7 +609,6 @@
     ids = jnp.stack([mu, seq // 2, seq % 2])
     qkv_weight = pltpu.with_memory_space_constraint(qkv_weight, pltpu.HBM)
     out_weight = pltpu.with_memory_space_constraint(out_weight, pltpu.HBM)
-    alone = lax.optimization_barrier
 
     def along(value, pairs):
         return lax.ppermute(value, "seq", chip_pairs(pairs))
@@ -570,12 +621,6 @@
         for d in range(1, mod_count):
             moved.append(lax.ppermute(pieces[d], "mod", [(i, i ^ d) for i in range(mod_count)]))
         return moved
-
-    def add(*shares):
-        total = shares[0].astype(jnp.float32)
-        for share in shares[1:]:
-            total = total + share.astype(jnp.float32)
-        return total.astype(jnp.bfloat16)
 
     in_hbm = [
         pltpu.with_memory_space_constraint(value, pltpu.HBM)
@@ -612,8 +657,8 @@
     late = exchange(late)
     sets = (((0,), own), ((2, 1), mid), ((3,), late))
 
-    def finish(pieces, kept, index, slot=None):
-        own_share, partner_share = output_rows(info, pieces, kept, index, 2, slot)
+    def finish(pieces, kept, index, turns):
+        own_share, partner_share = output_rows(info, pieces, kept, index, turns)
         return own_share, swap(partner_share)
 
     *first, kept_b = attend_slots(
@@ -625,31 +670,31 @@
         Prefetch(out_weight, (turn_b,), chips),
     )
     first = exchange(first)
-    sum_a = alone(add(*finish(first, kept_a, 0)))
-    own_b, partner_b = finish(first, kept_b, 1)
-    own_b, sum_a = alone((own_b, sum_a))
+    sum_a = add_rows(info, chips, *finish(first, kept_a, 0, 2))
+    own_b, partner_b = finish(first, kept_b, 1, 2)
     from_one = along(sum_a, [(i, i ^ 1) for i in range(chips)])
-    sum_b = alone(add(own_b, partner_b))
+    sum_b = add_rows(info, chips, own_b, partner_b)
     from_inner = along(sum_b, [(1, 2), (2, 1)])
-    *rest, kept_c = attend_slots(
-        info,
-        doc_lengths,
-        sets,
-        (turn_c, turn_d),
-        chips,
-        Prefetch(out_weight, (turn_c,), chips),
-    )
-    rest = exchange(rest)
-    sum_c = alone(add(*finish(rest, kept_c, 0)))
+    *rest_c, kept_c = attend_slots(
+        info, doc_lengths, sets, (turn_c,), chips, Prefetch(out_weight, (turn_c,), chips)
+    )
+    rest_c = exchange(rest_c)
+    sum_c = add_rows(info, chips, *finish(rest_c, kept_c, 0, 1))
     chip = seq // 2
     middle = (chip > 0) & (chip < chips - 1)
-    relay_sum = jnp.where(middle, add(sum_c, from_one), sum_b)
+    relay_sum = add_rows(info, chips, sum_c, from_one, sum_b)
     from_two = along(relay_sum, [(i, i ^ 2) for i in range(chips)])
     from_end = along(sum_c, [(i, i ^ 1) for i in range(chips)])
-    shares_d = finish(rest, out_weight, 1, slot=0)
+    *rest_d, kept_d = attend_slots(
+        info, doc_lengths, sets, (turn_d,), chips, Prefetch(out_weight, (turn_d,), chips)
+    )
+    rest_d = exchange(rest_d)
+    shares_d = finish(rest_d, kept_d, 0, 1)
     near = jnp.where(middle, from_inner, from_one)
-    far = jnp.where(middle, from_end, jnp.zeros_like(from_end))
-    return add(tokens, *shares_d, near, from_two, far)
+    early = tokens.astype(jnp.float32)
+    for share in (*shares_d, near):
+        early = early + share.astype(jnp.float32)
+    return last_rows(info, chips, early, from_two, from_end)
 
 
 def solution(mesh):

time: 171 us -> 164 us (0.959)
  starting transfers between devices: 32 us -> 40.3 us
  waiting for transfers between devices: 81.2 us -> 74.3 us
  local copies, waits for them, and re-layouts: 6.4 us -> 0.01 us
    ppermute x8, waiting for transfers between devices: 68.5 us -> 60.9 us  [along(): return lax.ppermute(value, 'seq', chip_pairs(pairs))]
    unnamed x12 -> x2, local copies, waits for them, and re-layouts: 6.4 us -> 0.01 us
    ppermute x8, starting transfers between devices: 12.7 us -> 17.5 us  [along(): return lax.ppermute(value, 'seq', chip_pairs(pairs))]
    pallas_call x0 -> x5, Pallas kernels: none -> 4 us  [the longest x4 2.57 us: add_rows(): pl.pallas_call(kernel, out_shape=pltpu.VMEM(first.shape, jnp.bfloat16), i...]
    ppermute x15 -> x18, starting transfers between devices: 17.6 us -> 21.2 us  [exchange(): lax.ppermute(pieces[d], 'mod', [(i, i ^ d) for i in range(mod_count)])]
    pallas_call x2 -> x3, Pallas kernels: 13.2 us -> 10.1 us  [attend_slots(): pl.pallas_call(kernel, out_shape=[pltpu.VMEM((len(turns) * block, HDIM),...]
    convert_element_type x4 -> x0, other arithmetic: 1.74 us -> none  [add(): return total.astype(jnp.bfloat16)]
    ppermute x15 -> x18, waiting for transfers between devices: 12.7 us -> 13.3 us  [exchange(): lax.ppermute(pieces[d], 'mod', [(i, i ^ d) for i in range(mod_count)])]
  transfers between devices with their start and end apart: 32 -> 35, of which waited for: 11 -> 12; matrix products, arithmetic and copies ran while one was open for 0% -> 1% of each run, Pallas kernels for 22% -> 23%
where the time goes in v3:
time: 164 us
  waiting for transfers between devices  74.3 us (45%)
  Pallas kernels  47.8 us (29%)
  starting transfers between devices  40.3 us (25%)
    ppermute x8, waiting for transfers between devices, along(): return lax.ppermute(value, 'seq', chip_pairs(pairs))  60.9 us
    ppermute x18, starting transfers between devices, exchange(): lax.ppermute(pieces[d], 'mod', [(i, i ^ d) for i in range(mod_count)])  21.2 us
    ppermute x8, starting transfers between devices, along(): return lax.ppermute(value, 'seq', chip_pairs(pairs))  17.5 us
    ppermute x18, waiting for transfers between devices, exchange(): lax.ppermute(pieces[d], 'mod', [(i, i ^ d) for i in range(mod_count)])  13.3 us
    pallas_call x2, Pallas kernels, project_slots(): pl.pallas_call(kernel, out_shape=[pltpu.VMEM((count * block, cols), jnp.b...  12.7 us
    pallas_call x3, Pallas kernels, attend_slots(): pl.pallas_call(kernel, out_shape=[pltpu.VMEM((len(turns) * block, HDIM),...  10.1 us
    pallas_call x1, Pallas kernels, fetch_weights(): pl.pallas_call(kernel, out_shape=[pltpu.VMEM(shape, jnp.bfloat16)] * coun...  8.91 us
    pallas_call x4, Pallas kernels, output_rows(): pl.pallas_call(kernel, out_shape=[pltpu.VMEM((half, width), jnp.bfloat16)...  6.67 us
  transfers between devices with their start and end apart: 35, of which 12 were waited for; matrix products, arithmetic and copies ran while one was open for 1% of the time, Pallas kernels for 23%

profile of v3, /device:TPU:0, one launch (start us, length us, event | category | flops | bytes accessed | tf_op | source)
XLA Modules:
  0.0 164.2 jit_solution(2527697502703324349)
XLA Ops:
  0.0 0.1 pad_add_fusion.ids_ref
  0.1 2.7 %norm_rows.1 = (bf16[64,4096]{1,0:T(8,128)(2,1)S(1)}, s32[7]{0:T(128)S(1)}) custom-call(s32[3]{0:T(128)S(1)} %pad_add_fusion.ids_ref, s32[16]{0:T(128)} %modality_ref.1, bf16[64,4096]{1,0:T(8,128)(2,1)} %tokens_ref.1, f32[3,4096]{1,0:T(4,128)} %gain_ref.1), custom_call_target="tpu_custom_call" | custom-call | flops 4000000 | bytes 1048576 | tf_op jit(solution)/shard_map/norm_rows/pallas_call | solution.py:173
  2.7 4.1 %collective-permute-start.4 = (bf16[64,4096]{1,0:T(8,128)(2,1)S(1)}, bf16[64,4096]{1,0:T(8,128)(2,1)S(1)}, u32[]{:S(2)}, u32[]{:S(2)}) collective-permute-start(bf16[64,4096]{1,0:T(8,128)(2,1)S(1)} %get-tuple-element.46.refs_0_), channel_id=1, source_target_pairs={{0,4},{1,5},{2,6},{3,7},{4,0},{5,1},{6,2},{7,3},{8,12},{9,13},{10,... | collective-permute-start | bytes 1572872 | tf_op jit(solution)/shard_map/ppermute | solution.py:614
  6.9 1.6 collective-permute-start.6
  8.5 0.7 collective-permute-start.11
  9.1 21.8 %collective-permute-done.4.refs_0_ = bf16[64,4096]{1,0:T(8,128)(2,1)S(1)} collective-permute-done((bf16[64,4096]{1,0:T(8,128)(2,1)S(1)}, bf16[64,4096]{1,0:T(8,128)(2,1)S(1)}, u32[]{:S(2)}, u32[]{:S(2)}) %collective-permute-start.4) | collective-permute-done | bytes 524320 | tf_op jit(solution)/shard_map/ppermute | solution.py:614
  30.9 0.0 collective-permute-start.13
  30.9 0.5 collective-permute-start.5
  31.4 0.0 collective-permute-start.7
  31.5 0.0 collective-permute-done.11.inner_own
  31.5 0.5 collective-permute-start.12
  32.0 11.2 %collective-permute-done.13.relayed_own = bf16[64,4096]{1,0:T(8,128)(2,1)S(1)} collective-permute-done((bf16[64,4096]{1,0:T(8,128)(2,1)S(1)}, bf16[64,4096]{1,0:T(8,128)(2,1)S(1)}, u32[]{:S(2)}, u32[]{:S(2)}) %collective-permute-start.13) | collective-permute-done | bytes 524320 | tf_op jit(solution)/shard_map/ppermute | solution.py:614
  43.2 0.0 collective-permute-start.14
  43.2 8.9 %fetch_weights.1 = (bf16[2,4,1024,768]{3,2,1,0:T(8,128)(2,1)S(1)}, bf16[2,4,1024,768]{3,2,1,0:T(8,128)(2,1)S(1)}) custom-call(s32[7]{0:T(128)S(1)} %get-tuple-element.45.info_ref, bf16[3,4096,1536]{2,1,0:T(8,128)(2,1)} %refs_5_.1), custom_call_target="tpu_custom_call" | custom-call | flops 6000000000 | bytes 26214400 | tf_op jit(solution)/shard_map/fetch_weights/pallas_call | solution.py:231
  52.1 6.3 %project_slots.2 = (bf16[128,384]{1,0:T(8,128)(2,1)S(1)}, bf16[128,384]{1,0:T(8,128)(2,1)S(1)}, bf16[128,384]{1,0:T(8,128)(2,1)S(1)}, bf16[128,384]{1,0:T(8,128)(2,1)S(1)}) custom-call(s32[7]{0:T(128)S(1)} %get-tuple-element.45.info_ref, bf16[64,4096]{1,0:T(8,128)(2,1)S(1)} %get-tuple-element.46.refs_0_, bf16[64,4096]{1,0:T(8,128)(2,1)S(1)} %collective-permute-done.refs_1_, ...), custom_call_target="tpu_custom_call" | custom-call | flops 1610612736 | bytes 12582912 | tf_op jit(solution)/shard_map/project_slots/pallas_call | solution.py:322
  58.4 1.3 collective-permute-start.1
  59.8 6.4 %project_slots.3 = (bf16[256,384]{1,0:T(8,128)(2,1)S(1)}, bf16[256,384]{1,0:T(8,128)(2,1)S(1)}, bf16[256,384]{1,0:T(8,128)(2,1)S(1)}, bf16[256,384]{1,0:T(8,128)(2,1)S(1)}) custom-call(s32[7]{0:T(128)S(1)} %get-tuple-element.45.info_ref, bf16[64,4096]{1,0:T(8,128)(2,1)S(1)} %collective-permute-done.4.refs_0_, ...), custom_call_target="tpu_custom_call" | custom-call | flops 3221225472 | bytes 25165824 | tf_op jit(solution)/shard_map/project_slots/pallas_call | solution.py:322
  66.1 0.8 collective-permute-start.8
  67.0 1.4 collective-permute-start.2
  68.4 1.3 collective-permute-start.3
  69.7 1.5 collective-permute-start.9
  71.2 0.7 collective-permute-start.10
  71.9 2.7 %project_late.1 = (bf16[128,384]{1,0:T(8,128)(2,1)S(1)}, bf16[128,384]{1,0:T(8,128)(2,1)S(1)}, bf16[128,384]{1,0:T(8,128)(2,1)S(1)}, bf16[128,384]{1,0:T(8,128)(2,1)S(1)}, bf16[512,4096]{1,0:T(8,128)(2,1)S(1)}) custom-call(s32[7]{0:T(128)S(1)} %get-tuple-element.45.info_ref, bf16[64,4096]{1,0:T(8,128)(2,1)S(1)} %collective-permute-done.11.inner_own, ...), custom_call_target="tpu_custom_call" | custom-call | flops 1610612736 | bytes 12582912 | tf_op jit(solution)/shard_map/project_late/pallas_call | solution.py:377
  74.7 1.3 collective-permute-start.15
  76.0 1.1 collective-permute-done.3.refs_3_
  77.1 0.5 collective-permute-start.16
  77.7 1.6 collective-permute-start.17
  79.2 6.1 %collective-permute-done.9.refs_6_ = bf16[256,384]{1,0:T(8,128)(2,1)S(1)} collective-permute-done((bf16[256,384]{1,0:T(8,128)(2,1)S(1)}, bf16[256,384]{1,0:T(8,128)(2,1)S(1)}, u32[]{:S(2)}, u32[]{:S(2)}) %collective-permute-start.9) | collective-permute-done | bytes 196640 | tf_op jit(solution)/shard_map/ppermute | solution.py:622
  85.4 1.0 collective-permute-done.16.refs_10_
  86.4 4.6 %attend_slots.4 = (bf16[256,128]{1,0:T(8,128)(2,1)S(1)}, bf16[256,128]{1,0:T(8,128)(2,1)S(1)}, bf16[256,128]{1,0:T(8,128)(2,1)S(1)}, bf16[256,128]{1,0:T(8,128)(2,1)S(1)}, bf16[512,4096]{1,0:T(8,128)(2,1)S(1)}) custom-call(s32[7]{0:T(128)S(1)} %get-tuple-element.45.info_ref, s32[4]{0:T(128)S(1)} %copy-done, bf16[128,384]{1,0:T(8,128)(2,1)S(1)} %get-tuple-element.47.refs_0_, ...), custom_call_target="tpu_custom_call" | custom-call | flops 1207959552 | bytes 1572864 | tf_op jit(solution)/shard_map/attend_slots/pallas_call | solution.py:477
  91.0 1.3 collective-permute-start.22
  92.3 1.5 collective-permute-start.23
  93.8 0.8 collective-permute-start.24
  94.6 1.1 collective-permute-done.22.refs_1_
  95.7 1.6 collective-permute-done.23.refs_2_
  97.3 1.7 %collective-permute-done.24.refs_3_ = bf16[256,128]{1,0:T(8,128)(2,1)S(1)} collective-permute-done((bf16[256,128]{1,0:T(8,128)(2,1)S(1)}, bf16[256,128]{1,0:T(8,128)(2,1)S(1)}, u32[]{:S(2)}, u32[]{:S(2)}) %collective-permute-start.24) | collective-permute-done | bytes 65568 | tf_op jit(solution)/shard_map/ppermute | solution.py:622
  99.0 1.3 output_rows.6
  100.3 0.1 collective-permute-start.27
  100.3 1.3 output_rows.5
  101.6 0.6 collective-permute-start.25
  102.2 2.7 %attend_slots.3 = (bf16[128,128]{1,0:T(8,128)(2,1)S(1)}, bf16[128,128]{1,0:T(8,128)(2,1)S(1)}, bf16[128,128]{1,0:T(8,128)(2,1)S(1)}, bf16[128,128]{1,0:T(8,128)(2,1)S(1)}, bf16[512,4096]{1,0:T(8,128)(2,1)S(1)}) custom-call(s32[7]{0:T(128)S(1)} %get-tuple-element.45.info_ref, s32[4]{0:T(128)S(1)} %copy-done, bf16[128,384]{1,0:T(8,128)(2,1)S(1)} %get-tuple-element.47.refs_0_, ...), custom_call_target="tpu_custom_call" | custom-call | flops 603979776 | bytes 1572864 | tf_op jit(solution)/shard_map/attend_slots/pallas_call | solution.py:477
  104.9 0.9 collective-permute-start.18
  105.8 0.5 collective-permute-start.19
  106.3 2.1 %collective-permute-start.20 = (bf16[128,128]{1,0:T(8,128)(2,1)S(1)}, bf16[128,128]{1,0:T(8,128)(2,1)S(1)}, u32[]{:S(2)}, u32[]{:S(2)}) collective-permute-start(bf16[128,128]{1,0:T(8,128)(2,1)S(1)} %get-tuple-element.64), channel_id=1, source_target_pairs={{0,24},{8,16},{16,8},{24,0},{1,25},{9,17},{17,9},{25,1},{2,26},{10... | collective-permute-start | bytes 98312 | tf_op jit(solution)/shard_map/ppermute | solution.py:622
  108.5 2.7 %attend_slots.5 = (bf16[128,128]{1,0:T(8,128)(2,1)S(1)}, bf16[128,128]{1,0:T(8,128)(2,1)S(1)}, bf16[128,128]{1,0:T(8,128)(2,1)S(1)}, bf16[128,128]{1,0:T(8,128)(2,1)S(1)}, bf16[512,4096]{1,0:T(8,128)(2,1)S(1)}) custom-call(s32[7]{0:T(128)S(1)} %get-tuple-element.45.info_ref, s32[4]{0:T(128)S(1)} %copy-done, bf16[128,384]{1,0:T(8,128)(2,1)S(1)} %get-tuple-element.47.refs_0_, ...), custom_call_target="tpu_custom_call" | custom-call | flops 603979776 | bytes 1572864 | tf_op jit(solution)/shard_map/attend_slots/pallas_call | solution.py:477
  111.2 0.9 collective-permute-start.29
  112.1 0.5 collective-permute-start.30
  112.7 2.1 %collective-permute-start.31 = (bf16[128,128]{1,0:T(8,128)(2,1)S(1)}, bf16[128,128]{1,0:T(8,128)(2,1)S(1)}, u32[]{:S(2)}, u32[]{:S(2)}) collective-permute-start(bf16[128,128]{1,0:T(8,128)(2,1)S(1)} %get-tuple-element.81), channel_id=1, source_target_pairs={{0,24},{8,16},{16,8},{24,0},{1,25},{9,17},{17,9},{25,1},{2,26},{10... | collective-permute-start | bytes 98312 | tf_op jit(solution)/shard_map/ppermute | solution.py:622
  114.8 2.1 %output_rows.4 = (bf16[64,4096]{1,0:T(8,128)(2,1)S(1)}, bf16[64,4096]{1,0:T(8,128)(2,1)}) custom-call(s32[7]{0:T(128)S(1)} %get-tuple-element.45.info_ref, bf16[128,128]{1,0:T(8,128)(2,1)S(1)} %get-tuple-element.61.refs_0_, bf16[128,128]{1,0:T(8,128)(2,1)S(1)} %collective-permute-done.18.refs_1_, bf16[128,128]{1,0:T(8,128)(2,1)S(1)} %collective-permute-done.19.refs_2_, ...), custom_call_target="tpu_custom_call" | custom-call | flops 536870912 | bytes 4194304 | tf_op jit(solution)/shard_map/output_rows/pallas_call | solution.py:519
  116.9 0.6 collective-permute-done.31.refs_3_
  117.5 2.1 %output_rows.7 = (bf16[64,4096]{1,0:T(8,128)(2,1)S(1)}, bf16[64,4096]{1,0:T(8,128)(2,1)}) custom-call(s32[7]{0:T(128)S(1)} %get-tuple-element.45.info_ref, bf16[128,128]{1,0:T(8,128)(2,1)S(1)} %get-tuple-element.78.refs_0_, bf16[128,128]{1,0:T(8,128)(2,1)S(1)} %collective-permute-done.29.refs_1_, bf16[128,128]{1,0:T(8,128)(2,1)S(1)} %collective-permute-done.30.refs_2_, ...), custom_call_target="tpu_custom_call" | custom-call | flops 536870912 | bytes 4194304 | tf_op jit(solution)/shard_map/output_rows/pallas_call | solution.py:519
  119.6 0.7 add_rows.5
  120.2 1.7 %collective-permute-start.28 = (bf16[64,4096]{1,0:T(8,128)(2,1)S(1)}, bf16[64,4096]{1,0:T(8,128)(2,1)S(1)}, u32[]{:S(2)}, u32[]{:S(2)}) collective-permute-start(bf16[64,4096]{1,0:T(8,128)(2,1)S(1)} %add_rows.5), channel_id=1, source_target_pairs={{0,2},{1,3},{2,0},{3,1},{4,6},{5,7},{6,4},{7,5},{8,10},{9,11},{10,... | collective-permute-start | bytes 1572872 | tf_op jit(solution)/shard_map/ppermute | solution.py:614
  122.0 0.7 add_rows.4.refs_0_
  122.6 1.5 collective-permute-start.26
  124.1 0.7 add_rows.6.first_ref
  124.8 4.4 %collective-permute-start.34 = (bf16[64,4096]{1,0:T(8,128)(2,1)S(1)}, bf16[64,4096]{1,0:T(8,128)(2,1)S(1)}, u32[]{:S(2)}, u32[]{:S(2)}) collective-permute-start(bf16[64,4096]{1,0:T(8,128)(2,1)S(1)} %add_rows.6.first_ref), channel_id=1, source_target_pairs={{0,2},{1,3},{2,0},{3,1},{4,6},{5,7},{6,4},{7,5},{8,10},{9,11},{10,... | collective-permute-start | bytes 1572872 | tf_op jit(solution)/shard_map/ppermute | solution.py:614
  129.2 5.9 %collective-permute-done.28.second_ref = bf16[64,4096]{1,0:T(8,128)(2,1)S(1)} collective-permute-done((bf16[64,4096]{1,0:T(8,128)(2,1)S(1)}, bf16[64,4096]{1,0:T(8,128)(2,1)S(1)}, u32[]{:S(2)}, u32[]{:S(2)}) %collective-permute-start.28) | collective-permute-done | bytes 524320 | tf_op jit(solution)/shard_map/ppermute | solution.py:614
  135.1 0.6 add_rows.7
  135.7 3.4 %collective-permute-start.33 = (bf16[64,4096]{1,0:T(8,128)(2,1)S(1)}, bf16[64,4096]{1,0:T(8,128)(2,1)S(1)}, u32[]{:S(2)}, u32[]{:S(2)}) collective-permute-start(bf16[64,4096]{1,0:T(8,128)(2,1)S(1)} %add_rows.7), channel_id=1, source_target_pairs={{0,4},{1,5},{2,6},{3,7},{4,0},{5,1},{6,2},{7,3},{8,12},{9,13},{10,... | collective-permute-start | bytes 1572872 | tf_op jit(solution)/shard_map/ppermute | solution.py:614
  139.1 1.5 convert_add_fusion.early_ref
  140.7 13.7 %collective-permute-done.34.middle_ref = bf16[64,4096]{1,0:T(8,128)(2,1)S(1)} collective-permute-done((bf16[64,4096]{1,0:T(8,128)(2,1)S(1)}, bf16[64,4096]{1,0:T(8,128)(2,1)S(1)}, u32[]{:S(2)}, u32[]{:S(2)}) %collective-permute-start.34) | collective-permute-done | bytes 524320 | tf_op jit(solution)/shard_map/ppermute | solution.py:614
  154.3 8.4 %collective-permute-done.33.far_ref = bf16[64,4096]{1,0:T(8,128)(2,1)S(1)} collective-permute-done((bf16[64,4096]{1,0:T(8,128)(2,1)S(1)}, bf16[64,4096]{1,0:T(8,128)(2,1)S(1)}, u32[]{:S(2)}, u32[]{:S(2)}) %collective-permute-start.33) | collective-permute-done | bytes 524320 | tf_op jit(solution)/shard_map/ppermute | solution.py:614
  162.7 1.4 last_rows.1
  (27 shorter events, 0.1 us)
Async XLA Ops:
  2.7 28.2 %collective-permute-start.4 = (bf16[64,4096]{1,0:T(8,128)(2,1)S(1)}, bf16[64,4096]{1,0:T(8,128)(2,1)S(1)}, u32[]{:S(2)}, u32[]{:S(2)}) collective-permute-start(bf16[64,4096]{1,0:T(8,128)(2,1)S(1)} %get-tuple-element.46.refs_0_), channel_id=1, source_target_pairs={{0,4},{1,5},{2,6},{3,7},{4,0},{5,1},{6,2},{7,3},{8,12},{9,13},{10,... | collective-permute-start | bytes 1572872 | tf_op jit(solution)/shard_map/ppermute | solution.py:614
  6.9 24.6 %collective-permute-start.6 = (bf16[64,4096]{1,0:T(8,128)(2,1)S(1)}, bf16[64,4096]{1,0:T(8,128)(2,1)S(1)}, u32[]{:S(2)}, u32[]{:S(2)}) collective-permute-start(bf16[64,4096]{1,0:T(8,128)(2,1)S(1)} %get-tuple-element.46.refs_0_), channel_id=1, source_target_pairs={{0,2},{1,3},{2,0},{3,1},{4,6},{5,7},{6,4},{7,5},{8,10},{9,11},{10,... | collective-permute-start | bytes 1572872 | tf_op jit(solution)/shard_map/ppermute | solution.py:614
  8.5 23.0 %collective-permute-start.11 = (bf16[64,4096]{1,0:T(8,128)(2,1)S(1)}, bf16[64,4096]{1,0:T(8,128)(2,1)S(1)}, u32[]{:S(2)}, u32[]{:S(2)}) collective-permute-start(bf16[64,4096]{1,0:T(8,128)(2,1)S(1)} %get-tuple-element.46.refs_0_), channel_id=1, source_target_pairs={{2,4},{3,5},{4,2},{5,3},{10,12},{11,13},{12,10},{13,11},{18,20},{1... | collective-permute-start | bytes 1572872 | tf_op jit(solution)/shard_map/ppermute | solution.py:614
  30.9 12.2 %collective-permute-start.13 = (bf16[64,4096]{1,0:T(8,128)(2,1)S(1)}, bf16[64,4096]{1,0:T(8,128)(2,1)S(1)}, u32[]{:S(2)}, u32[]{:S(2)}) collective-permute-start(bf16[64,4096]{1,0:T(8,128)(2,1)S(1)} %collective-permute-done.4.refs_0_), channel_id=1, source_target_pairs={{0,2},{1,3},{2,0},{3,1},{4,6},{5,7},{6,4},{7,5},{8,10},{9,11},{10,... | collective-permute-start | bytes 1572872 | tf_op jit(solution)/shard_map/ppermute | solution.py:614
  30.9 21.2 %collective-permute-start = (bf16[64,4096]{1,0:T(8,128)(2,1)S(1)}, bf16[64,4096]{1,0:T(8,128)(2,1)S(1)}, u32[]{:S(2)}, u32[]{:S(2)}) collective-permute-start(bf16[64,4096]{1,0:T(8,128)(2,1)S(1)} %get-tuple-element.46.refs_0_), channel_id=1, source_target_pairs={{0,1},{1,0},{2,3},{3,2},{4,5},{5,4},{6,7},{7,6},{8,9},{9,8},{10,11... | collective-permute-start | bytes 1572872 | tf_op jit(solution)/shard_map/ppermute | solution.py:617
  30.9 28.8 %collective-permute-start.5 = (bf16[64,4096]{1,0:T(8,128)(2,1)S(1)}, bf16[64,4096]{1,0:T(8,128)(2,1)S(1)}, u32[]{:S(2)}, u32[]{:S(2)}) collective-permute-start(bf16[64,4096]{1,0:T(8,128)(2,1)S(1)} %collective-permute-done.4.refs_0_), channel_id=1, source_target_pairs={{0,1},{1,0},{2,3},{3,2},{4,5},{5,4},{6,7},{7,6},{8,9},{9,8},{10,11... | collective-permute-start | bytes 1572872 | tf_op jit(solution)/shard_map/ppermute | solution.py:617
  31.4 28.3 %collective-permute-start.7 = (bf16[64,4096]{1,0:T(8,128)(2,1)S(1)}, bf16[64,4096]{1,0:T(8,128)(2,1)S(1)}, u32[]{:S(2)}, u32[]{:S(2)}) collective-permute-start(bf16[64,4096]{1,0:T(8,128)(2,1)S(1)} %collective-permute-done.6.refs_2_), channel_id=1, source_target_pairs={{0,1},{1,0},{2,3},{3,2},{4,5},{5,4},{6,7},{7,6},{8,9},{9,8},{10,11... | collective-permute-start | bytes 1572872 | tf_op jit(solution)/shard_map/ppermute | solution.py:617
  31.5 38.2 %collective-permute-start.12 = (bf16[64,4096]{1,0:T(8,128)(2,1)S(1)}, bf16[64,4096]{1,0:T(8,128)(2,1)S(1)}, u32[]{:S(2)}, u32[]{:S(2)}) collective-permute-start(bf16[64,4096]{1,0:T(8,128)(2,1)S(1)} %collective-permute-done.11.inner_own), channel_id=1, source_target_pairs={{0,1},{1,0},{2,3},{3,2},{4,5},{5,4},{6,7},{7,6},{8,9},{9,8},{10,11... | collective-permute-start | bytes 1572872 | tf_op jit(solution)/shard_map/ppermute | solution.py:617
  43.2 28.1 %collective-permute-start.14 = (bf16[64,4096]{1,0:T(8,128)(2,1)S(1)}, bf16[64,4096]{1,0:T(8,128)(2,1)S(1)}, u32[]{:S(2)}, u32[]{:S(2)}) collective-permute-start(bf16[64,4096]{1,0:T(8,128)(2,1)S(1)} %collective-permute-done.13.relayed_own), channel_id=1, source_target_pairs={{0,1},{1,0},{2,3},{3,2},{4,5},{5,4},{6,7},{7,6},{8,9},{9,8},{10,11... | collective-permute-start | bytes 1572872 | tf_op jit(solution)/shard_map/ppermute | solution.py:617
  58.4 9.9 %collective-permute-start.1 = (bf16[128,384]{1,0:T(8,128)(2,1)S(1)}, bf16[128,384]{1,0:T(8,128)(2,1)S(1)}, u32[]{:S(2)}, u32[]{:S(2)}) collective-permute-start(bf16[128,384]{1,0:T(8,128)(2,1)S(1)} %get-tuple-element.48), channel_id=1, source_target_pairs={{0,8},{8,0},{16,24},{24,16},{1,9},{9,1},{17,25},{25,17},{2,10},{10... | collective-permute-start | bytes 294920 | tf_op jit(solution)/shard_map/ppermute | solution.py:622
  66.1 11.5 %collective-permute-start.8 = (bf16[256,384]{1,0:T(8,128)(2,1)S(1)}, bf16[256,384]{1,0:T(8,128)(2,1)S(1)}, u32[]{:S(2)}, u32[]{:S(2)}) collective-permute-start(bf16[256,384]{1,0:T(8,128)(2,1)S(1)} %get-tuple-element.53), channel_id=1, source_target_pairs={{0,8},{8,0},{16,24},{24,16},{1,9},{9,1},{17,25},{25,17},{2,10},{10... | collective-permute-start | bytes 589832 | tf_op jit(solution)/shard_map/ppermute | solution.py:622
  67.0 7.7 %collective-permute-start.2 = (bf16[128,384]{1,0:T(8,128)(2,1)S(1)}, bf16[128,384]{1,0:T(8,128)(2,1)S(1)}, u32[]{:S(2)}, u32[]{:S(2)}) collective-permute-start(bf16[128,384]{1,0:T(8,128)(2,1)S(1)} %get-tuple-element.49), channel_id=1, source_target_pairs={{0,16},{8,24},{16,0},{24,8},{1,17},{9,25},{17,1},{25,9},{2,18},{10... | collective-permute-start | bytes 294920 | tf_op jit(solution)/shard_map/ppermute | solution.py:622
  68.4 8.8 %collective-permute-start.3 = (bf16[128,384]{1,0:T(8,128)(2,1)S(1)}, bf16[128,384]{1,0:T(8,128)(2,1)S(1)}, u32[]{:S(2)}, u32[]{:S(2)}) collective-permute-start(bf16[128,384]{1,0:T(8,128)(2,1)S(1)} %get-tuple-element.50), channel_id=1, source_target_pairs={{0,24},{8,16},{16,8},{24,0},{1,25},{9,17},{17,9},{25,1},{2,26},{10... | collective-permute-start | bytes 294920 | tf_op jit(solution)/shard_map/ppermute | solution.py:622
  69.7 15.7 %collective-permute-start.9 = (bf16[256,384]{1,0:T(8,128)(2,1)S(1)}, bf16[256,384]{1,0:T(8,128)(2,1)S(1)}, u32[]{:S(2)}, u32[]{:S(2)}) collective-permute-start(bf16[256,384]{1,0:T(8,128)(2,1)S(1)} %get-tuple-element.54), channel_id=1, source_target_pairs={{0,16},{8,24},{16,0},{24,8},{1,17},{9,25},{17,1},{25,9},{2,18},{10... | collective-permute-start | bytes 589832 | tf_op jit(solution)/shard_map/ppermute | solution.py:622
  71.2 14.2 %collective-permute-start.10 = (bf16[256,384]{1,0:T(8,128)(2,1)S(1)}, bf16[256,384]{1,0:T(8,128)(2,1)S(1)}, u32[]{:S(2)}, u32[]{:S(2)}) collective-permute-start(bf16[256,384]{1,0:T(8,128)(2,1)S(1)} %get-tuple-element.55), channel_id=1, source_target_pairs={{0,24},{8,16},{16,8},{24,0},{1,25},{9,17},{17,9},{25,1},{2,26},{10... | collective-permute-start | bytes 589832 | tf_op jit(solution)/shard_map/ppermute | solution.py:622
  71.9 14.5 %copy-start = (s32[4]{0:T(128)S(1)}, s32[4]{0:T(128)}, u32[]{:S(2)}) copy-start(s32[4]{0:T(128)} %docs_ref.5) | copy-start | bytes 52
  74.7 10.7 %collective-permute-start.15 = (bf16[128,384]{1,0:T(8,128)(2,1)S(1)}, bf16[128,384]{1,0:T(8,128)(2,1)S(1)}, u32[]{:S(2)}, u32[]{:S(2)}) collective-permute-start(bf16[128,384]{1,0:T(8,128)(2,1)S(1)} %get-tuple-element.58), channel_id=1, source_target_pairs={{0,8},{8,0},{16,24},{24,16},{1,9},{9,1},{17,25},{25,17},{2,10},{10... | collective-permute-start | bytes 294920 | tf_op jit(solution)/shard_map/ppermute | solution.py:622
  77.1 9.3 %collective-permute-start.16 = (bf16[128,384]{1,0:T(8,128)(2,1)S(1)}, bf16[128,384]{1,0:T(8,128)(2,1)S(1)}, u32[]{:S(2)}, u32[]{:S(2)}) collective-permute-start(bf16[128,384]{1,0:T(8,128)(2,1)S(1)} %get-tuple-element.59), channel_id=1, source_target_pairs={{0,16},{8,24},{16,0},{24,8},{1,17},{9,25},{17,1},{25,9},{2,18},{10... | collective-permute-start | bytes 294920 | tf_op jit(solution)/shard_map/ppermute | solution.py:622
  77.7 8.8 %collective-permute-start.17 = (bf16[128,384]{1,0:T(8,128)(2,1)S(1)}, bf16[128,384]{1,0:T(8,128)(2,1)S(1)}, u32[]{:S(2)}, u32[]{:S(2)}) collective-permute-start(bf16[128,384]{1,0:T(8,128)(2,1)S(1)} %get-tuple-element.60), channel_id=1, source_target_pairs={{0,24},{8,16},{16,8},{24,0},{1,25},{9,17},{17,9},{25,1},{2,26},{10... | collective-permute-start | bytes 294920 | tf_op jit(solution)/shard_map/ppermute | solution.py:622
  91.0 4.7 %collective-permute-start.22 = (bf16[256,128]{1,0:T(8,128)(2,1)S(1)}, bf16[256,128]{1,0:T(8,128)(2,1)S(1)}, u32[]{:S(2)}, u32[]{:S(2)}) collective-permute-start(bf16[256,128]{1,0:T(8,128)(2,1)S(1)} %get-tuple-element.69), channel_id=1, source_target_pairs={{0,8},{8,0},{16,24},{24,16},{1,9},{9,1},{17,25},{25,17},{2,10},{10... | collective-permute-start | bytes 196616 | tf_op jit(solution)/shard_map/ppermute | solution.py:622
  92.3 5.0 %collective-permute-start.23 = (bf16[256,128]{1,0:T(8,128)(2,1)S(1)}, bf16[256,128]{1,0:T(8,128)(2,1)S(1)}, u32[]{:S(2)}, u32[]{:S(2)}) collective-permute-start(bf16[256,128]{1,0:T(8,128)(2,1)S(1)} %get-tuple-element.70), channel_id=1, source_target_pairs={{0,16},{8,24},{16,0},{24,8},{1,17},{9,25},{17,1},{25,9},{2,18},{10... | collective-permute-start | bytes 196616 | tf_op jit(solution)/shard_map/ppermute | solution.py:622
  93.8 5.2 %collective-permute-start.24 = (bf16[256,128]{1,0:T(8,128)(2,1)S(1)}, bf16[256,128]{1,0:T(8,128)(2,1)S(1)}, u32[]{:S(2)}, u32[]{:S(2)}) collective-permute-start(bf16[256,128]{1,0:T(8,128)(2,1)S(1)} %get-tuple-element.71), channel_id=1, source_target_pairs={{0,24},{8,16},{16,8},{24,0},{1,25},{9,17},{17,9},{25,1},{2,26},{10... | collective-permute-start | bytes 196616 | tf_op jit(solution)/shard_map/ppermute | solution.py:622
  100.3 19.3 %collective-permute-start.27 = (bf16[64,4096]{1,0:T(8,128)(2,1)S(1)}, bf16[64,4096]{1,0:T(8,128)(2,1)S(1)}, u32[]{:S(2)}, u32[]{:S(2)}) collective-permute-start(bf16[64,4096]{1,0:T(8,128)(2,1)S(1)} %get-tuple-element.77), channel_id=1, source_target_pairs={{0,1},{1,0},{2,3},{3,2},{4,5},{5,4},{6,7},{7,6},{8,9},{9,8},{10,11... | collective-permute-start | bytes 1572872 | tf_op jit(solution)/shard_map/ppermute | solution.py:617
  101.6 20.3 %collective-permute-start.25 = (bf16[64,4096]{1,0:T(8,128)(2,1)S(1)}, bf16[64,4096]{1,0:T(8,128)(2,1)S(1)}, u32[]{:S(2)}, u32[]{:S(2)}) collective-permute-start(bf16[64,4096]{1,0:T(8,128)(2,1)S(1)} %get-tuple-element.74), channel_id=1, source_target_pairs={{0,1},{1,0},{2,3},{3,2},{4,5},{5,4},{6,7},{7,6},{8,9},{9,8},{10,11... | collective-permute-start | bytes 1572872 | tf_op jit(solution)/shard_map/ppermute | solution.py:617
  104.9 6.3 %collective-permute-start.18 = (bf16[128,128]{1,0:T(8,128)(2,1)S(1)}, bf16[128,128]{1,0:T(8,128)(2,1)S(1)}, u32[]{:S(2)}, u32[]{:S(2)}) collective-permute-start(bf16[128,128]{1,0:T(8,128)(2,1)S(1)} %get-tuple-element.62), channel_id=1, source_target_pairs={{0,8},{8,0},{16,24},{24,16},{1,9},{9,1},{17,25},{25,17},{2,10},{10... | collective-permute-start | bytes 98312 | tf_op jit(solution)/shard_map/ppermute | solution.py:622
  105.8 6.3 %collective-permute-start.19 = (bf16[128,128]{1,0:T(8,128)(2,1)S(1)}, bf16[128,128]{1,0:T(8,128)(2,1)S(1)}, u32[]{:S(2)}, u32[]{:S(2)}) collective-permute-start(bf16[128,128]{1,0:T(8,128)(2,1)S(1)} %get-tuple-element.63), channel_id=1, source_target_pairs={{0,16},{8,24},{16,0},{24,8},{1,17},{9,25},{17,1},{25,9},{2,18},{10... | collective-permute-start | bytes 98312 | tf_op jit(solution)/shard_map/ppermute | solution.py:622
  106.3 6.3 %collective-permute-start.20 = (bf16[128,128]{1,0:T(8,128)(2,1)S(1)}, bf16[128,128]{1,0:T(8,128)(2,1)S(1)}, u32[]{:S(2)}, u32[]{:S(2)}) collective-permute-start(bf16[128,128]{1,0:T(8,128)(2,1)S(1)} %get-tuple-element.64), channel_id=1, source_target_pairs={{0,24},{8,16},{16,8},{24,0},{1,25},{9,17},{17,9},{25,1},{2,26},{10... | collective-permute-start | bytes 98312 | tf_op jit(solution)/shard_map/ppermute | solution.py:622
  111.2 5.6 %collective-permute-start.29 = (bf16[128,128]{1,0:T(8,128)(2,1)S(1)}, bf16[128,128]{1,0:T(8,128)(2,1)S(1)}, u32[]{:S(2)}, u32[]{:S(2)}) collective-permute-start(bf16[128,128]{1,0:T(8,128)(2,1)S(1)} %get-tuple-element.79), channel_id=1, source_target_pairs={{0,8},{8,0},{16,24},{24,16},{1,9},{9,1},{17,25},{25,17},{2,10},{10... | collective-permute-start | bytes 98312 | tf_op jit(solution)/shard_map/ppermute | solution.py:622
  112.1 4.7 %collective-permute-start.30 = (bf16[128,128]{1,0:T(8,128)(2,1)S(1)}, bf16[128,128]{1,0:T(8,128)(2,1)S(1)}, u32[]{:S(2)}, u32[]{:S(2)}) collective-permute-start(bf16[128,128]{1,0:T(8,128)(2,1)S(1)} %get-tuple-element.80), channel_id=1, source_target_pairs={{0,16},{8,24},{16,0},{24,8},{1,17},{9,25},{17,1},{25,9},{2,18},{10... | collective-permute-start | bytes 98312 | tf_op jit(solution)/shard_map/ppermute | solution.py:622
  112.7 4.8 %collective-permute-start.31 = (bf16[128,128]{1,0:T(8,128)(2,1)S(1)}, bf16[128,128]{1,0:T(8,128)(2,1)S(1)}, u32[]{:S(2)}, u32[]{:S(2)}) collective-permute-start(bf16[128,128]{1,0:T(8,128)(2,1)S(1)} %get-tuple-element.81), channel_id=1, source_target_pairs={{0,24},{8,16},{16,8},{24,0},{1,25},{9,17},{17,9},{25,1},{2,26},{10... | collective-permute-start | bytes 98312 | tf_op jit(solution)/shard_map/ppermute | solution.py:622
  116.9 22.3 %collective-permute-start.21 = (bf16[64,4096]{1,0:T(8,128)(2,1)}, bf16[64,4096]{1,0:T(8,128)(2,1)}, u32[]{:S(2)}, u32[]{:S(2)}) collective-permute-start(bf16[64,4096]{1,0:T(8,128)(2,1)} %get-tuple-element.67), channel_id=1, source_target_pairs={{0,1},{1,0},{2,3},{3,2},{4,5},{5,4},{6,7},{7,6},{8,9},{9,8},{10,11... | collective-permute-start | bytes 1572872 | tf_op jit(solution)/shard_map/ppermute | solution.py:617
  119.6 4.6 %collective-permute-start.32 = (bf16[64,4096]{1,0:T(8,128)(2,1)}, bf16[64,4096]{1,0:T(8,128)(2,1)S(1)}, u32[]{:S(2)}, u32[]{:S(2)}) collective-permute-start(bf16[64,4096]{1,0:T(8,128)(2,1)} %get-tuple-element.84), channel_id=1, source_target_pairs={{0,1},{1,0},{2,3},{3,2},{4,5},{5,4},{6,7},{7,6},{8,9},{9,8},{10,11... | collective-permute-start | bytes 1572872 | tf_op jit(solution)/shard_map/ppermute | solution.py:617
  120.2 14.9 %collective-permute-start.28 = (bf16[64,4096]{1,0:T(8,128)(2,1)S(1)}, bf16[64,4096]{1,0:T(8,128)(2,1)S(1)}, u32[]{:S(2)}, u32[]{:S(2)}) collective-permute-start(bf16[64,4096]{1,0:T(8,128)(2,1)S(1)} %add_rows.5), channel_id=1, source_target_pairs={{0,2},{1,3},{2,0},{3,1},{4,6},{5,7},{6,4},{7,5},{8,10},{9,11},{10,... | collective-permute-start | bytes 1572872 | tf_op jit(solution)/shard_map/ppermute | solution.py:614
  122.6 16.5 %collective-permute-start.26 = (bf16[64,4096]{1,0:T(8,128)(2,1)S(1)}, bf16[64,4096]{1,0:T(8,128)(2,1)}, u32[]{:S(2)}, u32[]{:S(2)}) collective-permute-start(bf16[64,4096]{1,0:T(8,128)(2,1)S(1)} %add_rows.4.refs_0_), channel_id=1, source_target_pairs={{2,4},{3,5},{4,2},{5,3},{10,12},{11,13},{12,10},{13,11},{18,20},{1... | collective-permute-start | bytes 1572872 | tf_op jit(solution)/shard_map/ppermute | solution.py:614
  124.8 29.5 %collective-permute-start.34 = (bf16[64,4096]{1,0:T(8,128)(2,1)S(1)}, bf16[64,4096]{1,0:T(8,128)(2,1)S(1)}, u32[]{:S(2)}, u32[]{:S(2)}) collective-permute-start(bf16[64,4096]{1,0:T(8,128)(2,1)S(1)} %add_rows.6.first_ref), channel_id=1, source_target_pairs={{0,2},{1,3},{2,0},{3,1},{4,6},{5,7},{6,4},{7,5},{8,10},{9,11},{10,... | collective-permute-start | bytes 1572872 | tf_op jit(solution)/shard_map/ppermute | solution.py:614
  135.7 27.0 %collective-permute-start.33 = (bf16[64,4096]{1,0:T(8,128)(2,1)S(1)}, bf16[64,4096]{1,0:T(8,128)(2,1)S(1)}, u32[]{:S(2)}, u32[]{:S(2)}) collective-permute-start(bf16[64,4096]{1,0:T(8,128)(2,1)S(1)} %add_rows.7), channel_id=1, source_target_pairs={{0,4},{1,5},{2,6},{3,7},{4,0},{5,1},{6,2},{7,3},{8,12},{9,13},{10,... | collective-permute-start | bytes 1572872 | tf_op jit(solution)/shard_map/ppermute | solution.py:614

commit v4 on v3

--- a/solution.py
+++ b/solution.py
@@ -191,38 +191,41 @@
     )(ids, modality, tokens, norm_gain)
 
 
-def weight_copies(info_ref, weight_ref, buffer_ref, sems, slot):
-    pairs, pieces, piece, pair_cols = buffer_ref.shape
-    copies = {}
-    for p in range(pairs):
-        first = jnp.bitwise_xor(info_ref[0] // 2, p) * pair_cols
-        for k in range(pieces):
-            copies[p, k] = pltpu.make_async_copy(
-                weight_ref.at[
-                    mode_of(info_ref, slot),
-                    pl.ds(k * piece, piece),
-                    pl.ds(pl.multiple_of(first, 128), pair_cols),
-                ],
-                buffer_ref.at[p, k],
-                sems.at[p, k],
+def weight_copies(info_ref, weight_ref, buffer_ref, sems, slot, pair, at):
+    pieces, piece, pair_cols = buffer_ref.shape[1:]
+    first = jnp.bitwise_xor(info_ref[0] // 2, pair) * pair_cols
+    return [
+        pltpu.make_async_copy(
+            weight_ref.at[
+                mode_of(info_ref, slot),
+                pl.ds(k * piece, piece),
+                pl.ds(pl.multiple_of(first, 128), pair_cols),
+            ],
+            buffer_ref.at[at, k],
+            sems.at[at, k],
+        )
+        for k in range(pieces)
+    ]
+
+
+def weight_shape(weight, pairs):
+    width, cols = weight.shape[1:]
+    return (pairs, PIECES, width // PIECES, cols // 2)
+
+
+def fetch_weights(info, weight, ahead):
+    shapes = [weight_shape(weight, n_pairs) for _, n_pairs in ahead]
+    count = len(ahead)
+
+    def kernel(info_ref, weight_ref, *refs):
+        copies = [
+            copy
+            for i, (slot, n_pairs) in enumerate(ahead)
+            for p in range(n_pairs)
+            for copy in weight_copies(
+                info_ref, weight_ref, refs[i], refs[count + i], slot, p, p
             )
-    return copies
-
-
-def weight_shape(weight):
-    width, cols = weight.shape[1:]
-    return (2, PIECES, width // PIECES, cols // 2)
-
-
-def fetch_weights(info, qkv_weight, slots):
-    shape = weight_shape(qkv_weight)
-    count = len(slots)
-
-    def kernel(info_ref, qkv_ref, *refs):
-        sems = refs[count]
-        copies = []
-        for i, slot in enumerate(slots):
-            copies += weight_copies(info_ref, qkv_ref, refs[i], sems.at[i], slot).values()
+        ]
         for copy in copies:
             copy.start()
         for copy in copies:
@@ -230,16 +233,16 @@
 
     return pl.pallas_call(
         kernel,
-        out_shape=[pltpu.VMEM(shape, jnp.bfloat16)] * count,
+        out_shape=[pltpu.VMEM(shape, jnp.bfloat16) for shape in shapes],
         in_specs=[SMEM, HBM],
         out_specs=[VMEM] * count,
-        scratch_shapes=[pltpu.SemaphoreType.DMA((count, *shape[:2]))],
+        scratch_shapes=[pltpu.SemaphoreType.DMA(shape[:2]) for shape in shapes],
         compiler_params=params(1),
         cost_estimate=pl.CostEstimate(
             flops=6_000_000_000, bytes_accessed=25 << 20, transcendentals=0
         ),
         name="fetch_weights",
-    )(info, qkv_weight)
+    )(info, weight)
 
 
 class Prefetch:
@@ -278,57 +281,73 @@
         outs[2 * p + e][rows, :] = jnp.where(odd, last, first)
 
 
-def project_slots(info, parts, weight, slots, ready=()):
+def project_slots(info, parts, weight, slots, ready=(), ahead=()):
     half, width = parts[0][0].shape
     block = 2 * half
     cols = 3 * HDIM
     heads = weight.shape[2] // cols
-    shape = weight_shape(weight)
-    pairs, pieces, piece, _ = shape
+    pairs = 2
     count, given = len(slots), len(ready)
+    steps = [(n, p) for n in range(count) for p in range(pairs)]
+    places = [(i, j) for i, array in enumerate(ready) for j in range(array.shape[0])]
+    streamed = steps[len(places) :]
+    shape = weight_shape(weight, len(streamed))
+    ahead_shapes = [weight_shape(weight, n_pairs) for _, n_pairs in ahead]
 
     def kernel(info_ref, *refs):
         ins, refs = refs[: 2 * count], refs[2 * count :]
         ready_refs, weight_ref, refs = refs[:given], refs[given], refs[given + 1 :]
-        outs, (buffer_ref, sems) = refs[:heads], refs[heads:]
-        fetched = [
-            weight_copies(info_ref, weight_ref, buffer_ref, sems, slot) for slot in slots[given:]
+        outs, refs = refs[:heads], refs[heads:]
+        ahead_refs, refs = refs[: len(ahead)], refs[len(ahead) :]
+        buffer_ref, sems, ahead_sems = refs[0], refs[1], refs[2:]
+        fetched = {
+            step: weight_copies(info_ref, weight_ref, buffer_ref, sems, slots[step[0]], step[1], i)
+            for i, step in enumerate(streamed)
+        }
+        later = [
+            copy
+            for i, (slot, n_pairs) in enumerate(ahead)
+            for p in range(n_pairs)
+            for copy in weight_copies(
+                info_ref, weight_ref, ahead_refs[i], ahead_sems[i], slot, p, p
+            )
         ]
-        for copy in fetched[0].values():
+        for copy in [copy for copies in fetched.values() for copy in copies] + later:
             copy.start()
 
-        def project(n):
-            source_ref = ready_refs[n] if n < given else buffer_ref
-            for p in range(pairs):
+        @pl.when(info_ref[1] >= 0)
+        def _():
+            for i, (n, p) in enumerate(steps):
                 result = None
-                for k in range(pieces):
-                    if n >= given:
-                        fetched[n - given][p, k].wait()
+                piece = width // PIECES
+                for k in range(PIECES):
+                    if (n, p) in fetched:
+                        fetched[n, p][k].wait()
+                        part_ref, at = buffer_ref, streamed.index((n, p))
+                    else:
+                        part_ref, at = ready_refs[places[i][0]], places[i][1]
                     rows = jnp.concatenate(
                         [ins[2 * n + i][:, k * piece : (k + 1) * piece] for i in range(2)], axis=0
                     )
-                    part = jnp.dot(rows, source_ref[p, k], preferred_element_type=jnp.float32)
+                    part = jnp.dot(rows, part_ref[at, k], preferred_element_type=jnp.float32)
                     result = part if result is None else result + part
-                    if given <= n < count - 1:
-                        fetched[n - given + 1][p, k].start()
                 store_pair(info_ref, outs, pl.ds(n * block, block), p, result)
 
-        for n in range(count):
-            if n < given:
-                pl.when(info_ref[1] >= 0)(lambda: project(n))
-            else:
-                project(n)
-
-    return pl.pallas_call(
-        kernel,
-        out_shape=[pltpu.VMEM((count * block, cols), jnp.bfloat16)] * heads,
+        for copy in later:
+            copy.wait()
+
+    return pl.pallas_call(
+        kernel,
+        out_shape=[pltpu.VMEM((count * block, cols), jnp.bfloat16)] * heads
+        + [pltpu.VMEM(ahead_shape, jnp.bfloat16) for ahead_shape in ahead_shapes],
         in_specs=[SMEM] + [VMEM] * (2 * count + given) + [HBM],
-        out_specs=[VMEM] * heads,
+        out_specs=[VMEM] * (heads + len(ahead)),
         scratch_shapes=[
             pltpu.VMEM(shape, jnp.bfloat16),
             pltpu.SemaphoreType.DMA(shape[:2]),
-        ],
-        compiler_params=params(16),
+        ]
+        + [pltpu.SemaphoreType.DMA(ahead_shape[:2]) for ahead_shape in ahead_shapes],
+        compiler_params=params(4 + 3 * len(streamed) * 2),
         cost_estimate=pl.CostEstimate(
             flops=2 * count * block * width * cols * heads,
             bytes_accessed=count * width * cols * heads * 2,
@@ -532,68 +551,91 @@
     )(info, *pieces, weight)
 
 
-def add_rows(info, chips, first, second, otherwise=None):
-    values = [first, second] + ([] if otherwise is None else [otherwise])
-    values = [pltpu.with_memory_space_constraint(value, pltpu.VMEM) for value in values]
-
-    def kernel(info_ref, first_ref, second_ref, *refs):
-        def add():
-            total = first_ref[...].astype(jnp.float32) + second_ref[...].astype(jnp.float32)
-            refs[-1][...] = total.astype(jnp.bfloat16)
-
-        if otherwise is None:
-            add()
-            return
-        middle = is_middle(info_ref, chips)
-        pl.when(middle)(lambda: add())
-
-        @pl.when(jnp.logical_not(middle))
-        def _():
-            refs[-1][...] = refs[0][...]
+def in_vmem(*values):
+    return [pltpu.with_memory_space_constraint(value, pltpu.VMEM) for value in values]
+
+
+def add_rows(first, second):
+    def kernel(first_ref, second_ref, out_ref):
+        total = first_ref[...].astype(jnp.float32) + second_ref[...].astype(jnp.float32)
+        out_ref[...] = total.astype(jnp.bfloat16)
 
     return pl.pallas_call(
         kernel,
         out_shape=pltpu.VMEM(first.shape, jnp.bfloat16),
-        in_specs=[SMEM] + [VMEM] * len(values),
+        in_specs=[VMEM, VMEM],
         out_specs=VMEM,
         compiler_params=params(4),
         cost_estimate=pl.CostEstimate(
             flops=4 * first.size, bytes_accessed=6 * first.size, transcendentals=0
         ),
         name="add_rows",
-    )(info, *values)
-
-
-def last_rows(info, chips, early, far, middle_only):
-    values = [
-        pltpu.with_memory_space_constraint(value, pltpu.VMEM)
-        for value in (early, far, middle_only)
-    ]
-
-    def kernel(info_ref, early_ref, far_ref, middle_ref, out_ref):
+    )(*in_vmem(first, second))
+
+
+def relay_rows(info, chips, own, partner, passing, otherwise):
+    def kernel(info_ref, own_ref, partner_ref, passing_ref, otherwise_ref, sum_ref, relay_ref):
         middle = is_middle(info_ref, chips)
 
         @pl.when(middle)
         def _():
-            total = early_ref[...] + far_ref[...].astype(jnp.float32)
-            out_ref[...] = (total + middle_ref[...].astype(jnp.float32)).astype(jnp.bfloat16)
+            total = own_ref[...].astype(jnp.float32) + partner_ref[...].astype(jnp.float32)
+            sum_ref[...] = total.astype(jnp.bfloat16)
+            total = total + passing_ref[...].astype(jnp.float32)
+            relay_ref[...] = total.astype(jnp.bfloat16)
 
         @pl.when(jnp.logical_not(middle))
         def _():
-            total = early_ref[...] + far_ref[...].astype(jnp.float32)
-            out_ref[...] = total.astype(jnp.bfloat16)
-
-    return pl.pallas_call(
-        kernel,
-        out_shape=jax.ShapeDtypeStruct(far.shape, jnp.bfloat16),
+            total = own_ref[...].astype(jnp.float32) + partner_ref[...].astype(jnp.float32)
+            sum_ref[...] = total.astype(jnp.bfloat16)
+            relay_ref[...] = otherwise_ref[...]
+
+    return pl.pallas_call(
+        kernel,
+        out_shape=[pltpu.VMEM(own.shape, jnp.bfloat16)] * 2,
+        in_specs=[SMEM] + [VMEM] * 4,
+        out_specs=[VMEM] * 2,
+        compiler_params=params(4),
+        cost_estimate=pl.CostEstimate(
+            flops=4 * own.size, bytes_accessed=12 * own.size, transcendentals=0
+        ),
+        name="relay_rows",
+    )(info, *in_vmem(own, partner, passing, otherwise))
+
+
+def last_rows(info, chips, early, far, middle_only):
+    rows, width = far.shape
+    parts = 4
+    part = rows // parts
+
+    def kernel(info_ref, early_ref, far_ref, middle_ref, out_ref, done_ref, sems):
+        factor = jnp.where(is_middle(info_ref, chips), 1.0, 0.0)
+        copies = []
+        for i in range(parts):
+            at = pl.ds(i * part, part)
+            total = early_ref[at] + far_ref[at].astype(jnp.float32)
+            total = total + middle_ref[at].astype(jnp.float32) * factor
+            done_ref[at] = total.astype(jnp.bfloat16)
+            copies.append(pltpu.make_async_copy(done_ref.at[at], out_ref.at[at], sems.at[i]))
+            copies[i].start()
+        for copy in copies:
+            copy.wait()
+
+    return pl.pallas_call(
+        kernel,
+        out_shape=pltpu.HBM(far.shape, jnp.bfloat16),
         in_specs=[SMEM, VMEM, VMEM, VMEM],
-        out_specs=VMEM,
+        out_specs=HBM,
+        scratch_shapes=[
+            pltpu.VMEM((rows, width), jnp.bfloat16),
+            pltpu.SemaphoreType.DMA((parts,)),
+        ],
         compiler_params=params(6),
         cost_estimate=pl.CostEstimate(
             flops=4 * far.size, bytes_accessed=10 * far.size, transcendentals=0
         ),
         name="last_rows",
-    )(info, *values)
+    )(info, *in_vmem(early, far, middle_only))
 
 
 def chip_pairs(pairs):
@@ -638,11 +680,13 @@
     relayed_pair = (relayed, swap(relayed))
     turn_a, turn_b, turn_c, turn_d = (3, 1), (2, 3), (1, 2), (0, 0)
 
-    own = project_slots(info, [own_pair], qkv_weight, (0,))
+    *own, late_weight = project_slots(
+        info, [own_pair], qkv_weight, (0,), ahead=((3, 2),)
+    )
     own = exchange(own)
-    late_weight, two_weight = fetch_weights(info, qkv_weight, (3, 2))
+    two_weight, one_weight = fetch_weights(info, qkv_weight, ((2, 2), (1, 1)))
     mid = project_slots(
-        info, [two_pair, one_pair], qkv_weight, (2, 1), ready=(two_weight,)
+        info, [two_pair, one_pair], qkv_weight, (2, 1), ready=(two_weight, one_weight)
     )
     mid = exchange(mid)
     *late, kept_a = project_late(
@@ -670,19 +714,19 @@
         Prefetch(out_weight, (turn_b,), chips),
     )
     first = exchange(first)
-    sum_a = add_rows(info, chips, *finish(first, kept_a, 0, 2))
+    *rest_c, kept_c = attend_slots(
+        info, doc_lengths, sets, (turn_c,), chips, Prefetch(out_weight, (turn_c,), chips)
+    )
+    sum_a = add_rows(*finish(first, kept_a, 0, 2))
     own_b, partner_b = finish(first, kept_b, 1, 2)
     from_one = along(sum_a, [(i, i ^ 1) for i in range(chips)])
-    sum_b = add_rows(info, chips, own_b, partner_b)
+    sum_b = add_rows(own_b, partner_b)
     from_inner = along(sum_b, [(1, 2), (2, 1)])
-    *rest_c, kept_c = attend_slots(
-        info, doc_lengths, sets, (turn_c,), chips, Prefetch(out_weight, (turn_c,), chips)
-    )
     rest_c = exchange(rest_c)
-    sum_c = add_rows(info, chips, *finish(rest_c, kept_c, 0, 1))
+    shares_c = finish(rest_c, kept_c, 0, 1)
     chip = seq // 2
     middle = (chip > 0) & (chip < chips - 1)
-    relay_sum = add_rows(info, chips, sum_c, from_one, sum_b)
+    sum_c, relay_sum = relay_rows(info, chips, *shares_c, from_one, sum_b)
     from_two = along(relay_sum, [(i, i ^ 2) for i in range(chips)])
     from_end = along(sum_c, [(i, i ^ 1) for i in range(chips)])
     *rest_d, kept_d = attend_slots(

time: 164 us -> 163 us (level)
  starting transfers between devices: 40.3 us -> 37.8 us
  waiting for transfers between devices: 74.3 us -> 76.7 us
    ppermute x8, waiting for transfers between devices: 60.9 us -> 64.3 us  [along(): return lax.ppermute(value, 'seq', chip_pairs(pairs))]
    ppermute x8, starting transfers between devices: 17.5 us -> 14.7 us  [along(): return lax.ppermute(value, 'seq', chip_pairs(pairs))]
    pallas_call x2, Pallas kernels: 12.7 us -> 15 us  [project_slots(): pl.pallas_call(kernel, out_shape=[pltpu.VMEM((count * block, cols), jnp.b...]
    pallas_call x4 -> x2, Pallas kernels: 2.57 us -> 0.24 us  [add_rows(): pl.pallas_call(kernel, out_shape=pltpu.VMEM(first.shape, jnp.bfloat16), i...]
    pallas_call x2 -> x3, Pallas kernels: 10.3 us -> 9.2 us  [the longest x1 7.08 us: fetch_weights(): pl.pallas_call(kernel, out_shape=[pltpu.VMEM(shape, jnp.bfloat16) for sha...]
  transfers between devices with their start and end apart: 35 -> 35, of which waited for: 12 -> 11; matrix products, arithmetic and copies ran while one was open for 1% -> 1% of each run, Pallas kernels for 23% -> 22%
where the time goes in v4:
time: 163 us
  waiting for transfers between devices  76.7 us (47%)
  Pallas kernels  46.7 us (29%)
  starting transfers between devices  37.8 us (23%)
    ppermute x8, waiting for transfers between devices, along(): return lax.ppermute(value, 'seq', chip_pairs(pairs))  64.3 us
    ppermute x18, starting transfers between devices, exchange(): lax.ppermute(pieces[d], 'mod', [(i, i ^ d) for i in range(mod_count)])  21.3 us
    pallas_call x2, Pallas kernels, project_slots(): pl.pallas_call(kernel, out_shape=[pltpu.VMEM((count * block, cols), jnp.b...  15 us
    ppermute x8, starting transfers between devices, along(): return lax.ppermute(value, 'seq', chip_pairs(pairs))  14.7 us
    ppermute x18, waiting for transfers between devices, exchange(): lax.ppermute(pieces[d], 'mod', [(i, i ^ d) for i in range(mod_count)])  12.4 us
    pallas_call x3, Pallas kernels, attend_slots(): pl.pallas_call(kernel, out_shape=[pltpu.VMEM((len(turns) * block, HDIM),...  10.1 us
    pallas_call x1, Pallas kernels, fetch_weights(): pl.pallas_call(kernel, out_shape=[pltpu.VMEM(shape, jnp.bfloat16) for sha...  7.08 us
    pallas_call x4, Pallas kernels, output_rows(): pl.pallas_call(kernel, out_shape=[pltpu.VMEM((half, width), jnp.bfloat16)...  6.7 us
  transfers between devices with their start and end apart: 35, of which 11 were waited for; matrix products, arithmetic and copies ran while one was open for 1% of the time, Pallas kernels for 22%

profile of v4, /device:TPU:0, one launch (start us, length us, event | category | flops | bytes accessed | tf_op | source)
XLA Modules:
  0.0 163.1 jit_solution(7648585084065375226)
XLA Ops:
  0.0 0.1 pad_add_fusion.ids_ref
  0.1 2.7 %norm_rows.1 = (bf16[64,4096]{1,0:T(8,128)(2,1)S(1)}, s32[7]{0:T(128)S(1)}) custom-call(s32[3]{0:T(128)S(1)} %pad_add_fusion.ids_ref, s32[16]{0:T(128)} %modality_ref.1, bf16[64,4096]{1,0:T(8,128)(2,1)} %tokens_ref.1, f32[3,4096]{1,0:T(4,128)} %gain_ref.1), custom_call_target="tpu_custom_call" | custom-call | flops 4000000 | bytes 1048576 | tf_op jit(solution)/shard_map/norm_rows/pallas_call | solution.py:173
  2.7 4.1 %collective-permute-start.4 = (bf16[64,4096]{1,0:T(8,128)(2,1)S(1)}, bf16[64,4096]{1,0:T(8,128)(2,1)S(1)}, u32[]{:S(2)}, u32[]{:S(2)}) collective-permute-start(bf16[64,4096]{1,0:T(8,128)(2,1)S(1)} %get-tuple-element.49.refs_0_), channel_id=1, source_target_pairs={{0,4},{1,5},{2,6},{3,7},{4,0},{5,1},{6,2},{7,3},{8,12},{9,13},{10,... | collective-permute-start | bytes 1572872 | tf_op jit(solution)/shard_map/ppermute | solution.py:656
  6.9 1.6 collective-permute-start.6
  8.5 0.7 collective-permute-start.11
  9.1 21.8 %collective-permute-done.4.refs_0_ = bf16[64,4096]{1,0:T(8,128)(2,1)S(1)} collective-permute-done((bf16[64,4096]{1,0:T(8,128)(2,1)S(1)}, bf16[64,4096]{1,0:T(8,128)(2,1)S(1)}, u32[]{:S(2)}, u32[]{:S(2)}) %collective-permute-start.4) | collective-permute-done | bytes 524320 | tf_op jit(solution)/shard_map/ppermute | solution.py:656
  30.9 0.0 collective-permute-start.13
  30.9 0.5 collective-permute-start.5
  31.4 0.0 collective-permute-start.7
  31.5 0.0 collective-permute-done.11.inner_own
  31.5 0.5 collective-permute-start.12
  32.0 11.2 %collective-permute-done.13.relayed_own = bf16[64,4096]{1,0:T(8,128)(2,1)S(1)} collective-permute-done((bf16[64,4096]{1,0:T(8,128)(2,1)S(1)}, bf16[64,4096]{1,0:T(8,128)(2,1)S(1)}, u32[]{:S(2)}, u32[]{:S(2)}) %collective-permute-start.13) | collective-permute-done | bytes 524320 | tf_op jit(solution)/shard_map/ppermute | solution.py:656
  43.2 0.0 collective-permute-start.14
  43.2 7.1 %fetch_weights.1 = (bf16[2,4,1024,768]{3,2,1,0:T(8,128)(2,1)S(1)}, bf16[1,4,1024,768]{3,2,1,0:T(8,128)(2,1)S(1)}) custom-call(s32[7]{0:T(128)S(1)} %get-tuple-element.48.info_ref, bf16[3,4096,1536]{2,1,0:T(8,128)(2,1)} %refs_6_.1), custom_call_target="tpu_custom_call" | custom-call | flops 6000000000 | bytes 26214400 | tf_op jit(solution)/shard_map/fetch_weights/pallas_call | solution.py:234
  50.3 0.0 collective-permute-done.refs_1_
  50.3 9.0 %project_slots.2 = (bf16[128,384]{1,0:T(8,128)(2,1)S(1)}, bf16[128,384]{1,0:T(8,128)(2,1)S(1)}, bf16[128,384]{1,0:T(8,128)(2,1)S(1)}, bf16[128,384]{1,0:T(8,128)(2,1)S(1)}, bf16[2,4,1024,768]{3,2,1,0:T(8,128)(2,1)S(1)}) custom-call(s32[7]{0:T(128)S(1)} %get-tuple-element.48.info_ref, bf16[64,4096]{1,0:T(8,128)(2,1)S(1)} %get-tuple-element.49.refs_0_, ...), custom_call_target="tpu_custom_call" | custom-call | flops 1610612736 | bytes 12582912 | tf_op jit(solution)/shard_map/project_slots/pallas_call | solution.py:339
  59.3 1.7 %collective-permute-start.1 = (bf16[128,384]{1,0:T(8,128)(2,1)S(1)}, bf16[128,384]{1,0:T(8,128)(2,1)S(1)}, u32[]{:S(2)}, u32[]{:S(2)}) collective-permute-start(bf16[128,384]{1,0:T(8,128)(2,1)S(1)} %get-tuple-element.51), channel_id=1, source_target_pairs={{0,8},{8,0},{16,24},{24,16},{1,9},{9,1},{17,25},{25,17},{2,10},{10... | collective-permute-start | bytes 294920 | tf_op jit(solution)/shard_map/ppermute | solution.py:664
  61.1 6.0 %project_slots.3 = (bf16[256,384]{1,0:T(8,128)(2,1)S(1)}, bf16[256,384]{1,0:T(8,128)(2,1)S(1)}, bf16[256,384]{1,0:T(8,128)(2,1)S(1)}, bf16[256,384]{1,0:T(8,128)(2,1)S(1)}) custom-call(s32[7]{0:T(128)S(1)} %get-tuple-element.48.info_ref, bf16[64,4096]{1,0:T(8,128)(2,1)S(1)} %collective-permute-done.4.refs_0_, ...), custom_call_target="tpu_custom_call" | custom-call | flops 3221225472 | bytes 25165824 | tf_op jit(solution)/shard_map/project_slots/pallas_call | solution.py:339
  67.0 1.2 collective-permute-start.10
  68.2 0.7 collective-permute-start.2
  68.9 2.2 %collective-permute-start.3 = (bf16[128,384]{1,0:T(8,128)(2,1)S(1)}, bf16[128,384]{1,0:T(8,128)(2,1)S(1)}, u32[]{:S(2)}, u32[]{:S(2)}) collective-permute-start(bf16[128,384]{1,0:T(8,128)(2,1)S(1)} %get-tuple-element.53), channel_id=1, source_target_pairs={{0,24},{8,16},{16,8},{24,0},{1,25},{9,17},{17,9},{25,1},{2,26},{10... | collective-permute-start | bytes 294920 | tf_op jit(solution)/shard_map/ppermute | solution.py:664
  71.2 0.5 collective-permute-start.8
  71.7 0.7 collective-permute-start.9
  72.4 2.7 %project_late.1 = (bf16[128,384]{1,0:T(8,128)(2,1)S(1)}, bf16[128,384]{1,0:T(8,128)(2,1)S(1)}, bf16[128,384]{1,0:T(8,128)(2,1)S(1)}, bf16[128,384]{1,0:T(8,128)(2,1)S(1)}, bf16[512,4096]{1,0:T(8,128)(2,1)S(1)}) custom-call(s32[7]{0:T(128)S(1)} %get-tuple-element.48.info_ref, bf16[64,4096]{1,0:T(8,128)(2,1)S(1)} %collective-permute-done.11.inner_own, ...), custom_call_target="tpu_custom_call" | custom-call | flops 1610612736 | bytes 12582912 | tf_op jit(solution)/shard_map/project_late/pallas_call | solution.py:396
  75.2 4.2 %collective-permute-done.2.refs_2_ = bf16[128,384]{1,0:T(8,128)(2,1)S(1)} collective-permute-done((bf16[128,384]{1,0:T(8,128)(2,1)S(1)}, bf16[128,384]{1,0:T(8,128)(2,1)S(1)}, u32[]{:S(2)}, u32[]{:S(2)}) %collective-permute-start.2) | collective-permute-done | bytes 98336 | tf_op jit(solution)/shard_map/ppermute | solution.py:664
  79.3 0.4 collective-permute-start.15
  79.7 1.3 collective-permute-start.16
  81.0 1.8 %collective-permute-start.17 = (bf16[128,384]{1,0:T(8,128)(2,1)S(1)}, bf16[128,384]{1,0:T(8,128)(2,1)S(1)}, u32[]{:S(2)}, u32[]{:S(2)}) collective-permute-start(bf16[128,384]{1,0:T(8,128)(2,1)S(1)} %get-tuple-element.64), channel_id=1, source_target_pairs={{0,24},{8,16},{16,8},{24,0},{1,25},{9,17},{17,9},{25,1},{2,26},{10... | collective-permute-start | bytes 294920 | tf_op jit(solution)/shard_map/ppermute | solution.py:664
  82.8 0.7 collective-permute-done.9.refs_6_
  83.6 1.2 collective-permute-done.15.refs_9_
  84.8 2.8 %collective-permute-done.16.refs_10_ = bf16[128,384]{1,0:T(8,128)(2,1)S(1)} collective-permute-done((bf16[128,384]{1,0:T(8,128)(2,1)S(1)}, bf16[128,384]{1,0:T(8,128)(2,1)S(1)}, u32[]{:S(2)}, u32[]{:S(2)}) %collective-permute-start.16) | collective-permute-done | bytes 98336 | tf_op jit(solution)/shard_map/ppermute | solution.py:664
  87.6 4.6 %attend_slots.4 = (bf16[256,128]{1,0:T(8,128)(2,1)S(1)}, bf16[256,128]{1,0:T(8,128)(2,1)S(1)}, bf16[256,128]{1,0:T(8,128)(2,1)S(1)}, bf16[256,128]{1,0:T(8,128)(2,1)S(1)}, bf16[512,4096]{1,0:T(8,128)(2,1)S(1)}) custom-call(s32[7]{0:T(128)S(1)} %get-tuple-element.48.info_ref, s32[4]{0:T(128)S(1)} %copy-done, bf16[128,384]{1,0:T(8,128)(2,1)S(1)} %get-tuple-element.50.refs_0_, ...), custom_call_target="tpu_custom_call" | custom-call | flops 1207959552 | bytes 1572864 | tf_op jit(solution)/shard_map/attend_slots/pallas_call | solution.py:496
  92.2 0.5 collective-permute-start.22
  92.7 1.3 collective-permute-start.23
  94.0 1.8 %collective-permute-start.24 = (bf16[256,128]{1,0:T(8,128)(2,1)S(1)}, bf16[256,128]{1,0:T(8,128)(2,1)S(1)}, u32[]{:S(2)}, u32[]{:S(2)}) collective-permute-start(bf16[256,128]{1,0:T(8,128)(2,1)S(1)} %get-tuple-element.75), channel_id=1, source_target_pairs={{0,24},{8,16},{16,8},{24,0},{1,25},{9,17},{17,9},{25,1},{2,26},{10... | collective-permute-start | bytes 196616 | tf_op jit(solution)/shard_map/ppermute | solution.py:664
  95.8 1.3 collective-permute-done.22.refs_1_
  97.0 0.5 collective-permute-done.23.refs_2_
  97.5 1.7 %collective-permute-done.24.refs_3_ = bf16[256,128]{1,0:T(8,128)(2,1)S(1)} collective-permute-done((bf16[256,128]{1,0:T(8,128)(2,1)S(1)}, bf16[256,128]{1,0:T(8,128)(2,1)S(1)}, u32[]{:S(2)}, u32[]{:S(2)}) %collective-permute-start.24) | collective-permute-done | bytes 65568 | tf_op jit(solution)/shard_map/ppermute | solution.py:664
  99.2 1.3 output_rows.6
  100.5 0.1 collective-permute-start.27
  100.5 1.3 output_rows.5
  101.8 0.6 collective-permute-start.25
  102.4 2.7 %attend_slots.5 = (bf16[128,128]{1,0:T(8,128)(2,1)S(1)}, bf16[128,128]{1,0:T(8,128)(2,1)S(1)}, bf16[128,128]{1,0:T(8,128)(2,1)S(1)}, bf16[128,128]{1,0:T(8,128)(2,1)S(1)}, bf16[512,4096]{1,0:T(8,128)(2,1)S(1)}) custom-call(s32[7]{0:T(128)S(1)} %get-tuple-element.48.info_ref, s32[4]{0:T(128)S(1)} %copy-done, bf16[128,384]{1,0:T(8,128)(2,1)S(1)} %get-tuple-element.50.refs_0_, ...), custom_call_target="tpu_custom_call" | custom-call | flops 603979776 | bytes 1572864 | tf_op jit(solution)/shard_map/attend_slots/pallas_call | solution.py:496
  105.1 1.1 collective-permute-start.29
  106.2 1.3 collective-permute-start.30
  107.5 1.2 collective-permute-start.31
  108.7 2.7 %attend_slots.3 = (bf16[128,128]{1,0:T(8,128)(2,1)S(1)}, bf16[128,128]{1,0:T(8,128)(2,1)S(1)}, bf16[128,128]{1,0:T(8,128)(2,1)S(1)}, bf16[128,128]{1,0:T(8,128)(2,1)S(1)}, bf16[512,4096]{1,0:T(8,128)(2,1)S(1)}) custom-call(s32[7]{0:T(128)S(1)} %get-tuple-element.48.info_ref, s32[4]{0:T(128)S(1)} %copy-done, bf16[128,384]{1,0:T(8,128)(2,1)S(1)} %get-tuple-element.50.refs_0_, ...), custom_call_target="tpu_custom_call" | custom-call | flops 603979776 | bytes 1572864 | tf_op jit(solution)/shard_map/attend_slots/pallas_call | solution.py:496
  111.5 1.1 collective-permute-start.18
  112.5 1.3 collective-permute-start.19
  113.8 1.2 collective-permute-start.20
  115.0 2.1 %output_rows.7 = (bf16[64,4096]{1,0:T(8,128)(2,1)S(1)}, bf16[64,4096]{1,0:T(8,128)(2,1)}) custom-call(s32[7]{0:T(128)S(1)} %get-tuple-element.48.info_ref, bf16[128,128]{1,0:T(8,128)(2,1)S(1)} %get-tuple-element.82.refs_0_, bf16[128,128]{1,0:T(8,128)(2,1)S(1)} %collective-permute-done.29.refs_1_, bf16[128,128]{1,0:T(8,128)(2,1)S(1)} %collective-permute-done.30.refs_2_, ...), custom_call_target="tpu_custom_call" | custom-call | flops 536870912 | bytes 4194304 | tf_op jit(solution)/shard_map/output_rows/pallas_call | solution.py:538
  117.1 0.1 add_rows.3
  117.3 1.7 %collective-permute-start.28 = (bf16[64,4096]{1,0:T(8,128)(2,1)S(1)}, bf16[64,4096]{1,0:T(8,128)(2,1)S(1)}, u32[]{:S(2)}, u32[]{:S(2)}) collective-permute-start(bf16[64,4096]{1,0:T(8,128)(2,1)S(1)} %add_rows.3), channel_id=1, source_target_pairs={{0,2},{1,3},{2,0},{3,1},{4,6},{5,7},{6,4},{7,5},{8,10},{9,11},{10,... | collective-permute-start | bytes 1572872 | tf_op jit(solution)/shard_map/ppermute | solution.py:656
  119.0 2.1 %output_rows.4 = (bf16[64,4096]{1,0:T(8,128)(2,1)S(1)}, bf16[64,4096]{1,0:T(8,128)(2,1)}) custom-call(s32[7]{0:T(128)S(1)} %get-tuple-element.48.info_ref, bf16[128,128]{1,0:T(8,128)(2,1)S(1)} %get-tuple-element.65.refs_0_, bf16[128,128]{1,0:T(8,128)(2,1)S(1)} %collective-permute-done.18.refs_1_, bf16[128,128]{1,0:T(8,128)(2,1)S(1)} %collective-permute-done.19.refs_2_, ...), custom_call_target="tpu_custom_call" | custom-call | flops 536870912 | bytes 4194304 | tf_op jit(solution)/shard_map/output_rows/pallas_call | solution.py:538
  121.0 0.2 collective-permute-start.21
  121.3 0.1 add_rows.2.otherwise_ref
  121.4 1.5 collective-permute-start.26
  122.9 8.8 %collective-permute-done.28.passing_ref = bf16[64,4096]{1,0:T(8,128)(2,1)S(1)} collective-permute-done((bf16[64,4096]{1,0:T(8,128)(2,1)S(1)}, bf16[64,4096]{1,0:T(8,128)(2,1)S(1)}, u32[]{:S(2)}, u32[]{:S(2)}) %collective-permute-start.28) | collective-permute-done | bytes 524320 | tf_op jit(solution)/shard_map/ppermute | solution.py:656
  131.7 0.7 relay_rows.1
  132.3 3.5 %collective-permute-start.33 = (bf16[64,4096]{1,0:T(8,128)(2,1)S(1)}, bf16[64,4096]{1,0:T(8,128)(2,1)S(1)}, u32[]{:S(2)}, u32[]{:S(2)}) collective-permute-start(bf16[64,4096]{1,0:T(8,128)(2,1)S(1)} %get-tuple-element.89), channel_id=1, source_target_pairs={{0,4},{1,5},{2,6},{3,7},{4,0},{5,1},{6,2},{7,3},{8,12},{9,13},{10,... | collective-permute-start | bytes 1572872 | tf_op jit(solution)/shard_map/ppermute | solution.py:656
  135.8 1.6 %collective-permute-start.34 = (bf16[64,4096]{1,0:T(8,128)(2,1)S(1)}, bf16[64,4096]{1,0:T(8,128)(2,1)S(1)}, u32[]{:S(2)}, u32[]{:S(2)}) collective-permute-start(bf16[64,4096]{1,0:T(8,128)(2,1)S(1)} %get-tuple-element.90), channel_id=1, source_target_pairs={{0,2},{1,3},{2,0},{3,1},{4,6},{5,7},{6,4},{7,5},{8,10},{9,11},{10,... | collective-permute-start | bytes 1572872 | tf_op jit(solution)/shard_map/ppermute | solution.py:656
  137.5 1.5 convert_add_fusion.early_ref
  139.0 22.5 %collective-permute-done.33.far_ref = bf16[64,4096]{1,0:T(8,128)(2,1)S(1)} collective-permute-done((bf16[64,4096]{1,0:T(8,128)(2,1)S(1)}, bf16[64,4096]{1,0:T(8,128)(2,1)S(1)}, u32[]{:S(2)}, u32[]{:S(2)}) %collective-permute-start.33) | collective-permute-done | bytes 524320 | tf_op jit(solution)/shard_map/ppermute | solution.py:656
  161.5 1.4 last_rows.1
  (26 shorter events, 0.1 us)
Async XLA Ops:
  2.7 28.2 %collective-permute-start.4 = (bf16[64,4096]{1,0:T(8,128)(2,1)S(1)}, bf16[64,4096]{1,0:T(8,128)(2,1)S(1)}, u32[]{:S(2)}, u32[]{:S(2)}) collective-permute-start(bf16[64,4096]{1,0:T(8,128)(2,1)S(1)} %get-tuple-element.49.refs_0_), channel_id=1, source_target_pairs={{0,4},{1,5},{2,6},{3,7},{4,0},{5,1},{6,2},{7,3},{8,12},{9,13},{10,... | collective-permute-start | bytes 1572872 | tf_op jit(solution)/shard_map/ppermute | solution.py:656
  6.9 24.6 %collective-permute-start.6 = (bf16[64,4096]{1,0:T(8,128)(2,1)S(1)}, bf16[64,4096]{1,0:T(8,128)(2,1)S(1)}, u32[]{:S(2)}, u32[]{:S(2)}) collective-permute-start(bf16[64,4096]{1,0:T(8,128)(2,1)S(1)} %get-tuple-element.49.refs_0_), channel_id=1, source_target_pairs={{0,2},{1,3},{2,0},{3,1},{4,6},{5,7},{6,4},{7,5},{8,10},{9,11},{10,... | collective-permute-start | bytes 1572872 | tf_op jit(solution)/shard_map/ppermute | solution.py:656
  8.5 23.0 %collective-permute-start.11 = (bf16[64,4096]{1,0:T(8,128)(2,1)S(1)}, bf16[64,4096]{1,0:T(8,128)(2,1)S(1)}, u32[]{:S(2)}, u32[]{:S(2)}) collective-permute-start(bf16[64,4096]{1,0:T(8,128)(2,1)S(1)} %get-tuple-element.49.refs_0_), channel_id=1, source_target_pairs={{2,4},{3,5},{4,2},{5,3},{10,12},{11,13},{12,10},{13,11},{18,20},{1... | collective-permute-start | bytes 1572872 | tf_op jit(solution)/shard_map/ppermute | solution.py:656
  30.9 12.2 %collective-permute-start.13 = (bf16[64,4096]{1,0:T(8,128)(2,1)S(1)}, bf16[64,4096]{1,0:T(8,128)(2,1)S(1)}, u32[]{:S(2)}, u32[]{:S(2)}) collective-permute-start(bf16[64,4096]{1,0:T(8,128)(2,1)S(1)} %collective-permute-done.4.refs_0_), channel_id=1, source_target_pairs={{0,2},{1,3},{2,0},{3,1},{4,6},{5,7},{6,4},{7,5},{8,10},{9,11},{10,... | collective-permute-start | bytes 1572872 | tf_op jit(solution)/shard_map/ppermute | solution.py:656
  30.9 19.3 %collective-permute-start = (bf16[64,4096]{1,0:T(8,128)(2,1)S(1)}, bf16[64,4096]{1,0:T(8,128)(2,1)S(1)}, u32[]{:S(2)}, u32[]{:S(2)}) collective-permute-start(bf16[64,4096]{1,0:T(8,128)(2,1)S(1)} %get-tuple-element.49.refs_0_), channel_id=1, source_target_pairs={{0,1},{1,0},{2,3},{3,2},{4,5},{5,4},{6,7},{7,6},{8,9},{9,8},{10,11... | collective-permute-start | bytes 1572872 | tf_op jit(solution)/shard_map/ppermute | solution.py:659
  30.9 30.1 %collective-permute-start.5 = (bf16[64,4096]{1,0:T(8,128)(2,1)S(1)}, bf16[64,4096]{1,0:T(8,128)(2,1)S(1)}, u32[]{:S(2)}, u32[]{:S(2)}) collective-permute-start(bf16[64,4096]{1,0:T(8,128)(2,1)S(1)} %collective-permute-done.4.refs_0_), channel_id=1, source_target_pairs={{0,1},{1,0},{2,3},{3,2},{4,5},{5,4},{6,7},{7,6},{8,9},{9,8},{10,11... | collective-permute-start | bytes 1572872 | tf_op jit(solution)/shard_map/ppermute | solution.py:659
  31.4 29.6 %collective-permute-start.7 = (bf16[64,4096]{1,0:T(8,128)(2,1)S(1)}, bf16[64,4096]{1,0:T(8,128)(2,1)S(1)}, u32[]{:S(2)}, u32[]{:S(2)}) collective-permute-start(bf16[64,4096]{1,0:T(8,128)(2,1)S(1)} %collective-permute-done.6.refs_2_), channel_id=1, source_target_pairs={{0,1},{1,0},{2,3},{3,2},{4,5},{5,4},{6,7},{7,6},{8,9},{9,8},{10,11... | collective-permute-start | bytes 1572872 | tf_op jit(solution)/shard_map/ppermute | solution.py:659
  31.5 39.7 %collective-permute-start.12 = (bf16[64,4096]{1,0:T(8,128)(2,1)S(1)}, bf16[64,4096]{1,0:T(8,128)(2,1)S(1)}, u32[]{:S(2)}, u32[]{:S(2)}) collective-permute-start(bf16[64,4096]{1,0:T(8,128)(2,1)S(1)} %collective-permute-done.11.inner_own), channel_id=1, source_target_pairs={{0,1},{1,0},{2,3},{3,2},{4,5},{5,4},{6,7},{7,6},{8,9},{9,8},{10,11... | collective-permute-start | bytes 1572872 | tf_op jit(solution)/shard_map/ppermute | solution.py:659
  43.2 28.5 %collective-permute-start.14 = (bf16[64,4096]{1,0:T(8,128)(2,1)S(1)}, bf16[64,4096]{1,0:T(8,128)(2,1)S(1)}, u32[]{:S(2)}, u32[]{:S(2)}) collective-permute-start(bf16[64,4096]{1,0:T(8,128)(2,1)S(1)} %collective-permute-done.13.relayed_own), channel_id=1, source_target_pairs={{0,1},{1,0},{2,3},{3,2},{4,5},{5,4},{6,7},{7,6},{8,9},{9,8},{10,11... | collective-permute-start | bytes 1572872 | tf_op jit(solution)/shard_map/ppermute | solution.py:659
  59.3 9.6 %collective-permute-start.1 = (bf16[128,384]{1,0:T(8,128)(2,1)S(1)}, bf16[128,384]{1,0:T(8,128)(2,1)S(1)}, u32[]{:S(2)}, u32[]{:S(2)}) collective-permute-start(bf16[128,384]{1,0:T(8,128)(2,1)S(1)} %get-tuple-element.51), channel_id=1, source_target_pairs={{0,8},{8,0},{16,24},{24,16},{1,9},{9,1},{17,25},{25,17},{2,10},{10... | collective-permute-start | bytes 294920 | tf_op jit(solution)/shard_map/ppermute | solution.py:664
  67.0 14.0 %collective-permute-start.10 = (bf16[256,384]{1,0:T(8,128)(2,1)S(1)}, bf16[256,384]{1,0:T(8,128)(2,1)S(1)}, u32[]{:S(2)}, u32[]{:S(2)}) collective-permute-start(bf16[256,384]{1,0:T(8,128)(2,1)S(1)} %get-tuple-element.59), channel_id=1, source_target_pairs={{0,24},{8,16},{16,8},{24,0},{1,25},{9,17},{17,9},{25,1},{2,26},{10... | collective-permute-start | bytes 589832 | tf_op jit(solution)/shard_map/ppermute | solution.py:664
  68.2 11.1 %collective-permute-start.2 = (bf16[128,384]{1,0:T(8,128)(2,1)S(1)}, bf16[128,384]{1,0:T(8,128)(2,1)S(1)}, u32[]{:S(2)}, u32[]{:S(2)}) collective-permute-start(bf16[128,384]{1,0:T(8,128)(2,1)S(1)} %get-tuple-element.52), channel_id=1, source_target_pairs={{0,16},{8,24},{16,0},{24,8},{1,17},{9,25},{17,1},{25,9},{2,18},{10... | collective-permute-start | bytes 294920 | tf_op jit(solution)/shard_map/ppermute | solution.py:664
  68.9 10.8 %collective-permute-start.3 = (bf16[128,384]{1,0:T(8,128)(2,1)S(1)}, bf16[128,384]{1,0:T(8,128)(2,1)S(1)}, u32[]{:S(2)}, u32[]{:S(2)}) collective-permute-start(bf16[128,384]{1,0:T(8,128)(2,1)S(1)} %get-tuple-element.53), channel_id=1, source_target_pairs={{0,24},{8,16},{16,8},{24,0},{1,25},{9,17},{17,9},{25,1},{2,26},{10... | collective-permute-start | bytes 294920 | tf_op jit(solution)/shard_map/ppermute | solution.py:664
  71.2 11.7 %collective-permute-start.8 = (bf16[256,384]{1,0:T(8,128)(2,1)S(1)}, bf16[256,384]{1,0:T(8,128)(2,1)S(1)}, u32[]{:S(2)}, u32[]{:S(2)}) collective-permute-start(bf16[256,384]{1,0:T(8,128)(2,1)S(1)} %get-tuple-element.57), channel_id=1, source_target_pairs={{0,8},{8,0},{16,24},{24,16},{1,9},{9,1},{17,25},{25,17},{2,10},{10... | collective-permute-start | bytes 589832 | tf_op jit(solution)/shard_map/ppermute | solution.py:664
  71.7 11.9 %collective-permute-start.9 = (bf16[256,384]{1,0:T(8,128)(2,1)S(1)}, bf16[256,384]{1,0:T(8,128)(2,1)S(1)}, u32[]{:S(2)}, u32[]{:S(2)}) collective-permute-start(bf16[256,384]{1,0:T(8,128)(2,1)S(1)} %get-tuple-element.58), channel_id=1, source_target_pairs={{0,16},{8,24},{16,0},{24,8},{1,17},{9,25},{17,1},{25,9},{2,18},{10... | collective-permute-start | bytes 589832 | tf_op jit(solution)/shard_map/ppermute | solution.py:664
  72.4 15.2 %copy-start = (s32[4]{0:T(128)S(1)}, s32[4]{0:T(128)}, u32[]{:S(2)}) copy-start(s32[4]{0:T(128)} %docs_ref.5) | copy-start | bytes 52
  79.3 5.4 %collective-permute-start.15 = (bf16[128,384]{1,0:T(8,128)(2,1)S(1)}, bf16[128,384]{1,0:T(8,128)(2,1)S(1)}, u32[]{:S(2)}, u32[]{:S(2)}) collective-permute-start(bf16[128,384]{1,0:T(8,128)(2,1)S(1)} %get-tuple-element.62), channel_id=1, source_target_pairs={{0,8},{8,0},{16,24},{24,16},{1,9},{9,1},{17,25},{25,17},{2,10},{10... | collective-permute-start | bytes 294920 | tf_op jit(solution)/shard_map/ppermute | solution.py:664
  79.7 7.9 %collective-permute-start.16 = (bf16[128,384]{1,0:T(8,128)(2,1)S(1)}, bf16[128,384]{1,0:T(8,128)(2,1)S(1)}, u32[]{:S(2)}, u32[]{:S(2)}) collective-permute-start(bf16[128,384]{1,0:T(8,128)(2,1)S(1)} %get-tuple-element.63), channel_id=1, source_target_pairs={{0,16},{8,24},{16,0},{24,8},{1,17},{9,25},{17,1},{25,9},{2,18},{10... | collective-permute-start | bytes 294920 | tf_op jit(solution)/shard_map/ppermute | solution.py:664
  81.0 6.6 %collective-permute-start.17 = (bf16[128,384]{1,0:T(8,128)(2,1)S(1)}, bf16[128,384]{1,0:T(8,128)(2,1)S(1)}, u32[]{:S(2)}, u32[]{:S(2)}) collective-permute-start(bf16[128,384]{1,0:T(8,128)(2,1)S(1)} %get-tuple-element.64), channel_id=1, source_target_pairs={{0,24},{8,16},{16,8},{24,0},{1,25},{9,17},{17,9},{25,1},{2,26},{10... | collective-permute-start | bytes 294920 | tf_op jit(solution)/shard_map/ppermute | solution.py:664
  92.2 4.8 %collective-permute-start.22 = (bf16[256,128]{1,0:T(8,128)(2,1)S(1)}, bf16[256,128]{1,0:T(8,128)(2,1)S(1)}, u32[]{:S(2)}, u32[]{:S(2)}) collective-permute-start(bf16[256,128]{1,0:T(8,128)(2,1)S(1)} %get-tuple-element.73), channel_id=1, source_target_pairs={{0,8},{8,0},{16,24},{24,16},{1,9},{9,1},{17,25},{25,17},{2,10},{10... | collective-permute-start | bytes 196616 | tf_op jit(solution)/shard_map/ppermute | solution.py:664
  92.7 4.8 %collective-permute-start.23 = (bf16[256,128]{1,0:T(8,128)(2,1)S(1)}, bf16[256,128]{1,0:T(8,128)(2,1)S(1)}, u32[]{:S(2)}, u32[]{:S(2)}) collective-permute-start(bf16[256,128]{1,0:T(8,128)(2,1)S(1)} %get-tuple-element.74), channel_id=1, source_target_pairs={{0,16},{8,24},{16,0},{24,8},{1,17},{9,25},{17,1},{25,9},{2,18},{10... | collective-permute-start | bytes 196616 | tf_op jit(solution)/shard_map/ppermute | solution.py:664
  94.0 5.2 %collective-permute-start.24 = (bf16[256,128]{1,0:T(8,128)(2,1)S(1)}, bf16[256,128]{1,0:T(8,128)(2,1)S(1)}, u32[]{:S(2)}, u32[]{:S(2)}) collective-permute-start(bf16[256,128]{1,0:T(8,128)(2,1)S(1)} %get-tuple-element.75), channel_id=1, source_target_pairs={{0,24},{8,16},{16,8},{24,0},{1,25},{9,17},{17,9},{25,1},{2,26},{10... | collective-permute-start | bytes 196616 | tf_op jit(solution)/shard_map/ppermute | solution.py:664
  100.5 16.7 %collective-permute-start.27 = (bf16[64,4096]{1,0:T(8,128)(2,1)S(1)}, bf16[64,4096]{1,0:T(8,128)(2,1)S(1)}, u32[]{:S(2)}, u32[]{:S(2)}) collective-permute-start(bf16[64,4096]{1,0:T(8,128)(2,1)S(1)} %get-tuple-element.81), channel_id=1, source_target_pairs={{0,1},{1,0},{2,3},{3,2},{4,5},{5,4},{6,7},{7,6},{8,9},{9,8},{10,11... | collective-permute-start | bytes 1572872 | tf_op jit(solution)/shard_map/ppermute | solution.py:659
  101.8 19.4 %collective-permute-start.25 = (bf16[64,4096]{1,0:T(8,128)(2,1)S(1)}, bf16[64,4096]{1,0:T(8,128)(2,1)S(1)}, u32[]{:S(2)}, u32[]{:S(2)}) collective-permute-start(bf16[64,4096]{1,0:T(8,128)(2,1)S(1)} %get-tuple-element.78), channel_id=1, source_target_pairs={{0,1},{1,0},{2,3},{3,2},{4,5},{5,4},{6,7},{7,6},{8,9},{9,8},{10,11... | collective-permute-start | bytes 1572872 | tf_op jit(solution)/shard_map/ppermute | solution.py:659
  105.1 6.3 %collective-permute-start.29 = (bf16[128,128]{1,0:T(8,128)(2,1)S(1)}, bf16[128,128]{1,0:T(8,128)(2,1)S(1)}, u32[]{:S(2)}, u32[]{:S(2)}) collective-permute-start(bf16[128,128]{1,0:T(8,128)(2,1)S(1)} %get-tuple-element.83), channel_id=1, source_target_pairs={{0,8},{8,0},{16,24},{24,16},{1,9},{9,1},{17,25},{25,17},{2,10},{10... | collective-permute-start | bytes 98312 | tf_op jit(solution)/shard_map/ppermute | solution.py:664
  106.2 6.3 %collective-permute-start.30 = (bf16[128,128]{1,0:T(8,128)(2,1)S(1)}, bf16[128,128]{1,0:T(8,128)(2,1)S(1)}, u32[]{:S(2)}, u32[]{:S(2)}) collective-permute-start(bf16[128,128]{1,0:T(8,128)(2,1)S(1)} %get-tuple-element.84), channel_id=1, source_target_pairs={{0,16},{8,24},{16,0},{24,8},{1,17},{9,25},{17,1},{25,9},{2,18},{10... | collective-permute-start | bytes 98312 | tf_op jit(solution)/shard_map/ppermute | solution.py:664
  107.5 6.3 %collective-permute-start.31 = (bf16[128,128]{1,0:T(8,128)(2,1)S(1)}, bf16[128,128]{1,0:T(8,128)(2,1)S(1)}, u32[]{:S(2)}, u32[]{:S(2)}) collective-permute-start(bf16[128,128]{1,0:T(8,128)(2,1)S(1)} %get-tuple-element.85), channel_id=1, source_target_pairs={{0,24},{8,16},{16,8},{24,0},{1,25},{9,17},{17,9},{25,1},{2,26},{10... | collective-permute-start | bytes 98312 | tf_op jit(solution)/shard_map/ppermute | solution.py:664
  111.5 5.8 %collective-permute-start.18 = (bf16[128,128]{1,0:T(8,128)(2,1)S(1)}, bf16[128,128]{1,0:T(8,128)(2,1)S(1)}, u32[]{:S(2)}, u32[]{:S(2)}) collective-permute-start(bf16[128,128]{1,0:T(8,128)(2,1)S(1)} %get-tuple-element.66), channel_id=1, source_target_pairs={{0,8},{8,0},{16,24},{24,16},{1,9},{9,1},{17,25},{25,17},{2,10},{10... | collective-permute-start | bytes 98312 | tf_op jit(solution)/shard_map/ppermute | solution.py:664
  112.5 6.4 %collective-permute-start.19 = (bf16[128,128]{1,0:T(8,128)(2,1)S(1)}, bf16[128,128]{1,0:T(8,128)(2,1)S(1)}, u32[]{:S(2)}, u32[]{:S(2)}) collective-permute-start(bf16[128,128]{1,0:T(8,128)(2,1)S(1)} %get-tuple-element.67), channel_id=1, source_target_pairs={{0,16},{8,24},{16,0},{24,8},{1,17},{9,25},{17,1},{25,9},{2,18},{10... | collective-permute-start | bytes 98312 | tf_op jit(solution)/shard_map/ppermute | solution.py:664
  113.8 5.1 %collective-permute-start.20 = (bf16[128,128]{1,0:T(8,128)(2,1)S(1)}, bf16[128,128]{1,0:T(8,128)(2,1)S(1)}, u32[]{:S(2)}, u32[]{:S(2)}) collective-permute-start(bf16[128,128]{1,0:T(8,128)(2,1)S(1)} %get-tuple-element.68), channel_id=1, source_target_pairs={{0,24},{8,16},{16,8},{24,0},{1,25},{9,17},{17,9},{25,1},{2,26},{10... | collective-permute-start | bytes 98312 | tf_op jit(solution)/shard_map/ppermute | solution.py:664
  117.1 5.8 %collective-permute-start.32 = (bf16[64,4096]{1,0:T(8,128)(2,1)}, bf16[64,4096]{1,0:T(8,128)(2,1)S(1)}, u32[]{:S(2)}, u32[]{:S(2)}) collective-permute-start(bf16[64,4096]{1,0:T(8,128)(2,1)} %get-tuple-element.88), channel_id=1, source_target_pairs={{0,1},{1,0},{2,3},{3,2},{4,5},{5,4},{6,7},{7,6},{8,9},{9,8},{10,11... | collective-permute-start | bytes 1572872 | tf_op jit(solution)/shard_map/ppermute | solution.py:659
  117.3 14.4 %collective-permute-start.28 = (bf16[64,4096]{1,0:T(8,128)(2,1)S(1)}, bf16[64,4096]{1,0:T(8,128)(2,1)S(1)}, u32[]{:S(2)}, u32[]{:S(2)}) collective-permute-start(bf16[64,4096]{1,0:T(8,128)(2,1)S(1)} %add_rows.3), channel_id=1, source_target_pairs={{0,2},{1,3},{2,0},{3,1},{4,6},{5,7},{6,4},{7,5},{8,10},{9,11},{10,... | collective-permute-start | bytes 1572872 | tf_op jit(solution)/shard_map/ppermute | solution.py:656
  121.0 16.4 %collective-permute-start.21 = (bf16[64,4096]{1,0:T(8,128)(2,1)}, bf16[64,4096]{1,0:T(8,128)(2,1)}, u32[]{:S(2)}, u32[]{:S(2)}) collective-permute-start(bf16[64,4096]{1,0:T(8,128)(2,1)} %get-tuple-element.71), channel_id=1, source_target_pairs={{0,1},{1,0},{2,3},{3,2},{4,5},{5,4},{6,7},{7,6},{8,9},{9,8},{10,11... | collective-permute-start | bytes 1572872 | tf_op jit(solution)/shard_map/ppermute | solution.py:659
  121.4 16.1 %collective-permute-start.26 = (bf16[64,4096]{1,0:T(8,128)(2,1)S(1)}, bf16[64,4096]{1,0:T(8,128)(2,1)}, u32[]{:S(2)}, u32[]{:S(2)}) collective-permute-start(bf16[64,4096]{1,0:T(8,128)(2,1)S(1)} %add_rows.2.otherwise_ref), channel_id=1, source_target_pairs={{2,4},{3,5},{4,2},{5,3},{10,12},{11,13},{12,10},{13,11},{18,20},{1... | collective-permute-start | bytes 1572872 | tf_op jit(solution)/shard_map/ppermute | solution.py:656
  132.3 29.2 %collective-permute-start.33 = (bf16[64,4096]{1,0:T(8,128)(2,1)S(1)}, bf16[64,4096]{1,0:T(8,128)(2,1)S(1)}, u32[]{:S(2)}, u32[]{:S(2)}) collective-permute-start(bf16[64,4096]{1,0:T(8,128)(2,1)S(1)} %get-tuple-element.89), channel_id=1, source_target_pairs={{0,4},{1,5},{2,6},{3,7},{4,0},{5,1},{6,2},{7,3},{8,12},{9,13},{10,... | collective-permute-start | bytes 1572872 | tf_op jit(solution)/shard_map/ppermute | solution.py:656
  135.8 25.7 %collective-permute-start.34 = (bf16[64,4096]{1,0:T(8,128)(2,1)S(1)}, bf16[64,4096]{1,0:T(8,128)(2,1)S(1)}, u32[]{:S(2)}, u32[]{:S(2)}) collective-permute-start(bf16[64,4096]{1,0:T(8,128)(2,1)S(1)} %get-tuple-element.90), channel_id=1, source_target_pairs={{0,2},{1,3},{2,0},{3,1},{4,6},{5,7},{6,4},{7,5},{8,10},{9,11},{10,... | collective-permute-start | bytes 1572872 | tf_op jit(solution)/shard_map/ppermute | solution.py:656

commit v5 on v4

--- a/solution.py
+++ b/solution.py
@@ -118,29 +118,38 @@
 PIECES = 4
 
 
-def is_middle(info, chips):
-    return (info[1] > 0) & (info[1] < chips - 1)
+def mesh_place():
+    seq = lax.axis_index("seq")
+    return lax.axis_index("mod"), seq // 2, seq % 2
+
+
+def is_middle(chips):
+    chip = mesh_place()[1]
+    return (chip > 0) & (chip < chips - 1)
 
 
 def mode_of(info, slot):
-    return info[3 + slot]
+    return info[slot]
 
 
 def params(mib):
     return pltpu.CompilerParams(vmem_limit_bytes=mib << 20)
 
 
-def norm_rows(ids, modality, tokens, norm_gain, chips):
+def norm_rows(modality, doc_lengths, tokens, norm_gain, chips):
     rows, width = tokens.shape
     modes = norm_gain.shape[0]
     step = 16
     parts = 4
     part = rows // parts
-
-    def kernel(ids_ref, modality_ref, tokens_ref, gain_ref, out_ref, info_ref, *scratch):
-        rows_ref, gains_ref, table_ref, row_sems, sems = scratch
+    docs = doc_lengths.shape[0]
+
+    def kernel(modality_ref, docs_ref, tokens_ref, gain_ref, out_ref, info_ref, *scratch):
+        rows_ref, gains_ref, table_ref, lengths_ref, row_sems, sems = scratch
         table_copy = pltpu.make_async_copy(modality_ref, table_ref, sems.at[0])
         table_copy.start()
+        lengths_copy = pltpu.make_async_copy(docs_ref, lengths_ref, sems.at[2])
+        lengths_copy.start()
         gain_copy = pltpu.make_async_copy(gain_ref, gains_ref, sems.at[1])
         gain_copy.start()
         row_copies = [
@@ -154,12 +163,15 @@
         for copy in row_copies:
             copy.start()
         table_copy.wait()
-        for i in range(3):
-            info_ref[i] = ids_ref[i]
+        lengths_copy.wait()
+        mu, chip, _ = mesh_place()
         for slot in range(chips):
-            at = ids_ref[0] * chips + jnp.bitwise_xor(ids_ref[1], slot)
-            info_ref[3 + slot] = table_ref[at]
-        mode = table_ref[ids_ref[0] * chips + ids_ref[1]]
+            info_ref[slot] = table_ref[mu * chips + jnp.bitwise_xor(chip, slot)]
+        end = jnp.int32(0)
+        for i in range(docs):
+            end = end + lengths_ref[i]
+            info_ref[chips + i] = end
+        mode = table_ref[mu * chips + chip]
         gain_copy.wait()
         gain = gains_ref[pl.ds(mode, 1), :]
         for i in range(parts):
@@ -174,26 +186,27 @@
         kernel,
         out_shape=[
             pltpu.VMEM((rows, width), jnp.bfloat16),
-            jax.ShapeDtypeStruct((3 + chips,), jnp.int32),
+            jax.ShapeDtypeStruct((chips + docs,), jnp.int32),
         ],
-        in_specs=[SMEM, HBM, HBM, HBM],
+        in_specs=[HBM] * 4,
         out_specs=[VMEM, SMEM],
         scratch_shapes=[
             pltpu.VMEM((rows, width), jnp.bfloat16),
             pltpu.VMEM((modes, width), jnp.float32),
             pltpu.SMEM(modality.shape, jnp.int32),
+            pltpu.SMEM(doc_lengths.shape, jnp.int32),
             pltpu.SemaphoreType.DMA((parts,)),
-            pltpu.SemaphoreType.DMA((2,)),
+            pltpu.SemaphoreType.DMA((3,)),
         ],
         compiler_params=params(8),
         cost_estimate=pl.CostEstimate(flops=4_000_000, bytes_accessed=1 << 20, transcendentals=64),
         name="norm_rows",
-    )(ids, modality, tokens, norm_gain)
+    )(modality, doc_lengths, tokens, norm_gain)
 
 
 def weight_copies(info_ref, weight_ref, buffer_ref, sems, slot, pair, at):
     pieces, piece, pair_cols = buffer_ref.shape[1:]
-    first = jnp.bitwise_xor(info_ref[0] // 2, pair) * pair_cols
+    first = jnp.bitwise_xor(mesh_place()[0] // 2, pair) * pair_cols
     return [
         pltpu.make_async_copy(
             weight_ref.at[
@@ -252,7 +265,7 @@
         self.scratch = pltpu.SemaphoreType.DMA((len(turns),))
 
     def copies(self, info_ref, weight_ref, kept_refs, sems):
-        middle = is_middle(info_ref, self.chips)
+        middle = is_middle(self.chips)
         return [
             pltpu.make_async_copy(
                 weight_ref.at[mode_of(info_ref, jnp.where(middle, turn[1], turn[0]))],
@@ -272,10 +285,10 @@
             copy.wait()
 
 
-def store_pair(info_ref, outs, rows, p, result):
+def store_pair(outs, rows, p, result):
     result = result.astype(jnp.bfloat16)
     cols = result.shape[1] // 2
-    odd = info_ref[0] % 2 == 1
+    odd = mesh_place()[0] % 2 == 1
     for e in range(2):
         first, last = result[:, e * cols : (e + 1) * cols], result[:, (1 - e) * cols : (2 - e) * cols]
         outs[2 * p + e][rows, :] = jnp.where(odd, last, first)
@@ -315,7 +328,7 @@
         for copy in [copy for copies in fetched.values() for copy in copies] + later:
             copy.start()
 
-        @pl.when(info_ref[1] >= 0)
+        @pl.when(mesh_place()[1] >= 0)
         def _():
             for i, (n, p) in enumerate(steps):
                 result = None
@@ -331,7 +344,7 @@
                     )
                     part = jnp.dot(rows, part_ref[at, k], preferred_element_type=jnp.float32)
                     result = part if result is None else result + part
-                store_pair(info_ref, outs, pl.ds(n * block, block), p, result)
+                store_pair(outs, pl.ds(n * block, block), p, result)
 
         for copy in later:
             copy.wait()
@@ -357,19 +370,15 @@
     )(info, *[piece for pair in parts for piece in pair], *ready, weight)
 
 
-def project_late(info, inner, relayed, weight, cols, chips, prefetch):
+def project_late(inner, relayed, weight, cols, chips):
     half, width = inner[0].shape
     block = 2 * half
     pairs, pieces, piece, pair_cols = weight.shape
     heads = pairs * pair_cols // cols
 
-    kept = len(prefetch.turns)
-
-    def kernel(info_ref, inner_own, inner_partner, relayed_own, relayed_partner, weight_ref, *refs):
-        next_ref, outs, kept_refs = refs[0], refs[1 : 1 + heads], refs[1 + heads : 1 + heads + kept]
-        rows_ref, sems = refs[1 + heads + kept :]
-        prefetch.start(info_ref, next_ref, kept_refs, sems)
-        middle = is_middle(info_ref, chips)
+    def kernel(inner_own, inner_partner, relayed_own, relayed_partner, weight_ref, *refs):
+        outs, rows_ref = refs[:heads], refs[heads]
+        middle = is_middle(chips)
 
         @pl.when(middle)
         def _():
@@ -390,15 +399,14 @@
                     preferred_element_type=jnp.float32,
                 )
                 result = part if result is None else result + part
-            store_pair(info_ref, outs, pl.ds(0, block), p, result)
-        prefetch.wait(info_ref, next_ref, kept_refs, sems)
-
-    return pl.pallas_call(
-        kernel,
-        out_shape=[pltpu.VMEM((block, cols), jnp.bfloat16)] * heads + prefetch.shapes,
-        in_specs=[SMEM] + [VMEM] * 5 + [HBM],
-        out_specs=[VMEM] * (heads + kept),
-        scratch_shapes=[pltpu.VMEM((block, width), jnp.bfloat16), prefetch.scratch],
+            store_pair(outs, pl.ds(0, block), p, result)
+
+    return pl.pallas_call(
+        kernel,
+        out_shape=[pltpu.VMEM((block, cols), jnp.bfloat16)] * heads,
+        in_specs=[VMEM] * 5,
+        out_specs=[VMEM] * heads,
+        scratch_shapes=[pltpu.VMEM((block, width), jnp.bfloat16)],
         compiler_params=params(8),
         cost_estimate=pl.CostEstimate(
             flops=2 * block * width * cols * heads,
@@ -406,29 +414,29 @@
             transcendentals=0,
         ),
         name="project_late",
-    )(info, *inner, *relayed, weight, prefetch.weight)
-
-
-def attend_slots(info, doc_lengths, sets, turns, chips, prefetch):
+    )(*inner, *relayed, weight)
+
+
+def attend_slots(info, docs, sets, turns, chips, prefetch):
     count = len(sets[0][1])
     block = sets[0][1][0].shape[0] // len(sets[0][0])
     total = count * chips * block
     window = min(total // 2 + block, total)
     scale = 1.0 / math.sqrt(HDIM)
-    docs = doc_lengths.shape[0]
 
     kept = len(prefetch.turns)
 
-    def kernel(info_ref, docs_ref, *refs):
+    def kernel(info_ref, *refs):
         ins, refs = refs[: len(sets) * count], refs[len(sets) * count :]
         next_ref, outs, kept_refs = refs[0], refs[1 : 1 + count], refs[1 + count : 1 + count + kept]
         keys_ref, values_ref, sems = refs[1 + count + kept :]
         prefetch.start(info_ref, next_ref, kept_refs, sems)
 
-        @pl.when(info_ref[1] >= 0)
+        @pl.when(mesh_place()[1] >= 0)
         def _():
-            middle = is_middle(info_ref, chips)
-            mu, chip, own_first = info_ref[0], info_ref[1], info_ref[2] * (block // 2)
+            middle = is_middle(chips)
+            mu, chip, core = mesh_place()
+            own_first = core * (block // 2)
 
             def slot_rows(d, slot, part):
                 for i, (slots, _) in enumerate(sets):
@@ -443,11 +451,7 @@
                     keys_ref[place, :] = slot_rows(d, slot, 1)
                     values_ref[place, :] = slot_rows(d, slot, 2)
 
-            ends = []
-            end = jnp.int32(0)
-            for i in range(docs):
-                end = end + docs_ref[i]
-                ends.append(end)
+            ends = [info_ref[chips + i] for i in range(docs)]
             row_place = lax.broadcasted_iota(jnp.int32, (block, 1), 0) + own_first
             row_place = jnp.where(row_place >= block, row_place - block, row_place)
             key_iota = lax.broadcasted_iota(jnp.int32, (1, window), 1)
@@ -497,7 +501,7 @@
         kernel,
         out_shape=[pltpu.VMEM((len(turns) * block, HDIM), jnp.bfloat16)] * count
         + prefetch.shapes,
-        in_specs=[SMEM, SMEM] + [VMEM] * (len(sets) * count) + [HBM],
+        in_specs=[SMEM] + [VMEM] * (len(sets) * count) + [HBM],
         out_specs=[VMEM] * (count + kept),
         scratch_shapes=[
             pltpu.VMEM((total, HDIM), jnp.bfloat16),
@@ -511,10 +515,10 @@
             transcendentals=n_queries * block * window,
         ),
         name="attend_slots",
-    )(info, doc_lengths, *[piece for _, pieces in sets for piece in pieces], prefetch.weight)
-
-
-def output_rows(info, pieces, weight, index, turns):
+    )(info, *[piece for _, pieces in sets for piece in pieces], prefetch.weight)
+
+
+def output_rows(pieces, weight, index, turns):
     count = len(pieces)
     block = pieces[0].shape[0] // turns
     half = block // 2
@@ -522,11 +526,11 @@
     depth, width = weight.shape
     tile = min(1024, width)
 
-    def kernel(info_ref, *refs):
+    def kernel(*refs):
         ins = refs[:count]
         weight_ref, own_ref, partner_ref, heads_ref = refs[count:]
         for d in range(count):
-            heads_ref[jnp.bitwise_xor(info_ref[0], d)] = ins[d][at : at + block, :]
+            heads_ref[jnp.bitwise_xor(mesh_place()[0], d)] = ins[d][at : at + block, :]
         rows = jnp.concatenate([heads_ref[h] for h in range(count)], axis=1)
         for first in range(0, width, tile):
             cols = slice(first, first + tile)
@@ -538,7 +542,7 @@
     return pl.pallas_call(
         kernel,
         out_shape=[pltpu.VMEM((half, width), jnp.bfloat16)] * 2,
-        in_specs=[SMEM] + [VMEM] * (count + 1),
+        in_specs= [VMEM] * (count + 1),
         out_specs=[VMEM] * 2,
         scratch_shapes=[pltpu.VMEM((count, block, HDIM), jnp.bfloat16)],
         compiler_params=params(8),
@@ -548,7 +552,7 @@
             transcendentals=0,
         ),
         name="output_rows",
-    )(info, *pieces, weight)
+    )(*pieces, weight)
 
 
 def in_vmem(*values):
@@ -573,9 +577,9 @@
     )(*in_vmem(first, second))
 
 
-def relay_rows(info, chips, own, partner, passing, otherwise):
-    def kernel(info_ref, own_ref, partner_ref, passing_ref, otherwise_ref, sum_ref, relay_ref):
-        middle = is_middle(info_ref, chips)
+def relay_rows(chips, own, partner, passing, otherwise):
+    def kernel(own_ref, partner_ref, passing_ref, otherwise_ref, sum_ref, relay_ref):
+        middle = is_middle(chips)
 
         @pl.when(middle)
         def _():
@@ -593,23 +597,23 @@
     return pl.pallas_call(
         kernel,
         out_shape=[pltpu.VMEM(own.shape, jnp.bfloat16)] * 2,
-        in_specs=[SMEM] + [VMEM] * 4,
+        in_specs=[VMEM] * 4,
         out_specs=[VMEM] * 2,
         compiler_params=params(4),
         cost_estimate=pl.CostEstimate(
             flops=4 * own.size, bytes_accessed=12 * own.size, transcendentals=0
         ),
         name="relay_rows",
-    )(info, *in_vmem(own, partner, passing, otherwise))
-
-
-def last_rows(info, chips, early, far, middle_only):
+    )(*in_vmem(own, partner, passing, otherwise))
+
+
+def last_rows(chips, early, far, middle_only):
     rows, width = far.shape
     parts = 4
     part = rows // parts
 
-    def kernel(info_ref, early_ref, far_ref, middle_ref, out_ref, done_ref, sems):
-        factor = jnp.where(is_middle(info_ref, chips), 1.0, 0.0)
+    def kernel(early_ref, far_ref, middle_ref, out_ref, done_ref, sems):
+        factor = jnp.where(is_middle(chips), 1.0, 0.0)
         copies = []
         for i in range(parts):
             at = pl.ds(i * part, part)
@@ -624,7 +628,7 @@
     return pl.pallas_call(
         kernel,
         out_shape=pltpu.HBM(far.shape, jnp.bfloat16),
-        in_specs=[SMEM, VMEM, VMEM, VMEM],
+        in_specs=[VMEM] * 3,
         out_specs=HBM,
         scratch_shapes=[
             pltpu.VMEM((rows, width), jnp.bfloat16),
@@ -635,7 +639,7 @@
             flops=4 * far.size, bytes_accessed=10 * far.size, transcendentals=0
         ),
         name="last_rows",
-    )(info, *in_vmem(early, far, middle_only))
+    )(*in_vmem(early, far, middle_only))
 
 
 def chip_pairs(pairs):
@@ -646,9 +650,7 @@
     seq_count = lax.axis_size("seq")
     mod_count = lax.axis_size("mod")
     chips = seq_count // 2
-    mu = lax.axis_index("mod").astype(jnp.int32)
-    seq = lax.axis_index("seq").astype(jnp.int32)
-    ids = jnp.stack([mu, seq // 2, seq % 2])
+    seq = lax.axis_index("seq")
     qkv_weight = pltpu.with_memory_space_constraint(qkv_weight, pltpu.HBM)
     out_weight = pltpu.with_memory_space_constraint(out_weight, pltpu.HBM)
 
@@ -666,9 +668,10 @@
 
     in_hbm = [
         pltpu.with_memory_space_constraint(value, pltpu.HBM)
-        for value in (modality, tokens, norm_gain)
+        for value in (modality, doc_lengths, tokens, norm_gain)
     ]
-    normed, info = norm_rows(ids, *in_hbm, chips)
+    normed, info = norm_rows(*in_hbm, chips)
+    docs = doc_lengths.shape[0]
     two = along(normed, [(i, i ^ 2) for i in range(chips)])
     one = along(normed, [(i, i ^ 1) for i in range(chips)])
     inner = along(normed, [(1, 2), (2, 1)])
@@ -689,33 +692,25 @@
         info, [two_pair, one_pair], qkv_weight, (2, 1), ready=(two_weight, one_weight)
     )
     mid = exchange(mid)
-    *late, kept_a = project_late(
-        info,
-        inner_pair,
-        relayed_pair,
-        late_weight,
-        3 * HDIM,
-        chips,
-        Prefetch(out_weight, (turn_a,), chips),
-    )
+    late = project_late(inner_pair, relayed_pair, late_weight, 3 * HDIM, chips)
     late = exchange(late)
     sets = (((0,), own), ((2, 1), mid), ((3,), late))
 
     def finish(pieces, kept, index, turns):
-        own_share, partner_share = output_rows(info, pieces, kept, index, turns)
+        own_share, partner_share = output_rows(pieces, kept, index, turns)
         return own_share, swap(partner_share)
 
-    *first, kept_b = attend_slots(
+    *first, kept_a, kept_b = attend_slots(
         info,
-        doc_lengths,
+        docs,
         sets,
         (turn_a, turn_b),
         chips,
-        Prefetch(out_weight, (turn_b,), chips),
+        Prefetch(out_weight, (turn_a, turn_b), chips),
     )
     first = exchange(first)
     *rest_c, kept_c = attend_slots(
-        info, doc_lengths, sets, (turn_c,), chips, Prefetch(out_weight, (turn_c,), chips)
+        info, docs, sets, (turn_c,), chips, Prefetch(out_weight, (turn_c,), chips)
     )
     sum_a = add_rows(*finish(first, kept_a, 0, 2))
     own_b, partner_b = finish(first, kept_b, 1, 2)
@@ -726,11 +721,11 @@
     shares_c = finish(rest_c, kept_c, 0, 1)
     chip = seq // 2
     middle = (chip > 0) & (chip < chips - 1)
-    sum_c, relay_sum = relay_rows(info, chips, *shares_c, from_one, sum_b)
+    sum_c, relay_sum = relay_rows(chips, *shares_c, from_one, sum_b)
     from_two = along(relay_sum, [(i, i ^ 2) for i in range(chips)])
     from_end = along(sum_c, [(i, i ^ 1) for i in range(chips)])
     *rest_d, kept_d = attend_slots(
-        info, doc_lengths, sets, (turn_d,), chips, Prefetch(out_weight, (turn_d,), chips)
+        info, docs, sets, (turn_d,), chips, Prefetch(out_weight, (turn_d,), chips)
     )
     rest_d = exchange(rest_d)
     shares_d = finish(rest_d, kept_d, 0, 1)
@@ -738,7 +733,7 @@
     early = tokens.astype(jnp.float32)
     for share in (*shares_d, near):
         early = early + share.astype(jnp.float32)
-    return last_rows(info, chips, early, from_two, from_end)
+    return last_rows(chips, early, from_two, from_end)
 
 
 def solution(mesh):

time: 163 us -> 160 us (0.982)
  Pallas kernels: 46.7 us -> 42.3 us
    pallas_call x4, Pallas kernels: 6.7 us -> 4.63 us  [output_rows(): pl.pallas_call(kernel, out_shape=[pltpu.VMEM((half, width), jnp.bfloat16)...]
    ppermute x18, waiting for transfers between devices: 12.4 us -> 14.1 us  [exchange(): lax.ppermute(pieces[d], 'mod', [(i, i ^ d) for i in range(mod_count)])]
  transfers between devices with their start and end apart: 35 -> 35, of which waited for: 11 -> 13; matrix products, arithmetic and copies ran while one was open for 1% -> 1% of each run, Pallas kernels for 22% -> 21%
where the time goes in v5:
time: 160 us
  waiting for transfers between devices  78.3 us (49%)
  Pallas kernels  42.3 us (26%)
  starting transfers between devices  37.5 us (23%)
  other arithmetic  1.63 us (1%)
    ppermute x8, waiting for transfers between devices, along(): return lax.ppermute(value, 'seq', chip_pairs(pairs))  64.2 us
    ppermute x18, starting transfers between devices, exchange(): lax.ppermute(pieces[d], 'mod', [(i, i ^ d) for i in range(mod_count)])  21.3 us
    ppermute x8, starting transfers between devices, along(): return lax.ppermute(value, 'seq', chip_pairs(pairs))  15.1 us
    pallas_call x2, Pallas kernels, project_slots(): pl.pallas_call(kernel, out_shape=[pltpu.VMEM((count * block, cols), jnp.b...  15 us
    ppermute x18, waiting for transfers between devices, exchange(): lax.ppermute(pieces[d], 'mod', [(i, i ^ d) for i in range(mod_count)])  14.1 us
    pallas_call x3, Pallas kernels, attend_slots(): pl.pallas_call(kernel, out_shape=[pltpu.VMEM((len(turns) * block, HDIM),...  10.2 us
    pallas_call x1, Pallas kernels, fetch_weights(): pl.pallas_call(kernel, out_shape=[pltpu.VMEM(shape, jnp.bfloat16) for sha...  7.08 us
    pallas_call x4, Pallas kernels, output_rows(): pl.pallas_call(kernel, out_shape=[pltpu.VMEM((half, width), jnp.bfloat16)...  4.63 us
  transfers between devices with their start and end apart: 35, of which 13 were waited for; matrix products, arithmetic and copies ran while one was open for 1% of the time, Pallas kernels for 21%

profile of v5, /device:TPU:0, one launch (start us, length us, event | category | flops | bytes accessed | tf_op | source)
XLA Modules:
  0.0 160.1 jit_solution(15701634401049121613)
XLA Ops:
  0.0 2.1 %norm_rows.1 = (bf16[64,4096]{1,0:T(8,128)(2,1)S(1)}, s32[8]{0:T(128)S(1)}) custom-call(s32[16]{0:T(128)} %modality_ref.1, s32[4]{0:T(128)} %docs_ref.1, bf16[64,4096]{1,0:T(8,128)(2,1)} %tokens_ref.1, f32[3,4096]{1,0:T(4,128)} %gain_ref.1), custom_call_target="tpu_custom_call" | custom-call | flops 4000000 | bytes 1048576 | tf_op jit(solution)/shard_map/norm_rows/pallas_call | solution.py:185
  2.1 4.1 %collective-permute-start.4 = (bf16[64,4096]{1,0:T(8,128)(2,1)S(1)}, bf16[64,4096]{1,0:T(8,128)(2,1)S(1)}, u32[]{:S(2)}, u32[]{:S(2)}) collective-permute-start(bf16[64,4096]{1,0:T(8,128)(2,1)S(1)} %get-tuple-element.49.refs_0_), channel_id=1, source_target_pairs={{0,4},{1,5},{2,6},{3,7},{4,0},{5,1},{6,2},{7,3},{8,12},{9,13},{10,... | collective-permute-start | bytes 1572872 | tf_op jit(solution)/shard_map/ppermute | solution.py:658
  6.3 0.7 collective-permute-start.11
  7.0 2.9 %collective-permute-start.6 = (bf16[64,4096]{1,0:T(8,128)(2,1)S(1)}, bf16[64,4096]{1,0:T(8,128)(2,1)S(1)}, u32[]{:S(2)}, u32[]{:S(2)}) collective-permute-start(bf16[64,4096]{1,0:T(8,128)(2,1)S(1)} %get-tuple-element.49.refs_0_), channel_id=1, source_target_pairs={{0,2},{1,3},{2,0},{3,1},{4,6},{5,7},{6,4},{7,5},{8,10},{9,11},{10,... | collective-permute-start | bytes 1572872 | tf_op jit(solution)/shard_map/ppermute | solution.py:658
  9.8 20.5 %collective-permute-done.4.refs_0_ = bf16[64,4096]{1,0:T(8,128)(2,1)S(1)} collective-permute-done((bf16[64,4096]{1,0:T(8,128)(2,1)S(1)}, bf16[64,4096]{1,0:T(8,128)(2,1)S(1)}, u32[]{:S(2)}, u32[]{:S(2)}) %collective-permute-start.4) | collective-permute-done | bytes 524320 | tf_op jit(solution)/shard_map/ppermute | solution.py:658
  30.3 0.5 collective-permute-start.5
  30.8 0.0 collective-permute-start.12
  30.8 0.9 collective-permute-done.6.refs_2_
  31.8 0.0 collective-permute-start.7
  31.8 11.0 %collective-permute-done.13.relayed_own = bf16[64,4096]{1,0:T(8,128)(2,1)S(1)} collective-permute-done((bf16[64,4096]{1,0:T(8,128)(2,1)S(1)}, bf16[64,4096]{1,0:T(8,128)(2,1)S(1)}, u32[]{:S(2)}, u32[]{:S(2)}) %collective-permute-start.13) | collective-permute-done | bytes 524320 | tf_op jit(solution)/shard_map/ppermute | solution.py:658
  42.8 7.1 %fetch_weights.1 = (bf16[2,4,1024,768]{3,2,1,0:T(8,128)(2,1)S(1)}, bf16[1,4,1024,768]{3,2,1,0:T(8,128)(2,1)S(1)}) custom-call(s32[8]{0:T(128)S(1)} %get-tuple-element.48.info_ref, bf16[3,4096,1536]{2,1,0:T(8,128)(2,1)} %refs_6_.1), custom_call_target="tpu_custom_call" | custom-call | flops 6000000000 | bytes 26214400 | tf_op jit(solution)/shard_map/fetch_weights/pallas_call | solution.py:247
  49.9 0.0 collective-permute-done.refs_1_
  49.9 9.0 %project_slots.2 = (bf16[128,384]{1,0:T(8,128)(2,1)S(1)}, bf16[128,384]{1,0:T(8,128)(2,1)S(1)}, bf16[128,384]{1,0:T(8,128)(2,1)S(1)}, bf16[128,384]{1,0:T(8,128)(2,1)S(1)}, bf16[2,4,1024,768]{3,2,1,0:T(8,128)(2,1)S(1)}) custom-call(s32[8]{0:T(128)S(1)} %get-tuple-element.48.info_ref, bf16[64,4096]{1,0:T(8,128)(2,1)S(1)} %get-tuple-element.49.refs_0_, ...), custom_call_target="tpu_custom_call" | custom-call | flops 1610612736 | bytes 12582912 | tf_op jit(solution)/shard_map/project_slots/pallas_call | solution.py:352
  58.9 2.0 %collective-permute-start.1 = (bf16[128,384]{1,0:T(8,128)(2,1)S(1)}, bf16[128,384]{1,0:T(8,128)(2,1)S(1)}, u32[]{:S(2)}, u32[]{:S(2)}) collective-permute-start(bf16[128,384]{1,0:T(8,128)(2,1)S(1)} %get-tuple-element.51), channel_id=1, source_target_pairs={{0,8},{8,0},{16,24},{24,16},{1,9},{9,1},{17,25},{25,17},{2,10},{10... | collective-permute-start | bytes 294920 | tf_op jit(solution)/shard_map/ppermute | solution.py:666
  60.9 6.0 %project_slots.3 = (bf16[256,384]{1,0:T(8,128)(2,1)S(1)}, bf16[256,384]{1,0:T(8,128)(2,1)S(1)}, bf16[256,384]{1,0:T(8,128)(2,1)S(1)}, bf16[256,384]{1,0:T(8,128)(2,1)S(1)}) custom-call(s32[8]{0:T(128)S(1)} %get-tuple-element.48.info_ref, bf16[64,4096]{1,0:T(8,128)(2,1)S(1)} %collective-permute-done.4.refs_0_, ...), custom_call_target="tpu_custom_call" | custom-call | flops 3221225472 | bytes 25165824 | tf_op jit(solution)/shard_map/project_slots/pallas_call | solution.py:352
  66.9 1.2 collective-permute-start.10
  68.1 0.5 collective-permute-start.2
  68.6 0.0 collective-permute-done.1.refs_1_
  68.6 2.5 %collective-permute-start.3 = (bf16[128,384]{1,0:T(8,128)(2,1)S(1)}, bf16[128,384]{1,0:T(8,128)(2,1)S(1)}, u32[]{:S(2)}, u32[]{:S(2)}) collective-permute-start(bf16[128,384]{1,0:T(8,128)(2,1)S(1)} %get-tuple-element.53), channel_id=1, source_target_pairs={{0,24},{8,16},{16,8},{24,0},{1,25},{9,17},{17,9},{25,1},{2,26},{10... | collective-permute-start | bytes 294920 | tf_op jit(solution)/shard_map/ppermute | solution.py:666
  71.1 0.0 collective-permute-done.12.inner_partner
  71.1 0.5 collective-permute-start.8
  71.6 0.0 collective-permute-done.14.relayed_partner
  71.6 0.5 collective-permute-start.9
  72.1 1.9 %project_late.1 = (bf16[128,384]{1,0:T(8,128)(2,1)S(1)}, bf16[128,384]{1,0:T(8,128)(2,1)S(1)}, bf16[128,384]{1,0:T(8,128)(2,1)S(1)}, bf16[128,384]{1,0:T(8,128)(2,1)S(1)}) custom-call(bf16[64,4096]{1,0:T(8,128)(2,1)S(1)} %collective-permute-done.11.inner_own, bf16[64,4096]{1,0:T(8,128)(2,1)S(1)} %collective-permute-done.12.inner_partner, ...), custom_call_target="tpu_custom_call" | custom-call | flops 1610612736 | bytes 12582912 | tf_op jit(solution)/shard_map/project_late/pallas_call | solution.py:404
  74.0 5.3 %collective-permute-done.2.refs_2_ = bf16[128,384]{1,0:T(8,128)(2,1)S(1)} collective-permute-done((bf16[128,384]{1,0:T(8,128)(2,1)S(1)}, bf16[128,384]{1,0:T(8,128)(2,1)S(1)}, u32[]{:S(2)}, u32[]{:S(2)}) %collective-permute-start.2) | collective-permute-done | bytes 98336 | tf_op jit(solution)/shard_map/ppermute | solution.py:666
  79.3 0.3 collective-permute-start.15
  79.6 1.4 collective-permute-start.16
  80.9 1.8 %collective-permute-start.17 = (bf16[128,384]{1,0:T(8,128)(2,1)S(1)}, bf16[128,384]{1,0:T(8,128)(2,1)S(1)}, u32[]{:S(2)}, u32[]{:S(2)}) collective-permute-start(bf16[128,384]{1,0:T(8,128)(2,1)S(1)} %get-tuple-element.64), channel_id=1, source_target_pairs={{0,24},{8,16},{16,8},{24,0},{1,25},{9,17},{17,9},{25,1},{2,26},{10... | collective-permute-start | bytes 294920 | tf_op jit(solution)/shard_map/ppermute | solution.py:666
  82.8 0.7 collective-permute-done.9.refs_6_
  83.5 1.3 collective-permute-done.15.refs_9_
  84.7 2.8 %collective-permute-done.16.refs_10_ = bf16[128,384]{1,0:T(8,128)(2,1)S(1)} collective-permute-done((bf16[128,384]{1,0:T(8,128)(2,1)S(1)}, bf16[128,384]{1,0:T(8,128)(2,1)S(1)}, u32[]{:S(2)}, u32[]{:S(2)}) %collective-permute-start.16) | collective-permute-done | bytes 98336 | tf_op jit(solution)/shard_map/ppermute | solution.py:666
  87.5 4.7 %attend_slots.4 = (bf16[256,128]{1,0:T(8,128)(2,1)S(1)}, bf16[256,128]{1,0:T(8,128)(2,1)S(1)}, bf16[256,128]{1,0:T(8,128)(2,1)S(1)}, bf16[256,128]{1,0:T(8,128)(...) custom-call(s32[8]{0:T(128)S(1)} %get-tuple-element.48.info_ref, ...), custom_call_target="tpu_custom_call" | custom-call | flops 1207959552 | bytes 1572864 | tf_op jit(solution)/shard_map/attend_slots/pallas_call | solution.py:500
  92.2 0.5 collective-permute-start.22
  92.7 1.3 collective-permute-start.23
  94.0 1.7 %collective-permute-start.24 = (bf16[256,128]{1,0:T(8,128)(2,1)S(1)}, bf16[256,128]{1,0:T(8,128)(2,1)S(1)}, u32[]{:S(2)}, u32[]{:S(2)}) collective-permute-start(bf16[256,128]{1,0:T(8,128)(2,1)S(1)} %get-tuple-element.75), channel_id=1, source_target_pairs={{0,24},{8,16},{16,8},{24,0},{1,25},{9,17},{17,9},{25,1},{2,26},{10... | collective-permute-start | bytes 196616 | tf_op jit(solution)/shard_map/ppermute | solution.py:666
  95.8 1.3 collective-permute-done.22.refs_1_
  97.0 0.5 collective-permute-done.23.refs_2_
  97.5 1.7 %collective-permute-done.24.refs_3_ = bf16[256,128]{1,0:T(8,128)(2,1)S(1)} collective-permute-done((bf16[256,128]{1,0:T(8,128)(2,1)S(1)}, bf16[256,128]{1,0:T(8,128)(2,1)S(1)}, u32[]{:S(2)}, u32[]{:S(2)}) %collective-permute-start.24) | collective-permute-done | bytes 65568 | tf_op jit(solution)/shard_map/ppermute | solution.py:666
  99.2 0.8 output_rows.6
  100.0 0.1 collective-permute-start.27
  100.0 0.8 output_rows.5
  100.8 0.6 collective-permute-start.25
  101.4 2.8 %attend_slots.5 = (bf16[128,128]{1,0:T(8,128)(2,1)S(1)}, bf16[128,128]{1,0:T(8,128)(2,1)S(1)}, bf16[128,128]{1,0:T(8,128)(2,1)S(1)}, bf16[128,128]{1,0:T(8,128)(2,1)S(1)}, bf16[512,4096]{1,0:T(8,128)(2,1)S(1)}) custom-call(s32[8]{0:T(128)S(1)} %get-tuple-element.48.info_ref, bf16[128,384]{1,0:T(8,128)(2,1)S(1)} %get-tuple-element.50.refs_0_, ...), custom_call_target="tpu_custom_call" | custom-call | flops 603979776 | bytes 1572864 | tf_op jit(solution)/shard_map/attend_slots/pallas_call | solution.py:500
  104.1 1.0 collective-permute-start.29
  105.2 1.4 collective-permute-start.30
  106.5 1.2 collective-permute-start.31
  107.7 2.8 %attend_slots.3 = (bf16[128,128]{1,0:T(8,128)(2,1)S(1)}, bf16[128,128]{1,0:T(8,128)(2,1)S(1)}, bf16[128,128]{1,0:T(8,128)(2,1)S(1)}, bf16[128,128]{1,0:T(8,128)(2,1)S(1)}, bf16[512,4096]{1,0:T(8,128)(2,1)S(1)}) custom-call(s32[8]{0:T(128)S(1)} %get-tuple-element.48.info_ref, bf16[128,384]{1,0:T(8,128)(2,1)S(1)} %get-tuple-element.50.refs_0_, ...), custom_call_target="tpu_custom_call" | custom-call | flops 603979776 | bytes 1572864 | tf_op jit(solution)/shard_map/attend_slots/pallas_call | solution.py:500
  110.5 1.0 collective-permute-start.18
  111.5 1.4 collective-permute-start.19
  112.8 1.2 collective-permute-start.20
  114.0 1.6 output_rows.7
  115.6 0.1 add_rows.3
  115.7 1.3 collective-permute-start.28
  117.0 0.7 collective-permute-done.20.refs_3_
  117.7 1.6 output_rows.4
  119.2 0.1 add_rows.2.otherwise_ref
  119.3 1.5 collective-permute-start.26
  120.8 9.3 %collective-permute-done.28.passing_ref = bf16[64,4096]{1,0:T(8,128)(2,1)S(1)} collective-permute-done((bf16[64,4096]{1,0:T(8,128)(2,1)S(1)}, bf16[64,4096]{1,0:T(8,128)(2,1)S(1)}, u32[]{:S(2)}, u32[]{:S(2)}) %collective-permute-start.28) | collective-permute-done | bytes 524320 | tf_op jit(solution)/shard_map/ppermute | solution.py:658
  130.1 0.1 relay_rows.1
  130.3 3.0 %collective-permute-start.33 = (bf16[64,4096]{1,0:T(8,128)(2,1)S(1)}, bf16[64,4096]{1,0:T(8,128)(2,1)S(1)}, u32[]{:S(2)}, u32[]{:S(2)}) collective-permute-start(bf16[64,4096]{1,0:T(8,128)(2,1)S(1)} %get-tuple-element.89), channel_id=1, source_target_pairs={{0,4},{1,5},{2,6},{3,7},{4,0},{5,1},{6,2},{7,3},{8,12},{9,13},{10,... | collective-permute-start | bytes 1572872 | tf_op jit(solution)/shard_map/ppermute | solution.py:658
  133.3 1.6 %collective-permute-start.34 = (bf16[64,4096]{1,0:T(8,128)(2,1)S(1)}, bf16[64,4096]{1,0:T(8,128)(2,1)S(1)}, u32[]{:S(2)}, u32[]{:S(2)}) collective-permute-start(bf16[64,4096]{1,0:T(8,128)(2,1)S(1)} %get-tuple-element.90), channel_id=1, source_target_pairs={{0,2},{1,3},{2,0},{3,1},{4,6},{5,7},{6,4},{7,5},{8,10},{9,11},{10,... | collective-permute-start | bytes 1572872 | tf_op jit(solution)/shard_map/ppermute | solution.py:658
  134.9 1.6 %convert_add_fusion.early_ref = f32[64,4096]{1,0:T(8,128)S(1)} fusion(bf16[64,4096]{1,0:T(8,128)(2,1)} %collective-permute-done.21, bf16[64,4096]{1,0:T(8,128)(2,1)S(1)} %get-tuple-element.70, bf16[64,4096]{1,0:T(8,128)(2,1)} %tokens_ref.1, bf16[64,4096]{1,0:T(8,128)(2,1)} %collective-permute-done.26, ...), kind=kLoop, calls=%fused_computation | loop fusion | flops 2097152 | bytes 3670017 | tf_op jit(solution)/shard_map/add | solution.py:735
  136.6 22.5 %collective-permute-done.33.far_ref = bf16[64,4096]{1,0:T(8,128)(2,1)S(1)} collective-permute-done((bf16[64,4096]{1,0:T(8,128)(2,1)S(1)}, bf16[64,4096]{1,0:T(8,128)(2,1)S(1)}, u32[]{:S(2)}, u32[]{:S(2)}) %collective-permute-start.33) | collective-permute-done | bytes 524320 | tf_op jit(solution)/shard_map/ppermute | solution.py:658
  159.0 0.9 last_rows.1
  (23 shorter events, 0.1 us)
Async XLA Ops:
  2.1 28.2 %collective-permute-start.4 = (bf16[64,4096]{1,0:T(8,128)(2,1)S(1)}, bf16[64,4096]{1,0:T(8,128)(2,1)S(1)}, u32[]{:S(2)}, u32[]{:S(2)}) collective-permute-start(bf16[64,4096]{1,0:T(8,128)(2,1)S(1)} %get-tuple-element.49.refs_0_), channel_id=1, source_target_pairs={{0,4},{1,5},{2,6},{3,7},{4,0},{5,1},{6,2},{7,3},{8,12},{9,13},{10,... | collective-permute-start | bytes 1572872 | tf_op jit(solution)/shard_map/ppermute | solution.py:658
  6.3 24.6 %collective-permute-start.11 = (bf16[64,4096]{1,0:T(8,128)(2,1)S(1)}, bf16[64,4096]{1,0:T(8,128)(2,1)S(1)}, u32[]{:S(2)}, u32[]{:S(2)}) collective-permute-start(bf16[64,4096]{1,0:T(8,128)(2,1)S(1)} %get-tuple-element.49.refs_0_), channel_id=1, source_target_pairs={{2,4},{3,5},{4,2},{5,3},{10,12},{11,13},{12,10},{13,11},{18,20},{1... | collective-permute-start | bytes 1572872 | tf_op jit(solution)/shard_map/ppermute | solution.py:658
  7.0 24.8 %collective-permute-start.6 = (bf16[64,4096]{1,0:T(8,128)(2,1)S(1)}, bf16[64,4096]{1,0:T(8,128)(2,1)S(1)}, u32[]{:S(2)}, u32[]{:S(2)}) collective-permute-start(bf16[64,4096]{1,0:T(8,128)(2,1)S(1)} %get-tuple-element.49.refs_0_), channel_id=1, source_target_pairs={{0,2},{1,3},{2,0},{3,1},{4,6},{5,7},{6,4},{7,5},{8,10},{9,11},{10,... | collective-permute-start | bytes 1572872 | tf_op jit(solution)/shard_map/ppermute | solution.py:658
  30.3 12.5 %collective-permute-start.13 = (bf16[64,4096]{1,0:T(8,128)(2,1)S(1)}, bf16[64,4096]{1,0:T(8,128)(2,1)S(1)}, u32[]{:S(2)}, u32[]{:S(2)}) collective-permute-start(bf16[64,4096]{1,0:T(8,128)(2,1)S(1)} %collective-permute-done.4.refs_0_), channel_id=1, source_target_pairs={{0,2},{1,3},{2,0},{3,1},{4,6},{5,7},{6,4},{7,5},{8,10},{9,11},{10,... | collective-permute-start | bytes 1572872 | tf_op jit(solution)/shard_map/ppermute | solution.py:658
  30.3 19.5 %collective-permute-start = (bf16[64,4096]{1,0:T(8,128)(2,1)S(1)}, bf16[64,4096]{1,0:T(8,128)(2,1)S(1)}, u32[]{:S(2)}, u32[]{:S(2)}) collective-permute-start(bf16[64,4096]{1,0:T(8,128)(2,1)S(1)} %get-tuple-element.49.refs_0_), channel_id=1, source_target_pairs={{0,1},{1,0},{2,3},{3,2},{4,5},{5,4},{6,7},{7,6},{8,9},{9,8},{10,11... | collective-permute-start | bytes 1572872 | tf_op jit(solution)/shard_map/ppermute | solution.py:661
  30.3 30.6 %collective-permute-start.5 = (bf16[64,4096]{1,0:T(8,128)(2,1)S(1)}, bf16[64,4096]{1,0:T(8,128)(2,1)S(1)}, u32[]{:S(2)}, u32[]{:S(2)}) collective-permute-start(bf16[64,4096]{1,0:T(8,128)(2,1)S(1)} %collective-permute-done.4.refs_0_), channel_id=1, source_target_pairs={{0,1},{1,0},{2,3},{3,2},{4,5},{5,4},{6,7},{7,6},{8,9},{9,8},{10,11... | collective-permute-start | bytes 1572872 | tf_op jit(solution)/shard_map/ppermute | solution.py:661
  30.8 40.2 %collective-permute-start.12 = (bf16[64,4096]{1,0:T(8,128)(2,1)S(1)}, bf16[64,4096]{1,0:T(8,128)(2,1)S(1)}, u32[]{:S(2)}, u32[]{:S(2)}) collective-permute-start(bf16[64,4096]{1,0:T(8,128)(2,1)S(1)} %collective-permute-done.11.inner_own), channel_id=1, source_target_pairs={{0,1},{1,0},{2,3},{3,2},{4,5},{5,4},{6,7},{7,6},{8,9},{9,8},{10,11... | collective-permute-start | bytes 1572872 | tf_op jit(solution)/shard_map/ppermute | solution.py:661
  31.8 29.2 %collective-permute-start.7 = (bf16[64,4096]{1,0:T(8,128)(2,1)S(1)}, bf16[64,4096]{1,0:T(8,128)(2,1)S(1)}, u32[]{:S(2)}, u32[]{:S(2)}) collective-permute-start(bf16[64,4096]{1,0:T(8,128)(2,1)S(1)} %collective-permute-done.6.refs_2_), channel_id=1, source_target_pairs={{0,1},{1,0},{2,3},{3,2},{4,5},{5,4},{6,7},{7,6},{8,9},{9,8},{10,11... | collective-permute-start | bytes 1572872 | tf_op jit(solution)/shard_map/ppermute | solution.py:661
  42.8 28.8 %collective-permute-start.14 = (bf16[64,4096]{1,0:T(8,128)(2,1)S(1)}, bf16[64,4096]{1,0:T(8,128)(2,1)S(1)}, u32[]{:S(2)}, u32[]{:S(2)}) collective-permute-start(bf16[64,4096]{1,0:T(8,128)(2,1)S(1)} %collective-permute-done.13.relayed_own), channel_id=1, source_target_pairs={{0,1},{1,0},{2,3},{3,2},{4,5},{5,4},{6,7},{7,6},{8,9},{9,8},{10,11... | collective-permute-start | bytes 1572872 | tf_op jit(solution)/shard_map/ppermute | solution.py:661
  58.9 9.6 %collective-permute-start.1 = (bf16[128,384]{1,0:T(8,128)(2,1)S(1)}, bf16[128,384]{1,0:T(8,128)(2,1)S(1)}, u32[]{:S(2)}, u32[]{:S(2)}) collective-permute-start(bf16[128,384]{1,0:T(8,128)(2,1)S(1)} %get-tuple-element.51), channel_id=1, source_target_pairs={{0,8},{8,0},{16,24},{24,16},{1,9},{9,1},{17,25},{25,17},{2,10},{10... | collective-permute-start | bytes 294920 | tf_op jit(solution)/shard_map/ppermute | solution.py:666
  66.9 14.0 %collective-permute-start.10 = (bf16[256,384]{1,0:T(8,128)(2,1)S(1)}, bf16[256,384]{1,0:T(8,128)(2,1)S(1)}, u32[]{:S(2)}, u32[]{:S(2)}) collective-permute-start(bf16[256,384]{1,0:T(8,128)(2,1)S(1)} %get-tuple-element.59), channel_id=1, source_target_pairs={{0,24},{8,16},{16,8},{24,0},{1,25},{9,17},{17,9},{25,1},{2,26},{10... | collective-permute-start | bytes 589832 | tf_op jit(solution)/shard_map/ppermute | solution.py:666
  68.1 11.1 %collective-permute-start.2 = (bf16[128,384]{1,0:T(8,128)(2,1)S(1)}, bf16[128,384]{1,0:T(8,128)(2,1)S(1)}, u32[]{:S(2)}, u32[]{:S(2)}) collective-permute-start(bf16[128,384]{1,0:T(8,128)(2,1)S(1)} %get-tuple-element.52), channel_id=1, source_target_pairs={{0,16},{8,24},{16,0},{24,8},{1,17},{9,25},{17,1},{25,9},{2,18},{10... | collective-permute-start | bytes 294920 | tf_op jit(solution)/shard_map/ppermute | solution.py:666
  68.6 11.0 %collective-permute-start.3 = (bf16[128,384]{1,0:T(8,128)(2,1)S(1)}, bf16[128,384]{1,0:T(8,128)(2,1)S(1)}, u32[]{:S(2)}, u32[]{:S(2)}) collective-permute-start(bf16[128,384]{1,0:T(8,128)(2,1)S(1)} %get-tuple-element.53), channel_id=1, source_target_pairs={{0,24},{8,16},{16,8},{24,0},{1,25},{9,17},{17,9},{25,1},{2,26},{10... | collective-permute-start | bytes 294920 | tf_op jit(solution)/shard_map/ppermute | solution.py:666
  71.1 11.7 %collective-permute-start.8 = (bf16[256,384]{1,0:T(8,128)(2,1)S(1)}, bf16[256,384]{1,0:T(8,128)(2,1)S(1)}, u32[]{:S(2)}, u32[]{:S(2)}) collective-permute-start(bf16[256,384]{1,0:T(8,128)(2,1)S(1)} %get-tuple-element.57), channel_id=1, source_target_pairs={{0,8},{8,0},{16,24},{24,16},{1,9},{9,1},{17,25},{25,17},{2,10},{10... | collective-permute-start | bytes 589832 | tf_op jit(solution)/shard_map/ppermute | solution.py:666
  71.6 11.9 %collective-permute-start.9 = (bf16[256,384]{1,0:T(8,128)(2,1)S(1)}, bf16[256,384]{1,0:T(8,128)(2,1)S(1)}, u32[]{:S(2)}, u32[]{:S(2)}) collective-permute-start(bf16[256,384]{1,0:T(8,128)(2,1)S(1)} %get-tuple-element.58), channel_id=1, source_target_pairs={{0,16},{8,24},{16,0},{24,8},{1,17},{9,25},{17,1},{25,9},{2,18},{10... | collective-permute-start | bytes 589832 | tf_op jit(solution)/shard_map/ppermute | solution.py:666
  79.3 5.5 %collective-permute-start.15 = (bf16[128,384]{1,0:T(8,128)(2,1)S(1)}, bf16[128,384]{1,0:T(8,128)(2,1)S(1)}, u32[]{:S(2)}, u32[]{:S(2)}) collective-permute-start(bf16[128,384]{1,0:T(8,128)(2,1)S(1)} %get-tuple-element.62), channel_id=1, source_target_pairs={{0,8},{8,0},{16,24},{24,16},{1,9},{9,1},{17,25},{25,17},{2,10},{10... | collective-permute-start | bytes 294920 | tf_op jit(solution)/shard_map/ppermute | solution.py:666
  79.6 7.9 %collective-permute-start.16 = (bf16[128,384]{1,0:T(8,128)(2,1)S(1)}, bf16[128,384]{1,0:T(8,128)(2,1)S(1)}, u32[]{:S(2)}, u32[]{:S(2)}) collective-permute-start(bf16[128,384]{1,0:T(8,128)(2,1)S(1)} %get-tuple-element.63), channel_id=1, source_target_pairs={{0,16},{8,24},{16,0},{24,8},{1,17},{9,25},{17,1},{25,9},{2,18},{10... | collective-permute-start | bytes 294920 | tf_op jit(solution)/shard_map/ppermute | solution.py:666
  80.9 6.6 %collective-permute-start.17 = (bf16[128,384]{1,0:T(8,128)(2,1)S(1)}, bf16[128,384]{1,0:T(8,128)(2,1)S(1)}, u32[]{:S(2)}, u32[]{:S(2)}) collective-permute-start(bf16[128,384]{1,0:T(8,128)(2,1)S(1)} %get-tuple-element.64), channel_id=1, source_target_pairs={{0,24},{8,16},{16,8},{24,0},{1,25},{9,17},{17,9},{25,1},{2,26},{10... | collective-permute-start | bytes 294920 | tf_op jit(solution)/shard_map/ppermute | solution.py:666
  92.2 4.8 %collective-permute-start.22 = (bf16[256,128]{1,0:T(8,128)(2,1)S(1)}, bf16[256,128]{1,0:T(8,128)(2,1)S(1)}, u32[]{:S(2)}, u32[]{:S(2)}) collective-permute-start(bf16[256,128]{1,0:T(8,128)(2,1)S(1)} %get-tuple-element.73), channel_id=1, source_target_pairs={{0,8},{8,0},{16,24},{24,16},{1,9},{9,1},{17,25},{25,17},{2,10},{10... | collective-permute-start | bytes 196616 | tf_op jit(solution)/shard_map/ppermute | solution.py:666
  92.7 4.8 %collective-permute-start.23 = (bf16[256,128]{1,0:T(8,128)(2,1)S(1)}, bf16[256,128]{1,0:T(8,128)(2,1)S(1)}, u32[]{:S(2)}, u32[]{:S(2)}) collective-permute-start(bf16[256,128]{1,0:T(8,128)(2,1)S(1)} %get-tuple-element.74), channel_id=1, source_target_pairs={{0,16},{8,24},{16,0},{24,8},{1,17},{9,25},{17,1},{25,9},{2,18},{10... | collective-permute-start | bytes 196616 | tf_op jit(solution)/shard_map/ppermute | solution.py:666
  94.0 5.2 %collective-permute-start.24 = (bf16[256,128]{1,0:T(8,128)(2,1)S(1)}, bf16[256,128]{1,0:T(8,128)(2,1)S(1)}, u32[]{:S(2)}, u32[]{:S(2)}) collective-permute-start(bf16[256,128]{1,0:T(8,128)(2,1)S(1)} %get-tuple-element.75), channel_id=1, source_target_pairs={{0,24},{8,16},{16,8},{24,0},{1,25},{9,17},{17,9},{25,1},{2,26},{10... | collective-permute-start | bytes 196616 | tf_op jit(solution)/shard_map/ppermute | solution.py:666
  100.0 15.6 %collective-permute-start.27 = (bf16[64,4096]{1,0:T(8,128)(2,1)S(1)}, bf16[64,4096]{1,0:T(8,128)(2,1)S(1)}, u32[]{:S(2)}, u32[]{:S(2)}) collective-permute-start(bf16[64,4096]{1,0:T(8,128)(2,1)S(1)} %get-tuple-element.81), channel_id=1, source_target_pairs={{0,1},{1,0},{2,3},{3,2},{4,5},{5,4},{6,7},{7,6},{8,9},{9,8},{10,11... | collective-permute-start | bytes 1572872 | tf_op jit(solution)/shard_map/ppermute | solution.py:661
  100.8 18.4 %collective-permute-start.25 = (bf16[64,4096]{1,0:T(8,128)(2,1)S(1)}, bf16[64,4096]{1,0:T(8,128)(2,1)S(1)}, u32[]{:S(2)}, u32[]{:S(2)}) collective-permute-start(bf16[64,4096]{1,0:T(8,128)(2,1)S(1)} %get-tuple-element.78), channel_id=1, source_target_pairs={{0,1},{1,0},{2,3},{3,2},{4,5},{5,4},{6,7},{7,6},{8,9},{9,8},{10,11... | collective-permute-start | bytes 1572872 | tf_op jit(solution)/shard_map/ppermute | solution.py:661
  104.1 6.3 %collective-permute-start.29 = (bf16[128,128]{1,0:T(8,128)(2,1)S(1)}, bf16[128,128]{1,0:T(8,128)(2,1)S(1)}, u32[]{:S(2)}, u32[]{:S(2)}) collective-permute-start(bf16[128,128]{1,0:T(8,128)(2,1)S(1)} %get-tuple-element.83), channel_id=1, source_target_pairs={{0,8},{8,0},{16,24},{24,16},{1,9},{9,1},{17,25},{25,17},{2,10},{10... | collective-permute-start | bytes 98312 | tf_op jit(solution)/shard_map/ppermute | solution.py:666
  105.2 6.3 %collective-permute-start.30 = (bf16[128,128]{1,0:T(8,128)(2,1)S(1)}, bf16[128,128]{1,0:T(8,128)(2,1)S(1)}, u32[]{:S(2)}, u32[]{:S(2)}) collective-permute-start(bf16[128,128]{1,0:T(8,128)(2,1)S(1)} %get-tuple-element.84), channel_id=1, source_target_pairs={{0,16},{8,24},{16,0},{24,8},{1,17},{9,25},{17,1},{25,9},{2,18},{10... | collective-permute-start | bytes 98312 | tf_op jit(solution)/shard_map/ppermute | solution.py:666
  106.5 6.3 %collective-permute-start.31 = (bf16[128,128]{1,0:T(8,128)(2,1)S(1)}, bf16[128,128]{1,0:T(8,128)(2,1)S(1)}, u32[]{:S(2)}, u32[]{:S(2)}) collective-permute-start(bf16[128,128]{1,0:T(8,128)(2,1)S(1)} %get-tuple-element.85), channel_id=1, source_target_pairs={{0,24},{8,16},{16,8},{24,0},{1,25},{9,17},{17,9},{25,1},{2,26},{10... | collective-permute-start | bytes 98312 | tf_op jit(solution)/shard_map/ppermute | solution.py:666
  110.5 5.3 %collective-permute-start.18 = (bf16[128,128]{1,0:T(8,128)(2,1)S(1)}, bf16[128,128]{1,0:T(8,128)(2,1)S(1)}, u32[]{:S(2)}, u32[]{:S(2)}) collective-permute-start(bf16[128,128]{1,0:T(8,128)(2,1)S(1)} %get-tuple-element.66), channel_id=1, source_target_pairs={{0,8},{8,0},{16,24},{24,16},{1,9},{9,1},{17,25},{25,17},{2,10},{10... | collective-permute-start | bytes 98312 | tf_op jit(solution)/shard_map/ppermute | solution.py:666
  111.5 5.5 %collective-permute-start.19 = (bf16[128,128]{1,0:T(8,128)(2,1)S(1)}, bf16[128,128]{1,0:T(8,128)(2,1)S(1)}, u32[]{:S(2)}, u32[]{:S(2)}) collective-permute-start(bf16[128,128]{1,0:T(8,128)(2,1)S(1)} %get-tuple-element.67), channel_id=1, source_target_pairs={{0,16},{8,24},{16,0},{24,8},{1,17},{9,25},{17,1},{25,9},{2,18},{10... | collective-permute-start | bytes 98312 | tf_op jit(solution)/shard_map/ppermute | solution.py:666
  112.8 4.8 %collective-permute-start.20 = (bf16[128,128]{1,0:T(8,128)(2,1)S(1)}, bf16[128,128]{1,0:T(8,128)(2,1)S(1)}, u32[]{:S(2)}, u32[]{:S(2)}) collective-permute-start(bf16[128,128]{1,0:T(8,128)(2,1)S(1)} %get-tuple-element.68), channel_id=1, source_target_pairs={{0,24},{8,16},{16,8},{24,0},{1,25},{9,17},{17,9},{25,1},{2,26},{10... | collective-permute-start | bytes 98312 | tf_op jit(solution)/shard_map/ppermute | solution.py:666
  115.6 5.3 %collective-permute-start.32 = (bf16[64,4096]{1,0:T(8,128)(2,1)}, bf16[64,4096]{1,0:T(8,128)(2,1)S(1)}, u32[]{:S(2)}, u32[]{:S(2)}) collective-permute-start(bf16[64,4096]{1,0:T(8,128)(2,1)} %get-tuple-element.88), channel_id=1, source_target_pairs={{0,1},{1,0},{2,3},{3,2},{4,5},{5,4},{6,7},{7,6},{8,9},{9,8},{10,11... | collective-permute-start | bytes 1572872 | tf_op jit(solution)/shard_map/ppermute | solution.py:661
  115.7 14.4 %collective-permute-start.28 = (bf16[64,4096]{1,0:T(8,128)(2,1)S(1)}, bf16[64,4096]{1,0:T(8,128)(2,1)S(1)}, u32[]{:S(2)}, u32[]{:S(2)}) collective-permute-start(bf16[64,4096]{1,0:T(8,128)(2,1)S(1)} %add_rows.3), channel_id=1, source_target_pairs={{0,2},{1,3},{2,0},{3,1},{4,6},{5,7},{6,4},{7,5},{8,10},{9,11},{10,... | collective-permute-start | bytes 1572872 | tf_op jit(solution)/shard_map/ppermute | solution.py:658
  119.2 15.7 %collective-permute-start.21 = (bf16[64,4096]{1,0:T(8,128)(2,1)}, bf16[64,4096]{1,0:T(8,128)(2,1)}, u32[]{:S(2)}, u32[]{:S(2)}) collective-permute-start(bf16[64,4096]{1,0:T(8,128)(2,1)} %get-tuple-element.71), channel_id=1, source_target_pairs={{0,1},{1,0},{2,3},{3,2},{4,5},{5,4},{6,7},{7,6},{8,9},{9,8},{10,11... | collective-permute-start | bytes 1572872 | tf_op jit(solution)/shard_map/ppermute | solution.py:661
  119.3 15.6 %collective-permute-start.26 = (bf16[64,4096]{1,0:T(8,128)(2,1)S(1)}, bf16[64,4096]{1,0:T(8,128)(2,1)}, u32[]{:S(2)}, u32[]{:S(2)}) collective-permute-start(bf16[64,4096]{1,0:T(8,128)(2,1)S(1)} %add_rows.2.otherwise_ref), channel_id=1, source_target_pairs={{2,4},{3,5},{4,2},{5,3},{10,12},{11,13},{12,10},{13,11},{18,20},{1... | collective-permute-start | bytes 1572872 | tf_op jit(solution)/shard_map/ppermute | solution.py:658
  130.3 28.8 %collective-permute-start.33 = (bf16[64,4096]{1,0:T(8,128)(2,1)S(1)}, bf16[64,4096]{1,0:T(8,128)(2,1)S(1)}, u32[]{:S(2)}, u32[]{:S(2)}) collective-permute-start(bf16[64,4096]{1,0:T(8,128)(2,1)S(1)} %get-tuple-element.89), channel_id=1, source_target_pairs={{0,4},{1,5},{2,6},{3,7},{4,0},{5,1},{6,2},{7,3},{8,12},{9,13},{10,... | collective-permute-start | bytes 1572872 | tf_op jit(solution)/shard_map/ppermute | solution.py:658
  133.3 25.8 %collective-permute-start.34 = (bf16[64,4096]{1,0:T(8,128)(2,1)S(1)}, bf16[64,4096]{1,0:T(8,128)(2,1)S(1)}, u32[]{:S(2)}, u32[]{:S(2)}) collective-permute-start(bf16[64,4096]{1,0:T(8,128)(2,1)S(1)} %get-tuple-element.90), channel_id=1, source_target_pairs={{0,2},{1,3},{2,0},{3,1},{4,6},{5,7},{6,4},{7,5},{8,10},{9,11},{10,... | collective-permute-start | bytes 1572872 | tf_op jit(solution)/shard_map/ppermute | solution.py:658

commit v6 on v5

--- a/solution.py
+++ b/solution.py
@@ -259,22 +259,16 @@
 
 
 class Prefetch:
-    def __init__(self, out_weight, turns, chips):
-        self.weight, self.turns, self.chips = out_weight, turns, chips
-        self.shapes = [pltpu.VMEM(out_weight.shape[1:], jnp.bfloat16)] * len(turns)
-        self.scratch = pltpu.SemaphoreType.DMA((len(turns),))
+    def __init__(self, out_weight, slots):
+        self.weight, self.slots = out_weight, slots
+        self.shapes = [pltpu.VMEM(out_weight.shape[1:], jnp.bfloat16)] * len(slots)
+        self.scratch = pltpu.SemaphoreType.DMA((len(slots),))
 
     def copies(self, info_ref, weight_ref, kept_refs, sems):
-        middle = is_middle(self.chips)
         return [
-            pltpu.make_async_copy(
-                weight_ref.at[mode_of(info_ref, jnp.where(middle, turn[1], turn[0]))],
-                kept_refs[i],
-                sems.at[i],
-            )
-            for i, turn in enumerate(self.turns)
+            pltpu.make_async_copy(weight_ref.at[mode_of(info_ref, slot)], kept_refs[i], sems.at[i])
+            for i, slot in enumerate(self.slots)
         ]
-
 
     def start(self, *refs):
         for copy in self.copies(*refs):
@@ -312,7 +306,7 @@
         ready_refs, weight_ref, refs = refs[:given], refs[given], refs[given + 1 :]
         outs, refs = refs[:heads], refs[heads:]
         ahead_refs, refs = refs[: len(ahead)], refs[len(ahead) :]
-        buffer_ref, sems, ahead_sems = refs[0], refs[1], refs[2:]
+        rows_ref, buffer_ref, sems, ahead_sems = refs[0], refs[1], refs[2], refs[3:]
         fetched = {
             step: weight_copies(info_ref, weight_ref, buffer_ref, sems, slots[step[0]], step[1], i)
             for i, step in enumerate(streamed)
@@ -330,6 +324,9 @@
 
         @pl.when(mesh_place()[1] >= 0)
         def _():
+            for n in range(count):
+                rows_ref[n, :half, :] = ins[2 * n][...]
+                rows_ref[n, half:, :] = ins[2 * n + 1][...]
             for i, (n, p) in enumerate(steps):
                 result = None
                 piece = width // PIECES
@@ -339,9 +336,7 @@
                         part_ref, at = buffer_ref, streamed.index((n, p))
                     else:
                         part_ref, at = ready_refs[places[i][0]], places[i][1]
-                    rows = jnp.concatenate(
-                        [ins[2 * n + i][:, k * piece : (k + 1) * piece] for i in range(2)], axis=0
-                    )
+                    rows = rows_ref[n, :, k * piece : (k + 1) * piece]
                     part = jnp.dot(rows, part_ref[at, k], preferred_element_type=jnp.float32)
                     result = part if result is None else result + part
                 store_pair(outs, pl.ds(n * block, block), p, result)
@@ -356,11 +351,12 @@
         in_specs=[SMEM] + [VMEM] * (2 * count + given) + [HBM],
         out_specs=[VMEM] * (heads + len(ahead)),
         scratch_shapes=[
+            pltpu.VMEM((count, block, width), jnp.bfloat16),
             pltpu.VMEM(shape, jnp.bfloat16),
             pltpu.SemaphoreType.DMA(shape[:2]),
         ]
         + [pltpu.SemaphoreType.DMA(ahead_shape[:2]) for ahead_shape in ahead_shapes],
-        compiler_params=params(4 + 3 * len(streamed) * 2),
+        compiler_params=params(6 + 6 * len(streamed)),
         cost_estimate=pl.CostEstimate(
             flops=2 * count * block * width * cols * heads,
             bytes_accessed=count * width * cols * heads * 2,
@@ -417,14 +413,14 @@
     )(*inner, *relayed, weight)
 
 
-def attend_slots(info, docs, sets, turns, chips, prefetch):
+def attend_slots(info, docs, sets, query_slots, chips, prefetch):
     count = len(sets[0][1])
     block = sets[0][1][0].shape[0] // len(sets[0][0])
     total = count * chips * block
     window = min(total // 2 + block, total)
     scale = 1.0 / math.sqrt(HDIM)
 
-    kept = len(prefetch.turns)
+    kept = len(prefetch.slots)
 
     def kernel(info_ref, *refs):
         ins, refs = refs[: len(sets) * count], refs[len(sets) * count :]
@@ -434,7 +430,6 @@
 
         @pl.when(mesh_place()[1] >= 0)
         def _():
-            middle = is_middle(chips)
             mu, chip, core = mesh_place()
             own_first = core * (block // 2)
 
@@ -458,8 +453,7 @@
             key_in_block = key_iota % block + own_first
             key_in_block = jnp.where(key_in_block >= block, key_in_block - block, key_in_block)
             key_place = (key_iota // block) * block + key_in_block
-            for n, turn in enumerate(turns):
-                slot = jnp.where(middle, turn[1], turn[0])
+            for n, slot in enumerate(query_slots):
                 for d in range(count):
                     index = jnp.bitwise_xor(mu, d) * chips + jnp.bitwise_xor(chip, slot)
                     first_row = index * block
@@ -474,11 +468,8 @@
                         row_first = jnp.where(row_pos >= e, e, row_first)
                     key_pos = key_place + start
                     allowed = (key_pos <= row_pos) & (key_pos >= row_first)
-                    query = slot_rows(d, turn[0], 0)
-                    if turn[1] != turn[0]:
-                        query = jnp.where(middle, slot_rows(d, turn[1], 0), query)
                     scores = lax.dot_general(
-                        query,
+                        slot_rows(d, slot, 0),
                         keys_ref[pl.ds(start, window), :],
                         (((1,), (1,)), ((), ())),
                         preferred_element_type=jnp.float32,
@@ -496,10 +487,10 @@
 
         prefetch.wait(info_ref, next_ref, kept_refs, sems)
 
-    n_queries = len(turns) * count
-    return pl.pallas_call(
-        kernel,
-        out_shape=[pltpu.VMEM((len(turns) * block, HDIM), jnp.bfloat16)] * count
+    n_queries = len(query_slots) * count
+    return pl.pallas_call(
+        kernel,
+        out_shape=[pltpu.VMEM((len(query_slots) * block, HDIM), jnp.bfloat16)] * count
         + prefetch.shapes,
         in_specs=[SMEM] + [VMEM] * (len(sets) * count) + [HBM],
         out_specs=[VMEM] * (count + kept),
@@ -518,11 +509,10 @@
     )(info, *[piece for _, pieces in sets for piece in pieces], prefetch.weight)
 
 
-def output_rows(pieces, weight, index, turns):
+def output_rows(pieces, weight):
     count = len(pieces)
-    block = pieces[0].shape[0] // turns
+    block = pieces[0].shape[0]
     half = block // 2
-    at = index * block
     depth, width = weight.shape
     tile = min(1024, width)
 
@@ -530,7 +520,7 @@
         ins = refs[:count]
         weight_ref, own_ref, partner_ref, heads_ref = refs[count:]
         for d in range(count):
-            heads_ref[jnp.bitwise_xor(mesh_place()[0], d)] = ins[d][at : at + block, :]
+            heads_ref[jnp.bitwise_xor(mesh_place()[0], d)] = ins[d][...]
         rows = jnp.concatenate([heads_ref[h] for h in range(count)], axis=1)
         for first in range(0, width, tile):
             cols = slice(first, first + tile)
@@ -577,48 +567,45 @@
     )(*in_vmem(first, second))
 
 
-def relay_rows(chips, own, partner, passing, otherwise):
-    def kernel(own_ref, partner_ref, passing_ref, otherwise_ref, sum_ref, relay_ref):
+def relay_rows(chips, own, partner, passing):
+    def kernel(own_ref, partner_ref, passing_ref, out_ref):
         middle = is_middle(chips)
 
         @pl.when(middle)
         def _():
             total = own_ref[...].astype(jnp.float32) + partner_ref[...].astype(jnp.float32)
-            sum_ref[...] = total.astype(jnp.bfloat16)
             total = total + passing_ref[...].astype(jnp.float32)
-            relay_ref[...] = total.astype(jnp.bfloat16)
+            out_ref[...] = total.astype(jnp.bfloat16)
 
         @pl.when(jnp.logical_not(middle))
         def _():
             total = own_ref[...].astype(jnp.float32) + partner_ref[...].astype(jnp.float32)
-            sum_ref[...] = total.astype(jnp.bfloat16)
-            relay_ref[...] = otherwise_ref[...]
-
-    return pl.pallas_call(
-        kernel,
-        out_shape=[pltpu.VMEM(own.shape, jnp.bfloat16)] * 2,
-        in_specs=[VMEM] * 4,
-        out_specs=[VMEM] * 2,
+            out_ref[...] = total.astype(jnp.bfloat16)
+
+    return pl.pallas_call(
+        kernel,
+        out_shape=pltpu.VMEM(own.shape, jnp.bfloat16),
+        in_specs=[VMEM] * 3,
+        out_specs=VMEM,
         compiler_params=params(4),
         cost_estimate=pl.CostEstimate(
-            flops=4 * own.size, bytes_accessed=12 * own.size, transcendentals=0
+            flops=4 * own.size, bytes_accessed=8 * own.size, transcendentals=0
         ),
         name="relay_rows",
-    )(*in_vmem(own, partner, passing, otherwise))
-
-
-def last_rows(chips, early, far, middle_only):
-    rows, width = far.shape
+    )(*in_vmem(own, partner, passing))
+
+
+def last_rows(early, first, second):
+    rows, width = first.shape
     parts = 4
     part = rows // parts
 
-    def kernel(early_ref, far_ref, middle_ref, out_ref, done_ref, sems):
-        factor = jnp.where(is_middle(chips), 1.0, 0.0)
+    def kernel(early_ref, first_ref, second_ref, out_ref, done_ref, sems):
         copies = []
         for i in range(parts):
             at = pl.ds(i * part, part)
-            total = early_ref[at] + far_ref[at].astype(jnp.float32)
-            total = total + middle_ref[at].astype(jnp.float32) * factor
+            total = early_ref[at] + first_ref[at].astype(jnp.float32)
+            total = total + second_ref[at].astype(jnp.float32)
             done_ref[at] = total.astype(jnp.bfloat16)
             copies.append(pltpu.make_async_copy(done_ref.at[at], out_ref.at[at], sems.at[i]))
             copies[i].start()
@@ -627,7 +614,7 @@
 
     return pl.pallas_call(
         kernel,
-        out_shape=pltpu.HBM(far.shape, jnp.bfloat16),
+        out_shape=pltpu.HBM(first.shape, jnp.bfloat16),
         in_specs=[VMEM] * 3,
         out_specs=HBM,
         scratch_shapes=[
@@ -636,10 +623,10 @@
         ],
         compiler_params=params(6),
         cost_estimate=pl.CostEstimate(
-            flops=4 * far.size, bytes_accessed=10 * far.size, transcendentals=0
+            flops=4 * first.size, bytes_accessed=10 * first.size, transcendentals=0
         ),
         name="last_rows",
-    )(*in_vmem(early, far, middle_only))
+    )(*in_vmem(early, first, second))
 
 
 def chip_pairs(pairs):
@@ -650,7 +637,6 @@
     seq_count = lax.axis_size("seq")
     mod_count = lax.axis_size("mod")
     chips = seq_count // 2
-    seq = lax.axis_index("seq")
     qkv_weight = pltpu.with_memory_space_constraint(qkv_weight, pltpu.HBM)
     out_weight = pltpu.with_memory_space_constraint(out_weight, pltpu.HBM)
 
@@ -681,7 +667,6 @@
     one_pair = (one, swap(one))
     inner_pair = (inner, swap(inner))
     relayed_pair = (relayed, swap(relayed))
-    turn_a, turn_b, turn_c, turn_d = (3, 1), (2, 3), (1, 2), (0, 0)
 
     *own, late_weight = project_slots(
         info, [own_pair], qkv_weight, (0,), ahead=((3, 2),)
@@ -696,44 +681,25 @@
     late = exchange(late)
     sets = (((0,), own), ((2, 1), mid), ((3,), late))
 
-    def finish(pieces, kept, index, turns):
-        own_share, partner_share = output_rows(pieces, kept, index, turns)
+    def attend(slot):
+        *rows, kept = attend_slots(info, docs, sets, (slot,), chips, Prefetch(out_weight, (slot,)))
+        return exchange(rows), kept
+
+    def finish(pieces, kept):
+        own_share, partner_share = output_rows(pieces, kept)
         return own_share, swap(partner_share)
 
-    *first, kept_a, kept_b = attend_slots(
-        info,
-        docs,
-        sets,
-        (turn_a, turn_b),
-        chips,
-        Prefetch(out_weight, (turn_a, turn_b), chips),
-    )
-    first = exchange(first)
-    *rest_c, kept_c = attend_slots(
-        info, docs, sets, (turn_c,), chips, Prefetch(out_weight, (turn_c,), chips)
-    )
-    sum_a = add_rows(*finish(first, kept_a, 0, 2))
-    own_b, partner_b = finish(first, kept_b, 1, 2)
+    sum_a = add_rows(*finish(*attend(3)))
     from_one = along(sum_a, [(i, i ^ 1) for i in range(chips)])
-    sum_b = add_rows(own_b, partner_b)
-    from_inner = along(sum_b, [(1, 2), (2, 1)])
-    rest_c = exchange(rest_c)
-    shares_c = finish(rest_c, kept_c, 0, 1)
-    chip = seq // 2
-    middle = (chip > 0) & (chip < chips - 1)
-    sum_c, relay_sum = relay_rows(chips, *shares_c, from_one, sum_b)
-    from_two = along(relay_sum, [(i, i ^ 2) for i in range(chips)])
+    from_inner = along(sum_a, [(1, 2), (2, 1)])
+    sum_b = relay_rows(chips, *finish(*attend(2)), from_one)
+    from_two = along(sum_b, [(i, i ^ 2) for i in range(chips)])
+    sum_c = add_rows(*finish(*attend(1)))
     from_end = along(sum_c, [(i, i ^ 1) for i in range(chips)])
-    *rest_d, kept_d = attend_slots(
-        info, docs, sets, (turn_d,), chips, Prefetch(out_weight, (turn_d,), chips)
-    )
-    rest_d = exchange(rest_d)
-    shares_d = finish(rest_d, kept_d, 0, 1)
-    near = jnp.where(middle, from_inner, from_one)
     early = tokens.astype(jnp.float32)
-    for share in (*shares_d, near):
+    for share in (*finish(*attend(0)), from_inner):
         early = early + share.astype(jnp.float32)
-    return last_rows(chips, early, from_two, from_end)
+    return last_rows(early, from_two, from_end)
 
 
 def solution(mesh):

time: 160 us -> 163 us (1.019)
  starting transfers between devices: 37.5 us -> 43.6 us
    ppermute x18 -> x21, starting transfers between devices: 21.3 us -> 24.9 us  [exchange(): lax.ppermute(pieces[d], 'mod', [(i, i ^ d) for i in range(mod_count)])]
    ppermute x8, starting transfers between devices: 15.1 us -> 17 us  [along(): return lax.ppermute(value, 'seq', chip_pairs(pairs))]
    pallas_call x4, Pallas kernels: 4.63 us -> 2.99 us  [output_rows(): pl.pallas_call(kernel, out_shape=[pltpu.VMEM((half, width), jnp.bfloat16)...]
    pallas_call x5 -> x6, Pallas kernels: 11.3 us -> 12.1 us  [the longest x4 11.1 us: attend_slots(): pl.pallas_call(kernel, out_shape=[pltpu.VMEM((len(query_slots) * block, H...]
    ppermute x18 -> x21, waiting for transfers between devices: 14.1 us -> 13.3 us  [exchange(): lax.ppermute(pieces[d], 'mod', [(i, i ^ d) for i in range(mod_count)])]
  transfers between devices with their start and end apart: 35 -> 38, of which waited for: 13 -> 13; matrix products, arithmetic and copies ran while one was open for 1% -> 0% of each run, Pallas kernels for 21% -> 21%
where the time goes in v6:
time: 163 us
  waiting for transfers between devices  76.9 us (47%)
  starting transfers between devices  43.6 us (27%)
  Pallas kernels  41.5 us (25%)
    ppermute x8, waiting for transfers between devices, along(): return lax.ppermute(value, 'seq', chip_pairs(pairs))  63.5 us
    ppermute x21, starting transfers between devices, exchange(): lax.ppermute(pieces[d], 'mod', [(i, i ^ d) for i in range(mod_count)])  24.9 us
    ppermute x8, starting transfers between devices, along(): return lax.ppermute(value, 'seq', chip_pairs(pairs))  17 us
    pallas_call x2, Pallas kernels, project_slots(): pl.pallas_call(kernel, out_shape=[pltpu.VMEM((count * block, cols), jnp.b...  15 us
    ppermute x21, waiting for transfers between devices, exchange(): lax.ppermute(pieces[d], 'mod', [(i, i ^ d) for i in range(mod_count)])  13.3 us
    pallas_call x4, Pallas kernels, attend_slots(): pl.pallas_call(kernel, out_shape=[pltpu.VMEM((len(query_slots) * block, H...  11.1 us
    pallas_call x1, Pallas kernels, fetch_weights(): pl.pallas_call(kernel, out_shape=[pltpu.VMEM(shape, jnp.bfloat16) for sha...  7.08 us
  transfers between devices with their start and end apart: 38, of which 13 were waited for; matrix products, arithmetic and copies ran while one was open for 0% of the time, Pallas kernels for 21%

profile of v6, /device:TPU:0, one launch (start us, length us, event | category | flops | bytes accessed | tf_op | source)
XLA Modules:
  0.0 162.6 jit_solution(6711156672245412226)
XLA Ops:
  0.0 2.1 %norm_rows.1 = (bf16[64,4096]{1,0:T(8,128)(2,1)S(1)}, s32[8]{0:T(128)S(1)}) custom-call(s32[16]{0:T(128)} %modality_ref.1, s32[4]{0:T(128)} %docs_ref.1, bf16[64,4096]{1,0:T(8,128)(2,1)} %tokens_ref.1, f32[3,4096]{1,0:T(4,128)} %gain_ref.1), custom_call_target="tpu_custom_call" | custom-call | flops 4000000 | bytes 1048576 | tf_op jit(solution)/shard_map/norm_rows/pallas_call | solution.py:185
  2.1 4.1 %collective-permute-start.4 = (bf16[64,4096]{1,0:T(8,128)(2,1)S(1)}, bf16[64,4096]{1,0:T(8,128)(2,1)S(1)}, u32[]{:S(2)}, u32[]{:S(2)}) collective-permute-start(bf16[64,4096]{1,0:T(8,128)(2,1)S(1)} %get-tuple-element.51.refs_0_), channel_id=1, source_target_pairs={{0,4},{1,5},{2,6},{3,7},{4,0},{5,1},{6,2},{7,3},{8,12},{9,13},{10,... | collective-permute-start | bytes 1572872 | tf_op jit(solution)/shard_map/ppermute | solution.py:644
  6.3 1.6 collective-permute-start.6
  7.8 0.7 collective-permute-start.11
  8.5 21.8 %collective-permute-done.4.refs_0_ = bf16[64,4096]{1,0:T(8,128)(2,1)S(1)} collective-permute-done((bf16[64,4096]{1,0:T(8,128)(2,1)S(1)}, bf16[64,4096]{1,0:T(8,128)(2,1)S(1)}, u32[]{:S(2)}, u32[]{:S(2)}) %collective-permute-start.4) | collective-permute-done | bytes 524320 | tf_op jit(solution)/shard_map/ppermute | solution.py:644
  30.3 0.5 collective-permute-start.5
  30.8 0.5 collective-permute-start.12
  31.4 11.2 %collective-permute-done.13.relayed_own = bf16[64,4096]{1,0:T(8,128)(2,1)S(1)} collective-permute-done((bf16[64,4096]{1,0:T(8,128)(2,1)S(1)}, bf16[64,4096]{1,0:T(8,128)(2,1)S(1)}, u32[]{:S(2)}, u32[]{:S(2)}) %collective-permute-start.13) | collective-permute-done | bytes 524320 | tf_op jit(solution)/shard_map/ppermute | solution.py:644
  42.6 7.1 %fetch_weights.1 = (bf16[2,4,1024,768]{3,2,1,0:T(8,128)(2,1)S(1)}, bf16[1,4,1024,768]{3,2,1,0:T(8,128)(2,1)S(1)}) custom-call(s32[8]{0:T(128)S(1)} %get-tuple-element.50.info_ref, bf16[3,4096,1536]{2,1,0:T(8,128)(2,1)} %refs_6_.1), custom_call_target="tpu_custom_call" | custom-call | flops 6000000000 | bytes 26214400 | tf_op jit(solution)/shard_map/fetch_weights/pallas_call | solution.py:247
  49.7 9.0 %project_slots.2 = (bf16[128,384]{1,0:T(8,128)(2,1)S(1)}, bf16[128,384]{1,0:T(8,128)(2,1)S(1)}, bf16[128,384]{1,0:T(8,128)(2,1)S(1)}, bf16[128,384]{1,0:T(8,128)(2,1)S(1)}, bf16[2,4,1024,768]{3,2,1,0:T(8,128)(2,1)S(1)}) custom-call(s32[8]{0:T(128)S(1)} %get-tuple-element.50.info_ref, bf16[64,4096]{1,0:T(8,128)(2,1)S(1)} %get-tuple-element.51.refs_0_, ...), custom_call_target="tpu_custom_call" | custom-call | flops 1610612736 | bytes 12582912 | tf_op jit(solution)/shard_map/project_slots/pallas_call | solution.py:347
  58.7 1.7 %collective-permute-start.1 = (bf16[128,384]{1,0:T(8,128)(2,1)S(1)}, bf16[128,384]{1,0:T(8,128)(2,1)S(1)}, u32[]{:S(2)}, u32[]{:S(2)}) collective-permute-start(bf16[128,384]{1,0:T(8,128)(2,1)S(1)} %get-tuple-element.53), channel_id=1, source_target_pairs={{0,8},{8,0},{16,24},{24,16},{1,9},{9,1},{17,25},{25,17},{2,10},{10... | collective-permute-start | bytes 294920 | tf_op jit(solution)/shard_map/ppermute | solution.py:652
  60.5 6.0 %project_slots.3 = (bf16[256,384]{1,0:T(8,128)(2,1)S(1)}, bf16[256,384]{1,0:T(8,128)(2,1)S(1)}, bf16[256,384]{1,0:T(8,128)(2,1)S(1)}, bf16[256,384]{1,0:T(8,128)(2,1)S(1)}) custom-call(s32[8]{0:T(128)S(1)} %get-tuple-element.50.info_ref, bf16[64,4096]{1,0:T(8,128)(2,1)S(1)} %collective-permute-done.4.refs_0_, ...), custom_call_target="tpu_custom_call" | custom-call | flops 3221225472 | bytes 25165824 | tf_op jit(solution)/shard_map/project_slots/pallas_call | solution.py:347
  66.5 1.2 collective-permute-start.10
  67.6 0.7 collective-permute-start.2
  68.3 2.2 %collective-permute-start.3 = (bf16[128,384]{1,0:T(8,128)(2,1)S(1)}, bf16[128,384]{1,0:T(8,128)(2,1)S(1)}, u32[]{:S(2)}, u32[]{:S(2)}) collective-permute-start(bf16[128,384]{1,0:T(8,128)(2,1)S(1)} %get-tuple-element.55), channel_id=1, source_target_pairs={{0,24},{8,16},{16,8},{24,0},{1,25},{9,17},{17,9},{25,1},{2,26},{10... | collective-permute-start | bytes 294920 | tf_op jit(solution)/shard_map/ppermute | solution.py:652
  70.6 0.5 collective-permute-start.8
  71.1 0.7 collective-permute-start.9
  71.8 1.9 %project_late.1 = (bf16[128,384]{1,0:T(8,128)(2,1)S(1)}, bf16[128,384]{1,0:T(8,128)(2,1)S(1)}, bf16[128,384]{1,0:T(8,128)(2,1)S(1)}, bf16[128,384]{1,0:T(8,128)(2,1)S(1)}) custom-call(bf16[64,4096]{1,0:T(8,128)(2,1)S(1)} %collective-permute-done.11.inner_own, bf16[64,4096]{1,0:T(8,128)(2,1)S(1)} %collective-permute-done.12.inner_partner, ...), custom_call_target="tpu_custom_call" | custom-call | flops 1610612736 | bytes 12582912 | tf_op jit(solution)/shard_map/project_late/pallas_call | solution.py:400
  73.7 5.0 %collective-permute-done.2.refs_2_ = bf16[128,384]{1,0:T(8,128)(2,1)S(1)} collective-permute-done((bf16[128,384]{1,0:T(8,128)(2,1)S(1)}, bf16[128,384]{1,0:T(8,128)(2,1)S(1)}, u32[]{:S(2)}, u32[]{:S(2)}) %collective-permute-start.2) | collective-permute-done | bytes 98336 | tf_op jit(solution)/shard_map/ppermute | solution.py:652
  78.8 0.3 collective-permute-start.15
  79.1 1.3 collective-permute-start.16
  80.4 1.8 %collective-permute-start.17 = (bf16[128,384]{1,0:T(8,128)(2,1)S(1)}, bf16[128,384]{1,0:T(8,128)(2,1)S(1)}, u32[]{:S(2)}, u32[]{:S(2)}) collective-permute-start(bf16[128,384]{1,0:T(8,128)(2,1)S(1)} %get-tuple-element.66), channel_id=1, source_target_pairs={{0,24},{8,16},{16,8},{24,0},{1,25},{9,17},{17,9},{25,1},{2,26},{10... | collective-permute-start | bytes 294920 | tf_op jit(solution)/shard_map/ppermute | solution.py:652
  82.3 0.7 collective-permute-done.9.refs_6_
  83.0 1.2 collective-permute-done.15.refs_9_
  84.2 2.8 %collective-permute-done.16.refs_10_ = bf16[128,384]{1,0:T(8,128)(2,1)S(1)} collective-permute-done((bf16[128,384]{1,0:T(8,128)(2,1)S(1)}, bf16[128,384]{1,0:T(8,128)(2,1)S(1)}, u32[]{:S(2)}, u32[]{:S(2)}) %collective-permute-start.16) | collective-permute-done | bytes 98336 | tf_op jit(solution)/shard_map/ppermute | solution.py:652
  87.0 2.9 %attend_slots.5 = (bf16[128,128]{1,0:T(8,128)(2,1)S(1)}, bf16[128,128]{1,0:T(8,128)(2,1)S(1)}, bf16[128,128]{1,0:T(8,128)(2,1)S(1)}, bf16[128,128]{1,0:T(8,128)(2,1)S(1)}, bf16[512,4096]{1,0:T(8,128)(2,1)S(1)}) custom-call(s32[8]{0:T(128)S(1)} %get-tuple-element.50.info_ref, bf16[128,384]{1,0:T(8,128)(2,1)S(1)} %get-tuple-element.52.refs_0_, ...), custom_call_target="tpu_custom_call" | custom-call | flops 603979776 | bytes 1572864 | tf_op jit(solution)/shard_map/attend_slots/pallas_call | solution.py:491
  89.9 0.5 collective-permute-start.22
  90.4 1.3 collective-permute-start.23
  91.7 1.8 %collective-permute-start.24 = (bf16[128,128]{1,0:T(8,128)(2,1)S(1)}, bf16[128,128]{1,0:T(8,128)(2,1)S(1)}, u32[]{:S(2)}, u32[]{:S(2)}) collective-permute-start(bf16[128,128]{1,0:T(8,128)(2,1)S(1)} %get-tuple-element.77), channel_id=1, source_target_pairs={{0,24},{8,16},{16,8},{24,0},{1,25},{9,17},{17,9},{25,1},{2,26},{10... | collective-permute-start | bytes 98312 | tf_op jit(solution)/shard_map/ppermute | solution.py:652
  93.5 0.6 collective-permute-done.22.refs_1_
  94.1 0.5 collective-permute-done.23.refs_2_
  94.5 2.0 %collective-permute-done.24.refs_3_ = bf16[128,128]{1,0:T(8,128)(2,1)S(1)} collective-permute-done((bf16[128,128]{1,0:T(8,128)(2,1)S(1)}, bf16[128,128]{1,0:T(8,128)(2,1)S(1)}, u32[]{:S(2)}, u32[]{:S(2)}) %collective-permute-start.24) | collective-permute-done | bytes 32800 | tf_op jit(solution)/shard_map/ppermute | solution.py:652
  96.5 0.7 output_rows.5
  97.3 0.1 collective-permute-start.25
  97.4 2.8 %attend_slots.7 = (bf16[128,128]{1,0:T(8,128)(2,1)S(1)}, bf16[128,128]{1,0:T(8,128)(2,1)S(1)}, bf16[128,128]{1,0:T(8,128)(2,1)S(1)}, bf16[128,128]{1,0:T(8,128)(2,1)S(1)}, bf16[512,4096]{1,0:T(8,128)(2,1)S(1)}) custom-call(s32[8]{0:T(128)S(1)} %get-tuple-element.50.info_ref, bf16[128,384]{1,0:T(8,128)(2,1)S(1)} %get-tuple-element.52.refs_0_, ...), custom_call_target="tpu_custom_call" | custom-call | flops 603979776 | bytes 1572864 | tf_op jit(solution)/shard_map/attend_slots/pallas_call | solution.py:491
  100.1 1.1 collective-permute-start.33
  101.2 1.3 collective-permute-start.34
  102.5 1.2 collective-permute-start.35
  103.7 2.7 %attend_slots.6 = (bf16[128,128]{1,0:T(8,128)(2,1)S(1)}, bf16[128,128]{1,0:T(8,128)(2,1)S(1)}, bf16[128,128]{1,0:T(8,128)(2,1)S(1)}, bf16[128,128]{1,0:T(8,128)(2,1)S(1)}, bf16[512,4096]{1,0:T(8,128)(2,1)S(1)}) custom-call(s32[8]{0:T(128)S(1)} %get-tuple-element.50.info_ref, bf16[128,384]{1,0:T(8,128)(2,1)S(1)} %get-tuple-element.52.refs_0_, ...), custom_call_target="tpu_custom_call" | custom-call | flops 603979776 | bytes 1572864 | tf_op jit(solution)/shard_map/attend_slots/pallas_call | solution.py:491
  106.4 1.1 collective-permute-start.27
  107.5 2.7 %attend_slots.4 = (bf16[128,128]{1,0:T(8,128)(2,1)S(1)}, bf16[128,128]{1,0:T(8,128)(2,1)S(1)}, bf16[128,128]{1,0:T(8,128)(2,1)S(1)}, bf16[128,128]{1,0:T(8,128)(2,1)S(1)}, bf16[512,4096]{1,0:T(8,128)(2,1)S(1)}) custom-call(s32[8]{0:T(128)S(1)} %get-tuple-element.50.info_ref, bf16[128,384]{1,0:T(8,128)(2,1)S(1)} %get-tuple-element.52.refs_0_, ...), custom_call_target="tpu_custom_call" | custom-call | flops 603979776 | bytes 1572864 | tf_op jit(solution)/shard_map/attend_slots/pallas_call | solution.py:491
  110.3 1.4 collective-permute-start.28
  111.7 1.2 collective-permute-start.29
  112.8 1.0 collective-permute-start.18
  113.8 0.7 output_rows.7
  114.6 1.4 collective-permute-start.19
  116.0 1.2 collective-permute-start.20
  117.2 0.7 output_rows.6
  117.9 0.6 collective-permute-start.30
  118.5 0.1 add_rows.2
  118.6 1.7 %collective-permute-start.31 = (bf16[64,4096]{1,0:T(8,128)(2,1)S(1)}, bf16[64,4096]{1,0:T(8,128)(2,1)S(1)}, u32[]{:S(2)}, u32[]{:S(2)}) collective-permute-start(bf16[64,4096]{1,0:T(8,128)(2,1)S(1)} %add_rows.2), channel_id=1, source_target_pairs={{0,2},{1,3},{2,0},{3,1},{4,6},{5,7},{6,4},{7,5},{8,10},{9,11},{10,... | collective-permute-start | bytes 1572872 | tf_op jit(solution)/shard_map/ppermute | solution.py:644
  120.3 0.5 collective-permute-done.20.refs_3_
  120.8 0.7 output_rows.4
  121.6 0.1 collective-permute-start.21
  121.6 0.7 collective-permute-start.26
  122.4 0.1 add_rows.3
  122.5 4.8 %collective-permute-start.37 = (bf16[64,4096]{1,0:T(8,128)(2,1)S(1)}, bf16[64,4096]{1,0:T(8,128)(2,1)S(1)}, u32[]{:S(2)}, u32[]{:S(2)}) collective-permute-start(bf16[64,4096]{1,0:T(8,128)(2,1)S(1)} %add_rows.3), channel_id=1, source_target_pairs={{0,2},{1,3},{2,0},{3,1},{4,6},{5,7},{6,4},{7,5},{8,10},{9,11},{10,... | collective-permute-start | bytes 1572872 | tf_op jit(solution)/shard_map/ppermute | solution.py:644
  127.3 6.2 %collective-permute-done.31.passing_ref = bf16[64,4096]{1,0:T(8,128)(2,1)S(1)} collective-permute-done((bf16[64,4096]{1,0:T(8,128)(2,1)S(1)}, bf16[64,4096]{1,0:T(8,128)(2,1)S(1)}, u32[]{:S(2)}, u32[]{:S(2)}) %collective-permute-start.31) | collective-permute-done | bytes 524320 | tf_op jit(solution)/shard_map/ppermute | solution.py:644
  133.5 0.1 relay_rows.1
  133.6 3.4 %collective-permute-start.32 = (bf16[64,4096]{1,0:T(8,128)(2,1)S(1)}, bf16[64,4096]{1,0:T(8,128)(2,1)S(1)}, u32[]{:S(2)}, u32[]{:S(2)}) collective-permute-start(bf16[64,4096]{1,0:T(8,128)(2,1)S(1)} %relay_rows.1), channel_id=1, source_target_pairs={{0,4},{1,5},{2,6},{3,7},{4,0},{5,1},{6,2},{7,3},{8,12},{9,13},{10,... | collective-permute-start | bytes 1572872 | tf_op jit(solution)/shard_map/ppermute | solution.py:644
  137.0 0.2 convert_add_fusion.early_ref
  137.3 14.0 %collective-permute-done.37.second_ref = bf16[64,4096]{1,0:T(8,128)(2,1)S(1)} collective-permute-done((bf16[64,4096]{1,0:T(8,128)(2,1)S(1)}, bf16[64,4096]{1,0:T(8,128)(2,1)S(1)}, u32[]{:S(2)}, u32[]{:S(2)}) %collective-permute-start.37) | collective-permute-done | bytes 524320 | tf_op jit(solution)/shard_map/ppermute | solution.py:644
  151.3 10.3 %collective-permute-done.32.first_ref = bf16[64,4096]{1,0:T(8,128)(2,1)S(1)} collective-permute-done((bf16[64,4096]{1,0:T(8,128)(2,1)S(1)}, bf16[64,4096]{1,0:T(8,128)(2,1)S(1)}, u32[]{:S(2)}, u32[]{:S(2)}) %collective-permute-start.32) | collective-permute-done | bytes 524320 | tf_op jit(solution)/shard_map/ppermute | solution.py:644
  161.6 0.9 last_rows.1
  (32 shorter events, 0.1 us)
Async XLA Ops:
  2.1 28.2 %collective-permute-start.4 = (bf16[64,4096]{1,0:T(8,128)(2,1)S(1)}, bf16[64,4096]{1,0:T(8,128)(2,1)S(1)}, u32[]{:S(2)}, u32[]{:S(2)}) collective-permute-start(bf16[64,4096]{1,0:T(8,128)(2,1)S(1)} %get-tuple-element.51.refs_0_), channel_id=1, source_target_pairs={{0,4},{1,5},{2,6},{3,7},{4,0},{5,1},{6,2},{7,3},{8,12},{9,13},{10,... | collective-permute-start | bytes 1572872 | tf_op jit(solution)/shard_map/ppermute | solution.py:644
  6.3 24.6 %collective-permute-start.6 = (bf16[64,4096]{1,0:T(8,128)(2,1)S(1)}, bf16[64,4096]{1,0:T(8,128)(2,1)S(1)}, u32[]{:S(2)}, u32[]{:S(2)}) collective-permute-start(bf16[64,4096]{1,0:T(8,128)(2,1)S(1)} %get-tuple-element.51.refs_0_), channel_id=1, source_target_pairs={{0,2},{1,3},{2,0},{3,1},{4,6},{5,7},{6,4},{7,5},{8,10},{9,11},{10,... | collective-permute-start | bytes 1572872 | tf_op jit(solution)/shard_map/ppermute | solution.py:644
  7.8 23.0 %collective-permute-start.11 = (bf16[64,4096]{1,0:T(8,128)(2,1)S(1)}, bf16[64,4096]{1,0:T(8,128)(2,1)S(1)}, u32[]{:S(2)}, u32[]{:S(2)}) collective-permute-start(bf16[64,4096]{1,0:T(8,128)(2,1)S(1)} %get-tuple-element.51.refs_0_), channel_id=1, source_target_pairs={{2,4},{3,5},{4,2},{5,3},{10,12},{11,13},{12,10},{13,11},{18,20},{1... | collective-permute-start | bytes 1572872 | tf_op jit(solution)/shard_map/ppermute | solution.py:644
  30.3 12.2 %collective-permute-start.13 = (bf16[64,4096]{1,0:T(8,128)(2,1)S(1)}, bf16[64,4096]{1,0:T(8,128)(2,1)S(1)}, u32[]{:S(2)}, u32[]{:S(2)}) collective-permute-start(bf16[64,4096]{1,0:T(8,128)(2,1)S(1)} %collective-permute-done.4.refs_0_), channel_id=1, source_target_pairs={{0,2},{1,3},{2,0},{3,1},{4,6},{5,7},{6,4},{7,5},{8,10},{9,11},{10,... | collective-permute-start | bytes 1572872 | tf_op jit(solution)/shard_map/ppermute | solution.py:644
  30.3 19.3 %collective-permute-start = (bf16[64,4096]{1,0:T(8,128)(2,1)S(1)}, bf16[64,4096]{1,0:T(8,128)(2,1)S(1)}, u32[]{:S(2)}, u32[]{:S(2)}) collective-permute-start(bf16[64,4096]{1,0:T(8,128)(2,1)S(1)} %get-tuple-element.51.refs_0_), channel_id=1, source_target_pairs={{0,1},{1,0},{2,3},{3,2},{4,5},{5,4},{6,7},{7,6},{8,9},{9,8},{10,11... | collective-permute-start | bytes 1572872 | tf_op jit(solution)/shard_map/ppermute | solution.py:647
  30.3 30.1 %collective-permute-start.5 = (bf16[64,4096]{1,0:T(8,128)(2,1)S(1)}, bf16[64,4096]{1,0:T(8,128)(2,1)S(1)}, u32[]{:S(2)}, u32[]{:S(2)}) collective-permute-start(bf16[64,4096]{1,0:T(8,128)(2,1)S(1)} %collective-permute-done.4.refs_0_), channel_id=1, source_target_pairs={{0,1},{1,0},{2,3},{3,2},{4,5},{5,4},{6,7},{7,6},{8,9},{9,8},{10,11... | collective-permute-start | bytes 1572872 | tf_op jit(solution)/shard_map/ppermute | solution.py:647
  30.8 29.6 %collective-permute-start.7 = (bf16[64,4096]{1,0:T(8,128)(2,1)S(1)}, bf16[64,4096]{1,0:T(8,128)(2,1)S(1)}, u32[]{:S(2)}, u32[]{:S(2)}) collective-permute-start(bf16[64,4096]{1,0:T(8,128)(2,1)S(1)} %collective-permute-done.6.refs_2_), channel_id=1, source_target_pairs={{0,1},{1,0},{2,3},{3,2},{4,5},{5,4},{6,7},{7,6},{8,9},{9,8},{10,11... | collective-permute-start | bytes 1572872 | tf_op jit(solution)/shard_map/ppermute | solution.py:647
  30.8 39.7 %collective-permute-start.12 = (bf16[64,4096]{1,0:T(8,128)(2,1)S(1)}, bf16[64,4096]{1,0:T(8,128)(2,1)S(1)}, u32[]{:S(2)}, u32[]{:S(2)}) collective-permute-start(bf16[64,4096]{1,0:T(8,128)(2,1)S(1)} %collective-permute-done.11.inner_own), channel_id=1, source_target_pairs={{0,1},{1,0},{2,3},{3,2},{4,5},{5,4},{6,7},{7,6},{8,9},{9,8},{10,11... | collective-permute-start | bytes 1572872 | tf_op jit(solution)/shard_map/ppermute | solution.py:647
  42.6 28.6 %collective-permute-start.14 = (bf16[64,4096]{1,0:T(8,128)(2,1)S(1)}, bf16[64,4096]{1,0:T(8,128)(2,1)S(1)}, u32[]{:S(2)}, u32[]{:S(2)}) collective-permute-start(bf16[64,4096]{1,0:T(8,128)(2,1)S(1)} %collective-permute-done.13.relayed_own), channel_id=1, source_target_pairs={{0,1},{1,0},{2,3},{3,2},{4,5},{5,4},{6,7},{7,6},{8,9},{9,8},{10,11... | collective-permute-start | bytes 1572872 | tf_op jit(solution)/shard_map/ppermute | solution.py:647
  58.7 9.6 %collective-permute-start.1 = (bf16[128,384]{1,0:T(8,128)(2,1)S(1)}, bf16[128,384]{1,0:T(8,128)(2,1)S(1)}, u32[]{:S(2)}, u32[]{:S(2)}) collective-permute-start(bf16[128,384]{1,0:T(8,128)(2,1)S(1)} %get-tuple-element.53), channel_id=1, source_target_pairs={{0,8},{8,0},{16,24},{24,16},{1,9},{9,1},{17,25},{25,17},{2,10},{10... | collective-permute-start | bytes 294920 | tf_op jit(solution)/shard_map/ppermute | solution.py:652
  66.5 14.0 %collective-permute-start.10 = (bf16[256,384]{1,0:T(8,128)(2,1)S(1)}, bf16[256,384]{1,0:T(8,128)(2,1)S(1)}, u32[]{:S(2)}, u32[]{:S(2)}) collective-permute-start(bf16[256,384]{1,0:T(8,128)(2,1)S(1)} %get-tuple-element.61), channel_id=1, source_target_pairs={{0,24},{8,16},{16,8},{24,0},{1,25},{9,17},{17,9},{25,1},{2,26},{10... | collective-permute-start | bytes 589832 | tf_op jit(solution)/shard_map/ppermute | solution.py:652
  67.6 11.1 %collective-permute-start.2 = (bf16[128,384]{1,0:T(8,128)(2,1)S(1)}, bf16[128,384]{1,0:T(8,128)(2,1)S(1)}, u32[]{:S(2)}, u32[]{:S(2)}) collective-permute-start(bf16[128,384]{1,0:T(8,128)(2,1)S(1)} %get-tuple-element.54), channel_id=1, source_target_pairs={{0,16},{8,24},{16,0},{24,8},{1,17},{9,25},{17,1},{25,9},{2,18},{10... | collective-permute-start | bytes 294920 | tf_op jit(solution)/shard_map/ppermute | solution.py:652
  68.3 10.8 %collective-permute-start.3 = (bf16[128,384]{1,0:T(8,128)(2,1)S(1)}, bf16[128,384]{1,0:T(8,128)(2,1)S(1)}, u32[]{:S(2)}, u32[]{:S(2)}) collective-permute-start(bf16[128,384]{1,0:T(8,128)(2,1)S(1)} %get-tuple-element.55), channel_id=1, source_target_pairs={{0,24},{8,16},{16,8},{24,0},{1,25},{9,17},{17,9},{25,1},{2,26},{10... | collective-permute-start | bytes 294920 | tf_op jit(solution)/shard_map/ppermute | solution.py:652
  70.6 11.7 %collective-permute-start.8 = (bf16[256,384]{1,0:T(8,128)(2,1)S(1)}, bf16[256,384]{1,0:T(8,128)(2,1)S(1)}, u32[]{:S(2)}, u32[]{:S(2)}) collective-permute-start(bf16[256,384]{1,0:T(8,128)(2,1)S(1)} %get-tuple-element.59), channel_id=1, source_target_pairs={{0,8},{8,0},{16,24},{24,16},{1,9},{9,1},{17,25},{25,17},{2,10},{10... | collective-permute-start | bytes 589832 | tf_op jit(solution)/shard_map/ppermute | solution.py:652
  71.1 11.9 %collective-permute-start.9 = (bf16[256,384]{1,0:T(8,128)(2,1)S(1)}, bf16[256,384]{1,0:T(8,128)(2,1)S(1)}, u32[]{:S(2)}, u32[]{:S(2)}) collective-permute-start(bf16[256,384]{1,0:T(8,128)(2,1)S(1)} %get-tuple-element.60), channel_id=1, source_target_pairs={{0,16},{8,24},{16,0},{24,8},{1,17},{9,25},{17,1},{25,9},{2,18},{10... | collective-permute-start | bytes 589832 | tf_op jit(solution)/shard_map/ppermute | solution.py:652
  78.8 5.5 %collective-permute-start.15 = (bf16[128,384]{1,0:T(8,128)(2,1)S(1)}, bf16[128,384]{1,0:T(8,128)(2,1)S(1)}, u32[]{:S(2)}, u32[]{:S(2)}) collective-permute-start(bf16[128,384]{1,0:T(8,128)(2,1)S(1)} %get-tuple-element.64), channel_id=1, source_target_pairs={{0,8},{8,0},{16,24},{24,16},{1,9},{9,1},{17,25},{25,17},{2,10},{10... | collective-permute-start | bytes 294920 | tf_op jit(solution)/shard_map/ppermute | solution.py:652
  79.1 7.9 %collective-permute-start.16 = (bf16[128,384]{1,0:T(8,128)(2,1)S(1)}, bf16[128,384]{1,0:T(8,128)(2,1)S(1)}, u32[]{:S(2)}, u32[]{:S(2)}) collective-permute-start(bf16[128,384]{1,0:T(8,128)(2,1)S(1)} %get-tuple-element.65), channel_id=1, source_target_pairs={{0,16},{8,24},{16,0},{24,8},{1,17},{9,25},{17,1},{25,9},{2,18},{10... | collective-permute-start | bytes 294920 | tf_op jit(solution)/shard_map/ppermute | solution.py:652
  80.4 6.6 %collective-permute-start.17 = (bf16[128,384]{1,0:T(8,128)(2,1)S(1)}, bf16[128,384]{1,0:T(8,128)(2,1)S(1)}, u32[]{:S(2)}, u32[]{:S(2)}) collective-permute-start(bf16[128,384]{1,0:T(8,128)(2,1)S(1)} %get-tuple-element.66), channel_id=1, source_target_pairs={{0,24},{8,16},{16,8},{24,0},{1,25},{9,17},{17,9},{25,1},{2,26},{10... | collective-permute-start | bytes 294920 | tf_op jit(solution)/shard_map/ppermute | solution.py:652
  89.9 4.1 %collective-permute-start.22 = (bf16[128,128]{1,0:T(8,128)(2,1)S(1)}, bf16[128,128]{1,0:T(8,128)(2,1)S(1)}, u32[]{:S(2)}, u32[]{:S(2)}) collective-permute-start(bf16[128,128]{1,0:T(8,128)(2,1)S(1)} %get-tuple-element.75), channel_id=1, source_target_pairs={{0,8},{8,0},{16,24},{24,16},{1,9},{9,1},{17,25},{25,17},{2,10},{10... | collective-permute-start | bytes 98312 | tf_op jit(solution)/shard_map/ppermute | solution.py:652
  90.4 4.1 %collective-permute-start.23 = (bf16[128,128]{1,0:T(8,128)(2,1)S(1)}, bf16[128,128]{1,0:T(8,128)(2,1)S(1)}, u32[]{:S(2)}, u32[]{:S(2)}) collective-permute-start(bf16[128,128]{1,0:T(8,128)(2,1)S(1)} %get-tuple-element.76), channel_id=1, source_target_pairs={{0,16},{8,24},{16,0},{24,8},{1,17},{9,25},{17,1},{25,9},{2,18},{10... | collective-permute-start | bytes 98312 | tf_op jit(solution)/shard_map/ppermute | solution.py:652
  91.7 4.8 %collective-permute-start.24 = (bf16[128,128]{1,0:T(8,128)(2,1)S(1)}, bf16[128,128]{1,0:T(8,128)(2,1)S(1)}, u32[]{:S(2)}, u32[]{:S(2)}) collective-permute-start(bf16[128,128]{1,0:T(8,128)(2,1)S(1)} %get-tuple-element.77), channel_id=1, source_target_pairs={{0,24},{8,16},{16,8},{24,0},{1,25},{9,17},{17,9},{25,1},{2,26},{10... | collective-permute-start | bytes 98312 | tf_op jit(solution)/shard_map/ppermute | solution.py:652
  97.3 20.6 %collective-permute-start.25 = (bf16[64,4096]{1,0:T(8,128)(2,1)S(1)}, bf16[64,4096]{1,0:T(8,128)(2,1)S(1)}, u32[]{:S(2)}, u32[]{:S(2)}) collective-permute-start(bf16[64,4096]{1,0:T(8,128)(2,1)S(1)} %get-tuple-element.80), channel_id=1, source_target_pairs={{0,1},{1,0},{2,3},{3,2},{4,5},{5,4},{6,7},{7,6},{8,9},{9,8},{10,11... | collective-permute-start | bytes 1572872 | tf_op jit(solution)/shard_map/ppermute | solution.py:647
  100.1 10.1 %collective-permute-start.33 = (bf16[128,128]{1,0:T(8,128)(2,1)S(1)}, bf16[128,128]{1,0:T(8,128)(2,1)S(1)}, u32[]{:S(2)}, u32[]{:S(2)}) collective-permute-start(bf16[128,128]{1,0:T(8,128)(2,1)S(1)} %get-tuple-element.89), channel_id=1, source_target_pairs={{0,8},{8,0},{16,24},{24,16},{1,9},{9,1},{17,25},{25,17},{2,10},{10... | collective-permute-start | bytes 98312 | tf_op jit(solution)/shard_map/ppermute | solution.py:652
  101.2 10.4 %collective-permute-start.34 = (bf16[128,128]{1,0:T(8,128)(2,1)S(1)}, bf16[128,128]{1,0:T(8,128)(2,1)S(1)}, u32[]{:S(2)}, u32[]{:S(2)}) collective-permute-start(bf16[128,128]{1,0:T(8,128)(2,1)S(1)} %get-tuple-element.90), channel_id=1, source_target_pairs={{0,16},{8,24},{16,0},{24,8},{1,17},{9,25},{17,1},{25,9},{2,18},{10... | collective-permute-start | bytes 98312 | tf_op jit(solution)/shard_map/ppermute | solution.py:652
  102.5 10.3 %collective-permute-start.35 = (bf16[128,128]{1,0:T(8,128)(2,1)S(1)}, bf16[128,128]{1,0:T(8,128)(2,1)S(1)}, u32[]{:S(2)}, u32[]{:S(2)}) collective-permute-start(bf16[128,128]{1,0:T(8,128)(2,1)S(1)} %get-tuple-element.91), channel_id=1, source_target_pairs={{0,24},{8,16},{16,8},{24,0},{1,25},{9,17},{17,9},{25,1},{2,26},{10... | collective-permute-start | bytes 98312 | tf_op jit(solution)/shard_map/ppermute | solution.py:652
  106.4 8.2 %collective-permute-start.27 = (bf16[128,128]{1,0:T(8,128)(2,1)S(1)}, bf16[128,128]{1,0:T(8,128)(2,1)S(1)}, u32[]{:S(2)}, u32[]{:S(2)}) collective-permute-start(bf16[128,128]{1,0:T(8,128)(2,1)S(1)} %get-tuple-element.82), channel_id=1, source_target_pairs={{0,8},{8,0},{16,24},{24,16},{1,9},{9,1},{17,25},{25,17},{2,10},{10... | collective-permute-start | bytes 98312 | tf_op jit(solution)/shard_map/ppermute | solution.py:652
  110.3 5.7 %collective-permute-start.28 = (bf16[128,128]{1,0:T(8,128)(2,1)S(1)}, bf16[128,128]{1,0:T(8,128)(2,1)S(1)}, u32[]{:S(2)}, u32[]{:S(2)}) collective-permute-start(bf16[128,128]{1,0:T(8,128)(2,1)S(1)} %get-tuple-element.83), channel_id=1, source_target_pairs={{0,16},{8,24},{16,0},{24,8},{1,17},{9,25},{17,1},{25,9},{2,18},{10... | collective-permute-start | bytes 98312 | tf_op jit(solution)/shard_map/ppermute | solution.py:652
  111.7 5.5 %collective-permute-start.29 = (bf16[128,128]{1,0:T(8,128)(2,1)S(1)}, bf16[128,128]{1,0:T(8,128)(2,1)S(1)}, u32[]{:S(2)}, u32[]{:S(2)}) collective-permute-start(bf16[128,128]{1,0:T(8,128)(2,1)S(1)} %get-tuple-element.84), channel_id=1, source_target_pairs={{0,24},{8,16},{16,8},{24,0},{1,25},{9,17},{17,9},{25,1},{2,26},{10... | collective-permute-start | bytes 98312 | tf_op jit(solution)/shard_map/ppermute | solution.py:652
  112.8 5.8 %collective-permute-start.18 = (bf16[128,128]{1,0:T(8,128)(2,1)S(1)}, bf16[128,128]{1,0:T(8,128)(2,1)S(1)}, u32[]{:S(2)}, u32[]{:S(2)}) collective-permute-start(bf16[128,128]{1,0:T(8,128)(2,1)S(1)} %get-tuple-element.68), channel_id=1, source_target_pairs={{0,8},{8,0},{16,24},{24,16},{1,9},{9,1},{17,25},{25,17},{2,10},{10... | collective-permute-start | bytes 98312 | tf_op jit(solution)/shard_map/ppermute | solution.py:652
  114.6 5.7 %collective-permute-start.19 = (bf16[128,128]{1,0:T(8,128)(2,1)S(1)}, bf16[128,128]{1,0:T(8,128)(2,1)S(1)}, u32[]{:S(2)}, u32[]{:S(2)}) collective-permute-start(bf16[128,128]{1,0:T(8,128)(2,1)S(1)} %get-tuple-element.69), channel_id=1, source_target_pairs={{0,16},{8,24},{16,0},{24,8},{1,17},{9,25},{17,1},{25,9},{2,18},{10... | collective-permute-start | bytes 98312 | tf_op jit(solution)/shard_map/ppermute | solution.py:652
  116.0 4.8 %collective-permute-start.20 = (bf16[128,128]{1,0:T(8,128)(2,1)S(1)}, bf16[128,128]{1,0:T(8,128)(2,1)S(1)}, u32[]{:S(2)}, u32[]{:S(2)}) collective-permute-start(bf16[128,128]{1,0:T(8,128)(2,1)S(1)} %get-tuple-element.70), channel_id=1, source_target_pairs={{0,24},{8,16},{16,8},{24,0},{1,25},{9,17},{17,9},{25,1},{2,26},{10... | collective-permute-start | bytes 98312 | tf_op jit(solution)/shard_map/ppermute | solution.py:652
  117.2 5.2 %collective-permute-start.36 = (bf16[64,4096]{1,0:T(8,128)(2,1)S(1)}, bf16[64,4096]{1,0:T(8,128)(2,1)S(1)}, u32[]{:S(2)}, u32[]{:S(2)}) collective-permute-start(bf16[64,4096]{1,0:T(8,128)(2,1)S(1)} %get-tuple-element.94), channel_id=1, source_target_pairs={{0,1},{1,0},{2,3},{3,2},{4,5},{5,4},{6,7},{7,6},{8,9},{9,8},{10,11... | collective-permute-start | bytes 1572872 | tf_op jit(solution)/shard_map/ppermute | solution.py:647
  117.2 19.9 %copy-start = (bf16[64,4096]{1,0:T(8,128)(2,1)S(1)}, bf16[64,4096]{1,0:T(8,128)(2,1)}, u32[]{:S(2)}) copy-start(bf16[64,4096]{1,0:T(8,128)(2,1)} %tokens_ref.1) | copy-start | bytes 1572868
  117.9 9.4 %collective-permute-start.30 = (bf16[64,4096]{1,0:T(8,128)(2,1)S(1)}, bf16[64,4096]{1,0:T(8,128)(2,1)S(1)}, u32[]{:S(2)}, u32[]{:S(2)}) collective-permute-start(bf16[64,4096]{1,0:T(8,128)(2,1)S(1)} %get-tuple-element.87), channel_id=1, source_target_pairs={{0,1},{1,0},{2,3},{3,2},{4,5},{5,4},{6,7},{7,6},{8,9},{9,8},{10,11... | collective-permute-start | bytes 1572872 | tf_op jit(solution)/shard_map/ppermute | solution.py:647
  118.6 14.9 %collective-permute-start.31 = (bf16[64,4096]{1,0:T(8,128)(2,1)S(1)}, bf16[64,4096]{1,0:T(8,128)(2,1)S(1)}, u32[]{:S(2)}, u32[]{:S(2)}) collective-permute-start(bf16[64,4096]{1,0:T(8,128)(2,1)S(1)} %add_rows.2), channel_id=1, source_target_pairs={{0,2},{1,3},{2,0},{3,1},{4,6},{5,7},{6,4},{7,5},{8,10},{9,11},{10,... | collective-permute-start | bytes 1572872 | tf_op jit(solution)/shard_map/ppermute | solution.py:644
  121.6 15.5 %collective-permute-start.21 = (bf16[64,4096]{1,0:T(8,128)(2,1)S(1)}, bf16[64,4096]{1,0:T(8,128)(2,1)S(1)}, u32[]{:S(2)}, u32[]{:S(2)}) collective-permute-start(bf16[64,4096]{1,0:T(8,128)(2,1)S(1)} %get-tuple-element.73), channel_id=1, source_target_pairs={{0,1},{1,0},{2,3},{3,2},{4,5},{5,4},{6,7},{7,6},{8,9},{9,8},{10,11... | collective-permute-start | bytes 1572872 | tf_op jit(solution)/shard_map/ppermute | solution.py:647
  121.6 15.4 %collective-permute-start.26 = (bf16[64,4096]{1,0:T(8,128)(2,1)S(1)}, bf16[64,4096]{1,0:T(8,128)(2,1)S(1)}, u32[]{:S(2)}, u32[]{:S(2)}) collective-permute-start(bf16[64,4096]{1,0:T(8,128)(2,1)S(1)} %add_rows.2), channel_id=1, source_target_pairs={{2,4},{3,5},{4,2},{5,3},{10,12},{11,13},{12,10},{13,11},{18,20},{1... | collective-permute-start | bytes 1572872 | tf_op jit(solution)/shard_map/ppermute | solution.py:644
  122.5 28.8 %collective-permute-start.37 = (bf16[64,4096]{1,0:T(8,128)(2,1)S(1)}, bf16[64,4096]{1,0:T(8,128)(2,1)S(1)}, u32[]{:S(2)}, u32[]{:S(2)}) collective-permute-start(bf16[64,4096]{1,0:T(8,128)(2,1)S(1)} %add_rows.3), channel_id=1, source_target_pairs={{0,2},{1,3},{2,0},{3,1},{4,6},{5,7},{6,4},{7,5},{8,10},{9,11},{10,... | collective-permute-start | bytes 1572872 | tf_op jit(solution)/shard_map/ppermute | solution.py:644
  133.6 28.0 %collective-permute-start.32 = (bf16[64,4096]{1,0:T(8,128)(2,1)S(1)}, bf16[64,4096]{1,0:T(8,128)(2,1)S(1)}, u32[]{:S(2)}, u32[]{:S(2)}) collective-permute-start(bf16[64,4096]{1,0:T(8,128)(2,1)S(1)} %relay_rows.1), channel_id=1, source_target_pairs={{0,4},{1,5},{2,6},{3,7},{4,0},{5,1},{6,2},{7,3},{8,12},{9,13},{10,... | collective-permute-start | bytes 1572872 | tf_op jit(solution)/shard_map/ppermute | solution.py:644

commit v7 on v6

--- a/solution.py
+++ b/solution.py
@@ -227,16 +227,16 @@
 
 
 def fetch_weights(info, weight, ahead):
-    shapes = [weight_shape(weight, n_pairs) for _, n_pairs in ahead]
+    shapes = [weight_shape(weight, n_pairs) for _, n_pairs, _ in ahead]
     count = len(ahead)
 
     def kernel(info_ref, weight_ref, *refs):
         copies = [
             copy
-            for i, (slot, n_pairs) in enumerate(ahead)
+            for i, (slot, n_pairs, skip) in enumerate(ahead)
             for p in range(n_pairs)
             for copy in weight_copies(
-                info_ref, weight_ref, refs[i], refs[count + i], slot, p, p
+                info_ref, weight_ref, refs[i], refs[count + i], slot, p + skip, p
             )
         ]
         for copy in copies:
@@ -299,24 +299,26 @@
     places = [(i, j) for i, array in enumerate(ready) for j in range(array.shape[0])]
     streamed = steps[len(places) :]
     shape = weight_shape(weight, len(streamed))
-    ahead_shapes = [weight_shape(weight, n_pairs) for _, n_pairs in ahead]
+    ahead_shapes = [weight_shape(weight, n_pairs) for _, n_pairs, _ in ahead]
 
     def kernel(info_ref, *refs):
         ins, refs = refs[: 2 * count], refs[2 * count :]
         ready_refs, weight_ref, refs = refs[:given], refs[given], refs[given + 1 :]
         outs, refs = refs[:heads], refs[heads:]
         ahead_refs, refs = refs[: len(ahead)], refs[len(ahead) :]
-        rows_ref, buffer_ref, sems, ahead_sems = refs[0], refs[1], refs[2], refs[3:]
+        rows_ref, refs = refs[0], refs[1:]
+        buffer_ref, sems = refs[:2] if streamed else (None, None)
+        ahead_sems = refs[2:] if streamed else refs
         fetched = {
             step: weight_copies(info_ref, weight_ref, buffer_ref, sems, slots[step[0]], step[1], i)
             for i, step in enumerate(streamed)
         }
         later = [
             copy
-            for i, (slot, n_pairs) in enumerate(ahead)
+            for i, (slot, n_pairs, skip) in enumerate(ahead)
             for p in range(n_pairs)
             for copy in weight_copies(
-                info_ref, weight_ref, ahead_refs[i], ahead_sems[i], slot, p, p
+                info_ref, weight_ref, ahead_refs[i], ahead_sems[i], slot, p + skip, p
             )
         ]
         for copy in [copy for copies in fetched.values() for copy in copies] + later:
@@ -352,9 +354,12 @@
         out_specs=[VMEM] * (heads + len(ahead)),
         scratch_shapes=[
             pltpu.VMEM((count, block, width), jnp.bfloat16),
-            pltpu.VMEM(shape, jnp.bfloat16),
-            pltpu.SemaphoreType.DMA(shape[:2]),
         ]
+        + (
+            [pltpu.VMEM(shape, jnp.bfloat16), pltpu.SemaphoreType.DMA(shape[:2])]
+            if streamed
+            else []
+        )
         + [pltpu.SemaphoreType.DMA(ahead_shape[:2]) for ahead_shape in ahead_shapes],
         compiler_params=params(6 + 6 * len(streamed)),
         cost_estimate=pl.CostEstimate(
@@ -366,13 +371,15 @@
     )(info, *[piece for pair in parts for piece in pair], *ready, weight)
 
 
-def project_late(inner, relayed, weight, cols, chips):
+def project_late(inner, relayed, weights, cols, chips):
     half, width = inner[0].shape
     block = 2 * half
-    pairs, pieces, piece, pair_cols = weight.shape
+    pairs = len(weights)
+    pieces, piece, pair_cols = weights[0].shape[1:]
     heads = pairs * pair_cols // cols
 
-    def kernel(inner_own, inner_partner, relayed_own, relayed_partner, weight_ref, *refs):
+    def kernel(inner_own, inner_partner, relayed_own, relayed_partner, *refs):
+        weight_refs, refs = refs[:pairs], refs[pairs:]
         outs, rows_ref = refs[:heads], refs[heads]
         middle = is_middle(chips)
 
@@ -391,7 +398,7 @@
             for k in range(pieces):
                 part = jnp.dot(
                     rows_ref[:, k * piece : (k + 1) * piece],
-                    weight_ref[p, k],
+                    weight_refs[p][0, k],
                     preferred_element_type=jnp.float32,
                 )
                 result = part if result is None else result + part
@@ -400,7 +407,7 @@
     return pl.pallas_call(
         kernel,
         out_shape=[pltpu.VMEM((block, cols), jnp.bfloat16)] * heads,
-        in_specs=[VMEM] * 5,
+        in_specs=[VMEM] * (4 + pairs),
         out_specs=[VMEM] * heads,
         scratch_shapes=[pltpu.VMEM((block, width), jnp.bfloat16)],
         compiler_params=params(8),
@@ -410,7 +417,7 @@
             transcendentals=0,
         ),
         name="project_late",
-    )(*inner, *relayed, weight)
+    )(*inner, *relayed, *weights)
 
 
 def attend_slots(info, docs, sets, query_slots, chips, prefetch):
@@ -668,16 +675,21 @@
     inner_pair = (inner, swap(inner))
     relayed_pair = (relayed, swap(relayed))
 
-    *own, late_weight = project_slots(
-        info, [own_pair], qkv_weight, (0,), ahead=((3, 2),)
+    *own, late_first = project_slots(
+        info, [own_pair], qkv_weight, (0,), ahead=((3, 1, 0),)
     )
     own = exchange(own)
-    two_weight, one_weight = fetch_weights(info, qkv_weight, ((2, 2), (1, 1)))
-    mid = project_slots(
-        info, [two_pair, one_pair], qkv_weight, (2, 1), ready=(two_weight, one_weight)
+    two_weight, one_weight = fetch_weights(info, qkv_weight, ((2, 2, 0), (1, 2, 0)))
+    *mid, late_second = project_slots(
+        info,
+        [two_pair, one_pair],
+        qkv_weight,
+        (2, 1),
+        ready=(two_weight, one_weight),
+        ahead=((3, 1, 1),),
     )
     mid = exchange(mid)
-    late = project_late(inner_pair, relayed_pair, late_weight, 3 * HDIM, chips)
+    late = project_late(inner_pair, relayed_pair, (late_first, late_second), 3 * HDIM, chips)
     late = exchange(late)
     sets = (((0,), own), ((2, 1), mid), ((3,), late))
 

time: 163 us -> 161 us (0.988)
  Pallas kernels: 41.5 us -> 39.6 us
    pallas_call x2, Pallas kernels: 15 us -> 11.3 us  [project_slots(): pl.pallas_call(kernel, out_shape=[pltpu.VMEM((count * block, cols), jnp.b...]
    pallas_call x1, Pallas kernels: 7.08 us -> 8.91 us  [fetch_weights(): pl.pallas_call(kernel, out_shape=[pltpu.VMEM(shape, jnp.bfloat16) for sha...]
  transfers between devices with their start and end apart: 38 -> 38, of which waited for: 13 -> 13; matrix products, arithmetic and copies ran while one was open for 0% -> 0% of each run, Pallas kernels for 21% -> 20%
where the time goes in v7:
time: 161 us
  waiting for transfers between devices  76.5 us (48%)
  starting transfers between devices  44.3 us (28%)
  Pallas kernels  39.6 us (25%)
    ppermute x8, waiting for transfers between devices, along(): return lax.ppermute(value, 'seq', chip_pairs(pairs))  63.5 us
    ppermute x21, starting transfers between devices, exchange(): lax.ppermute(pieces[d], 'mod', [(i, i ^ d) for i in range(mod_count)])  24.9 us
    ppermute x8, starting transfers between devices, along(): return lax.ppermute(value, 'seq', chip_pairs(pairs))  17.7 us
    ppermute x21, waiting for transfers between devices, exchange(): lax.ppermute(pieces[d], 'mod', [(i, i ^ d) for i in range(mod_count)])  13 us
    pallas_call x2, Pallas kernels, project_slots(): pl.pallas_call(kernel, out_shape=[pltpu.VMEM((count * block, cols), jnp.b...  11.3 us
    pallas_call x4, Pallas kernels, attend_slots(): pl.pallas_call(kernel, out_shape=[pltpu.VMEM((len(query_slots) * block, H...  11.1 us
    pallas_call x1, Pallas kernels, fetch_weights(): pl.pallas_call(kernel, out_shape=[pltpu.VMEM(shape, jnp.bfloat16) for sha...  8.91 us
  transfers between devices with their start and end apart: 38, of which 13 were waited for; matrix products, arithmetic and copies ran while one was open for 0% of the time, Pallas kernels for 20%

profile of v7, /device:TPU:0, one launch (start us, length us, event | category | flops | bytes accessed | tf_op | source)
XLA Modules:
  0.0 161.0 jit_solution(3184242611044740651)
XLA Ops:
  0.0 2.1 %norm_rows.1 = (bf16[64,4096]{1,0:T(8,128)(2,1)S(1)}, s32[8]{0:T(128)S(1)}) custom-call(s32[16]{0:T(128)} %modality_ref.1, s32[4]{0:T(128)} %docs_ref.1, bf16[64,4096]{1,0:T(8,128)(2,1)} %tokens_ref.1, f32[3,4096]{1,0:T(4,128)} %gain_ref.1), custom_call_target="tpu_custom_call" | custom-call | flops 4000000 | bytes 1048576 | tf_op jit(solution)/shard_map/norm_rows/pallas_call | solution.py:185
  2.1 4.1 %collective-permute-start.4 = (bf16[64,4096]{1,0:T(8,128)(2,1)S(1)}, bf16[64,4096]{1,0:T(8,128)(2,1)S(1)}, u32[]{:S(2)}, u32[]{:S(2)}) collective-permute-start(bf16[64,4096]{1,0:T(8,128)(2,1)S(1)} %get-tuple-element.52.refs_0_), channel_id=1, source_target_pairs={{0,4},{1,5},{2,6},{3,7},{4,0},{5,1},{6,2},{7,3},{8,12},{9,13},{10,... | collective-permute-start | bytes 1572872 | tf_op jit(solution)/shard_map/ppermute | solution.py:651
  6.3 1.6 collective-permute-start.6
  7.8 0.7 collective-permute-start.11
  8.5 21.8 %collective-permute-done.4.refs_0_ = bf16[64,4096]{1,0:T(8,128)(2,1)S(1)} collective-permute-done((bf16[64,4096]{1,0:T(8,128)(2,1)S(1)}, bf16[64,4096]{1,0:T(8,128)(2,1)S(1)}, u32[]{:S(2)}, u32[]{:S(2)}) %collective-permute-start.4) | collective-permute-done | bytes 524320 | tf_op jit(solution)/shard_map/ppermute | solution.py:651
  30.3 0.5 collective-permute-start.5
  30.8 0.5 collective-permute-start.12
  31.4 11.2 %collective-permute-done.13.relayed_own = bf16[64,4096]{1,0:T(8,128)(2,1)S(1)} collective-permute-done((bf16[64,4096]{1,0:T(8,128)(2,1)S(1)}, bf16[64,4096]{1,0:T(8,128)(2,1)S(1)}, u32[]{:S(2)}, u32[]{:S(2)}) %collective-permute-start.13) | collective-permute-done | bytes 524320 | tf_op jit(solution)/shard_map/ppermute | solution.py:651
  42.6 8.9 %fetch_weights.1 = (bf16[2,4,1024,768]{3,2,1,0:T(8,128)(2,1)S(1)}, bf16[2,4,1024,768]{3,2,1,0:T(8,128)(2,1)S(1)}) custom-call(s32[8]{0:T(128)S(1)} %get-tuple-element.51.info_ref, bf16[3,4096,1536]{2,1,0:T(8,128)(2,1)} %refs_6_.1), custom_call_target="tpu_custom_call" | custom-call | flops 6000000000 | bytes 26214400 | tf_op jit(solution)/shard_map/fetch_weights/pallas_call | solution.py:247
  51.5 7.2 %project_slots.2 = (bf16[128,384]{1,0:T(8,128)(2,1)S(1)}, bf16[128,384]{1,0:T(8,128)(2,1)S(1)}, bf16[128,384]{1,0:T(8,128)(2,1)S(1)}, bf16[128,384]{1,0:T(8,128)(2,1)S(1)}, bf16[1,4,1024,768]{3,2,1,0:T(8,128)(2,1)S(1)}) custom-call(s32[8]{0:T(128)S(1)} %get-tuple-element.51.info_ref, bf16[64,4096]{1,0:T(8,128)(2,1)S(1)} %get-tuple-element.52.refs_0_, ...), custom_call_target="tpu_custom_call" | custom-call | flops 1610612736 | bytes 12582912 | tf_op jit(solution)/shard_map/project_slots/pallas_call | solution.py:349
  58.7 1.3 collective-permute-start.1
  60.1 4.1 %project_slots.3 = (bf16[256,384]{1,0:T(8,128)(2,1)S(1)}, bf16[256,384]{1,0:T(8,128)(2,1)S(1)}, bf16[256,384]{1,0:T(8,128)(2,1)S(1)}, bf16[256,384]{1,0:T(8,128)(2,1)S(1)}, bf16[1,4,1024,768]{3,2,1,0:T(8,128)(2,1)S(1)}) custom-call(s32[8]{0:T(128)S(1)} %get-tuple-element.51.info_ref, bf16[64,4096]{1,0:T(8,128)(2,1)S(1)} %collective-permute-done.4.refs_0_, ...), custom_call_target="tpu_custom_call" | custom-call | flops 3221225472 | bytes 25165824 | tf_op jit(solution)/shard_map/project_slots/pallas_call | solution.py:349
  64.1 1.6 collective-permute-start.10
  65.7 0.7 collective-permute-start.2
  66.4 2.2 %collective-permute-start.3 = (bf16[128,384]{1,0:T(8,128)(2,1)S(1)}, bf16[128,384]{1,0:T(8,128)(2,1)S(1)}, u32[]{:S(2)}, u32[]{:S(2)}) collective-permute-start(bf16[128,384]{1,0:T(8,128)(2,1)S(1)} %get-tuple-element.56), channel_id=1, source_target_pairs={{0,24},{8,16},{16,8},{24,0},{1,25},{9,17},{17,9},{25,1},{2,26},{10... | collective-permute-start | bytes 294920 | tf_op jit(solution)/shard_map/ppermute | solution.py:659
  68.7 0.5 collective-permute-start.8
  69.2 0.7 collective-permute-start.9
  69.9 1.9 %project_late.1 = (bf16[128,384]{1,0:T(8,128)(2,1)S(1)}, bf16[128,384]{1,0:T(8,128)(2,1)S(1)}, bf16[128,384]{1,0:T(8,128)(2,1)S(1)}, bf16[128,384]{1,0:T(8,128)(2,1)S(1)}) custom-call(bf16[64,4096]{1,0:T(8,128)(2,1)S(1)} %collective-permute-done.11.inner_own, bf16[64,4096]{1,0:T(8,128)(2,1)S(1)} %collective-permute-done.12.inner_partner, ...), custom_call_target="tpu_custom_call" | custom-call | flops 1610612736 | bytes 12582912 | tf_op jit(solution)/shard_map/project_late/pallas_call | solution.py:407
  71.8 4.6 %collective-permute-done.2.refs_2_ = bf16[128,384]{1,0:T(8,128)(2,1)S(1)} collective-permute-done((bf16[128,384]{1,0:T(8,128)(2,1)S(1)}, bf16[128,384]{1,0:T(8,128)(2,1)S(1)}, u32[]{:S(2)}, u32[]{:S(2)}) %collective-permute-start.2) | collective-permute-done | bytes 98336 | tf_op jit(solution)/shard_map/ppermute | solution.py:659
  76.5 0.7 collective-permute-start.15
  77.2 1.3 collective-permute-start.16
  78.5 1.4 collective-permute-start.17
  80.0 0.7 collective-permute-done.9.refs_6_
  80.7 0.9 collective-permute-done.15.refs_9_
  81.5 3.3 %collective-permute-done.16.refs_10_ = bf16[128,384]{1,0:T(8,128)(2,1)S(1)} collective-permute-done((bf16[128,384]{1,0:T(8,128)(2,1)S(1)}, bf16[128,384]{1,0:T(8,128)(2,1)S(1)}, u32[]{:S(2)}, u32[]{:S(2)}) %collective-permute-start.16) | collective-permute-done | bytes 98336 | tf_op jit(solution)/shard_map/ppermute | solution.py:659
  84.8 2.9 %attend_slots.5 = (bf16[128,128]{1,0:T(8,128)(2,1)S(1)}, bf16[128,128]{1,0:T(8,128)(2,1)S(1)}, bf16[128,128]{1,0:T(8,128)(2,1)S(1)}, bf16[128,128]{1,0:T(8,128)(2,1)S(1)}, bf16[512,4096]{1,0:T(8,128)(2,1)S(1)}) custom-call(s32[8]{0:T(128)S(1)} %get-tuple-element.51.info_ref, bf16[128,384]{1,0:T(8,128)(2,1)S(1)} %get-tuple-element.53.refs_0_, ...), custom_call_target="tpu_custom_call" | custom-call | flops 603979776 | bytes 1572864 | tf_op jit(solution)/shard_map/attend_slots/pallas_call | solution.py:498
  87.7 0.8 collective-permute-start.22
  88.5 1.3 collective-permute-start.23
  89.8 1.4 collective-permute-start.24
  91.3 0.6 collective-permute-done.22.refs_1_
  91.8 0.6 collective-permute-done.23.refs_2_
  92.5 2.2 %collective-permute-done.24.refs_3_ = bf16[128,128]{1,0:T(8,128)(2,1)S(1)} collective-permute-done((bf16[128,128]{1,0:T(8,128)(2,1)S(1)}, bf16[128,128]{1,0:T(8,128)(2,1)S(1)}, u32[]{:S(2)}, u32[]{:S(2)}) %collective-permute-start.24) | collective-permute-done | bytes 32800 | tf_op jit(solution)/shard_map/ppermute | solution.py:659
  94.6 0.7 output_rows.5
  95.4 0.1 collective-permute-start.25
  95.5 2.8 %attend_slots.7 = (bf16[128,128]{1,0:T(8,128)(2,1)S(1)}, bf16[128,128]{1,0:T(8,128)(2,1)S(1)}, bf16[128,128]{1,0:T(8,128)(2,1)S(1)}, bf16[128,128]{1,0:T(8,128)(2,1)S(1)}, bf16[512,4096]{1,0:T(8,128)(2,1)S(1)}) custom-call(s32[8]{0:T(128)S(1)} %get-tuple-element.51.info_ref, bf16[128,384]{1,0:T(8,128)(2,1)S(1)} %get-tuple-element.53.refs_0_, ...), custom_call_target="tpu_custom_call" | custom-call | flops 603979776 | bytes 1572864 | tf_op jit(solution)/shard_map/attend_slots/pallas_call | solution.py:498
  98.2 1.1 collective-permute-start.33
  99.3 1.0 collective-permute-start.34
  100.3 1.5 collective-permute-start.35
  101.8 2.7 %attend_slots.6 = (bf16[128,128]{1,0:T(8,128)(2,1)S(1)}, bf16[128,128]{1,0:T(8,128)(2,1)S(1)}, bf16[128,128]{1,0:T(8,128)(2,1)S(1)}, bf16[128,128]{1,0:T(8,128)(2,1)S(1)}, bf16[512,4096]{1,0:T(8,128)(2,1)S(1)}) custom-call(s32[8]{0:T(128)S(1)} %get-tuple-element.51.info_ref, bf16[128,384]{1,0:T(8,128)(2,1)S(1)} %get-tuple-element.53.refs_0_, ...), custom_call_target="tpu_custom_call" | custom-call | flops 603979776 | bytes 1572864 | tf_op jit(solution)/shard_map/attend_slots/pallas_call | solution.py:498
  104.5 1.1 collective-permute-start.27
  105.6 2.7 %attend_slots.4 = (bf16[128,128]{1,0:T(8,128)(2,1)S(1)}, bf16[128,128]{1,0:T(8,128)(2,1)S(1)}, bf16[128,128]{1,0:T(8,128)(2,1)S(1)}, bf16[128,128]{1,0:T(8,128)(2,1)S(1)}, bf16[512,4096]{1,0:T(8,128)(2,1)S(1)}) custom-call(s32[8]{0:T(128)S(1)} %get-tuple-element.51.info_ref, bf16[128,384]{1,0:T(8,128)(2,1)S(1)} %get-tuple-element.53.refs_0_, ...), custom_call_target="tpu_custom_call" | custom-call | flops 603979776 | bytes 1572864 | tf_op jit(solution)/shard_map/attend_slots/pallas_call | solution.py:498
  108.4 1.1 collective-permute-start.28
  109.4 1.5 collective-permute-start.29
  110.9 1.0 collective-permute-start.18
  111.9 0.7 output_rows.7
  112.7 1.1 collective-permute-start.19
  113.8 1.5 collective-permute-start.20
  115.2 0.7 output_rows.6
  116.0 0.6 collective-permute-start.30
  116.6 0.1 add_rows.2
  116.7 1.7 %collective-permute-start.31 = (bf16[64,4096]{1,0:T(8,128)(2,1)S(1)}, bf16[64,4096]{1,0:T(8,128)(2,1)S(1)}, u32[]{:S(2)}, u32[]{:S(2)}) collective-permute-start(bf16[64,4096]{1,0:T(8,128)(2,1)S(1)} %add_rows.2), channel_id=1, source_target_pairs={{0,2},{1,3},{2,0},{3,1},{4,6},{5,7},{6,4},{7,5},{8,10},{9,11},{10,... | collective-permute-start | bytes 1572872 | tf_op jit(solution)/shard_map/ppermute | solution.py:651
  118.4 0.1 collective-permute-done.20.refs_3_
  118.6 0.7 output_rows.4
  119.3 0.1 collective-permute-start.21
  119.4 0.7 collective-permute-start.26
  120.1 0.1 add_rows.3
  120.2 5.4 %collective-permute-start.37 = (bf16[64,4096]{1,0:T(8,128)(2,1)S(1)}, bf16[64,4096]{1,0:T(8,128)(2,1)S(1)}, u32[]{:S(2)}, u32[]{:S(2)}) collective-permute-start(bf16[64,4096]{1,0:T(8,128)(2,1)S(1)} %add_rows.3), channel_id=1, source_target_pairs={{0,2},{1,3},{2,0},{3,1},{4,6},{5,7},{6,4},{7,5},{8,10},{9,11},{10,... | collective-permute-start | bytes 1572872 | tf_op jit(solution)/shard_map/ppermute | solution.py:651
  125.7 5.9 %collective-permute-done.31.passing_ref = bf16[64,4096]{1,0:T(8,128)(2,1)S(1)} collective-permute-done((bf16[64,4096]{1,0:T(8,128)(2,1)S(1)}, bf16[64,4096]{1,0:T(8,128)(2,1)S(1)}, u32[]{:S(2)}, u32[]{:S(2)}) %collective-permute-start.31) | collective-permute-done | bytes 524320 | tf_op jit(solution)/shard_map/ppermute | solution.py:651
  131.6 0.1 relay_rows.1
  131.7 3.4 %collective-permute-start.32 = (bf16[64,4096]{1,0:T(8,128)(2,1)S(1)}, bf16[64,4096]{1,0:T(8,128)(2,1)S(1)}, u32[]{:S(2)}, u32[]{:S(2)}) collective-permute-start(bf16[64,4096]{1,0:T(8,128)(2,1)S(1)} %relay_rows.1), channel_id=1, source_target_pairs={{0,4},{1,5},{2,6},{3,7},{4,0},{5,1},{6,2},{7,3},{8,12},{9,13},{10,... | collective-permute-start | bytes 1572872 | tf_op jit(solution)/shard_map/ppermute | solution.py:651
  135.1 0.2 convert_add_fusion.early_ref
  135.4 13.7 %collective-permute-done.37.second_ref = bf16[64,4096]{1,0:T(8,128)(2,1)S(1)} collective-permute-done((bf16[64,4096]{1,0:T(8,128)(2,1)S(1)}, bf16[64,4096]{1,0:T(8,128)(2,1)S(1)}, u32[]{:S(2)}, u32[]{:S(2)}) %collective-permute-start.37) | collective-permute-done | bytes 524320 | tf_op jit(solution)/shard_map/ppermute | solution.py:651
  149.0 10.9 %collective-permute-done.32.first_ref = bf16[64,4096]{1,0:T(8,128)(2,1)S(1)} collective-permute-done((bf16[64,4096]{1,0:T(8,128)(2,1)S(1)}, bf16[64,4096]{1,0:T(8,128)(2,1)S(1)}, u32[]{:S(2)}, u32[]{:S(2)}) %collective-permute-start.32) | collective-permute-done | bytes 524320 | tf_op jit(solution)/shard_map/ppermute | solution.py:651
  160.0 0.9 last_rows.1
  (32 shorter events, 0.1 us)
Async XLA Ops:
  2.1 28.2 %collective-permute-start.4 = (bf16[64,4096]{1,0:T(8,128)(2,1)S(1)}, bf16[64,4096]{1,0:T(8,128)(2,1)S(1)}, u32[]{:S(2)}, u32[]{:S(2)}) collective-permute-start(bf16[64,4096]{1,0:T(8,128)(2,1)S(1)} %get-tuple-element.52.refs_0_), channel_id=1, source_target_pairs={{0,4},{1,5},{2,6},{3,7},{4,0},{5,1},{6,2},{7,3},{8,12},{9,13},{10,... | collective-permute-start | bytes 1572872 | tf_op jit(solution)/shard_map/ppermute | solution.py:651
  6.3 24.6 %collective-permute-start.6 = (bf16[64,4096]{1,0:T(8,128)(2,1)S(1)}, bf16[64,4096]{1,0:T(8,128)(2,1)S(1)}, u32[]{:S(2)}, u32[]{:S(2)}) collective-permute-start(bf16[64,4096]{1,0:T(8,128)(2,1)S(1)} %get-tuple-element.52.refs_0_), channel_id=1, source_target_pairs={{0,2},{1,3},{2,0},{3,1},{4,6},{5,7},{6,4},{7,5},{8,10},{9,11},{10,... | collective-permute-start | bytes 1572872 | tf_op jit(solution)/shard_map/ppermute | solution.py:651
  7.8 23.0 %collective-permute-start.11 = (bf16[64,4096]{1,0:T(8,128)(2,1)S(1)}, bf16[64,4096]{1,0:T(8,128)(2,1)S(1)}, u32[]{:S(2)}, u32[]{:S(2)}) collective-permute-start(bf16[64,4096]{1,0:T(8,128)(2,1)S(1)} %get-tuple-element.52.refs_0_), channel_id=1, source_target_pairs={{2,4},{3,5},{4,2},{5,3},{10,12},{11,13},{12,10},{13,11},{18,20},{1... | collective-permute-start | bytes 1572872 | tf_op jit(solution)/shard_map/ppermute | solution.py:651
  30.3 12.2 %collective-permute-start.13 = (bf16[64,4096]{1,0:T(8,128)(2,1)S(1)}, bf16[64,4096]{1,0:T(8,128)(2,1)S(1)}, u32[]{:S(2)}, u32[]{:S(2)}) collective-permute-start(bf16[64,4096]{1,0:T(8,128)(2,1)S(1)} %collective-permute-done.4.refs_0_), channel_id=1, source_target_pairs={{0,2},{1,3},{2,0},{3,1},{4,6},{5,7},{6,4},{7,5},{8,10},{9,11},{10,... | collective-permute-start | bytes 1572872 | tf_op jit(solution)/shard_map/ppermute | solution.py:651
  30.3 21.2 %collective-permute-start = (bf16[64,4096]{1,0:T(8,128)(2,1)S(1)}, bf16[64,4096]{1,0:T(8,128)(2,1)S(1)}, u32[]{:S(2)}, u32[]{:S(2)}) collective-permute-start(bf16[64,4096]{1,0:T(8,128)(2,1)S(1)} %get-tuple-element.52.refs_0_), channel_id=1, source_target_pairs={{0,1},{1,0},{2,3},{3,2},{4,5},{5,4},{6,7},{7,6},{8,9},{9,8},{10,11... | collective-permute-start | bytes 1572872 | tf_op jit(solution)/shard_map/ppermute | solution.py:654
  30.3 29.7 %collective-permute-start.5 = (bf16[64,4096]{1,0:T(8,128)(2,1)S(1)}, bf16[64,4096]{1,0:T(8,128)(2,1)S(1)}, u32[]{:S(2)}, u32[]{:S(2)}) collective-permute-start(bf16[64,4096]{1,0:T(8,128)(2,1)S(1)} %collective-permute-done.4.refs_0_), channel_id=1, source_target_pairs={{0,1},{1,0},{2,3},{3,2},{4,5},{5,4},{6,7},{7,6},{8,9},{9,8},{10,11... | collective-permute-start | bytes 1572872 | tf_op jit(solution)/shard_map/ppermute | solution.py:654
  30.8 29.2 %collective-permute-start.7 = (bf16[64,4096]{1,0:T(8,128)(2,1)S(1)}, bf16[64,4096]{1,0:T(8,128)(2,1)S(1)}, u32[]{:S(2)}, u32[]{:S(2)}) collective-permute-start(bf16[64,4096]{1,0:T(8,128)(2,1)S(1)} %collective-permute-done.6.refs_2_), channel_id=1, source_target_pairs={{0,1},{1,0},{2,3},{3,2},{4,5},{5,4},{6,7},{7,6},{8,9},{9,8},{10,11... | collective-permute-start | bytes 1572872 | tf_op jit(solution)/shard_map/ppermute | solution.py:654
  30.8 37.8 %collective-permute-start.12 = (bf16[64,4096]{1,0:T(8,128)(2,1)S(1)}, bf16[64,4096]{1,0:T(8,128)(2,1)S(1)}, u32[]{:S(2)}, u32[]{:S(2)}) collective-permute-start(bf16[64,4096]{1,0:T(8,128)(2,1)S(1)} %collective-permute-done.11.inner_own), channel_id=1, source_target_pairs={{0,1},{1,0},{2,3},{3,2},{4,5},{5,4},{6,7},{7,6},{8,9},{9,8},{10,11... | collective-permute-start | bytes 1572872 | tf_op jit(solution)/shard_map/ppermute | solution.py:654
  42.6 26.6 %collective-permute-start.14 = (bf16[64,4096]{1,0:T(8,128)(2,1)S(1)}, bf16[64,4096]{1,0:T(8,128)(2,1)S(1)}, u32[]{:S(2)}, u32[]{:S(2)}) collective-permute-start(bf16[64,4096]{1,0:T(8,128)(2,1)S(1)} %collective-permute-done.13.relayed_own), channel_id=1, source_target_pairs={{0,1},{1,0},{2,3},{3,2},{4,5},{5,4},{6,7},{7,6},{8,9},{9,8},{10,11... | collective-permute-start | bytes 1572872 | tf_op jit(solution)/shard_map/ppermute | solution.py:654
  58.7 7.7 %collective-permute-start.1 = (bf16[128,384]{1,0:T(8,128)(2,1)S(1)}, bf16[128,384]{1,0:T(8,128)(2,1)S(1)}, u32[]{:S(2)}, u32[]{:S(2)}) collective-permute-start(bf16[128,384]{1,0:T(8,128)(2,1)S(1)} %get-tuple-element.54), channel_id=1, source_target_pairs={{0,8},{8,0},{16,24},{24,16},{1,9},{9,1},{17,25},{25,17},{2,10},{10... | collective-permute-start | bytes 294920 | tf_op jit(solution)/shard_map/ppermute | solution.py:659
  64.1 14.4 %collective-permute-start.10 = (bf16[256,384]{1,0:T(8,128)(2,1)S(1)}, bf16[256,384]{1,0:T(8,128)(2,1)S(1)}, u32[]{:S(2)}, u32[]{:S(2)}) collective-permute-start(bf16[256,384]{1,0:T(8,128)(2,1)S(1)} %get-tuple-element.62), channel_id=1, source_target_pairs={{0,24},{8,16},{16,8},{24,0},{1,25},{9,17},{17,9},{25,1},{2,26},{10... | collective-permute-start | bytes 589832 | tf_op jit(solution)/shard_map/ppermute | solution.py:659
  65.7 10.7 %collective-permute-start.2 = (bf16[128,384]{1,0:T(8,128)(2,1)S(1)}, bf16[128,384]{1,0:T(8,128)(2,1)S(1)}, u32[]{:S(2)}, u32[]{:S(2)}) collective-permute-start(bf16[128,384]{1,0:T(8,128)(2,1)S(1)} %get-tuple-element.55), channel_id=1, source_target_pairs={{0,16},{8,24},{16,0},{24,8},{1,17},{9,25},{17,1},{25,9},{2,18},{10... | collective-permute-start | bytes 294920 | tf_op jit(solution)/shard_map/ppermute | solution.py:659
  66.4 10.8 %collective-permute-start.3 = (bf16[128,384]{1,0:T(8,128)(2,1)S(1)}, bf16[128,384]{1,0:T(8,128)(2,1)S(1)}, u32[]{:S(2)}, u32[]{:S(2)}) collective-permute-start(bf16[128,384]{1,0:T(8,128)(2,1)S(1)} %get-tuple-element.56), channel_id=1, source_target_pairs={{0,24},{8,16},{16,8},{24,0},{1,25},{9,17},{17,9},{25,1},{2,26},{10... | collective-permute-start | bytes 294920 | tf_op jit(solution)/shard_map/ppermute | solution.py:659
  68.7 11.3 %collective-permute-start.8 = (bf16[256,384]{1,0:T(8,128)(2,1)S(1)}, bf16[256,384]{1,0:T(8,128)(2,1)S(1)}, u32[]{:S(2)}, u32[]{:S(2)}) collective-permute-start(bf16[256,384]{1,0:T(8,128)(2,1)S(1)} %get-tuple-element.60), channel_id=1, source_target_pairs={{0,8},{8,0},{16,24},{24,16},{1,9},{9,1},{17,25},{25,17},{2,10},{10... | collective-permute-start | bytes 589832 | tf_op jit(solution)/shard_map/ppermute | solution.py:659
  69.2 11.5 %collective-permute-start.9 = (bf16[256,384]{1,0:T(8,128)(2,1)S(1)}, bf16[256,384]{1,0:T(8,128)(2,1)S(1)}, u32[]{:S(2)}, u32[]{:S(2)}) collective-permute-start(bf16[256,384]{1,0:T(8,128)(2,1)S(1)} %get-tuple-element.61), channel_id=1, source_target_pairs={{0,16},{8,24},{16,0},{24,8},{1,17},{9,25},{17,1},{25,9},{2,18},{10... | collective-permute-start | bytes 589832 | tf_op jit(solution)/shard_map/ppermute | solution.py:659
  76.5 5.1 %collective-permute-start.15 = (bf16[128,384]{1,0:T(8,128)(2,1)S(1)}, bf16[128,384]{1,0:T(8,128)(2,1)S(1)}, u32[]{:S(2)}, u32[]{:S(2)}) collective-permute-start(bf16[128,384]{1,0:T(8,128)(2,1)S(1)} %get-tuple-element.66), channel_id=1, source_target_pairs={{0,8},{8,0},{16,24},{24,16},{1,9},{9,1},{17,25},{25,17},{2,10},{10... | collective-permute-start | bytes 294920 | tf_op jit(solution)/shard_map/ppermute | solution.py:659
  77.2 7.6 %collective-permute-start.16 = (bf16[128,384]{1,0:T(8,128)(2,1)S(1)}, bf16[128,384]{1,0:T(8,128)(2,1)S(1)}, u32[]{:S(2)}, u32[]{:S(2)}) collective-permute-start(bf16[128,384]{1,0:T(8,128)(2,1)S(1)} %get-tuple-element.67), channel_id=1, source_target_pairs={{0,16},{8,24},{16,0},{24,8},{1,17},{9,25},{17,1},{25,9},{2,18},{10... | collective-permute-start | bytes 294920 | tf_op jit(solution)/shard_map/ppermute | solution.py:659
  78.5 6.3 %collective-permute-start.17 = (bf16[128,384]{1,0:T(8,128)(2,1)S(1)}, bf16[128,384]{1,0:T(8,128)(2,1)S(1)}, u32[]{:S(2)}, u32[]{:S(2)}) collective-permute-start(bf16[128,384]{1,0:T(8,128)(2,1)S(1)} %get-tuple-element.68), channel_id=1, source_target_pairs={{0,24},{8,16},{16,8},{24,0},{1,25},{9,17},{17,9},{25,1},{2,26},{10... | collective-permute-start | bytes 294920 | tf_op jit(solution)/shard_map/ppermute | solution.py:659
  87.7 4.1 %collective-permute-start.22 = (bf16[128,128]{1,0:T(8,128)(2,1)S(1)}, bf16[128,128]{1,0:T(8,128)(2,1)S(1)}, u32[]{:S(2)}, u32[]{:S(2)}) collective-permute-start(bf16[128,128]{1,0:T(8,128)(2,1)S(1)} %get-tuple-element.77), channel_id=1, source_target_pairs={{0,8},{8,0},{16,24},{24,16},{1,9},{9,1},{17,25},{25,17},{2,10},{10... | collective-permute-start | bytes 98312 | tf_op jit(solution)/shard_map/ppermute | solution.py:659
  88.5 3.9 %collective-permute-start.23 = (bf16[128,128]{1,0:T(8,128)(2,1)S(1)}, bf16[128,128]{1,0:T(8,128)(2,1)S(1)}, u32[]{:S(2)}, u32[]{:S(2)}) collective-permute-start(bf16[128,128]{1,0:T(8,128)(2,1)S(1)} %get-tuple-element.78), channel_id=1, source_target_pairs={{0,16},{8,24},{16,0},{24,8},{1,17},{9,25},{17,1},{25,9},{2,18},{10... | collective-permute-start | bytes 98312 | tf_op jit(solution)/shard_map/ppermute | solution.py:659
  89.8 4.8 %collective-permute-start.24 = (bf16[128,128]{1,0:T(8,128)(2,1)S(1)}, bf16[128,128]{1,0:T(8,128)(2,1)S(1)}, u32[]{:S(2)}, u32[]{:S(2)}) collective-permute-start(bf16[128,128]{1,0:T(8,128)(2,1)S(1)} %get-tuple-element.79), channel_id=1, source_target_pairs={{0,24},{8,16},{16,8},{24,0},{1,25},{9,17},{17,9},{25,1},{2,26},{10... | collective-permute-start | bytes 98312 | tf_op jit(solution)/shard_map/ppermute | solution.py:659
  95.4 20.6 %collective-permute-start.25 = (bf16[64,4096]{1,0:T(8,128)(2,1)S(1)}, bf16[64,4096]{1,0:T(8,128)(2,1)S(1)}, u32[]{:S(2)}, u32[]{:S(2)}) collective-permute-start(bf16[64,4096]{1,0:T(8,128)(2,1)S(1)} %get-tuple-element.82), channel_id=1, source_target_pairs={{0,1},{1,0},{2,3},{3,2},{4,5},{5,4},{6,7},{7,6},{8,9},{9,8},{10,11... | collective-permute-start | bytes 1572872 | tf_op jit(solution)/shard_map/ppermute | solution.py:654
  98.2 10.1 %collective-permute-start.33 = (bf16[128,128]{1,0:T(8,128)(2,1)S(1)}, bf16[128,128]{1,0:T(8,128)(2,1)S(1)}, u32[]{:S(2)}, u32[]{:S(2)}) collective-permute-start(bf16[128,128]{1,0:T(8,128)(2,1)S(1)} %get-tuple-element.91), channel_id=1, source_target_pairs={{0,8},{8,0},{16,24},{24,16},{1,9},{9,1},{17,25},{25,17},{2,10},{10... | collective-permute-start | bytes 98312 | tf_op jit(solution)/shard_map/ppermute | solution.py:659
  99.3 10.1 %collective-permute-start.34 = (bf16[128,128]{1,0:T(8,128)(2,1)S(1)}, bf16[128,128]{1,0:T(8,128)(2,1)S(1)}, u32[]{:S(2)}, u32[]{:S(2)}) collective-permute-start(bf16[128,128]{1,0:T(8,128)(2,1)S(1)} %get-tuple-element.92), channel_id=1, source_target_pairs={{0,16},{8,24},{16,0},{24,8},{1,17},{9,25},{17,1},{25,9},{2,18},{10... | collective-permute-start | bytes 98312 | tf_op jit(solution)/shard_map/ppermute | solution.py:659
  100.3 10.6 %collective-permute-start.35 = (bf16[128,128]{1,0:T(8,128)(2,1)S(1)}, bf16[128,128]{1,0:T(8,128)(2,1)S(1)}, u32[]{:S(2)}, u32[]{:S(2)}) collective-permute-start(bf16[128,128]{1,0:T(8,128)(2,1)S(1)} %get-tuple-element.93), channel_id=1, source_target_pairs={{0,24},{8,16},{16,8},{24,0},{1,25},{9,17},{17,9},{25,1},{2,26},{10... | collective-permute-start | bytes 98312 | tf_op jit(solution)/shard_map/ppermute | solution.py:659
  104.5 8.2 %collective-permute-start.27 = (bf16[128,128]{1,0:T(8,128)(2,1)S(1)}, bf16[128,128]{1,0:T(8,128)(2,1)S(1)}, u32[]{:S(2)}, u32[]{:S(2)}) collective-permute-start(bf16[128,128]{1,0:T(8,128)(2,1)S(1)} %get-tuple-element.84), channel_id=1, source_target_pairs={{0,8},{8,0},{16,24},{24,16},{1,9},{9,1},{17,25},{25,17},{2,10},{10... | collective-permute-start | bytes 98312 | tf_op jit(solution)/shard_map/ppermute | solution.py:659
  108.4 5.4 %collective-permute-start.28 = (bf16[128,128]{1,0:T(8,128)(2,1)S(1)}, bf16[128,128]{1,0:T(8,128)(2,1)S(1)}, u32[]{:S(2)}, u32[]{:S(2)}) collective-permute-start(bf16[128,128]{1,0:T(8,128)(2,1)S(1)} %get-tuple-element.85), channel_id=1, source_target_pairs={{0,16},{8,24},{16,0},{24,8},{1,17},{9,25},{17,1},{25,9},{2,18},{10... | collective-permute-start | bytes 98312 | tf_op jit(solution)/shard_map/ppermute | solution.py:659
  109.4 5.8 %collective-permute-start.29 = (bf16[128,128]{1,0:T(8,128)(2,1)S(1)}, bf16[128,128]{1,0:T(8,128)(2,1)S(1)}, u32[]{:S(2)}, u32[]{:S(2)}) collective-permute-start(bf16[128,128]{1,0:T(8,128)(2,1)S(1)} %get-tuple-element.86), channel_id=1, source_target_pairs={{0,24},{8,16},{16,8},{24,0},{1,25},{9,17},{17,9},{25,1},{2,26},{10... | collective-permute-start | bytes 98312 | tf_op jit(solution)/shard_map/ppermute | solution.py:659
  110.9 5.8 %collective-permute-start.18 = (bf16[128,128]{1,0:T(8,128)(2,1)S(1)}, bf16[128,128]{1,0:T(8,128)(2,1)S(1)}, u32[]{:S(2)}, u32[]{:S(2)}) collective-permute-start(bf16[128,128]{1,0:T(8,128)(2,1)S(1)} %get-tuple-element.70), channel_id=1, source_target_pairs={{0,8},{8,0},{16,24},{24,16},{1,9},{9,1},{17,25},{25,17},{2,10},{10... | collective-permute-start | bytes 98312 | tf_op jit(solution)/shard_map/ppermute | solution.py:659
  112.7 5.7 %collective-permute-start.19 = (bf16[128,128]{1,0:T(8,128)(2,1)S(1)}, bf16[128,128]{1,0:T(8,128)(2,1)S(1)}, u32[]{:S(2)}, u32[]{:S(2)}) collective-permute-start(bf16[128,128]{1,0:T(8,128)(2,1)S(1)} %get-tuple-element.71), channel_id=1, source_target_pairs={{0,16},{8,24},{16,0},{24,8},{1,17},{9,25},{17,1},{25,9},{2,18},{10... | collective-permute-start | bytes 98312 | tf_op jit(solution)/shard_map/ppermute | solution.py:659
  113.8 4.8 %collective-permute-start.20 = (bf16[128,128]{1,0:T(8,128)(2,1)S(1)}, bf16[128,128]{1,0:T(8,128)(2,1)S(1)}, u32[]{:S(2)}, u32[]{:S(2)}) collective-permute-start(bf16[128,128]{1,0:T(8,128)(2,1)S(1)} %get-tuple-element.72), channel_id=1, source_target_pairs={{0,24},{8,16},{16,8},{24,0},{1,25},{9,17},{17,9},{25,1},{2,26},{10... | collective-permute-start | bytes 98312 | tf_op jit(solution)/shard_map/ppermute | solution.py:659
  115.2 4.9 %collective-permute-start.36 = (bf16[64,4096]{1,0:T(8,128)(2,1)S(1)}, bf16[64,4096]{1,0:T(8,128)(2,1)S(1)}, u32[]{:S(2)}, u32[]{:S(2)}) collective-permute-start(bf16[64,4096]{1,0:T(8,128)(2,1)S(1)} %get-tuple-element.96), channel_id=1, source_target_pairs={{0,1},{1,0},{2,3},{3,2},{4,5},{5,4},{6,7},{7,6},{8,9},{9,8},{10,11... | collective-permute-start | bytes 1572872 | tf_op jit(solution)/shard_map/ppermute | solution.py:654
  115.2 19.9 %copy-start = (bf16[64,4096]{1,0:T(8,128)(2,1)S(1)}, bf16[64,4096]{1,0:T(8,128)(2,1)}, u32[]{:S(2)}) copy-start(bf16[64,4096]{1,0:T(8,128)(2,1)} %tokens_ref.1) | copy-start | bytes 1572868
  116.0 9.7 %collective-permute-start.30 = (bf16[64,4096]{1,0:T(8,128)(2,1)S(1)}, bf16[64,4096]{1,0:T(8,128)(2,1)S(1)}, u32[]{:S(2)}, u32[]{:S(2)}) collective-permute-start(bf16[64,4096]{1,0:T(8,128)(2,1)S(1)} %get-tuple-element.89), channel_id=1, source_target_pairs={{0,1},{1,0},{2,3},{3,2},{4,5},{5,4},{6,7},{7,6},{8,9},{9,8},{10,11... | collective-permute-start | bytes 1572872 | tf_op jit(solution)/shard_map/ppermute | solution.py:654
  116.7 14.9 %collective-permute-start.31 = (bf16[64,4096]{1,0:T(8,128)(2,1)S(1)}, bf16[64,4096]{1,0:T(8,128)(2,1)S(1)}, u32[]{:S(2)}, u32[]{:S(2)}) collective-permute-start(bf16[64,4096]{1,0:T(8,128)(2,1)S(1)} %add_rows.2), channel_id=1, source_target_pairs={{0,2},{1,3},{2,0},{3,1},{4,6},{5,7},{6,4},{7,5},{8,10},{9,11},{10,... | collective-permute-start | bytes 1572872 | tf_op jit(solution)/shard_map/ppermute | solution.py:651
  119.3 15.8 %collective-permute-start.21 = (bf16[64,4096]{1,0:T(8,128)(2,1)S(1)}, bf16[64,4096]{1,0:T(8,128)(2,1)S(1)}, u32[]{:S(2)}, u32[]{:S(2)}) collective-permute-start(bf16[64,4096]{1,0:T(8,128)(2,1)S(1)} %get-tuple-element.75), channel_id=1, source_target_pairs={{0,1},{1,0},{2,3},{3,2},{4,5},{5,4},{6,7},{7,6},{8,9},{9,8},{10,11... | collective-permute-start | bytes 1572872 | tf_op jit(solution)/shard_map/ppermute | solution.py:654
  119.4 15.7 %collective-permute-start.26 = (bf16[64,4096]{1,0:T(8,128)(2,1)S(1)}, bf16[64,4096]{1,0:T(8,128)(2,1)S(1)}, u32[]{:S(2)}, u32[]{:S(2)}) collective-permute-start(bf16[64,4096]{1,0:T(8,128)(2,1)S(1)} %add_rows.2), channel_id=1, source_target_pairs={{2,4},{3,5},{4,2},{5,3},{10,12},{11,13},{12,10},{13,11},{18,20},{1... | collective-permute-start | bytes 1572872 | tf_op jit(solution)/shard_map/ppermute | solution.py:651
  120.2 28.8 %collective-permute-start.37 = (bf16[64,4096]{1,0:T(8,128)(2,1)S(1)}, bf16[64,4096]{1,0:T(8,128)(2,1)S(1)}, u32[]{:S(2)}, u32[]{:S(2)}) collective-permute-start(bf16[64,4096]{1,0:T(8,128)(2,1)S(1)} %add_rows.3), channel_id=1, source_target_pairs={{0,2},{1,3},{2,0},{3,1},{4,6},{5,7},{6,4},{7,5},{8,10},{9,11},{10,... | collective-permute-start | bytes 1572872 | tf_op jit(solution)/shard_map/ppermute | solution.py:651
  131.7 28.3 %collective-permute-start.32 = (bf16[64,4096]{1,0:T(8,128)(2,1)S(1)}, bf16[64,4096]{1,0:T(8,128)(2,1)S(1)}, u32[]{:S(2)}, u32[]{:S(2)}) collective-permute-start(bf16[64,4096]{1,0:T(8,128)(2,1)S(1)} %relay_rows.1), channel_id=1, source_target_pairs={{0,4},{1,5},{2,6},{3,7},{4,0},{5,1},{6,2},{7,3},{8,12},{9,13},{10,... | collective-permute-start | bytes 1572872 | tf_op jit(solution)/shard_map/ppermute | solution.py:651
